TPU v7x, 128 devices: a whole 4x4x4 slice. The times are simulated.
128 devices in a mesh: dom: 128 (over y, z, x, core).
Axes of the slice: x: 4, y: 4, z: 4, core: 2. Of those that a mesh axis runs over, the one named last changes fastest.
Arguments:
- right_side: float32 [131072, 3], P('dom'), may hold values from -10 to 10
- fine_diagonal: float32 [131072, 3], P('dom'), may hold values from 2 to 4
- fine_columns: int32 [131072, 27], P('dom'), may hold values from 0 to 131071, as said below
- fine_blocks: float32 [131072, 27, 3, 3], P('dom'), may hold values from -0.625 to 0.625
- aggregate_of_node: int32 [131072], P('dom'), may hold values from 0 to 31, as said below
- coarse_row_of_aggregate: int32 [4096], P('dom'), may hold values from 0 to 4095, as said below
- coarse_diagonal: float32 [4096, 3], P('dom'), may hold values from 2 to 4
- coarse_columns: int32 [4096, 27], P('dom'), may hold values from 0 to 4095
- coarse_blocks: float32 [4096, 27, 3, 3], P('dom'), may hold values from -0.625 to 0.625
Outputs:
- solution: float32 [131072, 3], P('dom')
- correction: float32 [4096, 3], P('dom')
Inputs may be any that keep to these rules, and one draw needn't show every extreme that they name: Every entry of fine_columns differs from its row number by at most 256, and some entry by exactly 256. `aggregate_of_node`: on each device every aggregate number 0 to 31 is used by at least one of its nodes. coarse_row_of_aggregate is a permutation of 0 to 4095; among the 32 aggregates of one device (an aligned block of entries) at most 8 get rows of any one owner, and exactly 8 for some owner.
All inputs are finite; a program needn't handle non-finite values.
Results may differ from a plain program's by a relative error of at most 0.0003.
Values sent between devices are 32-bit elements.
No kernel may reach another device: no remote copies, remote signals or barrier semaphores. Data moves between devices by JAX's collectives and lax.ppermute only.
A program may use at most 64 MiB of HBM per device.

v0:
```python
import jax
import jax.numpy as jnp
from jax import lax
from jax.sharding import Mesh
from jax.sharding import PartitionSpec as P

CAP = 8
WIN = 256
SWEEPS = 2
CSWEEPS = 6
DOM = ("dom_0", "dom_1", "dom_2", "dom_3")


damping = 0.7
highest = lax.Precision.HIGHEST


def padded_2(value, sides, width, wrap):
    for axis, dim in sides:
        peers, length = lax.axis_size(axis), value.shape[dim]
        up = [(i, (i + 1) % peers) for i in range(peers if wrap else peers - 1)]
        down = [(j, i) for i, j in up]
        last = lax.slice_in_dim(value, length - width, length, axis=dim)
        initial = lax.slice_in_dim(value, 0, width, axis=dim)
        before = lax.ppermute(last, axis, up)
        after = lax.ppermute(initial, axis, down)
        value = jnp.concatenate([before, value, after], axis=dim)
    return value


def split_up(value, dim, peers):
    return jnp.stack(jnp.split(value, peers, axis=dim))


def joined_along(tiles, dim):
    tiles = jnp.moveaxis(tiles, 0, dim)
    shape = tiles.shape
    return tiles.reshape(*shape[:dim], shape[dim] * shape[dim + 1], *shape[dim + 2 :])


def turned_blocks(tiles, axes, sequence):
    inside = tiles.shape[1:]
    whole = tiles.reshape(*(lax.axis_size(a) for a in axes), *inside)
    for k in sequence:
        whole = lax.all_to_all(whole, axes[k], k, k, tiled=True)
    return whole.reshape(-1, *inside)


def exchange_by_chip(value, groups, sequence, split_dim, concat_dim):
    peers = lax.axis_size(groups[0]) * lax.axis_size(groups[1])
    tiles = split_up(value, split_dim, peers)
    return joined_along(turned_blocks(tiles, groups, sequence), concat_dim)


def couple(blocks, nearby):
    return jnp.sum(blocks * nearby[:, :, None, :], axis=(1, 3))


def apply_fine(field, fine_diagonal, fine_columns, fine_blocks):
    row_count = fine_columns.shape[0]
    padded = padded_2(field, ((DOM, 0),), WIN, False)
    first_row = lax.axis_index(DOM) * row_count - WIN
    local_columns = (fine_columns - first_row).astype(jnp.int32)
    nearby = padded[local_columns]
    return fine_diagonal * field - couple(fine_blocks, nearby)


def apply_coarse(field, coarse_diagonal, coarse_columns, coarse_blocks):
    gathered = lax.all_gather(field, DOM, axis=0, tiled=True)
    nearby = gathered[coarse_columns]
    return coarse_diagonal * field - couple(coarse_blocks, nearby)


def body(
    right_side,
    fine_diagonal,
    fine_columns,
    fine_blocks,
    aggregate_of_node,
    coarse_row_of_aggregate,
    coarse_diagonal,
    coarse_columns,
    coarse_blocks,
):
    solution = damping * right_side / fine_diagonal
    for sweep in range(SWEEPS - 1):
        solution = (
            solution
            + damping
            * (right_side - apply_fine(solution, fine_diagonal, fine_columns, fine_blocks))
            / fine_diagonal
        )
    residual = right_side - apply_fine(solution, fine_diagonal, fine_columns, fine_blocks)
    aggregate_count = coarse_diagonal.shape[0]
    devices = lax.axis_size(DOM)
    aggregate_ids = jnp.arange(aggregate_count, dtype=jnp.int32)
    sums_here = jax.ops.segment_sum(residual, aggregate_of_node, num_segments=aggregate_count)
    owners = coarse_row_of_aggregate // aggregate_count
    member = (owners[:, None] == jnp.arange(devices, dtype=jnp.int32)[None, :]).astype(jnp.float32)
    earlier = (aggregate_ids[None, :] < aggregate_ids[:, None]).astype(jnp.float32)
    before = jnp.dot(earlier, member, precision=highest)
    position = jnp.sum(before * member, axis=1).astype(jnp.int32)
    bucket = (owners * CAP + position).astype(jnp.int32)
    local_rows = (coarse_row_of_aggregate - owners * aggregate_count).astype(jnp.int32)
    slot_out = jnp.full((devices * CAP,), aggregate_count, jnp.int32).at[bucket].set(local_rows)
    slot_in = exchange_by_chip(slot_out, (("dom_0", "dom_1", "dom_2"), "dom_3"), (0, 1), 0, 0)
    outgoing = jnp.zeros((devices * CAP, 3), jnp.float32).at[bucket].set(sums_here)
    arrived = exchange_by_chip(outgoing, (("dom_0", "dom_1", "dom_2"), "dom_3"), (0, 1), 0, 0)
    coarse_rhs = jnp.zeros((aggregate_count, 3), jnp.float32).at[slot_in].add(arrived, mode="drop")
    correction = damping * coarse_rhs / coarse_diagonal
    for sweep in range(CSWEEPS - 1):
        correction = (
            correction
            + damping
            * (
                coarse_rhs
                - apply_coarse(correction, coarse_diagonal, coarse_columns, coarse_blocks)
            )
            / coarse_diagonal
        )
    sending = jnp.take(correction, slot_in, axis=0, mode="fill", fill_value=0.0)
    returned = exchange_by_chip(sending, (("dom_0", "dom_1", "dom_2"), "dom_3"), (0, 1), 0, 0)
    label_values = returned[bucket]
    solution = solution + label_values[aggregate_of_node]
    for sweep in range(SWEEPS):
        solution = (
            solution
            + damping
            * (right_side - apply_fine(solution, fine_diagonal, fine_columns, fine_blocks))
            / fine_diagonal
        )
    return (solution, correction)


def solution(mesh):
    torus = Mesh(mesh.devices.reshape(4, 4, 4, 2), ("dom_0", "dom_1", "dom_2", "dom_3"))
    return jax.shard_map(
        body,
        mesh=torus,
        in_specs=(
            P(DOM, None),
            P(DOM, None),
            P(DOM, None),
            P(DOM, None, None, None),
            P(DOM),
            P(DOM),
            P(DOM, None),
            P(DOM, None),
            P(DOM, None, None, None),
        ),
        out_specs=(P(DOM, None), P(DOM, None)),
        check_vma=False,
    )
```

profile of v0, /device:TPU:0, one launch (start us, length us, event | category | flops | bytes accessed | tf_op | source)
XLA Modules:
  0.0 753.9 jit_solution(1142505852747501974)
XLA Ops:
  1.4 1.3 collective-permute-start
  2.7 1.3 collective-permute-start.1
  6.3 9.7 %stack.1289 = s32[128,8]{1,0:T(8,128)} concatenate(s32[1,8]{1,0:T(1,128)S(1)} %get-tuple-element.405, s32[1,8]{1,0:T(1,128)S(1)} %get-tuple-element.404, s32[1,8]{1,0:T(1,128)S(1)} %get-tuple-element.403, s32[1,8]{1,0:T(1,128)S(1)} %get-tuple-element.402, s32[1,8]{1,0:T(1,128)S(1)} %get-tuple-element.401, s32[1,8]{1,0:T(1,128)S(1)} %get-tuple-element.400, ...), dimensions={0} | concatenate | bytes 8192 | tf_op jit(solution)/shard_map/stack | solution.py:32
  16.0 14.5 %all-to-all-start = ((s32[64,2,8]{2,1,0:T(2,128)}), s32[64,2,8]{2,1,0:T(2,128)S(1)}, u32[]{:S(2)}, u32[]{:S(2)}) async-start(s32[64,2,8]{2,1,0:T(2,128)} %bitcast.128), calls=%async_computation | async-start | bytes 131072 | tf_op jit(solution)/shard_map/all_to_all | solution.py:45
  32.6 91.5 %gather_fusion = f32[27648,3]{1,0:T(8,128)} fusion(f32[1536,3]{1,0:T(8,128)S(1)} %copy.2716, s32[27648]{0:T(1024)S(1)} %broadcast_clamp_fusion), kind=kCustom, calls=%fused_computation | custom fusion | bytes 774144 | tf_op jit(solution)/shard_map/gather | solution.py:64
  124.1 8.3 %copy.2717 = f32[27648,3]{0,1:T(4,128)S(1)} copy(f32[27648,3]{1,0:T(8,128)} %gather_fusion) | data formatting | bytes 663552 | tf_op jit(solution)/shard_map/gather | solution.py:64
  132.4 3.0 reshape.61
  135.4 1.9 copy.2718
  138.8 1.3 collective-permute-start.3
  140.3 6.1 all_to_all.30
  148.4 91.5 %gather_fusion.1 = f32[27648,3]{1,0:T(8,128)} fusion(f32[1536,3]{1,0:T(8,128)S(1)} %copy.2722, s32[27648]{0:T(1024)S(1)} %broadcast_clamp_fusion), kind=kCustom, calls=%fused_computation.1 | custom fusion | bytes 774144 | tf_op jit(solution)/shard_map/gather | solution.py:64
  239.9 8.3 %copy.2723 = f32[27648,3]{0,1:T(4,128)S(1)} copy(f32[27648,3]{1,0:T(8,128)} %gather_fusion.1) | data formatting | bytes 663552 | tf_op jit(solution)/shard_map/gather | solution.py:64
  248.2 3.0 reshape.69
  251.2 1.9 copy.2724
  253.5 6.0 scatter_custom_fusion.1
  273.3 10.9 %all-to-all-start.2 = ((f32[64,2,8,3]{2,1,3,0:T(2,128)}), f32[64,2,8,3]{2,1,3,0:T(2,128)S(1)}, u32[]{:S(2)}, u32[]{:S(2)}) async-start(f32[64,2,8,3]{2,1,3,0:T(2,128)} %copy.2855), calls=%async_computation.2 | async-start | bytes 393216 | tf_op jit(solution)/shard_map/all_to_all | solution.py:45
  284.3 10.7 %all-to-all-done.2 = f32[64,2,8,3]{2,1,3,0:T(2,128)S(1)} async-done(((f32[64,2,8,3]{2,1,3,0:T(2,128)}), f32[64,2,8,3]{2,1,3,0:T(2,128)S(1)}, u32[]{:S(2)}, u32[]{:S(2)}) %all-to-all-start.2) | async-done | bytes 12320 | tf_op jit(solution)/shard_map/all_to_all | solution.py:45
  295.2 3.7 all_to_all.31
  300.5 6.0 scatter_custom_fusion.3
  306.6 33.4 %all-gather = f32[128,32,3]{1,2,0:T(4,128)S(1)} all-gather(f32[1,32,3]{1,2,0:T(4,128)S(1)} %fusion.11), channel_id=1, replica_groups=mesh['dom_0'=4,'dom_1'=4,'dom_2'=4,'dom_3'=2] {'dom_0','dom_1','dom_2','..., dimensions={0}, use_global_device_ids=true | all-gather | bytes 49536 | tf_op jit(solution)/shard_map/all_gather | solution.py:69
  340.9 1.9 gather_fusion.2
  343.2 33.4 %all-gather.1 = f32[128,32,3]{1,2,0:T(4,128)S(1)} all-gather(f32[1,32,3]{1,2,0:T(4,128)S(1)} %bitcast.827), channel_id=1, replica_groups=mesh['dom_0'=4,'dom_1'=4,'dom_2'=4,'dom_3'=2] {'dom_0','dom_1','dom_2','..., dimensions={0}, use_global_device_ids=true | all-gather | bytes 49536 | tf_op jit(solution)/shard_map/all_gather | solution.py:69
  377.4 1.9 gather_fusion.3
  379.7 33.4 %all-gather.2 = f32[128,32,3]{1,2,0:T(4,128)S(1)} all-gather(f32[1,32,3]{1,2,0:T(4,128)S(1)} %bitcast.825), channel_id=1, replica_groups=mesh['dom_0'=4,'dom_1'=4,'dom_2'=4,'dom_3'=2] {'dom_0','dom_1','dom_2','..., dimensions={0}, use_global_device_ids=true | all-gather | bytes 49536 | tf_op jit(solution)/shard_map/all_gather | solution.py:69
  413.9 1.9 gather_fusion.4
  416.2 33.6 %all-gather.3 = f32[128,32,3]{1,2,0:T(4,128)S(1)} all-gather(f32[1,32,3]{1,2,0:T(4,128)S(1)} %bitcast.826), channel_id=1, replica_groups=mesh['dom_0'=4,'dom_1'=4,'dom_2'=4,'dom_3'=2] {'dom_0','dom_1','dom_2','..., dimensions={0}, use_global_device_ids=true | all-gather | bytes 49536 | tf_op jit(solution)/shard_map/all_gather | solution.py:69
  450.7 1.9 gather_fusion.5
  453.0 33.4 %all-gather.4 = f32[128,32,3]{1,2,0:T(4,128)S(1)} all-gather(f32[1,32,3]{1,2,0:T(4,128)S(1)} %bitcast.824), channel_id=1, replica_groups=mesh['dom_0'=4,'dom_1'=4,'dom_2'=4,'dom_3'=2] {'dom_0','dom_1','dom_2','..., dimensions={0}, use_global_device_ids=true | all-gather | bytes 49536 | tf_op jit(solution)/shard_map/all_gather | solution.py:69
  487.2 1.9 gather_fusion.6
  489.6 2.8 gather_fusion.7
  505.5 5.9 all-to-all-start.4
  511.4 10.4 %all-to-all-done.4 = f32[64,2,8,3]{2,1,3,0:T(2,128)S(1)} async-done(((f32[64,2,8,3]{2,1,3,0:T(2,128)}), f32[64,2,8,3]{2,1,3,0:T(2,128)S(1)}, u32[]{:S(2)}, u32[]{:S(2)}) %all-to-all-start.4) | async-done | bytes 12320 | tf_op jit(solution)/shard_map/all_to_all | solution.py:45
  522.0 3.7 all_to_all.32
  527.4 2.8 gather_fusion.9
  530.4 2.1 collective-permute-start.4
  532.5 1.3 collective-permute-start.5
  533.8 1.8 collective-permute-done.5
  535.9 91.5 %gather_fusion.10 = f32[27648,3]{1,0:T(8,128)} fusion(f32[1536,3]{1,0:T(8,128)S(1)} %copy.3009, s32[27648]{0:T(1024)S(1)} %broadcast_clamp_fusion), kind=kCustom, calls=%fused_computation.10 | custom fusion | bytes 774144 | tf_op jit(solution)/shard_map/gather | solution.py:64
  627.4 8.3 %copy.3010 = f32[27648,3]{0,1:T(4,128)S(1)} copy(f32[27648,3]{1,0:T(8,128)} %gather_fusion.10) | data formatting | bytes 663552 | tf_op jit(solution)/shard_map/gather | solution.py:64
  635.7 3.0 reshape.141
  638.7 1.9 copy.3011
  640.8 4.3 collective-permute-start.6
  645.1 1.6 collective-permute-start.7
  646.7 1.5 collective-permute-done.7
  648.5 91.5 %gather_fusion.11 = f32[27648,3]{1,0:T(8,128)} fusion(f32[1536,3]{1,0:T(8,128)S(1)} %copy.3012, s32[27648]{0:T(1024)S(1)} %broadcast_clamp_fusion), kind=kCustom, calls=%fused_computation.11 | custom fusion | bytes 774144 | tf_op jit(solution)/shard_map/gather | solution.py:64
  740.0 8.3 %copy.3013 = f32[27648,3]{0,1:T(4,128)S(1)} copy(f32[27648,3]{1,0:T(8,128)} %gather_fusion.11) | data formatting | bytes 663552 | tf_op jit(solution)/shard_map/gather | solution.py:64
  748.2 3.0 reshape.149
  751.2 1.9 copy.3014
  (650 shorter events, 46.6 us)
Async XLA Ops:
  0.6 31.5 %copy-start.6 = (s32[32,27]{1,0:T(8,128)S(1)}, s32[32,27]{1,0:T(8,128)}, u32[]{:S(2)}) copy-start(s32[32,27]{1,0:T(8,128)} %param.16) | copy-start | bytes 10372
  1.4 30.8 %collective-permute-start = (f32[256,3]{0,1:T(4,128)S(1)}, f32[256,3]{0,1:T(4,128)S(1)}, u32[]{:S(2)}, u32[]{:S(2)}) collective-permute-start(f32[256,3]{0,1:T(4,128)S(1)} %get-tuple-element.276), channel_id=1, source_target_pairs={{0,1},{1,2},{2,3},{3,4},{4,5},{5,6},{6,7},{7,8},{8,9},{9,10},{10,1... | collective-permute-start | bytes 9224 | tf_op jit(solution)/shard_map/ppermute | solution.py:25
  2.7 29.5 %collective-permute-start.1 = (f32[256,3]{0,1:T(4,128)S(1)}, f32[256,3]{0,1:T(4,128)S(1)}, u32[]{:S(2)}, u32[]{:S(2)}) collective-permute-start(f32[256,3]{0,1:T(4,128)S(1)} %get-tuple-element.277), channel_id=1, source_target_pairs={{1,0},{2,1},{3,2},{4,3},{5,4},{6,5},{7,6},{8,7},{9,8},{10,9},{11,1... | collective-permute-start | bytes 9224 | tf_op jit(solution)/shard_map/ppermute | solution.py:26
  16.0 124.1 %all-to-all-start = ((s32[64,2,8]{2,1,0:T(2,128)}), s32[64,2,8]{2,1,0:T(2,128)S(1)}, u32[]{:S(2)}, u32[]{:S(2)}) async-start(s32[64,2,8]{2,1,0:T(2,128)} %bitcast.128), calls=%async_computation | async-start | bytes 131072 | tf_op jit(solution)/shard_map/all_to_all | solution.py:45
  132.4 4.9 copy-start
  135.4 2.1 copy-start.3
  135.4 2.1 copy-start.4
  137.5 10.6 %collective-permute-start.2 = (f32[256,3]{0,1:T(4,128)S(1)}, f32[256,3]{0,1:T(4,128)S(1)}, u32[]{:S(2)}, u32[]{:S(2)}) collective-permute-start(f32[256,3]{0,1:T(4,128)S(1)} %get-tuple-element.274), channel_id=1, source_target_pairs={{0,1},{1,2},{2,3},{3,4},{4,5},{5,6},{6,7},{7,8},{8,9},{9,10},{10,1... | collective-permute-start | bytes 9224 | tf_op jit(solution)/shard_map/ppermute | solution.py:25
  138.8 9.3 %collective-permute-start.3 = (f32[256,3]{0,1:T(4,128)S(1)}, f32[256,3]{0,1:T(4,128)S(1)}, u32[]{:S(2)}, u32[]{:S(2)}) collective-permute-start(f32[256,3]{0,1:T(4,128)S(1)} %get-tuple-element.275), channel_id=1, source_target_pairs={{1,0},{2,1},{3,2},{4,3},{5,4},{6,5},{7,6},{8,7},{9,8},{10,9},{11,1... | collective-permute-start | bytes 9224 | tf_op jit(solution)/shard_map/ppermute | solution.py:26
  251.2 2.3 copy-start.8
  260.6 46.1 %copy-start.5 = (f32[32,3]{0,1:T(4,128)S(1)}, f32[32,3]{0,1:T(4,128)}, u32[]{:S(2)}) copy-start(f32[32,3]{0,1:T(4,128)} %param.15) | copy-start | bytes 1156
  273.3 21.6 %all-to-all-start.2 = ((f32[64,2,8,3]{2,1,3,0:T(2,128)}), f32[64,2,8,3]{2,1,3,0:T(2,128)S(1)}, u32[]{:S(2)}, u32[]{:S(2)}) async-start(f32[64,2,8,3]{2,1,3,0:T(2,128)} %copy.2855), calls=%async_computation.2 | async-start | bytes 393216 | tf_op jit(solution)/shard_map/all_to_all | solution.py:45
  340.9 2.2 copy-start.2
  489.5 2.9 copy-start.7
  505.5 16.3 %all-to-all-start.4 = ((f32[64,2,8,3]{2,1,3,0:T(2,128)}), f32[64,2,8,3]{2,1,3,0:T(2,128)S(1)}, u32[]{:S(2)}, u32[]{:S(2)}) async-start(f32[64,2,8,3]{2,1,3,0:T(2,128)} %copy.3005), calls=%async_computation.4 | async-start | bytes 393216 | tf_op jit(solution)/shard_map/all_to_all | solution.py:45
  530.4 3.4 collective-permute-start.4
  532.5 3.1 collective-permute-start.5
  635.7 4.9 copy-start.1
  640.8 5.8 collective-permute-start.6
  645.1 3.1 collective-permute-start.7
where the time goes:
time: 764 us; the launch traced here: 754 us
  local copies, waits for them, and re-layouts  482 us (63%)
  blocking collectives  181 us (24%)
  starting transfers between devices  45.6 us (6%)
  waiting for transfers between devices  24.5 us (3%)
  other arithmetic  18.7 us (2%)
    gather x16, local copies, waits for them, and re-layouts, apply_fine(): nearby = padded[local_columns]  419 us
    all_gather x5, blocking collectives, apply_coarse(): gathered = lax.all_gather(field, DOM, axis=0, tiled=True)  167 us
    all_to_all x3, starting transfers between devices, turned_blocks(): whole = lax.all_to_all(whole, axes[k], k, k, tiled=True)  31.3 us
    all_to_all x3, waiting for transfers between devices, turned_blocks(): whole = lax.all_to_all(whole, axes[k], k, k, tiled=True)  21.2 us
    split x270, local copies, waits for them, and re-layouts, split_up(): return jnp.stack(jnp.split(value, peers, axis=dim))  20.8 us
  transfers between devices with their start and end apart: 11, of which 4 were waited for; matrix products, arithmetic and copies ran while one was open for 16% of the time, Pallas kernels for 0%

commit v1 on v0

v1 whole, which is shorter than its diff:
```python
import jax
import jax.numpy as jnp
from jax import lax
from jax.experimental import pallas as pl
from jax.experimental.pallas import tpu as pltpu
from jax.sharding import Mesh
from jax.sharding import PartitionSpec as P

DOM = ("dom_0", "dom_1", "dom_2", "dom_3")
SWEEPS = 2
CSWEEPS = 6
damping = 0.7
highest = lax.Precision.HIGHEST

ROWS = 1024
LANES = 128
SLOTS = 27
FULL = 24
HALO = 256
WIDE = 512
BLOCKS = ROWS // LANES
P_COL = 9 * FULL
P_BTAIL = P_COL + FULL
P_CTAIL = P_BTAIL + 27
P_RHS = P_CTAIL + 3
P_DIA = P_RHS + 6
P_ROW = P_DIA + 6
P_ALL = 288
f32 = jnp.float32
i32 = jnp.int32


def lanes(start, size=LANES):
    if isinstance(start, int):
        return slice(start, start + size)
    return pl.ds(pl.multiple_of(start, LANES), size)


def picked(row, where):
    return jnp.take_along_axis(
        jnp.broadcast_to(row, where.shape), where, axis=1, mode="promise_in_bounds"
    )


def pack_kernel(rhs, dia, col, blk, agg, owner_row, up, down, node_row):
    table = owner_row[...]
    found = picked(table, agg[...]).astype(f32)
    node_row[...] = found
    for out, near, wide in ((up, ROWS - HALO, ROWS - WIDE), (down, 0, 0)):
        for i in range(3):
            for j in range(3):
                g = 3 * i + j
                out[g * FULL : (g + 1) * FULL, :] = blk[i, j, 0:FULL, lanes(near, HALO)]
                out[P_BTAIL + 3 * g : P_BTAIL + 3 * g + 3, :] = blk[
                    i, j, FULL:SLOTS, lanes(near, HALO)
                ]
        out[P_COL : P_COL + FULL, :] = col[0:FULL, lanes(near, HALO)].astype(f32)
        out[P_CTAIL : P_CTAIL + 3, :] = col[FULL:SLOTS, lanes(near, HALO)].astype(f32)
        for h in range(2):
            out[P_RHS + 3 * h : P_RHS + 3 * h + 3, :] = rhs[:, lanes(wide + HALO * h, HALO)]
            out[P_DIA + 3 * h : P_DIA + 3 * h + 3, :] = dia[:, lanes(wide + HALO * h, HALO)]
            for q in range(2):
                s = wide // LANES + 2 * h + q
                out[P_ROW + h : P_ROW + h + 1, lanes(LANES * q)] = found[s : s + 1, :]
        out[P_ROW + 2 : P_ALL, :] = jnp.zeros((P_ALL - P_ROW - 2, HALO), f32)


def pulled_block(columns, blocks, table, first_chunk):
    total = [None, None, None]
    for part in range(4):
        where = columns(part)
        chunk = lax.shift_right_arithmetic(where, 7)
        lane = lax.bitwise_and(where, 127)
        near = [jnp.zeros(where.shape, f32) for _ in range(3)]
        for c in range(5):
            here = chunk == c
            for j in range(3):
                row = table[j : j + 1, lanes(first_chunk * LANES + c * LANES)]
                near[j] = jnp.where(here, picked(row, lane), near[j])
        for i in range(3):
            s = blocks(i, 0, part) * near[0]
            s = s + blocks(i, 1, part) * near[1]
            s = s + blocks(i, 2, part) * near[2]
            if part < 3:
                total[i] = s if total[i] is None else total[i] + s
            else:
                total[i] = jnp.sum(total[i], axis=0, keepdims=True) + jnp.sum(
                    s, axis=0, keepdims=True
                )
    return total


def local_getters(col, blk, start, b):
    def columns(part):
        lo, hi = 8 * part, min(8 * part + 8, SLOTS)
        return col[lo:hi, lanes(b * LANES)] - start

    def blocks(i, j, part):
        lo, hi = 8 * part, min(8 * part + 8, SLOTS)
        return blk[i, j, lo:hi, lanes(b * LANES)]

    return columns, blocks


def halo_getters(halo, start, b):
    def columns(part):
        if part < 3:
            got = halo[P_COL + 8 * part : P_COL + 8 * part + 8, lanes(b * LANES)]
        else:
            got = halo[P_CTAIL : P_CTAIL + 3, lanes(b * LANES)]
        return got.astype(i32) - start

    def blocks(i, j, part):
        g = 3 * i + j
        if part < 3:
            return halo[g * FULL + 8 * part : g * FULL + 8 * part + 8, lanes(b * LANES)]
        return halo[P_BTAIL + 3 * g : P_BTAIL + 3 * g + 3, lanes(b * LANES)]

    return columns, blocks


def wide_vector(out, local, before, after, row):
    out[:, lanes(WIDE, ROWS)] = local[...]
    for h in range(2):
        out[:, lanes(HALO * h, HALO)] = before[row + 3 * h : row + 3 * h + 3, :]
        out[:, lanes(WIDE + ROWS + HALO * h, HALO)] = after[row + 3 * h : row + 3 * h + 3, :]


def smoothed(table, pulled, rhs, dia, at):
    pull = jnp.concatenate(pulled, axis=0)
    s = table[:, lanes(at)]
    b = rhs[:, lanes(at)]
    d = dia[:, lanes(at)]
    return s + damping * (b - (d * s - pull)) / d


def sweep_halo(out, table, rhs, dia, halo, base, first):
    for b in range(2):
        at = first + LANES * b
        start = base + (at - WIDE) - 2 * LANES
        cols, blks = halo_getters(halo, start, b)
        pull = pulled_block(cols, blks, table, at // LANES - 2)
        out[:, lanes(at)] = smoothed(table, pull, rhs, dia, at)


def own_block(table, col, blk, base, b):
    start = base + b * LANES - 2 * LANES
    cols, blks = local_getters(col, blk, start, b)
    return pulled_block(cols, blks, table, b + WIDE // LANES - 2)


def pre_kernel(base_ref, rhs, dia, col, blk, agg, owner_row, before, after,
               send, first_iter, keep_rhs, keep_dia, up2, down2, one, two, res):
    base = base_ref[0]
    wide_vector(keep_rhs, rhs, before, after, P_RHS)
    wide_vector(keep_dia, dia, before, after, P_DIA)
    raw = keep_dia[...]
    keep_dia[...] = jnp.where(raw == 0.0, 1.0, raw)
    one[...] = damping * keep_rhs[...] / keep_dia[...]
    two[...] = jnp.zeros(two.shape, f32)
    sweep_halo(two, one, keep_rhs, keep_dia, before, base, WIDE - HALO)
    sweep_halo(two, one, keep_rhs, keep_dia, after, base, WIDE + ROWS)

    def second(b, carry):
        at = WIDE + b * LANES
        pull = own_block(one, col, blk, base, b)
        two[:, lanes(at)] = smoothed(one, pull, keep_rhs, keep_dia, at)
        return carry

    lax.fori_loop(0, BLOCKS, second, 0)

    def third(b, carry):
        at = WIDE + b * LANES
        pull = jnp.concatenate(own_block(two, col, blk, base, b), axis=0)
        s, d = two[:, lanes(at)], keep_dia[:, lanes(at)]
        res[0:3, lanes(b * LANES)] = keep_rhs[:, lanes(at)] - (d * s - pull)
        return carry

    res[...] = jnp.zeros(res.shape, f32)
    lax.fori_loop(0, BLOCKS, third, 0)
    first_iter[...] = two[...]
    up2[...] = two[:, lanes(WIDE + ROWS - WIDE, HALO)]
    down2[...] = two[:, lanes(WIDE + HALO, HALO)]
    label = lax.broadcasted_iota(i32, (32, LANES), 0)
    sums = None
    for b in range(BLOCKS):
        member = (label == jnp.broadcast_to(agg[b : b + 1, :], (32, LANES))).astype(f32)
        part = lax.dot_general(
            res[:, lanes(b * LANES)], member, (((1,), (1,)), ((), ())),
            precision=highest, preferred_element_type=f32,
        )
        sums = part if sums is None else sums + part
    row = jnp.concatenate(
        [sums[0:1], sums[1:2], sums[2:3], owner_row[0:1, 0:32].astype(f32)], axis=1
    )
    send[...] = jnp.broadcast_to(row, (LANES, LANES))


def spread(parts):
    group = lax.shift_right_logical(lax.broadcasted_iota(i32, (1, LANES), 1), 5)
    return jnp.where(group == 0, parts[0], jnp.where(group == 1, parts[1], parts[2]))


def coarse_setup_kernel(me_ref, sums, dia, col, blk, send, keep_rhs, keep_dia, where, weights):
    me = me_ref[0]
    got = sums[...]
    group = lax.shift_right_logical(lax.broadcasted_iota(i32, (LANES, LANES), 1), 5)
    rows = jnp.where(group == 3, got, 0.0)
    rows = rows + pltpu.roll(rows, 64, axis=1)
    rows = rows + pltpu.roll(rows, 32, axis=1)
    rows = rows.astype(i32) - me * 32
    lines = []
    for r in range(32):
        lines.append(jnp.sum(jnp.where(rows == r, got, 0.0), axis=0, keepdims=True))
    lines = jnp.concatenate(lines, axis=0)
    pick = lax.broadcasted_iota(i32, (8, LANES), 0) == lax.shift_right_logical(
        lax.broadcasted_iota(i32, (8, LANES), 1), 5
    )
    mine = lax.dot_general(
        pick.astype(f32), lines, (((1,), (1,)), ((), ())),
        precision=highest, preferred_element_type=f32,
    )
    pad = jnp.zeros((1, 32), f32)
    rhs = jnp.concatenate([mine[0:1], mine[1:2], mine[2:3], pad], axis=1)
    d = jnp.concatenate([dia[0:1, :], dia[1:2, :], dia[2:3, :], pad + 1.0], axis=1)
    keep_rhs[...] = rhs
    keep_dia[...] = d
    send[...] = jnp.broadcast_to(damping * rhs / d, (LANES, LANES))

    def folded(a):
        z = jnp.concatenate([a, jnp.zeros((32, 5), f32)], axis=1)
        z = jnp.transpose(z)
        return jnp.concatenate([z[8 * k : 8 * k + 8, :] for k in range(4)], axis=1)

    where[...] = folded(col[...].astype(f32)).astype(i32)
    for i in range(3):
        for j in range(3):
            weights[3 * i + j] = folded(blk[i, j])


def coarse_lookup(table, column, shape):
    chunk = lax.bitwise_and(column, 31)
    lane = lax.shift_right_logical(column, 5)
    near = [jnp.zeros(shape, f32) for _ in range(3)]
    for c in range(32):
        here = chunk == c
        for j in range(3):
            row = table[32 * j + c : 32 * j + c + 1, :]
            near[j] = jnp.where(here, picked(row, lane), near[j])
    return near


def coarse_kernel(got, own, rhs, dia, where, weights, send, mine, table):
    table[...] = jnp.transpose(got[...])
    near = coarse_lookup(table, where[...], (8, LANES))
    parts = []
    for i in range(3):
        s = weights[3 * i] * near[0] + weights[3 * i + 1] * near[1] + weights[3 * i + 2] * near[2]
        s = jnp.sum(s, axis=0, keepdims=True)
        s = s + pltpu.roll(s, 64, axis=1)
        parts.append(s + pltpu.roll(s, 32, axis=1))
    c, d = own[0:1, :], dia[...]
    new = c + damping * (rhs[...] - (d * c - spread(parts))) / d
    send[...] = jnp.broadcast_to(new, (LANES, LANES))
    mine[...] = jnp.concatenate([new[:, 32 * i : 32 * i + 32] for i in range(3)], axis=0)


def post_kernel(base_ref, got, first_iter, rhs, dia, col, blk, node_row, before, after,
                before2, after2, out, table, one, two):
    base = base_ref[0]
    table[...] = jnp.transpose(got[...])
    one[...] = first_iter[...]
    one[:, lanes(0, HALO)] = before2[...]
    one[:, lanes(WIDE + ROWS + HALO, HALO)] = after2[...]
    edge = [
        h[P_ROW + t : P_ROW + t + 1, lanes(LANES * q)]
        for h in (before, after) for t in range(2) for q in range(2)
    ]
    edge = jnp.concatenate(edge, axis=0)
    own = coarse_lookup(table, node_row[...].astype(i32), (8, LANES))
    far = coarse_lookup(table, edge.astype(i32), (8, LANES))
    for s in range(16):
        if s < 4:
            row = [f[s : s + 1, :] for f in far]
        elif s < 12:
            row = [f[s - 4 : s - 3, :] for f in own]
        else:
            row = [f[s - 8 : s - 7, :] for f in far]
        one[:, lanes(s * LANES)] = one[:, lanes(s * LANES)] + jnp.concatenate(row, axis=0)
    two[...] = jnp.zeros(two.shape, f32)
    sweep_halo(two, one, rhs, dia, before, base, WIDE - HALO)
    sweep_halo(two, one, rhs, dia, after, base, WIDE + ROWS)

    def first(b, carry):
        at = WIDE + b * LANES
        pull = own_block(one, col, blk, base, b)
        two[:, lanes(at)] = smoothed(one, pull, rhs, dia, at)
        return carry

    def second(b, carry):
        at = WIDE + b * LANES
        pull = own_block(two, col, blk, base, b)
        out[:, lanes(b * LANES)] = smoothed(two, pull, rhs, dia, at)
        return carry

    lax.fori_loop(0, BLOCKS, first, 0)
    lax.fori_loop(0, BLOCKS, second, 0)


def call(kernel, name, outs, args, scratch=(), scalar=False):
    vmem = pl.BlockSpec(memory_space=pltpu.VMEM)
    specs = [vmem] * len(args)
    if scalar:
        specs[0] = pl.BlockSpec(memory_space=pltpu.SMEM)
    return pl.pallas_call(
        kernel,
        name=name,
        in_specs=specs,
        out_specs=[vmem] * len(outs),
        out_shape=[jax.ShapeDtypeStruct(o, t) for o, t in outs],
        scratch_shapes=[pltpu.VMEM(s, f32) for s in scratch],
    )(*args)


def everywhere(row):
    return lax.all_to_all(row, DOM, 0, 0, tiled=True)


def shifts(up, down):
    count = lax.axis_size(DOM)
    forward = [(i, i + 1) for i in range(count - 1)]
    backward = [(i + 1, i) for i in range(count - 1)]
    return lax.ppermute(up, DOM, forward), lax.ppermute(down, DOM, backward)


def body(right_side, fine_diagonal, fine_columns, fine_blocks, aggregate_of_node,
         coarse_row_of_aggregate, coarse_diagonal, coarse_columns, coarse_blocks):
    rhs, dia = right_side.T, fine_diagonal.T
    col, blk = fine_columns.T, fine_blocks.transpose(2, 3, 1, 0)
    agg = aggregate_of_node.reshape(8, LANES)
    owner = jnp.pad(coarse_row_of_aggregate, (0, 96)).reshape(1, LANES)
    cdia, cblk = coarse_diagonal.T, coarse_blocks.transpose(2, 3, 0, 1)
    me = lax.axis_index(DOM).astype(i32).reshape(1)
    base = me * ROWS
    wide = WIDE + ROWS + WIDE

    up, down, node_row = call(
        pack_kernel, "pack",
        [((P_ALL, HALO), f32), ((P_ALL, HALO), f32), ((8, LANES), f32)],
        [rhs, dia, col, blk, agg, owner],
    )
    before, after = shifts(up, down)
    square = ((LANES, LANES), f32)
    send, first_iter, wrhs, wdia, up2, down2 = call(
        pre_kernel, "pre",
        [square, ((3, wide), f32), ((3, wide), f32), ((3, wide), f32),
         ((3, HALO), f32), ((3, HALO), f32)],
        [base, rhs, dia, col, blk, agg, owner, before, after],
        scratch=[(3, wide), (3, wide), (8, ROWS)], scalar=True,
    )
    before2, after2 = shifts(up2, down2)
    sums = everywhere(send)
    line = ((1, LANES), f32)
    send, crhs, cd, where, weights = call(
        coarse_setup_kernel, "coarse_setup",
        [square, line, line, ((8, LANES), i32), ((9, 8, LANES), f32)],
        [me, sums, cdia, coarse_columns, cblk], scalar=True,
    )
    for sweep in range(CSWEEPS - 1):
        got = everywhere(send)
        send, mine = call(
            coarse_kernel, "coarse", [square, ((3, 32), f32)],
            [got, send, crhs, cd, where, weights], scratch=[(LANES, LANES)],
        )
    got = everywhere(send)
    solution, = call(
        post_kernel, "post", [((3, ROWS), f32)],
        [base, got, first_iter, wrhs, wdia, col, blk, node_row, before, after, before2, after2],
        scratch=[(LANES, LANES), (3, wide), (3, wide)], scalar=True,
    )
    return solution.T, mine.T


def solution(mesh):
    torus = Mesh(mesh.devices.reshape(4, 4, 4, 2), DOM)
    return jax.shard_map(
        body,
        mesh=torus,
        in_specs=(
            P(DOM, None),
            P(DOM, None),
            P(DOM, None),
            P(DOM, None, None, None),
            P(DOM),
            P(DOM),
            P(DOM, None),
            P(DOM, None),
            P(DOM, None, None, None),
        ),
        out_specs=(P(DOM, None), P(DOM, None)),
        check_vma=False,
    )
```

time: 764 us -> 156 us (0.20); the launches traced: 754 us -> 154 us
  local copies, waits for them, and re-layouts: 482 us -> 2.51 us
  blocking collectives: 181 us -> 104 us
  starting transfers between devices: 45.6 us -> 10 us
  Pallas kernels: 0 us -> 26 us
  other arithmetic: 18.7 us -> 0 us
  waiting for transfers between devices: 24.5 us -> 11.2 us
    gather x35 -> x0, local copies, waits for them, and re-layouts: 436 us -> none  [the longest x16 419 us: apply_fine(): nearby = padded[local_columns]]
    all_gather x5 -> x0, blocking collectives: 167 us -> none  [apply_coarse(): gathered = lax.all_gather(field, DOM, axis=0, tiled=True)]
    all_to_all x3 -> x6, blocking collectives: 13.6 us -> 104 us  [everywhere(): return lax.all_to_all(row, DOM, 0, 0, tiled=True)]
    all_to_all x3 -> x1, starting transfers between devices: 31.3 us -> 4.81 us  [everywhere(): return lax.all_to_all(row, DOM, 0, 0, tiled=True)]
    pallas_call x0 -> x9, Pallas kernels: none -> 26 us  [call(): pl.pallas_call(kernel, name=name, in_specs=specs, out_specs=[vmem] * len(...]
    split x270 -> x0, local copies, waits for them, and re-layouts: 20.8 us -> none  [split_up(): return jnp.stack(jnp.split(value, peers, axis=dim))]
    all_to_all x3 -> x1, waiting for transfers between devices: 21.2 us -> 4.13 us  [everywhere(): return lax.all_to_all(row, DOM, 0, 0, tiled=True)]
    scatter-add x2 -> x0, other arithmetic: 12 us -> none  [the longest x1 6.01 us: body(): jax.ops.segment_sum(residual, aggregate_of_node, num_segments=aggregate_c...]
  transfers between devices with their start and end apart: 11 -> 5, of which waited for: 4 -> 4; matrix products, arithmetic and copies ran while one was open for 16% -> 0% of each run, Pallas kernels for 0% -> 0%
where the time goes in v1:
time: 156 us; the launch traced here: 154 us
  blocking collectives  104 us (67%)
  Pallas kernels  26 us (17%)
  waiting for transfers between devices  11.2 us (7%)
  starting transfers between devices  10 us (6%)
  local copies, waits for them, and re-layouts  2.51 us (2%)
    all_to_all x6, blocking collectives, everywhere(): return lax.all_to_all(row, DOM, 0, 0, tiled=True)  104 us
    pallas_call x9, Pallas kernels, call(): pl.pallas_call(kernel, name=name, in_specs=specs, out_specs=[vmem] * len(...  26 us
    ppermute x4, waiting for transfers between devices, shifts(): return (lax.ppermute(up, DOM, forward), lax.ppermute(down, DOM, backward))  7.11 us
    ppermute x4, starting transfers between devices, shifts(): return (lax.ppermute(up, DOM, forward), lax.ppermute(down, DOM, backward))  5.23 us
    all_to_all x1, starting transfers between devices, everywhere(): return lax.all_to_all(row, DOM, 0, 0, tiled=True)  4.81 us
    all_to_all x1, waiting for transfers between devices, everywhere(): return lax.all_to_all(row, DOM, 0, 0, tiled=True)  4.13 us
  transfers between devices with their start and end apart: 5, of which 4 were waited for; matrix products, arithmetic and copies ran while one was open for 0% of the time, Pallas kernels for 0%

profile of v1, /device:TPU:0, one launch (start us, length us, event | category | flops | bytes accessed | tf_op | source)
XLA Modules:
  0.0 154.3 jit_solution(10167141849120909433)
XLA Ops:
  0.6 1.1 pad_bitcast_fusion.owner_row
  1.8 2.2 %pack.1 = (f32[288,256]{1,0:T(8,128)}, f32[288,256]{1,0:T(8,128)}, f32[8,128]{1,0:T(8,128)}) custom-call(f32[3,1024]{1,0:T(4,128)} %bitcast.59, f32[3,1024]{1,0:T(4,128)} %bitcast.61, s32[27,1024]{1,0:T(8,128)} %bitcast.43, f32[3,3,27,1024]{3,2,1,0:T(8,128)} %bitcast.40, s32[8,128]{1,0:T(8,128)} %bitcast.66, s32[1,128]{1,0:T(1,128)} %pad_bitcast_fusion.owner_row), custom_call_target="tpu_custom_call" | custom-call | tf_op jit(solution)/shard_map/pack/pallas_call | solution.py:315
  4.0 1.3 collective-permute-start
  5.3 1.3 collective-permute-start.1
  6.6 0.1 collective-permute-done.before
  6.7 0.0 copy-start
  6.7 4.2 %collective-permute-done.1.after = f32[288,256]{1,0:T(8,128)S(1)} collective-permute-done((f32[288,256]{1,0:T(8,128)}, f32[288,256]{1,0:T(8,128)S(1)}, u32[]{:S(2)}, u32[]{:S(2)}) %collective-permute-start.1) | collective-permute-done | bytes 294944 | tf_op jit(solution)/shard_map/ppermute | solution.py:333
  10.8 0.0 copy-done
  10.8 0.0 copy-start.1
  10.8 0.7 copy-done.1
  11.5 5.9 %pre.1 = (f32[128,128]{1,0:T(8,128)}, f32[3,2048]{1,0:T(4,128)}, f32[3,2048]{1,0:T(4,128)}, f32[3,2048]{1,0:T(4,128)}, f32[3,256]{1,0:T(4,128)}, /*index=5*/f32[3,256]{1,0:T(4,128)}) custom-call(s32[1]{0:T(128)S(6)} %mul.15.base_ref, f32[3,1024]{1,0:T(4,128)} %bitcast.60, f32[3,1024]{1,0:T(4,128)} %bitcast.62, s32[27,1024]{1,0:T(8,128)} %bitcast.44, ...), custom_call_target="tpu_custom_call" | custom-call | tf_op jit(solution)/shard_map/pre/pallas_call | solution.py:315
  17.4 0.0 copy-start.6
  17.4 0.0 copy-start.5
  17.5 28.0 %all_to_all.77 = f32[128,1,128]{2,1,0:T(1,128)} all-to-all(f32[128,1,128]{2,1,0:T(1,128)} %bitcast.64), channel_id=1, replica_groups=mesh['dom_0'=4,'dom_1'=4,'dom_2'=4,'dom_3'=2] {'dom_0','dom_1','dom_2','..., dimensions={0} | all-to-all | bytes 131072 | tf_op jit(solution)/shard_map/all_to_all | solution.py:326
  45.4 2.2 %coarse_setup.1 = (f32[128,128]{1,0:T(8,128)}, f32[1,128]{1,0:T(1,128)}, f32[1,128]{1,0:T(1,128)}, s32[8,128]{1,0:T(8,128)}, f32[9,8,128]{2,1,0:T(8,128)}) custom-call(s32[1]{0:T(128)} %bitcast.me_ref, f32[128,128]{1,0:T(8,128)} %bitcast.47, f32[3,32]{1,0:T(4,128)} %bitcast.68, s32[32,27]{1,0:T(8,128)} %col.1, f32[3,3,32,27]{3,2,1,0:T(8,128)} %bitcast.58), custom_call_target="tpu_custom_call" | custom-call | tf_op jit(solution)/shard_map/coarse_setup/pallas_call | solution.py:315
  47.6 15.1 %all_to_all.78 = f32[128,1,128]{2,1,0:T(1,128)} all-to-all(f32[128,1,128]{2,1,0:T(1,128)} %bitcast.49), channel_id=1, replica_groups=mesh['dom_0'=4,'dom_1'=4,'dom_2'=4,'dom_3'=2] {'dom_0','dom_1','dom_2','..., dimensions={0} | all-to-all | bytes 131072 | tf_op jit(solution)/shard_map/all_to_all | solution.py:326
  62.8 2.0 %coarse.5 = (f32[128,128]{1,0:T(8,128)}, f32[3,32]{1,0:T(4,128)}) custom-call(f32[128,128]{1,0:T(8,128)} %bitcast.54, f32[128,128]{1,0:T(8,128)} %get-tuple-element.25.own, f32[1,128]{1,0:T(1,128)} %get-tuple-element.26.rhs, f32[1,128]{1,0:T(1,128)} %get-tuple-element.27.dia, s32[8,128]{1,0:T(8,128)} %get-tuple-element.28.where, ...), custom_call_target="tpu_custom_call" | custom-call | tf_op jit(solution)/shard_map/coarse/pallas_call | solution.py:315
  64.7 15.1 %all_to_all.79 = f32[128,1,128]{2,1,0:T(1,128)} all-to-all(f32[128,1,128]{2,1,0:T(1,128)} %bitcast.50), channel_id=1, replica_groups=mesh['dom_0'=4,'dom_1'=4,'dom_2'=4,'dom_3'=2] {'dom_0','dom_1','dom_2','..., dimensions={0} | all-to-all | bytes 131072 | tf_op jit(solution)/shard_map/all_to_all | solution.py:326
  79.9 2.0 %coarse.6 = (f32[128,128]{1,0:T(8,128)}, f32[3,32]{1,0:T(4,128)}) custom-call(f32[128,128]{1,0:T(8,128)} %bitcast.55, f32[128,128]{1,0:T(8,128)} %get-tuple-element.30.own, f32[1,128]{1,0:T(1,128)} %get-tuple-element.26.rhs, f32[1,128]{1,0:T(1,128)} %get-tuple-element.27.dia, s32[8,128]{1,0:T(8,128)} %get-tuple-element.28.where, ...), custom_call_target="tpu_custom_call" | custom-call | tf_op jit(solution)/shard_map/coarse/pallas_call | solution.py:315
  81.8 15.2 %all_to_all.80 = f32[128,1,128]{2,1,0:T(1,128)} all-to-all(f32[128,1,128]{2,1,0:T(1,128)} %bitcast.51), channel_id=1, replica_groups=mesh['dom_0'=4,'dom_1'=4,'dom_2'=4,'dom_3'=2] {'dom_0','dom_1','dom_2','..., dimensions={0} | all-to-all | bytes 131072 | tf_op jit(solution)/shard_map/all_to_all | solution.py:326
  97.0 2.0 %coarse.7 = (f32[128,128]{1,0:T(8,128)}, f32[3,32]{1,0:T(4,128)}) custom-call(f32[128,128]{1,0:T(8,128)} %bitcast.56, f32[128,128]{1,0:T(8,128)} %get-tuple-element.31.own, f32[1,128]{1,0:T(1,128)} %get-tuple-element.26.rhs, f32[1,128]{1,0:T(1,128)} %get-tuple-element.27.dia, s32[8,128]{1,0:T(8,128)} %get-tuple-element.28.where, ...), custom_call_target="tpu_custom_call" | custom-call | tf_op jit(solution)/shard_map/coarse/pallas_call | solution.py:315
  99.0 15.3 %all_to_all.81 = f32[128,1,128]{2,1,0:T(1,128)} all-to-all(f32[128,1,128]{2,1,0:T(1,128)} %bitcast.52), channel_id=1, replica_groups=mesh['dom_0'=4,'dom_1'=4,'dom_2'=4,'dom_3'=2] {'dom_0','dom_1','dom_2','..., dimensions={0} | all-to-all | bytes 131072 | tf_op jit(solution)/shard_map/all_to_all | solution.py:326
  114.2 2.0 %coarse.8 = (f32[128,128]{1,0:T(8,128)}, f32[3,32]{1,0:T(4,128)}) custom-call(f32[128,128]{1,0:T(8,128)} %bitcast.57, f32[128,128]{1,0:T(8,128)} %get-tuple-element.32.own, f32[1,128]{1,0:T(1,128)} %get-tuple-element.26.rhs, f32[1,128]{1,0:T(1,128)} %get-tuple-element.27.dia, s32[8,128]{1,0:T(8,128)} %get-tuple-element.28.where, ...), custom_call_target="tpu_custom_call" | custom-call | tf_op jit(solution)/shard_map/coarse/pallas_call | solution.py:315
  116.2 15.1 %all_to_all.82 = f32[128,1,128]{2,1,0:T(1,128)} all-to-all(f32[128,1,128]{2,1,0:T(1,128)} %bitcast.48), channel_id=1, replica_groups=mesh['dom_0'=4,'dom_1'=4,'dom_2'=4,'dom_3'=2] {'dom_0','dom_1','dom_2','..., dimensions={0} | all-to-all | bytes 131072 | tf_op jit(solution)/shard_map/all_to_all | solution.py:326
  131.3 2.0 %coarse.9 = (f32[128,128]{1,0:T(8,128)}, f32[3,32]{1,0:T(4,128)}) custom-call(f32[128,128]{1,0:T(8,128)} %bitcast.53, f32[128,128]{1,0:T(8,128)} %get-tuple-element.33.own, f32[1,128]{1,0:T(1,128)} %get-tuple-element.26.rhs, f32[1,128]{1,0:T(1,128)} %get-tuple-element.27.dia, s32[8,128]{1,0:T(8,128)} %get-tuple-element.28.where, ...), custom_call_target="tpu_custom_call" | custom-call | tf_op jit(solution)/shard_map/coarse/pallas_call | solution.py:315
  133.3 4.8 %all-to-all-start.6 = ((f32[128,1,128]{2,1,0:T(1,128)}), f32[128,1,128]{2,1,0:T(1,128)S(1)}, u32[]{:S(2)}, u32[]{:S(2)}) async-start(f32[128,1,128]{2,1,0:T(1,128)} %bitcast.63), calls=%async_computation.6 | async-start | bytes 131072 | tf_op jit(solution)/shard_map/all_to_all | solution.py:326
  138.1 0.0 copy-done.6
  138.1 1.3 collective-permute-start.2
  139.5 0.0 copy-done.5
  139.5 1.3 collective-permute-start.3
  140.8 0.0 collective-permute-done.2.before2
  140.8 0.0 copy-start.3
  140.8 2.9 %collective-permute-done.3.after2 = f32[3,256]{1,0:T(4,128)S(1)} collective-permute-done((f32[3,256]{1,0:T(4,128)S(1)}, f32[3,256]{1,0:T(4,128)S(1)}, u32[]{:S(2)}, u32[]{:S(2)}) %collective-permute-start.3) | collective-permute-done | bytes 3104 | tf_op jit(solution)/shard_map/ppermute | solution.py:333
  143.7 0.0 copy-start.4
  143.7 4.1 %all-to-all-done.6 = f32[128,1,128]{2,1,0:T(1,128)S(1)} async-done(((f32[128,1,128]{2,1,0:T(1,128)}), f32[128,1,128]{2,1,0:T(1,128)S(1)}, u32[]{:S(2)}, u32[]{:S(2)}) %all-to-all-start.6) | async-done | bytes 65568 | tf_op jit(solution)/shard_map/all_to_all | solution.py:326
  147.8 0.0 copy-start.2
  147.8 0.0 copy-done.3
  147.8 0.0 copy-done.4
  147.8 0.6 copy-done.2
  148.4 5.9 %post.1 = f32[3,1024]{1,0:T(4,128)} custom-call(s32[1]{0:T(128)S(6)} %mul.15.base_ref, f32[128,128]{1,0:T(8,128)} %bitcast.46, f32[3,2048]{1,0:T(4,128)} %get-tuple-element.35.first_iter, f32[3,2048]{1,0:T(4,128)} %get-tuple-element.36.rhs, f32[3,2048]{1,0:T(4,128)} %get-tuple-element.37.dia, s32[27,1024]{1,0:T(8,128)} %bitcast.45, ...), custom_call_target="tpu_custom_call" | custom-call | tf_op jit(solution)/shard_map/post/pallas_call | solution.py:315
Async XLA Ops:
  4.0 2.7 %collective-permute-start = (f32[288,256]{1,0:T(8,128)}, f32[288,256]{1,0:T(8,128)S(1)}, u32[]{:S(2)}, u32[]{:S(2)}) collective-permute-start(f32[288,256]{1,0:T(8,128)} %get-tuple-element.22), channel_id=1, source_target_pairs={{0,1},{1,2},{2,3},{3,4},{4,5},{5,6},{6,7},{7,8},{8,9},{9,10},{10,1... | collective-permute-start | bytes 884744 | tf_op jit(solution)/shard_map/ppermute | solution.py:333
  5.3 5.5 %collective-permute-start.1 = (f32[288,256]{1,0:T(8,128)}, f32[288,256]{1,0:T(8,128)S(1)}, u32[]{:S(2)}, u32[]{:S(2)}) collective-permute-start(f32[288,256]{1,0:T(8,128)} %get-tuple-element.23), channel_id=1, source_target_pairs={{1,0},{2,1},{3,2},{4,3},{5,4},{6,5},{7,6},{8,7},{9,8},{10,9},{11,1... | collective-permute-start | bytes 884744 | tf_op jit(solution)/shard_map/ppermute | solution.py:333
  6.7 4.2 %copy-start = (f32[288,256]{1,0:T(8,128)}, f32[288,256]{1,0:T(8,128)S(1)}, u32[]{:S(2)}) copy-start(f32[288,256]{1,0:T(8,128)S(1)} %collective-permute-done.before) | copy-start | bytes 884740
  10.8 0.7 copy-start.1
  17.4 120.7 %copy-start.6 = (f32[3,256]{1,0:T(4,128)S(1)}, f32[3,256]{1,0:T(4,128)}, u32[]{:S(2)}) copy-start(f32[3,256]{1,0:T(4,128)} %get-tuple-element.39) | copy-start | bytes 9220
  17.4 122.0 %copy-start.5 = (f32[3,256]{1,0:T(4,128)S(1)}, f32[3,256]{1,0:T(4,128)}, u32[]{:S(2)}) copy-start(f32[3,256]{1,0:T(4,128)} %get-tuple-element.40) | copy-start | bytes 9220
  133.3 14.5 %all-to-all-start.6 = ((f32[128,1,128]{2,1,0:T(1,128)}), f32[128,1,128]{2,1,0:T(1,128)S(1)}, u32[]{:S(2)}, u32[]{:S(2)}) async-start(f32[128,1,128]{2,1,0:T(1,128)} %bitcast.63), calls=%async_computation.6 | async-start | bytes 131072 | tf_op jit(solution)/shard_map/all_to_all | solution.py:326
  138.1 2.7 %collective-permute-start.2 = (f32[3,256]{1,0:T(4,128)S(1)}, f32[3,256]{1,0:T(4,128)S(1)}, u32[]{:S(2)}, u32[]{:S(2)}) collective-permute-start(f32[3,256]{1,0:T(4,128)S(1)} %copy-done.6), channel_id=1, source_target_pairs={{0,1},{1,2},{2,3},{3,4},{4,5},{5,6},{6,7},{7,8},{8,9},{9,10},{10,1... | collective-permute-start | bytes 9224 | tf_op jit(solution)/shard_map/ppermute | solution.py:333
  139.5 4.2 %collective-permute-start.3 = (f32[3,256]{1,0:T(4,128)S(1)}, f32[3,256]{1,0:T(4,128)S(1)}, u32[]{:S(2)}, u32[]{:S(2)}) collective-permute-start(f32[3,256]{1,0:T(4,128)S(1)} %copy-done.5), channel_id=1, source_target_pairs={{1,0},{2,1},{3,2},{4,3},{5,4},{6,5},{7,6},{8,7},{9,8},{10,9},{11,1... | collective-permute-start | bytes 9224 | tf_op jit(solution)/shard_map/ppermute | solution.py:333
  140.8 7.0 %copy-start.3 = (f32[3,256]{1,0:T(4,128)}, f32[3,256]{1,0:T(4,128)S(1)}, u32[]{:S(2)}) copy-start(f32[3,256]{1,0:T(4,128)S(1)} %collective-permute-done.2.before2) | copy-start | bytes 9220
  143.7 4.1 %copy-start.4 = (f32[3,256]{1,0:T(4,128)}, f32[3,256]{1,0:T(4,128)S(1)}, u32[]{:S(2)}) copy-start(f32[3,256]{1,0:T(4,128)S(1)} %collective-permute-done.3.after2) | copy-start | bytes 9220
  147.8 0.6 copy-start.2

commit v2 on v1

--- a/solution.py
+++ b/solution.py
@@ -43,7 +43,7 @@
 
 
 def pack_kernel(rhs, dia, col, blk, agg, owner_row, up, down, node_row):
-    table = owner_row[...]
+    table = jnp.concatenate([owner_row[...]] * 4, axis=1)
     found = picked(table, agg[...]).astype(f32)
     node_row[...] = found
     for out, near, wide in ((up, ROWS - HALO, ROWS - WIDE), (down, 0, 0)):
@@ -191,7 +191,7 @@
         )
         sums = part if sums is None else sums + part
     row = jnp.concatenate(
-        [sums[0:1], sums[1:2], sums[2:3], owner_row[0:1, 0:32].astype(f32)], axis=1
+        [sums[0:1], sums[1:2], sums[2:3], owner_row[...].astype(f32)], axis=1
     )
     send[...] = jnp.broadcast_to(row, (LANES, LANES))
 
@@ -201,7 +201,7 @@
     return jnp.where(group == 0, parts[0], jnp.where(group == 1, parts[1], parts[2]))
 
 
-def coarse_setup_kernel(me_ref, sums, dia, col, blk, send, keep_rhs, keep_dia, where, weights):
+def coarse_setup_kernel(me_ref, sums, dia, col, blk, send, own, keep_rhs, keep_dia, where, weights):
     me = me_ref[0]
     got = sums[...]
     group = lax.shift_right_logical(lax.broadcasted_iota(i32, (LANES, LANES), 1), 5)
@@ -225,7 +225,8 @@
     d = jnp.concatenate([dia[0:1, :], dia[1:2, :], dia[2:3, :], pad + 1.0], axis=1)
     keep_rhs[...] = rhs
     keep_dia[...] = d
-    send[...] = jnp.broadcast_to(damping * rhs / d, (LANES, LANES))
+    own[...] = damping * rhs / d
+    send[...] = jnp.broadcast_to(own[...], (LANES, LANES))
 
     def folded(a):
         z = jnp.concatenate([a, jnp.zeros((32, 5), f32)], axis=1)
@@ -250,7 +251,7 @@
     return near
 
 
-def coarse_kernel(got, own, rhs, dia, where, weights, send, mine, table):
+def coarse_kernel(got, own, rhs, dia, where, weights, send, new_own, mine, table):
     table[...] = jnp.transpose(got[...])
     near = coarse_lookup(table, where[...], (8, LANES))
     parts = []
@@ -259,8 +260,9 @@
         s = jnp.sum(s, axis=0, keepdims=True)
         s = s + pltpu.roll(s, 64, axis=1)
         parts.append(s + pltpu.roll(s, 32, axis=1))
-    c, d = own[0:1, :], dia[...]
+    c, d = own[...], dia[...]
     new = c + damping * (rhs[...] - (d * c - spread(parts))) / d
+    new_own[...] = new
     send[...] = jnp.broadcast_to(new, (LANES, LANES))
     mine[...] = jnp.concatenate([new[:, 32 * i : 32 * i + 32] for i in range(3)], axis=0)
 
@@ -319,6 +321,7 @@
         out_specs=[vmem] * len(outs),
         out_shape=[jax.ShapeDtypeStruct(o, t) for o, t in outs],
         scratch_shapes=[pltpu.VMEM(s, f32) for s in scratch],
+        compiler_params=pltpu.CompilerParams(vmem_limit_bytes=12 * 2**20),
     )(*args)
 
 
@@ -338,7 +341,7 @@
     rhs, dia = right_side.T, fine_diagonal.T
     col, blk = fine_columns.T, fine_blocks.transpose(2, 3, 1, 0)
     agg = aggregate_of_node.reshape(8, LANES)
-    owner = jnp.pad(coarse_row_of_aggregate, (0, 96)).reshape(1, LANES)
+    owner = coarse_row_of_aggregate.reshape(1, 32)
     cdia, cblk = coarse_diagonal.T, coarse_blocks.transpose(2, 3, 0, 1)
     me = lax.axis_index(DOM).astype(i32).reshape(1)
     base = me * ROWS
@@ -361,16 +364,16 @@
     before2, after2 = shifts(up2, down2)
     sums = everywhere(send)
     line = ((1, LANES), f32)
-    send, crhs, cd, where, weights = call(
+    send, own, crhs, cd, where, weights = call(
         coarse_setup_kernel, "coarse_setup",
-        [square, line, line, ((8, LANES), i32), ((9, 8, LANES), f32)],
+        [square, line, line, line, ((8, LANES), i32), ((9, 8, LANES), f32)],
         [me, sums, cdia, coarse_columns, cblk], scalar=True,
     )
     for sweep in range(CSWEEPS - 1):
         got = everywhere(send)
-        send, mine = call(
-            coarse_kernel, "coarse", [square, ((3, 32), f32)],
-            [got, send, crhs, cd, where, weights], scratch=[(LANES, LANES)],
+        send, own, mine = call(
+            coarse_kernel, "coarse", [square, line, ((3, 32), f32)],
+            [got, own, crhs, cd, where, weights], scratch=[(LANES, LANES)],
         )
     got = everywhere(send)
     solution, = call(

time: 156 us -> 142 us (0.910)
  Pallas kernels: 26 us -> 14.2 us
  blocking collectives: 104 us -> 99.2 us
  local copies, waits for them, and re-layouts: 2.51 us -> 4.99 us
    pallas_call x9, Pallas kernels: 26 us -> 14.2 us  [call(): pl.pallas_call(kernel, name=name, in_specs=specs, out_specs=[vmem] * len(...]
    all_to_all x6, blocking collectives: 104 us -> 99.2 us  [everywhere(): return lax.all_to_all(row, DOM, 0, 0, tiled=True)]
    unnamed x14 -> x30, local copies, waits for them, and re-layouts: 1.37 us -> 4.99 us
  transfers between devices with their start and end apart: 5 -> 5, of which waited for: 4 -> 3; matrix products, arithmetic and copies ran while one was open for 0% -> 0% of each run, Pallas kernels for 0% -> 0%
where the time goes in v2:
time: 142 us; the launch traced here: 140 us
  blocking collectives  99.2 us (70%)
  Pallas kernels  14.2 us (10%)
  waiting for transfers between devices  11 us (8%)
  starting transfers between devices  10.2 us (7%)
  local copies, waits for them, and re-layouts  4.99 us (4%)
    all_to_all x6, blocking collectives, everywhere(): return lax.all_to_all(row, DOM, 0, 0, tiled=True)  99.2 us
    pallas_call x9, Pallas kernels, call(): pl.pallas_call(kernel, name=name, in_specs=specs, out_specs=[vmem] * len(...  14.2 us
    ppermute x4, waiting for transfers between devices, shifts(): return (lax.ppermute(up, DOM, forward), lax.ppermute(down, DOM, backward))  6.9 us
    ppermute x4, starting transfers between devices, shifts(): return (lax.ppermute(up, DOM, forward), lax.ppermute(down, DOM, backward))  5.37 us
    unnamed x30, local copies, waits for them, and re-layouts  4.99 us
    all_to_all x1, starting transfers between devices, everywhere(): return lax.all_to_all(row, DOM, 0, 0, tiled=True)  4.82 us
    all_to_all x1, waiting for transfers between devices, everywhere(): return lax.all_to_all(row, DOM, 0, 0, tiled=True)  4.1 us
  transfers between devices with their start and end apart: 5, of which 3 were waited for; matrix products, arithmetic and copies ran while one was open for 0% of the time, Pallas kernels for 0%

profile of v2, /device:TPU:0, one launch (start us, length us, event | category | flops | bytes accessed | tf_op | source)
XLA Modules:
  0.0 140.4 jit_solution(17511664147395157542)
XLA Ops:
  0.6 0.0 copy-start.13
  0.6 0.0 copy-start.10
  0.7 0.0 copy-start
  0.7 1.3 copy-done
  1.9 0.0 copy-start.2
  1.9 0.9 copy-done.2
  2.8 0.7 copy-done.5
  3.6 0.0 copy-start.7
  3.6 0.7 copy-done.7
  4.3 0.0 copy-start.9
  4.3 0.7 copy-done.9
  5.0 0.0 copy-start.12
  5.0 0.7 copy-done.12
  5.6 0.0 copy-start.1
  5.6 0.1 pack.1
  5.8 1.4 %collective-permute-start = (f32[288,256]{1,0:T(8,128)S(1)}, f32[288,256]{1,0:T(8,128)S(1)}, u32[]{:S(2)}, u32[]{:S(2)}) collective-permute-start(f32[288,256]{1,0:T(8,128)S(1)} %get-tuple-element.27), channel_id=1, source_target_pairs={{0,1},{1,2},{2,3},{3,4},{4,5},{5,6},{6,7},{7,8},{8,9},{9,10},{10,1... | collective-permute-start | bytes 884744 | tf_op jit(solution)/shard_map/ppermute | solution.py:336
  7.2 1.3 collective-permute-start.1
  8.5 0.0 collective-permute-done.before
  8.6 4.0 %collective-permute-done.1.after = f32[288,256]{1,0:T(8,128)S(1)} collective-permute-done((f32[288,256]{1,0:T(8,128)S(1)}, f32[288,256]{1,0:T(8,128)S(1)}, u32[]{:S(2)}, u32[]{:S(2)}) %collective-permute-start.1) | collective-permute-done | bytes 294944 | tf_op jit(solution)/shard_map/ppermute | solution.py:336
  12.6 0.0 copy-done.13
  12.6 0.0 copy-done.10
  12.6 0.0 copy-done.1
  12.6 0.0 copy-done.3
  12.6 0.0 copy-done.6
  12.6 0.0 copy-done.8
  12.6 3.7 %pre.1 = (f32[128,128]{1,0:T(8,128)S(1)}, f32[3,2048]{1,0:T(4,128)S(1)}, f32[3,2048]{1,0:T(4,128)S(1)}, f32[3,2048]{1,0:T(4,128)S(1)}, f32[3,256]{1,0:T(4,128)S(1)}, /*index=5*/f32[3,256]{1,0:T(4,128)S(1)}) custom-call(s32[1]{0:T(128)S(6)} %mul.15.base_ref, f32[3,1024]{1,0:T(4,128)S(1)} %bitcast.54, f32[3,1024]{1,0:T(4,128)S(1)} %bitcast.56, ...), custom_call_target="tpu_custom_call" | custom-call | tf_op jit(solution)/shard_map/pre/pallas_call | solution.py:317
  16.3 27.6 %all_to_all.77 = f32[128,1,128]{2,1,0:T(1,128)S(1)} all-to-all(f32[128,1,128]{2,1,0:T(1,128)S(1)} %bitcast.58), channel_id=1, replica_groups=mesh['dom_0'=4,'dom_1'=4,'dom_2'=4,'dom_3'=2] {'dom_0','dom_1','dom_2','..., dimensions={0} | all-to-all | bytes 131072 | tf_op jit(solution)/shard_map/all_to_all | solution.py:329
  43.9 0.0 copy-done.4
  43.9 0.0 copy-done.11
  43.9 0.0 copy-done.14
  43.9 0.6 coarse_setup.1
  44.5 14.3 %all_to_all.78 = f32[128,1,128]{2,1,0:T(1,128)S(1)} all-to-all(f32[128,1,128]{2,1,0:T(1,128)S(1)} %bitcast.57), channel_id=1, replica_groups=mesh['dom_0'=4,'dom_1'=4,'dom_2'=4,'dom_3'=2] {'dom_0','dom_1','dom_2','..., dimensions={0} | all-to-all | bytes 131072 | tf_op jit(solution)/shard_map/all_to_all | solution.py:329
  58.9 1.1 coarse.5
  59.9 14.3 %all_to_all.79 = f32[128,1,128]{2,1,0:T(1,128)S(1)} all-to-all(f32[128,1,128]{2,1,0:T(1,128)S(1)} %bitcast.59), channel_id=1, replica_groups=mesh['dom_0'=4,'dom_1'=4,'dom_2'=4,'dom_3'=2] {'dom_0','dom_1','dom_2','..., dimensions={0} | all-to-all | bytes 131072 | tf_op jit(solution)/shard_map/all_to_all | solution.py:329
  74.3 1.1 coarse.6
  75.3 14.3 %all_to_all.80 = f32[128,1,128]{2,1,0:T(1,128)S(1)} all-to-all(f32[128,1,128]{2,1,0:T(1,128)S(1)} %bitcast.60), channel_id=1, replica_groups=mesh['dom_0'=4,'dom_1'=4,'dom_2'=4,'dom_3'=2] {'dom_0','dom_1','dom_2','..., dimensions={0} | all-to-all | bytes 131072 | tf_op jit(solution)/shard_map/all_to_all | solution.py:329
  89.7 1.1 coarse.7
  90.7 14.3 %all_to_all.81 = f32[128,1,128]{2,1,0:T(1,128)S(1)} all-to-all(f32[128,1,128]{2,1,0:T(1,128)S(1)} %bitcast.61), channel_id=1, replica_groups=mesh['dom_0'=4,'dom_1'=4,'dom_2'=4,'dom_3'=2] {'dom_0','dom_1','dom_2','..., dimensions={0} | all-to-all | bytes 131072 | tf_op jit(solution)/shard_map/all_to_all | solution.py:329
  105.1 1.1 coarse.8
  106.1 14.3 %all_to_all.82 = f32[128,1,128]{2,1,0:T(1,128)S(1)} all-to-all(f32[128,1,128]{2,1,0:T(1,128)S(1)} %bitcast.62), channel_id=1, replica_groups=mesh['dom_0'=4,'dom_1'=4,'dom_2'=4,'dom_3'=2] {'dom_0','dom_1','dom_2','..., dimensions={0} | all-to-all | bytes 131072 | tf_op jit(solution)/shard_map/all_to_all | solution.py:329
  120.5 1.1 coarse.9
  121.6 4.8 %all-to-all-start.6 = ((f32[128,1,128]{2,1,0:T(1,128)}), f32[128,1,128]{2,1,0:T(1,128)S(1)}, u32[]{:S(2)}, u32[]{:S(2)}) async-start(f32[128,1,128]{2,1,0:T(1,128)} %bitcast.28), calls=%async_computation.6 | async-start | bytes 131072 | tf_op jit(solution)/shard_map/all_to_all | solution.py:329
  126.4 1.3 collective-permute-start.2
  127.7 1.3 collective-permute-start.3
  129.0 0.0 collective-permute-done.2.before2
  129.0 2.9 %collective-permute-done.3.after2 = f32[3,256]{1,0:T(4,128)S(1)} collective-permute-done((f32[3,256]{1,0:T(4,128)S(1)}, f32[3,256]{1,0:T(4,128)S(1)}, u32[]{:S(2)}, u32[]{:S(2)}) %collective-permute-start.3) | collective-permute-done | bytes 3104 | tf_op jit(solution)/shard_map/ppermute | solution.py:336
  131.9 4.1 %all-to-all-done.6 = f32[128,1,128]{2,1,0:T(1,128)S(1)} async-done(((f32[128,1,128]{2,1,0:T(1,128)}), f32[128,1,128]{2,1,0:T(1,128)S(1)}, u32[]{:S(2)}, u32[]{:S(2)}) %all-to-all-start.6) | async-done | bytes 65568 | tf_op jit(solution)/shard_map/all_to_all | solution.py:329
  136.0 4.3 %post.1 = f32[3,1024]{1,0:T(4,128)} custom-call(s32[1]{0:T(128)S(6)} %mul.15.base_ref, f32[128,128]{1,0:T(8,128)S(1)} %bitcast.45, f32[3,2048]{1,0:T(4,128)S(1)} %get-tuple-element.45.first_iter, f32[3,2048]{1,0:T(4,128)S(1)} %get-tuple-element.46.rhs, f32[3,2048]{1,0:T(4,128)S(1)} %get-tuple-element.47.dia, s32[27,1024]{1,0:T(8,128)S(1)} %bitcast.44, ...), custom_call_target="tpu_custom_call" | custom-call | tf_op jit(solution)/shard_map/post/pallas_call | solution.py:317
  (7 shorter events, 0.0 us)
Async XLA Ops:
  0.6 11.9 %copy-start.13 = (s32[32]{0:T(128)S(1)}, s32[32]{0:T(128)}, u32[]{:S(2)}) copy-start(s32[32]{0:T(128)} %param.14) | copy-start | bytes 388
  0.6 11.9 %copy-start.10 = (s32[1024]{0:T(1024)S(1)}, s32[1024]{0:T(1024)}, u32[]{:S(2)}) copy-start(s32[1024]{0:T(1024)} %param.13) | copy-start | bytes 12292
  0.7 1.3 copy-start
  1.9 0.9 copy-start.2
  2.8 0.7 copy-start.5
  3.6 0.7 copy-start.7
  4.3 0.7 copy-start.9
  5.0 0.7 copy-start.12
  5.6 7.0 %copy-start.1 = (f32[1024,27,3,3]{0,1,3,2:T(8,128)S(1)}, f32[1024,27,3,3]{0,1,3,2:T(8,128)}, u32[]{:S(2)}) copy-start(f32[1024,27,3,3]{0,1,3,2:T(8,128)} %param.12) | copy-start | bytes 2985988
  5.6 7.0 %copy-start.3 = (s32[1024,27]{0,1:T(8,128)S(1)}, s32[1024,27]{0,1:T(8,128)}, u32[]{:S(2)}) copy-start(s32[1024,27]{0,1:T(8,128)} %param.11) | copy-start | bytes 331780
  5.6 7.0 %copy-start.6 = (f32[1024,3]{0,1:T(4,128)S(1)}, f32[1024,3]{0,1:T(4,128)}, u32[]{:S(2)}) copy-start(f32[1024,3]{0,1:T(4,128)} %param.9) | copy-start | bytes 36868
  5.6 7.0 %copy-start.8 = (f32[1024,3]{0,1:T(4,128)S(1)}, f32[1024,3]{0,1:T(4,128)}, u32[]{:S(2)}) copy-start(f32[1024,3]{0,1:T(4,128)} %param.10) | copy-start | bytes 36868
  5.8 38.1 %copy-start.4 = (f32[32,27,3,3]{1,0,3,2:T(8,128)S(1)}, f32[32,27,3,3]{1,0,3,2:T(8,128)}, u32[]{:S(2)}) copy-start(f32[32,27,3,3]{1,0,3,2:T(8,128)} %param.17) | copy-start | bytes 93316
  5.8 38.1 %copy-start.11 = (s32[32,27]{1,0:T(8,128)S(1)}, s32[32,27]{1,0:T(8,128)}, u32[]{:S(2)}) copy-start(s32[32,27]{1,0:T(8,128)} %col.1) | copy-start | bytes 10372
  5.8 38.1 %copy-start.14 = (f32[32,3]{0,1:T(4,128)S(1)}, f32[32,3]{0,1:T(4,128)}, u32[]{:S(2)}) copy-start(f32[32,3]{0,1:T(4,128)} %param.15) | copy-start | bytes 1156
  5.8 2.8 %collective-permute-start = (f32[288,256]{1,0:T(8,128)S(1)}, f32[288,256]{1,0:T(8,128)S(1)}, u32[]{:S(2)}, u32[]{:S(2)}) collective-permute-start(f32[288,256]{1,0:T(8,128)S(1)} %get-tuple-element.27), channel_id=1, source_target_pairs={{0,1},{1,2},{2,3},{3,4},{4,5},{5,6},{6,7},{7,8},{8,9},{9,10},{10,1... | collective-permute-start | bytes 884744 | tf_op jit(solution)/shard_map/ppermute | solution.py:336
  7.2 5.3 %collective-permute-start.1 = (f32[288,256]{1,0:T(8,128)S(1)}, f32[288,256]{1,0:T(8,128)S(1)}, u32[]{:S(2)}, u32[]{:S(2)}) collective-permute-start(f32[288,256]{1,0:T(8,128)S(1)} %get-tuple-element.28), channel_id=1, source_target_pairs={{1,0},{2,1},{3,2},{4,3},{5,4},{6,5},{7,6},{8,7},{9,8},{10,9},{11,1... | collective-permute-start | bytes 884744 | tf_op jit(solution)/shard_map/ppermute | solution.py:336
  121.6 14.5 %all-to-all-start.6 = ((f32[128,1,128]{2,1,0:T(1,128)}), f32[128,1,128]{2,1,0:T(1,128)S(1)}, u32[]{:S(2)}, u32[]{:S(2)}) async-start(f32[128,1,128]{2,1,0:T(1,128)} %bitcast.28), calls=%async_computation.6 | async-start | bytes 131072 | tf_op jit(solution)/shard_map/all_to_all | solution.py:329
  126.4 2.7 %collective-permute-start.2 = (f32[3,256]{1,0:T(4,128)S(1)}, f32[3,256]{1,0:T(4,128)S(1)}, u32[]{:S(2)}, u32[]{:S(2)}) collective-permute-start(f32[3,256]{1,0:T(4,128)S(1)} %get-tuple-element.49), channel_id=1, source_target_pairs={{0,1},{1,2},{2,3},{3,4},{4,5},{5,6},{6,7},{7,8},{8,9},{9,10},{10,1... | collective-permute-start | bytes 9224 | tf_op jit(solution)/shard_map/ppermute | solution.py:336
  127.7 4.2 %collective-permute-start.3 = (f32[3,256]{1,0:T(4,128)S(1)}, f32[3,256]{1,0:T(4,128)S(1)}, u32[]{:S(2)}, u32[]{:S(2)}) collective-permute-start(f32[3,256]{1,0:T(4,128)S(1)} %get-tuple-element.50), channel_id=1, source_target_pairs={{1,0},{2,1},{3,2},{4,3},{5,4},{6,5},{7,6},{8,7},{9,8},{10,9},{11,1... | collective-permute-start | bytes 9224 | tf_op jit(solution)/shard_map/ppermute | solution.py:336

commit v3 on v2

--- a/solution.py
+++ b/solution.py
@@ -6,7 +6,10 @@
 from jax.sharding import Mesh
 from jax.sharding import PartitionSpec as P
 
-DOM = ("dom_0", "dom_1", "dom_2", "dom_3")
+DOM = ("dom_0", "dom_1", "dom_2", "dom_3", "dom_4", "dom_5")
+OTHERS = ("dom_0", "dom_1", "dom_3")
+PEERS = 16
+UNROLL = 8
 SWEEPS = 2
 CSWEEPS = 6
 damping = 0.7
@@ -149,7 +152,7 @@
     return pulled_block(cols, blks, table, b + WIDE // LANES - 2)
 
 
-def pre_kernel(base_ref, rhs, dia, col, blk, agg, owner_row, before, after,
+def pre_kernel(base_ref, rhs, dia, col, blk, agg, owner_row, cdia, before, after,
                send, first_iter, keep_rhs, keep_dia, up2, down2, one, two, res):
     base = base_ref[0]
     wide_vector(keep_rhs, rhs, before, after, P_RHS)
@@ -193,56 +196,50 @@
     row = jnp.concatenate(
         [sums[0:1], sums[1:2], sums[2:3], owner_row[...].astype(f32)], axis=1
     )
-    send[...] = jnp.broadcast_to(row, (LANES, LANES))
-
-
-def spread(parts):
-    group = lax.shift_right_logical(lax.broadcasted_iota(i32, (1, LANES), 1), 5)
-    return jnp.where(group == 0, parts[0], jnp.where(group == 1, parts[1], parts[2]))
-
-
-def coarse_setup_kernel(me_ref, sums, dia, col, blk, send, own, keep_rhs, keep_dia, where, weights):
-    me = me_ref[0]
-    got = sums[...]
-    group = lax.shift_right_logical(lax.broadcasted_iota(i32, (LANES, LANES), 1), 5)
-    rows = jnp.where(group == 3, got, 0.0)
-    rows = rows + pltpu.roll(rows, 64, axis=1)
-    rows = rows + pltpu.roll(rows, 32, axis=1)
-    rows = rows.astype(i32) - me * 32
-    lines = []
-    for r in range(32):
-        lines.append(jnp.sum(jnp.where(rows == r, got, 0.0), axis=0, keepdims=True))
-    lines = jnp.concatenate(lines, axis=0)
-    pick = lax.broadcasted_iota(i32, (8, LANES), 0) == lax.shift_right_logical(
-        lax.broadcasted_iota(i32, (8, LANES), 1), 5
-    )
-    mine = lax.dot_general(
-        pick.astype(f32), lines, (((1,), (1,)), ((), ())),
-        precision=highest, preferred_element_type=f32,
-    )
-    pad = jnp.zeros((1, 32), f32)
-    rhs = jnp.concatenate([mine[0:1], mine[1:2], mine[2:3], pad], axis=1)
-    d = jnp.concatenate([dia[0:1, :], dia[1:2, :], dia[2:3, :], pad + 1.0], axis=1)
-    keep_rhs[...] = rhs
-    keep_dia[...] = d
-    own[...] = damping * rhs / d
-    send[...] = jnp.broadcast_to(own[...], (LANES, LANES))
-
+    send[:, 0, :] = jnp.broadcast_to(row, (LANES, LANES))
+    row = jnp.concatenate(
+        [cdia[0:1], cdia[1:2], cdia[2:3], jnp.ones((1, 32), f32)], axis=1
+    )
+    send[:, 1, :] = jnp.broadcast_to(row, (LANES, LANES))
+
+
+def lane_of_device(p, me):
+    p = lax.bitwise_xor(p, lax.bitwise_and(me, 11))
+
+    def bit(at, to, mask=1):
+        return lax.shift_left(lax.bitwise_and(lax.shift_right_logical(p, at), mask), to)
+
+    return bit(3, 6) + bit(1, 5) + bit(0, 4) + bit(5, 2, 3) + bit(4, 1) + bit(2, 0)
+
+
+def device_of_lane(q, me):
+    def bit(at, to, mask=1):
+        return lax.shift_left(lax.bitwise_and(lax.shift_right_logical(q, at), mask), to)
+
+    p = bit(6, 3) + bit(5, 1) + bit(4, 0) + bit(2, 5, 3) + bit(1, 4) + bit(0, 2)
+    return lax.bitwise_xor(p, lax.bitwise_and(me, 11))
+
+
+def coarse_pack_kernel(col, blk, send):
     def folded(a):
         z = jnp.concatenate([a, jnp.zeros((32, 5), f32)], axis=1)
         z = jnp.transpose(z)
         return jnp.concatenate([z[8 * k : 8 * k + 8, :] for k in range(4)], axis=1)
 
-    where[...] = folded(col[...].astype(f32)).astype(i32)
-    for i in range(3):
-        for j in range(3):
-            weights[3 * i + j] = folded(blk[i, j])
-
-
-def coarse_lookup(table, column, shape):
-    chunk = lax.bitwise_and(column, 31)
-    lane = lax.shift_right_logical(column, 5)
-    near = [jnp.zeros(shape, f32) for _ in range(3)]
+    parts = [folded(blk[i, j]) for i in range(3) for j in range(3)]
+    parts.append(folded(col[...].astype(f32)))
+    for m in range(10):
+        for d in range(PEERS):
+            send[d, 8 * m : 8 * m + 8, :] = parts[m]
+
+
+def spread(parts):
+    group = lax.shift_right_logical(lax.broadcasted_iota(i32, parts[0].shape, 1), 5)
+    return jnp.where(group == 0, parts[0], jnp.where(group == 1, parts[1], parts[2]))
+
+
+def coarse_lookup(table, chunk, lane):
+    near = [jnp.zeros(chunk.shape, f32) for _ in range(3)]
     for c in range(32):
         here = chunk == c
         for j in range(3):
@@ -251,26 +248,105 @@
     return near
 
 
-def coarse_kernel(got, own, rhs, dia, where, weights, send, new_own, mine, table):
-    table[...] = jnp.transpose(got[...])
-    near = coarse_lookup(table, where[...], (8, LANES))
+def coarse_step(table, where, data, own, rhs, dia, gather):
+    def some(t, carry):
+        for u in range(UNROLL):
+            d = t * UNROLL + u
+            w = where[d]
+            near = coarse_lookup(table, lax.bitwise_and(w, 31), lax.shift_right_logical(w, 5))
+            for i in range(3):
+                a = data[d, lanes8(3 * i), :] * near[0]
+                a = a + data[d, lanes8(3 * i + 1), :] * near[1]
+                a = a + data[d, lanes8(3 * i + 2), :] * near[2]
+                gather[i, pl.ds(d, 1), :] = jnp.sum(a, axis=0, keepdims=True)
+        return carry
+
+    lax.fori_loop(0, PEERS // UNROLL, some, 0)
     parts = []
     for i in range(3):
-        s = weights[3 * i] * near[0] + weights[3 * i + 1] * near[1] + weights[3 * i + 2] * near[2]
-        s = jnp.sum(s, axis=0, keepdims=True)
+        s = gather[i]
         s = s + pltpu.roll(s, 64, axis=1)
         parts.append(s + pltpu.roll(s, 32, axis=1))
-    c, d = own[...], dia[...]
-    new = c + damping * (rhs[...] - (d * c - spread(parts))) / d
-    new_own[...] = new
-    send[...] = jnp.broadcast_to(new, (LANES, LANES))
-    mine[...] = jnp.concatenate([new[:, 32 * i : 32 * i + 32] for i in range(3)], axis=0)
-
-
-def post_kernel(base_ref, got, first_iter, rhs, dia, col, blk, node_row, before, after,
-                before2, after2, out, table, one, two):
+    return own + damping * (rhs - (dia * own - spread(parts))) / dia
+
+
+def lanes8(m):
+    return slice(8 * m, 8 * m + 8)
+
+
+def coarse_first_kernel(me_ref, sums, data, far_up, far_down, new, rhs, dia, where,
+                        table, gather, left, right):
+    me = me_ref[0]
+    got = jnp.transpose(sums[:, 0, :])
+    rows = got[96:128].astype(i32)
+    s = got[0:96]
+    split = []
+    for _ in range(3):
+        t = s.astype(jnp.bfloat16).astype(f32)
+        split.append(t)
+        s = s - t
+    chunk = lax.broadcasted_iota(i32, (32, LANES), 0)
+    place = lax.broadcasted_iota(i32, (LANES, LANES), 0)
+    low = lax.bitwise_and(rows, 31)
+    lane = lane_of_device(lax.shift_right_logical(rows, 5), me)
+    for a in range(32):
+        here = chunk == jnp.broadcast_to(low[a : a + 1], (32, LANES))
+        for t in range(3):
+            for i in range(3):
+                value = jnp.broadcast_to(split[t][32 * i + a : 32 * i + a + 1], (32, LANES))
+                left[96 * t + 32 * i : 96 * t + 32 * i + 32, lanes(LANES * a)] = jnp.where(
+                    here, value, 0.0
+                ).astype(jnp.bfloat16)
+        right[:, lanes(LANES * a)] = jnp.where(
+            place == jnp.broadcast_to(lane[a : a + 1], (LANES, LANES)), 1.0, 0.0
+        ).astype(jnp.bfloat16)
+    both = lax.dot_general(
+        left[...], right[...], (((1,), (1,)), ((), ())), preferred_element_type=f32
+    )
+    crhs = both[0:96] + both[96:192] + both[192:288]
+    order = device_of_lane(lax.broadcasted_iota(i32, (96, LANES), 1), me)
+    cdia = jnp.take_along_axis(
+        jnp.transpose(sums[:, 1, :])[0:96], order, axis=1, mode="promise_in_bounds"
+    )
+    pad = jnp.zeros((32, LANES), f32)
+    first = jnp.concatenate([damping * crhs / cdia, pad], axis=0)
+    table[...] = first
+    own = jnp.transpose(first)[0:PEERS]
+    rhs[...] = jnp.transpose(jnp.concatenate([crhs, pad], axis=0))[0:PEERS]
+    dia[...] = jnp.transpose(jnp.concatenate([cdia, pad + 1.0], axis=0))[0:PEERS]
+    for d in range(PEERS):
+        c = data[d, 72:80, :].astype(i32)
+        at = lane_of_device(lax.shift_right_logical(c, 5), me)
+        where[d] = lax.bitwise_and(c, 31) + lax.shift_left(at, 5)
+    new[...] = coarse_step(table, where, data, own, rhs[...], dia[...], gather)
+
+
+def gathered(table, pieces, mine):
+    row = 0
+    for piece in pieces:
+        size = piece.shape[0]
+        mine[row : row + size, :] = piece[...]
+        row += size
+    table[...] = jnp.transpose(mine[...])
+
+
+def coarse_kernel(me_ref, p0, p1, p2, p3, rhs, dia, where, data, new, correction,
+                  table, mine, gather):
+    gathered(table, (p0, p1, p2, p3), mine)
+    got = coarse_step(table, where, data, p0[...], rhs[...], dia[...], gather)
+    new[...] = got
+    mine[0:PEERS, :] = got
+    me = me_ref[0]
+    at = lane_of_device(me, me)
+    row = mine[pl.ds(at, 1), :]
+    correction[...] = jnp.concatenate([row[:, 32 * i : 32 * i + 32] for i in range(3)], axis=0)
+
+
+def post_kernel(base_ref, p0, p1, p2, p3, first_iter, rhs, dia, col, blk, node_row, before, after,
+                before2, after2, out, table, mine, one, two):
     base = base_ref[0]
-    table[...] = jnp.transpose(got[...])
+    me = lax.shift_right_logical(base, 10)
+    gathered(table, (p0, p1, p2, p3), mine)
     one[...] = first_iter[...]
     one[:, lanes(0, HALO)] = before2[...]
     one[:, lanes(WIDE + ROWS + HALO, HALO)] = after2[...]
@@ -279,8 +355,13 @@
         for h in (before, after) for t in range(2) for q in range(2)
     ]
     edge = jnp.concatenate(edge, axis=0)
-    own = coarse_lookup(table, node_row[...].astype(i32), (8, LANES))
-    far = coarse_lookup(table, edge.astype(i32), (8, LANES))
+
+    def found(rows):
+        rows = rows.astype(i32)
+        lane = lane_of_device(lax.shift_right_logical(rows, 5), me)
+        return coarse_lookup(table, lax.bitwise_and(rows, 31), lane)
+
+    own, far = found(node_row[...]), found(edge)
     for s in range(16):
         if s < 4:
             row = [f[s : s + 1, :] for f in far]
@@ -320,13 +401,21 @@
         in_specs=specs,
         out_specs=[vmem] * len(outs),
         out_shape=[jax.ShapeDtypeStruct(o, t) for o, t in outs],
-        scratch_shapes=[pltpu.VMEM(s, f32) for s in scratch],
+        scratch_shapes=[
+            pltpu.VMEM(*s) if isinstance(s[0], tuple) else pltpu.VMEM(s, f32) for s in scratch
+        ],
         compiler_params=pltpu.CompilerParams(vmem_limit_bytes=12 * 2**20),
     )(*args)
 
 
-def everywhere(row):
-    return lax.all_to_all(row, DOM, 0, 0, tiled=True)
+def in_group(new):
+    swap = [(0, 1), (1, 0)]
+    p1 = lax.ppermute(new, "dom_5", swap)
+    a = jnp.concatenate([new, p1], axis=0)
+    p2 = lax.ppermute(a, "dom_4", swap)
+    b = jnp.concatenate([a, p2], axis=0)
+    p3 = lax.ppermute(b, "dom_2", swap)
+    return new, p1, p2, p3
 
 
 def shifts(up, down):
@@ -347,45 +436,52 @@
     base = me * ROWS
     wide = WIDE + ROWS + WIDE
 
+    dsend, = call(
+        coarse_pack_kernel, "coarse_pack", [((PEERS, 80, LANES), f32)], [coarse_columns, cblk]
+    )
+    data = lax.all_to_all(dsend, OTHERS, 0, 0, tiled=True)
     up, down, node_row = call(
         pack_kernel, "pack",
         [((P_ALL, HALO), f32), ((P_ALL, HALO), f32), ((8, LANES), f32)],
         [rhs, dia, col, blk, agg, owner],
     )
     before, after = shifts(up, down)
-    square = ((LANES, LANES), f32)
     send, first_iter, wrhs, wdia, up2, down2 = call(
         pre_kernel, "pre",
-        [square, ((3, wide), f32), ((3, wide), f32), ((3, wide), f32),
+        [((LANES, 2, LANES), f32), ((3, wide), f32), ((3, wide), f32), ((3, wide), f32),
          ((3, HALO), f32), ((3, HALO), f32)],
-        [base, rhs, dia, col, blk, agg, owner, before, after],
+        [base, rhs, dia, col, blk, agg, owner, cdia, before, after],
         scratch=[(3, wide), (3, wide), (8, ROWS)], scalar=True,
     )
     before2, after2 = shifts(up2, down2)
-    sums = everywhere(send)
-    line = ((1, LANES), f32)
-    send, own, crhs, cd, where, weights = call(
-        coarse_setup_kernel, "coarse_setup",
-        [square, line, line, line, ((8, LANES), i32), ((9, 8, LANES), f32)],
-        [me, sums, cdia, coarse_columns, cblk], scalar=True,
-    )
-    for sweep in range(CSWEEPS - 1):
-        got = everywhere(send)
-        send, own, mine = call(
-            coarse_kernel, "coarse", [square, line, ((3, 32), f32)],
-            [got, own, crhs, cd, where, weights], scratch=[(LANES, LANES)],
+    sums = lax.all_to_all(send, DOM, 0, 0, tiled=True)
+    peers = ((PEERS, LANES), f32)
+    gather = (3, PEERS, LANES)
+    square = (LANES, LANES)
+    new, crhs, cd, where = call(
+        coarse_first_kernel, "coarse_first",
+        [peers, peers, peers, ((PEERS, 8, LANES), i32)],
+        [me, sums, data, before2, after2],
+        scratch=[square, gather, ((288, 4096), jnp.bfloat16), ((LANES, 4096), jnp.bfloat16)],
+        scalar=True,
+    )
+    for sweep in range(CSWEEPS - 2):
+        new, mine = call(
+            coarse_kernel, "coarse", [peers, ((3, 32), f32)],
+            [me, *in_group(new), crhs, cd, where, data],
+            scratch=[square, square, gather], scalar=True,
         )
-    got = everywhere(send)
     solution, = call(
         post_kernel, "post", [((3, ROWS), f32)],
-        [base, got, first_iter, wrhs, wdia, col, blk, node_row, before, after, before2, after2],
-        scratch=[(LANES, LANES), (3, wide), (3, wide)], scalar=True,
+        [base, *in_group(new), first_iter, wrhs, wdia, col, blk, node_row,
+         before, after, before2, after2],
+        scratch=[square, square, (3, wide), (3, wide)], scalar=True,
     )
     return solution.T, mine.T
 
 
 def solution(mesh):
-    torus = Mesh(mesh.devices.reshape(4, 4, 4, 2), DOM)
+    torus = Mesh(mesh.devices.reshape(4, 2, 2, 2, 2, 2), DOM)
     return jax.shard_map(
         body,
         mesh=torus,

time: 142 us -> 127 us (0.89)
  blocking collectives: 99.2 us -> 0 us
  waiting for transfers between devices: 11 us -> 61.6 us
  starting transfers between devices: 10.2 us -> 34.2 us
  Pallas kernels: 14.2 us -> 24.4 us
    all_to_all x6 -> x0, blocking collectives: 99.2 us -> none  [everywhere(): return lax.all_to_all(row, DOM, 0, 0, tiled=True)]
    ppermute x0 -> x15, waiting for transfers between devices: none -> 37.6 us  [the longest x5 17.5 us: in_group(): p3 = lax.ppermute(b, 'dom_2', swap)]
    all_to_all x1 -> x2, starting transfers between devices: 4.82 us -> 22.2 us  [the longest x1 18 us: body(): sums = lax.all_to_all(send, DOM, 0, 0, tiled=True)]
    all_to_all x1 -> x2, waiting for transfers between devices: 4.1 us -> 17.2 us  [the longest x1 8.66 us: body(): sums = lax.all_to_all(send, DOM, 0, 0, tiled=True)]
    pallas_call x9, Pallas kernels: 14.2 us -> 24.4 us  [call(): pl.pallas_call(kernel, name=name, in_specs=specs, out_specs=[vmem] * len(...]
    ppermute x0 -> x15, starting transfers between devices: none -> 6.57 us  [the longest x5 4.44 us: in_group(): p2 = lax.ppermute(a, 'dom_4', swap)]
  transfers between devices with their start and end apart: 5 -> 21, of which waited for: 3 -> 19; matrix products, arithmetic and copies ran while one was open for 0% -> 0% of each run, Pallas kernels for 0% -> 1%
where the time goes in v3:
time: 127 us; the launch traced here: 126 us
  waiting for transfers between devices  61.6 us (49%)
  starting transfers between devices  34.2 us (27%)
  Pallas kernels  24.4 us (19%)
  local copies, waits for them, and re-layouts  4.99 us (4%)
    pallas_call x9, Pallas kernels, call(): pl.pallas_call(kernel, name=name, in_specs=specs, out_specs=[vmem] * len(...  24.4 us
    all_to_all x1, starting transfers between devices, body(): sums = lax.all_to_all(send, DOM, 0, 0, tiled=True)  18 us
    ppermute x5, waiting for transfers between devices, in_group(): p3 = lax.ppermute(b, 'dom_2', swap)  17.5 us
    ppermute x5, waiting for transfers between devices, in_group(): p2 = lax.ppermute(a, 'dom_4', swap)  14.3 us
    all_to_all x1, waiting for transfers between devices, body(): sums = lax.all_to_all(send, DOM, 0, 0, tiled=True)  8.66 us
    all_to_all x1, waiting for transfers between devices, body(): data = lax.all_to_all(dsend, OTHERS, 0, 0, tiled=True)  8.56 us
    ppermute x4, waiting for transfers between devices, shifts(): return (lax.ppermute(up, DOM, forward), lax.ppermute(down, DOM, backward))  6.8 us
    ppermute x5, waiting for transfers between devices, in_group(): p1 = lax.ppermute(new, 'dom_5', swap)  5.84 us
  transfers between devices with their start and end apart: 21, of which 19 were waited for; matrix products, arithmetic and copies ran while one was open for 0% of the time, Pallas kernels for 1%

profile of v3, /device:TPU:0, one launch (start us, length us, event | category | flops | bytes accessed | tf_op | source)
XLA Modules:
  0.0 126.2 jit_solution(13580017712499904327)
XLA Ops:
  0.7 1.3 %copy-done = f32[1024,27,3,3]{0,1,3,2:T(8,128)S(1)} copy-done((f32[1024,27,3,3]{0,1,3,2:T(8,128)S(1)}, f32[1024,27,3,3]{0,1,3,2:T(8,128)}, u32[]{:S(2)}) %copy-start) | copy-done | bytes 995352
  2.0 0.9 copy-done.2
  2.9 0.7 copy-done.5
  3.6 0.7 copy-done.7
  4.3 0.7 copy-done.9
  5.0 0.7 copy-done.13
  5.8 1.4 %collective-permute-start = (f32[288,256]{1,0:T(8,128)S(1)}, f32[288,256]{1,0:T(8,128)S(1)}, u32[]{:S(2)}, u32[]{:S(2)}) collective-permute-start(f32[288,256]{1,0:T(8,128)S(1)} %get-tuple-element.20), channel_id=1, source_target_pairs={{0,1},{1,2},{2,3},{3,4},{4,5},{5,6},{6,7},{7,8},{8,9},{9,10},{10,1... | collective-permute-start | bytes 884744 | tf_op jit(solution)/shard_map/ppermute | solution.py:425
  7.2 1.3 %collective-permute-start.1 = (f32[288,256]{1,0:T(8,128)S(1)}, f32[288,256]{1,0:T(8,128)S(1)}, u32[]{:S(2)}, u32[]{:S(2)}) collective-permute-start(f32[288,256]{1,0:T(8,128)S(1)} %get-tuple-element.21), channel_id=1, source_target_pairs={{1,0},{2,1},{3,2},{4,3},{5,4},{6,5},{7,6},{8,7},{9,8},{10,9},{11,1... | collective-permute-start | bytes 884744 | tf_op jit(solution)/shard_map/ppermute | solution.py:425
  8.6 4.0 %collective-permute-done.1.after = f32[288,256]{1,0:T(8,128)S(1)} collective-permute-done((f32[288,256]{1,0:T(8,128)S(1)}, f32[288,256]{1,0:T(8,128)S(1)}, u32[]{:S(2)}, u32[]{:S(2)}) %collective-permute-start.1) | collective-permute-done | bytes 294944 | tf_op jit(solution)/shard_map/ppermute | solution.py:425
  12.6 4.5 %pre.1 = (f32[128,2,128]{2,1,0:T(2,128)}, f32[3,2048]{1,0:T(4,128)S(1)}, f32[3,2048]{1,0:T(4,128)S(1)}, f32[3,2048]{1,0:T(4,128)S(1)}, f32[3,256]{1,0:T(4,128)S(1)}, /*index=5*/f32[3,256]{1,0:T(4,128)S(1)}) custom-call(s32[1]{0:T(128)S(6)} %mul.23.base_ref, f32[3,1024]{1,0:T(4,128)S(1)} %bitcast.19, f32[3,1024]{1,0:T(4,128)S(1)} %bitcast.21, ...), custom_call_target="tpu_custom_call" | custom-call | tf_op jit(solution)/shard_map/pre/pallas_call | solution.py:398
  17.1 18.0 %all-to-all-start = ((f32[128,2,128]{2,1,0:T(2,128)}), f32[128,2,128]{2,1,0:T(2,128)S(1)}, u32[]{:S(2)}, u32[]{:S(2)}) async-start(f32[128,2,128]{2,1,0:T(2,128)} %get-tuple-element.22), calls=%async_computation | async-start | bytes 262144 | tf_op jit(solution)/shard_map/all_to_all | solution.py:457
  35.1 1.0 coarse_pack.1
  36.2 8.7 %all-to-all-done.sums = f32[128,2,128]{2,1,0:T(2,128)S(1)} async-done(((f32[128,2,128]{2,1,0:T(2,128)}), f32[128,2,128]{2,1,0:T(2,128)S(1)}, u32[]{:S(2)}, u32[]{:S(2)}) %all-to-all-start) | async-done | bytes 131104 | tf_op jit(solution)/shard_map/all_to_all | solution.py:457
  44.8 4.2 %all-to-all-start.1 = ((f32[16,80,128]{2,1,0:T(8,128)}), f32[16,80,128]{2,1,0:T(8,128)S(1)}, u32[]{:S(2)}, u32[]{:S(2)}) async-start(f32[16,80,128]{2,1,0:T(8,128)} %coarse_pack.1), calls=%async_computation.1 | async-start | bytes 1310720 | tf_op jit(solution)/shard_map/all_to_all | solution.py:442
  49.0 1.4 %collective-permute-start.2 = (f32[3,256]{1,0:T(4,128)S(1)}, f32[3,256]{1,0:T(4,128)S(1)}, u32[]{:S(2)}, u32[]{:S(2)}) collective-permute-start(f32[3,256]{1,0:T(4,128)S(1)} %get-tuple-element.23), channel_id=1, source_target_pairs={{0,1},{1,2},{2,3},{3,4},{4,5},{5,6},{6,7},{7,8},{8,9},{9,10},{10,1... | collective-permute-start | bytes 9224 | tf_op jit(solution)/shard_map/ppermute | solution.py:425
  50.5 1.3 %collective-permute-start.3 = (f32[3,256]{1,0:T(4,128)S(1)}, f32[3,256]{1,0:T(4,128)S(1)}, u32[]{:S(2)}, u32[]{:S(2)}) collective-permute-start(f32[3,256]{1,0:T(4,128)S(1)} %get-tuple-element.24), channel_id=1, source_target_pairs={{1,0},{2,1},{3,2},{4,3},{5,4},{6,5},{7,6},{8,7},{9,8},{10,9},{11,1... | collective-permute-start | bytes 9224 | tf_op jit(solution)/shard_map/ppermute | solution.py:425
  51.8 2.8 %collective-permute-done.3.far_down.after2 = f32[3,256]{1,0:T(4,128)S(1)} collective-permute-done((f32[3,256]{1,0:T(4,128)S(1)}, f32[3,256]{1,0:T(4,128)S(1)}, u32[]{:S(2)}, u32[]{:S(2)}) %collective-permute-start.3) | collective-permute-done | bytes 3104 | tf_op jit(solution)/shard_map/ppermute | solution.py:425
  54.6 8.6 %all-to-all-done.1.data = f32[16,80,128]{2,1,0:T(8,128)S(1)} async-done(((f32[16,80,128]{2,1,0:T(8,128)}), f32[16,80,128]{2,1,0:T(8,128)S(1)}, u32[]{:S(2)}, u32[]{:S(2)}) %all-to-all-start.1) | async-done | bytes 655392 | tf_op jit(solution)/shard_map/all_to_all | solution.py:442
  63.1 3.5 %coarse_first.1 = (f32[16,128]{1,0:T(8,128)S(1)}, f32[16,128]{1,0:T(8,128)S(1)}, f32[16,128]{1,0:T(8,128)S(1)}, s32[16,8,128]{2,1,0:T(8,128)S(1)}) custom-call(s32[1]{0:T(128)} %bitcast.me_ref, f32[128,2,128]{2,1,0:T(2,128)S(1)} %all-to-all-done.sums, f32[16,80,128]{2,1,0:T(8,128)S(1)} %all-to-all-done.1.data, ...), custom_call_target="tpu_custom_call" | custom-call | tf_op jit(solution)/shard_map/coarse_first/pallas_call | solution.py:398
  66.7 1.2 collective-permute-done.4.p1
  67.9 0.9 collective-permute-start.5
  68.8 2.9 %collective-permute-done.5.p2 = f32[32,128]{1,0:T(8,128)S(1)} collective-permute-done((f32[32,128]{1,0:T(8,128)S(1)}, f32[32,128]{1,0:T(8,128)S(1)}, u32[]{:S(2)}, u32[]{:S(2)}) %collective-permute-start.5) | collective-permute-done | bytes 16416 | tf_op jit(solution)/shard_map/ppermute | solution.py:415
  71.6 0.4 collective-permute-start.6
  72.1 3.5 %collective-permute-done.6.p3 = f32[64,128]{1,0:T(8,128)S(1)} collective-permute-done((f32[64,128]{1,0:T(8,128)S(1)}, f32[64,128]{1,0:T(8,128)S(1)}, u32[]{:S(2)}, u32[]{:S(2)}) %collective-permute-start.6) | collective-permute-done | bytes 32800 | tf_op jit(solution)/shard_map/ppermute | solution.py:417
  75.6 2.7 %coarse.4 = (f32[16,128]{1,0:T(8,128)S(1)}, f32[3,32]{1,0:T(4,128)}) custom-call(s32[1]{0:T(128)} %bitcast.me_ref, f32[16,128]{1,0:T(8,128)S(1)} %get-tuple-element.25.p0, f32[16,128]{1,0:T(8,128)S(1)} %collective-permute-done.4.p1, f32[32,128]{1,0:T(8,128)S(1)} %collective-permute-done.5.p2, f32[64,128]{1,0:T(8,128)S(1)} %collective-permute-done.6.p3, ...), custom_call_target="tpu_custom_call" | custom-call | tf_op jit(solution)/shard_map/coarse/pallas_call | solution.py:398
  78.3 1.2 collective-permute-done.7.p1
  79.5 0.9 collective-permute-start.8
  80.4 2.9 %collective-permute-done.8.p2 = f32[32,128]{1,0:T(8,128)S(1)} collective-permute-done((f32[32,128]{1,0:T(8,128)S(1)}, f32[32,128]{1,0:T(8,128)S(1)}, u32[]{:S(2)}, u32[]{:S(2)}) %collective-permute-start.8) | collective-permute-done | bytes 16416 | tf_op jit(solution)/shard_map/ppermute | solution.py:415
  83.2 0.4 collective-permute-start.9
  83.6 3.5 %collective-permute-done.9.p3 = f32[64,128]{1,0:T(8,128)S(1)} collective-permute-done((f32[64,128]{1,0:T(8,128)S(1)}, f32[64,128]{1,0:T(8,128)S(1)}, u32[]{:S(2)}, u32[]{:S(2)}) %collective-permute-start.9) | collective-permute-done | bytes 32800 | tf_op jit(solution)/shard_map/ppermute | solution.py:417
  87.1 2.7 %coarse.5 = (f32[16,128]{1,0:T(8,128)S(1)}, f32[3,32]{1,0:T(4,128)}) custom-call(s32[1]{0:T(128)} %bitcast.me_ref, f32[16,128]{1,0:T(8,128)S(1)} %get-tuple-element.29.p0, f32[16,128]{1,0:T(8,128)S(1)} %collective-permute-done.7.p1, f32[32,128]{1,0:T(8,128)S(1)} %collective-permute-done.8.p2, f32[64,128]{1,0:T(8,128)S(1)} %collective-permute-done.9.p3, ...), custom_call_target="tpu_custom_call" | custom-call | tf_op jit(solution)/shard_map/coarse/pallas_call | solution.py:398
  89.9 1.2 collective-permute-done.10.p1
  91.0 0.9 collective-permute-start.11
  91.9 2.9 %collective-permute-done.11.p2 = f32[32,128]{1,0:T(8,128)S(1)} collective-permute-done((f32[32,128]{1,0:T(8,128)S(1)}, f32[32,128]{1,0:T(8,128)S(1)}, u32[]{:S(2)}, u32[]{:S(2)}) %collective-permute-start.11) | collective-permute-done | bytes 16416 | tf_op jit(solution)/shard_map/ppermute | solution.py:415
  94.8 0.4 collective-permute-start.12
  95.2 3.5 %collective-permute-done.12.p3 = f32[64,128]{1,0:T(8,128)S(1)} collective-permute-done((f32[64,128]{1,0:T(8,128)S(1)}, f32[64,128]{1,0:T(8,128)S(1)}, u32[]{:S(2)}, u32[]{:S(2)}) %collective-permute-start.12) | collective-permute-done | bytes 32800 | tf_op jit(solution)/shard_map/ppermute | solution.py:417
  98.7 2.7 %coarse.6 = (f32[16,128]{1,0:T(8,128)S(1)}, f32[3,32]{1,0:T(4,128)}) custom-call(s32[1]{0:T(128)} %bitcast.me_ref, f32[16,128]{1,0:T(8,128)S(1)} %get-tuple-element.30.p0, f32[16,128]{1,0:T(8,128)S(1)} %collective-permute-done.10.p1, f32[32,128]{1,0:T(8,128)S(1)} %collective-permute-done.11.p2, f32[64,128]{1,0:T(8,128)S(1)} %collective-permute-done.12.p3, ...), custom_call_target="tpu_custom_call" | custom-call | tf_op jit(solution)/shard_map/coarse/pallas_call | solution.py:398
  101.4 1.2 collective-permute-done.13.p1
  102.6 0.9 collective-permute-start.14
  103.5 2.9 %collective-permute-done.14.p2 = f32[32,128]{1,0:T(8,128)S(1)} collective-permute-done((f32[32,128]{1,0:T(8,128)S(1)}, f32[32,128]{1,0:T(8,128)S(1)}, u32[]{:S(2)}, u32[]{:S(2)}) %collective-permute-start.14) | collective-permute-done | bytes 16416 | tf_op jit(solution)/shard_map/ppermute | solution.py:415
  106.7 3.5 %collective-permute-done.15.p3 = f32[64,128]{1,0:T(8,128)S(1)} collective-permute-done((f32[64,128]{1,0:T(8,128)S(1)}, f32[64,128]{1,0:T(8,128)S(1)}, u32[]{:S(2)}, u32[]{:S(2)}) %collective-permute-start.15) | collective-permute-done | bytes 32800 | tf_op jit(solution)/shard_map/ppermute | solution.py:417
  110.3 2.7 %coarse.7 = (f32[16,128]{1,0:T(8,128)S(1)}, f32[3,32]{1,0:T(4,128)}) custom-call(s32[1]{0:T(128)} %bitcast.me_ref, f32[16,128]{1,0:T(8,128)S(1)} %get-tuple-element.31.p0, f32[16,128]{1,0:T(8,128)S(1)} %collective-permute-done.13.p1, f32[32,128]{1,0:T(8,128)S(1)} %collective-permute-done.14.p2, f32[64,128]{1,0:T(8,128)S(1)} %collective-permute-done.15.p3, ...), custom_call_target="tpu_custom_call" | custom-call | tf_op jit(solution)/shard_map/coarse/pallas_call | solution.py:398
  113.0 1.2 collective-permute-done.16.p1
  114.2 0.9 collective-permute-start.17
  115.1 2.9 %collective-permute-done.17.p2 = f32[32,128]{1,0:T(8,128)S(1)} collective-permute-done((f32[32,128]{1,0:T(8,128)S(1)}, f32[32,128]{1,0:T(8,128)S(1)}, u32[]{:S(2)}, u32[]{:S(2)}) %collective-permute-start.17) | collective-permute-done | bytes 16416 | tf_op jit(solution)/shard_map/ppermute | solution.py:415
  117.9 0.4 collective-permute-start.18
  118.3 3.5 %collective-permute-done.18.p3 = f32[64,128]{1,0:T(8,128)S(1)} collective-permute-done((f32[64,128]{1,0:T(8,128)S(1)}, f32[64,128]{1,0:T(8,128)S(1)}, u32[]{:S(2)}, u32[]{:S(2)}) %collective-permute-start.18) | collective-permute-done | bytes 32800 | tf_op jit(solution)/shard_map/ppermute | solution.py:417
  121.8 4.3 %post.1 = f32[3,1024]{1,0:T(4,128)} custom-call(s32[1]{0:T(128)S(6)} %mul.23.base_ref, f32[16,128]{1,0:T(8,128)S(1)} %get-tuple-element.32.p0, f32[16,128]{1,0:T(8,128)S(1)} %collective-permute-done.16.p1, f32[32,128]{1,0:T(8,128)S(1)} %collective-permute-done.17.p2, f32[64,128]{1,0:T(8,128)S(1)} %collective-permute-done.18.p3, ...), custom_call_target="tpu_custom_call" | custom-call | tf_op jit(solution)/shard_map/post/pallas_call | solution.py:398
  (43 shorter events, 0.7 us)
Async XLA Ops:
  0.6 11.9 %copy-start.14 = (s32[32]{0:T(128)S(1)}, s32[32]{0:T(128)}, u32[]{:S(2)}) copy-start(s32[32]{0:T(128)} %param.14) | copy-start | bytes 388
  0.6 11.9 %copy-start.10 = (s32[1024]{0:T(1024)S(1)}, s32[1024]{0:T(1024)}, u32[]{:S(2)}) copy-start(s32[1024]{0:T(1024)} %param.13) | copy-start | bytes 12292
  0.7 11.9 %copy-start.12 = (f32[32,3]{0,1:T(4,128)S(1)}, f32[32,3]{0,1:T(4,128)}, u32[]{:S(2)}) copy-start(f32[32,3]{0,1:T(4,128)} %param.15) | copy-start | bytes 1156
  0.7 1.3 %copy-start = (f32[1024,27,3,3]{0,1,3,2:T(8,128)S(1)}, f32[1024,27,3,3]{0,1,3,2:T(8,128)}, u32[]{:S(2)}) copy-start(f32[1024,27,3,3]{0,1,3,2:T(8,128)} %param.12) | copy-start | bytes 2985988
  2.0 0.9 copy-start.2
  2.9 0.7 copy-start.5
  3.6 0.7 copy-start.7
  4.3 0.7 copy-start.9
  5.0 0.7 copy-start.13
  5.6 6.9 %copy-start.1 = (f32[1024,27,3,3]{0,1,3,2:T(8,128)S(1)}, f32[1024,27,3,3]{0,1,3,2:T(8,128)}, u32[]{:S(2)}) copy-start(f32[1024,27,3,3]{0,1,3,2:T(8,128)} %param.12) | copy-start | bytes 2985988
  5.6 7.0 %copy-start.3 = (s32[1024,27]{0,1:T(8,128)S(1)}, s32[1024,27]{0,1:T(8,128)}, u32[]{:S(2)}) copy-start(s32[1024,27]{0,1:T(8,128)} %param.11) | copy-start | bytes 331780
  5.6 7.0 %copy-start.6 = (f32[1024,3]{0,1:T(4,128)S(1)}, f32[1024,3]{0,1:T(4,128)}, u32[]{:S(2)}) copy-start(f32[1024,3]{0,1:T(4,128)} %param.9) | copy-start | bytes 36868
  5.6 7.0 %copy-start.8 = (f32[1024,3]{0,1:T(4,128)S(1)}, f32[1024,3]{0,1:T(4,128)}, u32[]{:S(2)}) copy-start(f32[1024,3]{0,1:T(4,128)} %param.10) | copy-start | bytes 36868
  5.8 29.3 %copy-start.4 = (f32[32,27,3,3]{1,0,3,2:T(8,128)S(1)}, f32[32,27,3,3]{1,0,3,2:T(8,128)}, u32[]{:S(2)}) copy-start(f32[32,27,3,3]{1,0,3,2:T(8,128)} %param.17) | copy-start | bytes 93316
  5.8 29.3 %copy-start.11 = (s32[32,27]{1,0:T(8,128)S(1)}, s32[32,27]{1,0:T(8,128)}, u32[]{:S(2)}) copy-start(s32[32,27]{1,0:T(8,128)} %col.1) | copy-start | bytes 10372
  5.8 2.8 %collective-permute-start = (f32[288,256]{1,0:T(8,128)S(1)}, f32[288,256]{1,0:T(8,128)S(1)}, u32[]{:S(2)}, u32[]{:S(2)}) collective-permute-start(f32[288,256]{1,0:T(8,128)S(1)} %get-tuple-element.20), channel_id=1, source_target_pairs={{0,1},{1,2},{2,3},{3,4},{4,5},{5,6},{6,7},{7,8},{8,9},{9,10},{10,1... | collective-permute-start | bytes 884744 | tf_op jit(solution)/shard_map/ppermute | solution.py:425
  7.2 5.3 %collective-permute-start.1 = (f32[288,256]{1,0:T(8,128)S(1)}, f32[288,256]{1,0:T(8,128)S(1)}, u32[]{:S(2)}, u32[]{:S(2)}) collective-permute-start(f32[288,256]{1,0:T(8,128)S(1)} %get-tuple-element.21), channel_id=1, source_target_pairs={{1,0},{2,1},{3,2},{4,3},{5,4},{6,5},{7,6},{8,7},{9,8},{10,9},{11,1... | collective-permute-start | bytes 884744 | tf_op jit(solution)/shard_map/ppermute | solution.py:425
  17.1 27.7 %all-to-all-start = ((f32[128,2,128]{2,1,0:T(2,128)}), f32[128,2,128]{2,1,0:T(2,128)S(1)}, u32[]{:S(2)}, u32[]{:S(2)}) async-start(f32[128,2,128]{2,1,0:T(2,128)} %get-tuple-element.22), calls=%async_computation | async-start | bytes 262144 | tf_op jit(solution)/shard_map/all_to_all | solution.py:457
  44.8 18.3 %all-to-all-start.1 = ((f32[16,80,128]{2,1,0:T(8,128)}), f32[16,80,128]{2,1,0:T(8,128)S(1)}, u32[]{:S(2)}, u32[]{:S(2)}) async-start(f32[16,80,128]{2,1,0:T(8,128)} %coarse_pack.1), calls=%async_computation.1 | async-start | bytes 1310720 | tf_op jit(solution)/shard_map/all_to_all | solution.py:442
  49.0 2.7 %collective-permute-start.2 = (f32[3,256]{1,0:T(4,128)S(1)}, f32[3,256]{1,0:T(4,128)S(1)}, u32[]{:S(2)}, u32[]{:S(2)}) collective-permute-start(f32[3,256]{1,0:T(4,128)S(1)} %get-tuple-element.23), channel_id=1, source_target_pairs={{0,1},{1,2},{2,3},{3,4},{4,5},{5,6},{6,7},{7,8},{8,9},{9,10},{10,1... | collective-permute-start | bytes 9224 | tf_op jit(solution)/shard_map/ppermute | solution.py:425
  50.5 4.1 %collective-permute-start.3 = (f32[3,256]{1,0:T(4,128)S(1)}, f32[3,256]{1,0:T(4,128)S(1)}, u32[]{:S(2)}, u32[]{:S(2)}) collective-permute-start(f32[3,256]{1,0:T(4,128)S(1)} %get-tuple-element.24), channel_id=1, source_target_pairs={{1,0},{2,1},{3,2},{4,3},{5,4},{6,5},{7,6},{8,7},{9,8},{10,9},{11,1... | collective-permute-start | bytes 9224 | tf_op jit(solution)/shard_map/ppermute | solution.py:425
  66.7 1.3 collective-permute-start.4
  67.9 3.7 %collective-permute-start.5 = (f32[32,128]{1,0:T(8,128)S(1)}, f32[32,128]{1,0:T(8,128)S(1)}, u32[]{:S(2)}, u32[]{:S(2)}) collective-permute-start(f32[32,128]{1,0:T(8,128)S(1)} %pad_maximum_fusion.5), channel_id=1, source_target_pairs={{0,2},{2,0},{1,3},{3,1},{4,6},{6,4},{5,7},{7,5},{8,10},{10,8},{9,1... | collective-permute-start | bytes 49160 | tf_op jit(solution)/shard_map/ppermute | solution.py:415
  71.6 3.9 %collective-permute-start.6 = (f32[64,128]{1,0:T(8,128)S(1)}, f32[64,128]{1,0:T(8,128)S(1)}, u32[]{:S(2)}, u32[]{:S(2)}) collective-permute-start(f32[64,128]{1,0:T(8,128)S(1)} %pad_maximum_fusion), channel_id=1, source_target_pairs={{0,8},{8,0},{1,9},{9,1},{2,10},{10,2},{3,11},{11,3},{4,12},{12,4},... | collective-permute-start | bytes 98312 | tf_op jit(solution)/shard_map/ppermute | solution.py:417
  78.3 1.2 collective-permute-start.7
  79.5 3.7 %collective-permute-start.8 = (f32[32,128]{1,0:T(8,128)S(1)}, f32[32,128]{1,0:T(8,128)S(1)}, u32[]{:S(2)}, u32[]{:S(2)}) collective-permute-start(f32[32,128]{1,0:T(8,128)S(1)} %pad_maximum_fusion.6), channel_id=1, source_target_pairs={{0,2},{2,0},{1,3},{3,1},{4,6},{6,4},{5,7},{7,5},{8,10},{10,8},{9,1... | collective-permute-start | bytes 49160 | tf_op jit(solution)/shard_map/ppermute | solution.py:415
  83.2 3.9 %collective-permute-start.9 = (f32[64,128]{1,0:T(8,128)S(1)}, f32[64,128]{1,0:T(8,128)S(1)}, u32[]{:S(2)}, u32[]{:S(2)}) collective-permute-start(f32[64,128]{1,0:T(8,128)S(1)} %pad_maximum_fusion.1), channel_id=1, source_target_pairs={{0,8},{8,0},{1,9},{9,1},{2,10},{10,2},{3,11},{11,3},{4,12},{12,4},... | collective-permute-start | bytes 98312 | tf_op jit(solution)/shard_map/ppermute | solution.py:417
  89.9 1.2 collective-permute-start.10
  91.0 3.7 %collective-permute-start.11 = (f32[32,128]{1,0:T(8,128)S(1)}, f32[32,128]{1,0:T(8,128)S(1)}, u32[]{:S(2)}, u32[]{:S(2)}) collective-permute-start(f32[32,128]{1,0:T(8,128)S(1)} %pad_maximum_fusion.7), channel_id=1, source_target_pairs={{0,2},{2,0},{1,3},{3,1},{4,6},{6,4},{5,7},{7,5},{8,10},{10,8},{9,1... | collective-permute-start | bytes 49160 | tf_op jit(solution)/shard_map/ppermute | solution.py:415
  94.8 3.9 %collective-permute-start.12 = (f32[64,128]{1,0:T(8,128)S(1)}, f32[64,128]{1,0:T(8,128)S(1)}, u32[]{:S(2)}, u32[]{:S(2)}) collective-permute-start(f32[64,128]{1,0:T(8,128)S(1)} %pad_maximum_fusion.2), channel_id=1, source_target_pairs={{0,8},{8,0},{1,9},{9,1},{2,10},{10,2},{3,11},{11,3},{4,12},{12,4},... | collective-permute-start | bytes 98312 | tf_op jit(solution)/shard_map/ppermute | solution.py:417
  101.4 1.2 collective-permute-start.13
  102.6 3.7 %collective-permute-start.14 = (f32[32,128]{1,0:T(8,128)S(1)}, f32[32,128]{1,0:T(8,128)S(1)}, u32[]{:S(2)}, u32[]{:S(2)}) collective-permute-start(f32[32,128]{1,0:T(8,128)S(1)} %pad_maximum_fusion.8), channel_id=1, source_target_pairs={{0,2},{2,0},{1,3},{3,1},{4,6},{6,4},{5,7},{7,5},{8,10},{10,8},{9,1... | collective-permute-start | bytes 49160 | tf_op jit(solution)/shard_map/ppermute | solution.py:415
  106.3 3.9 %collective-permute-start.15 = (f32[64,128]{1,0:T(8,128)S(1)}, f32[64,128]{1,0:T(8,128)S(1)}, u32[]{:S(2)}, u32[]{:S(2)}) collective-permute-start(f32[64,128]{1,0:T(8,128)S(1)} %pad_maximum_fusion.3), channel_id=1, source_target_pairs={{0,8},{8,0},{1,9},{9,1},{2,10},{10,2},{3,11},{11,3},{4,12},{12,4},... | collective-permute-start | bytes 98312 | tf_op jit(solution)/shard_map/ppermute | solution.py:417
  113.0 1.2 collective-permute-start.16
  114.2 3.7 %collective-permute-start.17 = (f32[32,128]{1,0:T(8,128)S(1)}, f32[32,128]{1,0:T(8,128)S(1)}, u32[]{:S(2)}, u32[]{:S(2)}) collective-permute-start(f32[32,128]{1,0:T(8,128)S(1)} %pad_maximum_fusion.9), channel_id=1, source_target_pairs={{0,2},{2,0},{1,3},{3,1},{4,6},{6,4},{5,7},{7,5},{8,10},{10,8},{9,1... | collective-permute-start | bytes 49160 | tf_op jit(solution)/shard_map/ppermute | solution.py:415
  117.9 3.9 %collective-permute-start.18 = (f32[64,128]{1,0:T(8,128)S(1)}, f32[64,128]{1,0:T(8,128)S(1)}, u32[]{:S(2)}, u32[]{:S(2)}) collective-permute-start(f32[64,128]{1,0:T(8,128)S(1)} %pad_maximum_fusion.4), channel_id=1, source_target_pairs={{0,8},{8,0},{1,9},{9,1},{2,10},{10,2},{3,11},{11,3},{4,12},{12,4},... | collective-permute-start | bytes 98312 | tf_op jit(solution)/shard_map/ppermute | solution.py:417

commit v4 on v3

--- a/solution.py
+++ b/solution.py
@@ -6,11 +6,11 @@
 from jax.sharding import Mesh
 from jax.sharding import PartitionSpec as P
 
+
 DOM = ("dom_0", "dom_1", "dom_2", "dom_3", "dom_4", "dom_5")
 OTHERS = ("dom_0", "dom_1", "dom_3")
 PEERS = 16
 UNROLL = 8
-SWEEPS = 2
 CSWEEPS = 6
 damping = 0.7
 highest = lax.Precision.HIGHEST
@@ -45,20 +45,28 @@
     )
 
 
-def pack_kernel(rhs, dia, col, blk, agg, owner_row, up, down, node_row):
-    table = jnp.concatenate([owner_row[...]] * 4, axis=1)
+def pack_kernel(rhs_in, dia_in, col_in, blk_in, agg_in, owner_in, up, down, node_row,
+                rhs, dia, col, blk, agg, owner, sem):
+    copies = [(rhs_in, rhs), (dia_in, dia), (agg_in, agg), (owner_in, owner)]
+    for t, near in enumerate((ROWS - HALO, 0)):
+        copies.append((col_in.at[:, lanes(near, HALO)], col.at[t]))
+        copies.append((blk_in.at[:, :, :, lanes(near, HALO)], blk.at[t]))
+    copies = [pltpu.make_async_copy(a, b, sem.at[n]) for n, (a, b) in enumerate(copies)]
+    for c in copies:
+        c.start()
+    for c in copies:
+        c.wait()
+    table = jnp.concatenate([owner[...]] * 4, axis=1)
     found = picked(table, agg[...]).astype(f32)
     node_row[...] = found
-    for out, near, wide in ((up, ROWS - HALO, ROWS - WIDE), (down, 0, 0)):
+    for t, (out, wide) in enumerate(((up, ROWS - WIDE), (down, 0))):
         for i in range(3):
             for j in range(3):
                 g = 3 * i + j
-                out[g * FULL : (g + 1) * FULL, :] = blk[i, j, 0:FULL, lanes(near, HALO)]
-                out[P_BTAIL + 3 * g : P_BTAIL + 3 * g + 3, :] = blk[
-                    i, j, FULL:SLOTS, lanes(near, HALO)
-                ]
-        out[P_COL : P_COL + FULL, :] = col[0:FULL, lanes(near, HALO)].astype(f32)
-        out[P_CTAIL : P_CTAIL + 3, :] = col[FULL:SLOTS, lanes(near, HALO)].astype(f32)
+                out[g * FULL : (g + 1) * FULL, :] = blk[t, i, j, 0:FULL, :]
+                out[P_BTAIL + 3 * g : P_BTAIL + 3 * g + 3, :] = blk[t, i, j, FULL:SLOTS, :]
+        out[P_COL : P_COL + FULL, :] = col[t, 0:FULL, :].astype(f32)
+        out[P_CTAIL : P_CTAIL + 3, :] = col[t, FULL:SLOTS, :].astype(f32)
         for h in range(2):
             out[P_RHS + 3 * h : P_RHS + 3 * h + 3, :] = rhs[:, lanes(wide + HALO * h, HALO)]
             out[P_DIA + 3 * h : P_DIA + 3 * h + 3, :] = dia[:, lanes(wide + HALO * h, HALO)]
@@ -390,14 +398,13 @@
     lax.fori_loop(0, BLOCKS, second, 0)
 
 
-def call(kernel, name, outs, args, scratch=(), scalar=False):
+def call(kernel, outs, args, scratch=(), scalar=False):
     vmem = pl.BlockSpec(memory_space=pltpu.VMEM)
     specs = [vmem] * len(args)
     if scalar:
         specs[0] = pl.BlockSpec(memory_space=pltpu.SMEM)
     return pl.pallas_call(
         kernel,
-        name=name,
         in_specs=specs,
         out_specs=[vmem] * len(outs),
         out_shape=[jax.ShapeDtypeStruct(o, t) for o, t in outs],
@@ -425,7 +432,7 @@
     return lax.ppermute(up, DOM, forward), lax.ppermute(down, DOM, backward)
 
 
-def body(right_side, fine_diagonal, fine_columns, fine_blocks, aggregate_of_node,
+def cycle(right_side, fine_diagonal, fine_columns, fine_blocks, aggregate_of_node,
          coarse_row_of_aggregate, coarse_diagonal, coarse_columns, coarse_blocks):
     rhs, dia = right_side.T, fine_diagonal.T
     col, blk = fine_columns.T, fine_blocks.transpose(2, 3, 1, 0)
@@ -436,18 +443,25 @@
     base = me * ROWS
     wide = WIDE + ROWS + WIDE
 
-    dsend, = call(
-        coarse_pack_kernel, "coarse_pack", [((PEERS, 80, LANES), f32)], [coarse_columns, cblk]
-    )
+    dsend, = call(coarse_pack_kernel, [((PEERS, 80, LANES), f32)], [coarse_columns, cblk])
     data = lax.all_to_all(dsend, OTHERS, 0, 0, tiled=True)
-    up, down, node_row = call(
-        pack_kernel, "pack",
-        [((P_ALL, HALO), f32), ((P_ALL, HALO), f32), ((8, LANES), f32)],
-        [rhs, dia, col, blk, agg, owner],
-    )
+    vmem, far = pl.BlockSpec(memory_space=pltpu.VMEM), pl.BlockSpec(memory_space=pltpu.HBM)
+    up, down, node_row = pl.pallas_call(
+        pack_kernel,
+        name="pack",
+        in_specs=[far] * 6,
+        out_specs=[vmem] * 3,
+        out_shape=[jax.ShapeDtypeStruct(o, f32) for o in ((P_ALL, HALO), (P_ALL, HALO), (8, LANES))],
+        scratch_shapes=[
+            pltpu.VMEM((3, ROWS), f32), pltpu.VMEM((3, ROWS), f32),
+            pltpu.VMEM((2, SLOTS, HALO), i32), pltpu.VMEM((2, 3, 3, SLOTS, HALO), f32),
+            pltpu.VMEM((8, LANES), i32), pltpu.VMEM((1, 32), i32), pltpu.SemaphoreType.DMA((8,)),
+        ],
+        compiler_params=pltpu.CompilerParams(vmem_limit_bytes=12 * 2**20),
+    )(rhs, dia, col, blk, agg, owner)
     before, after = shifts(up, down)
     send, first_iter, wrhs, wdia, up2, down2 = call(
-        pre_kernel, "pre",
+        pre_kernel,
         [((LANES, 2, LANES), f32), ((3, wide), f32), ((3, wide), f32), ((3, wide), f32),
          ((3, HALO), f32), ((3, HALO), f32)],
         [base, rhs, dia, col, blk, agg, owner, cdia, before, after],
@@ -459,20 +473,20 @@
     gather = (3, PEERS, LANES)
     square = (LANES, LANES)
     new, crhs, cd, where = call(
-        coarse_first_kernel, "coarse_first",
+        coarse_first_kernel,
         [peers, peers, peers, ((PEERS, 8, LANES), i32)],
         [me, sums, data, before2, after2],
         scratch=[square, gather, ((288, 4096), jnp.bfloat16), ((LANES, 4096), jnp.bfloat16)],
         scalar=True,
     )
-    for sweep in range(CSWEEPS - 2):
+    for _ in range(CSWEEPS - 2):
         new, mine = call(
-            coarse_kernel, "coarse", [peers, ((3, 32), f32)],
+            coarse_kernel, [peers, ((3, 32), f32)],
             [me, *in_group(new), crhs, cd, where, data],
             scratch=[square, square, gather], scalar=True,
         )
     solution, = call(
-        post_kernel, "post", [((3, ROWS), f32)],
+        post_kernel, [((3, ROWS), f32)],
         [base, *in_group(new), first_iter, wrhs, wdia, col, blk, node_row,
          before, after, before2, after2],
         scratch=[square, square, (3, wide), (3, wide)], scalar=True,
@@ -483,7 +497,7 @@
 def solution(mesh):
     torus = Mesh(mesh.devices.reshape(4, 2, 2, 2, 2, 2), DOM)
     return jax.shard_map(
-        body,
+        cycle,
         mesh=torus,
         in_specs=(
             P(DOM, None),

time: 127 us -> 126 us (level)
  starting transfers between devices: 34.2 us -> 32.8 us
where the time goes in v4:
time: 126 us; the launch traced here: 125 us
  waiting for transfers between devices  62 us (49%)
  starting transfers between devices  32.8 us (26%)
  Pallas kernels  24.7 us (20%)
  local copies, waits for them, and re-layouts  5 us (4%)
    pallas_call x8, Pallas kernels, call(): pl.pallas_call(kernel, in_specs=specs, out_specs=[vmem] * len(outs), out_...  24.3 us
    ppermute x5, waiting for transfers between devices, in_group(): p3 = lax.ppermute(b, 'dom_2', swap)  18.4 us
    all_to_all x1, starting transfers between devices, cycle(): sums = lax.all_to_all(send, DOM, 0, 0, tiled=True)  18 us
    ppermute x5, waiting for transfers between devices, in_group(): p2 = lax.ppermute(a, 'dom_4', swap)  14.9 us
    all_to_all x1, waiting for transfers between devices, cycle(): sums = lax.all_to_all(send, DOM, 0, 0, tiled=True)  8.33 us
    all_to_all x1, waiting for transfers between devices, cycle(): data = lax.all_to_all(dsend, OTHERS, 0, 0, tiled=True)  7.85 us
    ppermute x4, waiting for transfers between devices, shifts(): return (lax.ppermute(up, DOM, forward), lax.ppermute(down, DOM, backward))  6.67 us
    ppermute x5, waiting for transfers between devices, in_group(): p1 = lax.ppermute(new, 'dom_5', swap)  5.84 us
  transfers between devices with their start and end apart: 21, of which 19 were waited for; matrix products, arithmetic and copies ran while one was open for 0% of the time, Pallas kernels for 1%

profile of v4, /device:TPU:0, one launch (start us, length us, event | category | flops | bytes accessed | tf_op | source)
XLA Modules:
  0.0 125.4 jit_solution(9260079852376374155)
XLA Ops:
  0.7 1.3 %copy-done = f32[1024,27,3,3]{0,1,3,2:T(8,128)S(1)} copy-done((f32[1024,27,3,3]{0,1,3,2:T(8,128)S(1)}, f32[1024,27,3,3]{0,1,3,2:T(8,128)}, u32[]{:S(2)}) %copy-start) | copy-done | bytes 995352
  2.0 0.9 copy-done.2
  2.9 0.7 copy-done.5
  3.6 0.7 copy-done.7
  4.3 0.7 copy-done.9
  5.0 0.7 copy-done.13
  5.6 0.4 pack.1
  6.1 1.4 %collective-permute-start = (f32[288,256]{1,0:T(8,128)S(1)}, f32[288,256]{1,0:T(8,128)S(1)}, u32[]{:S(2)}, u32[]{:S(2)}) collective-permute-start(f32[288,256]{1,0:T(8,128)S(1)} %get-tuple-element.20), channel_id=1, source_target_pairs={{0,1},{1,2},{2,3},{3,4},{4,5},{5,6},{6,7},{7,8},{8,9},{9,10},{10,1... | collective-permute-start | bytes 884744 | tf_op jit(solution)/shard_map/ppermute | solution.py:432
  7.5 1.3 %collective-permute-start.1 = (f32[288,256]{1,0:T(8,128)S(1)}, f32[288,256]{1,0:T(8,128)S(1)}, u32[]{:S(2)}, u32[]{:S(2)}) collective-permute-start(f32[288,256]{1,0:T(8,128)S(1)} %get-tuple-element.21), channel_id=1, source_target_pairs={{1,0},{2,1},{3,2},{4,3},{5,4},{6,5},{7,6},{8,7},{9,8},{10,9},{11,1... | collective-permute-start | bytes 884744 | tf_op jit(solution)/shard_map/ppermute | solution.py:432
  8.8 4.0 %collective-permute-done.1.after = f32[288,256]{1,0:T(8,128)S(1)} collective-permute-done((f32[288,256]{1,0:T(8,128)S(1)}, f32[288,256]{1,0:T(8,128)S(1)}, u32[]{:S(2)}, u32[]{:S(2)}) %collective-permute-start.1) | collective-permute-done | bytes 294944 | tf_op jit(solution)/shard_map/ppermute | solution.py:432
  12.9 4.5 %shard_map.104 = (f32[128,2,128]{2,1,0:T(2,128)}, f32[3,2048]{1,0:T(4,128)S(1)}, f32[3,2048]{1,0:T(4,128)S(1)}, f32[3,2048]{1,0:T(4,128)S(1)}, f32[3,256]{1,0:T(4,128)S(1)}, /*index=5*/f32[3,256]{1,0:T(4,128)S(1)}) custom-call(s32[1]{0:T(128)S(6)} %mul.23.base_ref, f32[3,1024]{1,0:T(4,128)S(1)} %bitcast.19, f32[3,1024]{1,0:T(4,128)S(1)} %bitcast.21, ...), custom_call_target="tpu_custom_call" | custom-call | tf_op jit(solution)/shard_map/pallas_call | solution.py:406
  17.3 18.0 %all-to-all-start = ((f32[128,2,128]{2,1,0:T(2,128)}), f32[128,2,128]{2,1,0:T(2,128)S(1)}, u32[]{:S(2)}, u32[]{:S(2)}) async-start(f32[128,2,128]{2,1,0:T(2,128)} %get-tuple-element.22), calls=%async_computation | async-start | bytes 262144 | tf_op jit(solution)/shard_map/all_to_all | solution.py:471
  35.4 1.0 shard_map.105
  36.4 8.3 %all-to-all-done.sums = f32[128,2,128]{2,1,0:T(2,128)S(1)} async-done(((f32[128,2,128]{2,1,0:T(2,128)}), f32[128,2,128]{2,1,0:T(2,128)S(1)}, u32[]{:S(2)}, u32[]{:S(2)}) %all-to-all-start) | async-done | bytes 131104 | tf_op jit(solution)/shard_map/all_to_all | solution.py:471
  44.7 4.2 %all-to-all-start.1 = ((f32[16,80,128]{2,1,0:T(8,128)}), f32[16,80,128]{2,1,0:T(8,128)S(1)}, u32[]{:S(2)}, u32[]{:S(2)}) async-start(f32[16,80,128]{2,1,0:T(8,128)} %shard_map.105), calls=%async_computation.1 | async-start | bytes 1310720 | tf_op jit(solution)/shard_map/all_to_all | solution.py:447
  49.0 1.5 %collective-permute-start.2 = (f32[3,256]{1,0:T(4,128)S(1)}, f32[3,256]{1,0:T(4,128)S(1)}, u32[]{:S(2)}, u32[]{:S(2)}) collective-permute-start(f32[3,256]{1,0:T(4,128)S(1)} %get-tuple-element.23), channel_id=1, source_target_pairs={{0,1},{1,2},{2,3},{3,4},{4,5},{5,6},{6,7},{7,8},{8,9},{9,10},{10,1... | collective-permute-start | bytes 9224 | tf_op jit(solution)/shard_map/ppermute | solution.py:432
  50.5 1.3 %collective-permute-start.3 = (f32[3,256]{1,0:T(4,128)S(1)}, f32[3,256]{1,0:T(4,128)S(1)}, u32[]{:S(2)}, u32[]{:S(2)}) collective-permute-start(f32[3,256]{1,0:T(4,128)S(1)} %get-tuple-element.24), channel_id=1, source_target_pairs={{1,0},{2,1},{3,2},{4,3},{5,4},{6,5},{7,6},{8,7},{9,8},{10,9},{11,1... | collective-permute-start | bytes 9224 | tf_op jit(solution)/shard_map/ppermute | solution.py:432
  51.8 2.7 %collective-permute-done.3.far_down.after2 = f32[3,256]{1,0:T(4,128)S(1)} collective-permute-done((f32[3,256]{1,0:T(4,128)S(1)}, f32[3,256]{1,0:T(4,128)S(1)}, u32[]{:S(2)}, u32[]{:S(2)}) %collective-permute-start.3) | collective-permute-done | bytes 3104 | tf_op jit(solution)/shard_map/ppermute | solution.py:432
  54.5 7.8 %all-to-all-done.1.data = f32[16,80,128]{2,1,0:T(8,128)S(1)} async-done(((f32[16,80,128]{2,1,0:T(8,128)}), f32[16,80,128]{2,1,0:T(8,128)S(1)}, u32[]{:S(2)}, u32[]{:S(2)}) %all-to-all-start.1) | async-done | bytes 655392 | tf_op jit(solution)/shard_map/all_to_all | solution.py:447
  62.3 3.5 %shard_map.106 = (f32[16,128]{1,0:T(8,128)S(1)}, f32[16,128]{1,0:T(8,128)S(1)}, f32[16,128]{1,0:T(8,128)S(1)}, s32[16,8,128]{2,1,0:T(8,128)S(1)}) custom-call(s32[1]{0:T(128)} %bitcast.me_ref, f32[128,2,128]{2,1,0:T(2,128)S(1)} %all-to-all-done.sums, f32[16,80,128]{2,1,0:T(8,128)S(1)} %all-to-all-done.1.data, ...), custom_call_target="tpu_custom_call" | custom-call | tf_op jit(solution)/shard_map/pallas_call | solution.py:406
  66.0 1.2 collective-permute-done.4.p1
  67.1 0.8 collective-permute-start.5
  67.9 3.0 %collective-permute-done.5.p2 = f32[32,128]{1,0:T(8,128)S(1)} collective-permute-done((f32[32,128]{1,0:T(8,128)S(1)}, f32[32,128]{1,0:T(8,128)S(1)}, u32[]{:S(2)}, u32[]{:S(2)}) %collective-permute-start.5) | collective-permute-done | bytes 16416 | tf_op jit(solution)/shard_map/ppermute | solution.py:422
  70.9 0.2 collective-permute-start.6
  71.1 3.7 %collective-permute-done.6.p3 = f32[64,128]{1,0:T(8,128)S(1)} collective-permute-done((f32[64,128]{1,0:T(8,128)S(1)}, f32[64,128]{1,0:T(8,128)S(1)}, u32[]{:S(2)}, u32[]{:S(2)}) %collective-permute-start.6) | collective-permute-done | bytes 32800 | tf_op jit(solution)/shard_map/ppermute | solution.py:424
  74.8 2.7 %shard_map.107 = (f32[16,128]{1,0:T(8,128)S(1)}, f32[3,32]{1,0:T(4,128)}) custom-call(s32[1]{0:T(128)} %bitcast.me_ref, f32[16,128]{1,0:T(8,128)S(1)} %get-tuple-element.25.p0, f32[16,128]{1,0:T(8,128)S(1)} %collective-permute-done.4.p1, f32[32,128]{1,0:T(8,128)S(1)} %collective-permute-done.5.p2, f32[64,128]{1,0:T(8,128)S(1)} %collective-permute-done.6.p3, ...), custom_call_target="tpu_custom_call" | custom-call | tf_op jit(solution)/shard_map/pallas_call | solution.py:406
  77.5 1.2 collective-permute-done.7.p1
  78.7 0.8 collective-permute-start.8
  79.5 3.0 %collective-permute-done.8.p2 = f32[32,128]{1,0:T(8,128)S(1)} collective-permute-done((f32[32,128]{1,0:T(8,128)S(1)}, f32[32,128]{1,0:T(8,128)S(1)}, u32[]{:S(2)}, u32[]{:S(2)}) %collective-permute-start.8) | collective-permute-done | bytes 16416 | tf_op jit(solution)/shard_map/ppermute | solution.py:422
  82.4 0.2 collective-permute-start.9
  82.7 3.7 %collective-permute-done.9.p3 = f32[64,128]{1,0:T(8,128)S(1)} collective-permute-done((f32[64,128]{1,0:T(8,128)S(1)}, f32[64,128]{1,0:T(8,128)S(1)}, u32[]{:S(2)}, u32[]{:S(2)}) %collective-permute-start.9) | collective-permute-done | bytes 32800 | tf_op jit(solution)/shard_map/ppermute | solution.py:424
  86.4 2.7 %shard_map.108 = (f32[16,128]{1,0:T(8,128)S(1)}, f32[3,32]{1,0:T(4,128)}) custom-call(s32[1]{0:T(128)} %bitcast.me_ref, f32[16,128]{1,0:T(8,128)S(1)} %get-tuple-element.29.p0, f32[16,128]{1,0:T(8,128)S(1)} %collective-permute-done.7.p1, f32[32,128]{1,0:T(8,128)S(1)} %collective-permute-done.8.p2, f32[64,128]{1,0:T(8,128)S(1)} %collective-permute-done.9.p3, ...), custom_call_target="tpu_custom_call" | custom-call | tf_op jit(solution)/shard_map/pallas_call | solution.py:406
  89.1 1.2 collective-permute-done.10.p1
  90.3 0.8 collective-permute-start.11
  91.0 3.0 %collective-permute-done.11.p2 = f32[32,128]{1,0:T(8,128)S(1)} collective-permute-done((f32[32,128]{1,0:T(8,128)S(1)}, f32[32,128]{1,0:T(8,128)S(1)}, u32[]{:S(2)}, u32[]{:S(2)}) %collective-permute-start.11) | collective-permute-done | bytes 16416 | tf_op jit(solution)/shard_map/ppermute | solution.py:422
  94.0 0.2 collective-permute-start.12
  94.2 3.7 %collective-permute-done.12.p3 = f32[64,128]{1,0:T(8,128)S(1)} collective-permute-done((f32[64,128]{1,0:T(8,128)S(1)}, f32[64,128]{1,0:T(8,128)S(1)}, u32[]{:S(2)}, u32[]{:S(2)}) %collective-permute-start.12) | collective-permute-done | bytes 32800 | tf_op jit(solution)/shard_map/ppermute | solution.py:424
  97.9 2.7 %shard_map.109 = (f32[16,128]{1,0:T(8,128)S(1)}, f32[3,32]{1,0:T(4,128)}) custom-call(s32[1]{0:T(128)} %bitcast.me_ref, f32[16,128]{1,0:T(8,128)S(1)} %get-tuple-element.30.p0, f32[16,128]{1,0:T(8,128)S(1)} %collective-permute-done.10.p1, f32[32,128]{1,0:T(8,128)S(1)} %collective-permute-done.11.p2, f32[64,128]{1,0:T(8,128)S(1)} %collective-permute-done.12.p3, ...), custom_call_target="tpu_custom_call" | custom-call | tf_op jit(solution)/shard_map/pallas_call | solution.py:406
  100.7 1.2 collective-permute-done.13.p1
  101.8 0.8 collective-permute-start.14
  102.6 3.0 %collective-permute-done.14.p2 = f32[32,128]{1,0:T(8,128)S(1)} collective-permute-done((f32[32,128]{1,0:T(8,128)S(1)}, f32[32,128]{1,0:T(8,128)S(1)}, u32[]{:S(2)}, u32[]{:S(2)}) %collective-permute-start.14) | collective-permute-done | bytes 16416 | tf_op jit(solution)/shard_map/ppermute | solution.py:422
  105.8 3.7 %collective-permute-done.15.p3 = f32[64,128]{1,0:T(8,128)S(1)} collective-permute-done((f32[64,128]{1,0:T(8,128)S(1)}, f32[64,128]{1,0:T(8,128)S(1)}, u32[]{:S(2)}, u32[]{:S(2)}) %collective-permute-start.15) | collective-permute-done | bytes 32800 | tf_op jit(solution)/shard_map/ppermute | solution.py:424
  109.5 2.7 %shard_map.110 = (f32[16,128]{1,0:T(8,128)S(1)}, f32[3,32]{1,0:T(4,128)}) custom-call(s32[1]{0:T(128)} %bitcast.me_ref, f32[16,128]{1,0:T(8,128)S(1)} %get-tuple-element.31.p0, f32[16,128]{1,0:T(8,128)S(1)} %collective-permute-done.13.p1, f32[32,128]{1,0:T(8,128)S(1)} %collective-permute-done.14.p2, f32[64,128]{1,0:T(8,128)S(1)} %collective-permute-done.15.p3, ...), custom_call_target="tpu_custom_call" | custom-call | tf_op jit(solution)/shard_map/pallas_call | solution.py:406
  112.2 1.2 collective-permute-done.16.p1
  113.4 0.8 collective-permute-start.17
  114.2 3.0 %collective-permute-done.17.p2 = f32[32,128]{1,0:T(8,128)S(1)} collective-permute-done((f32[32,128]{1,0:T(8,128)S(1)}, f32[32,128]{1,0:T(8,128)S(1)}, u32[]{:S(2)}, u32[]{:S(2)}) %collective-permute-start.17) | collective-permute-done | bytes 16416 | tf_op jit(solution)/shard_map/ppermute | solution.py:422
  117.4 3.7 %collective-permute-done.18.p3 = f32[64,128]{1,0:T(8,128)S(1)} collective-permute-done((f32[64,128]{1,0:T(8,128)S(1)}, f32[64,128]{1,0:T(8,128)S(1)}, u32[]{:S(2)}, u32[]{:S(2)}) %collective-permute-start.18) | collective-permute-done | bytes 32800 | tf_op jit(solution)/shard_map/ppermute | solution.py:424
  121.1 4.3 %shard_map.111 = f32[3,1024]{1,0:T(4,128)} custom-call(s32[1]{0:T(128)S(6)} %mul.23.base_ref, f32[16,128]{1,0:T(8,128)S(1)} %get-tuple-element.32.p0, f32[16,128]{1,0:T(8,128)S(1)} %collective-permute-done.16.p1, f32[32,128]{1,0:T(8,128)S(1)} %collective-permute-done.17.p2, f32[64,128]{1,0:T(8,128)S(1)} %collective-permute-done.18.p3, ...), custom_call_target="tpu_custom_call" | custom-call | tf_op jit(solution)/shard_map/pallas_call | solution.py:406
  (43 shorter events, 0.6 us)
Async XLA Ops:
  0.6 12.2 %copy-start.14 = (s32[32]{0:T(128)S(1)}, s32[32]{0:T(128)}, u32[]{:S(2)}) copy-start(s32[32]{0:T(128)} %param.14) | copy-start | bytes 388
  0.6 12.2 %copy-start.10 = (s32[1024]{0:T(1024)S(1)}, s32[1024]{0:T(1024)}, u32[]{:S(2)}) copy-start(s32[1024]{0:T(1024)} %param.13) | copy-start | bytes 12292
  0.7 12.2 %copy-start.12 = (f32[32,3]{0,1:T(4,128)S(1)}, f32[32,3]{0,1:T(4,128)}, u32[]{:S(2)}) copy-start(f32[32,3]{0,1:T(4,128)} %param.15) | copy-start | bytes 1156
  0.7 1.3 %copy-start = (f32[1024,27,3,3]{0,1,3,2:T(8,128)S(1)}, f32[1024,27,3,3]{0,1,3,2:T(8,128)}, u32[]{:S(2)}) copy-start(f32[1024,27,3,3]{0,1,3,2:T(8,128)} %param.12) | copy-start | bytes 2985988
  2.0 0.9 copy-start.2
  2.9 0.7 copy-start.5
  3.6 0.7 copy-start.7
  4.3 0.7 copy-start.9
  5.0 0.7 copy-start.13
  5.6 7.2 %copy-start.1 = (f32[1024,27,3,3]{0,1,3,2:T(8,128)S(1)}, f32[1024,27,3,3]{0,1,3,2:T(8,128)}, u32[]{:S(2)}) copy-start(f32[1024,27,3,3]{0,1,3,2:T(8,128)} %param.12) | copy-start | bytes 2985988
  5.6 7.2 %copy-start.3 = (s32[1024,27]{0,1:T(8,128)S(1)}, s32[1024,27]{0,1:T(8,128)}, u32[]{:S(2)}) copy-start(s32[1024,27]{0,1:T(8,128)} %param.11) | copy-start | bytes 331780
  5.6 7.2 %copy-start.6 = (f32[1024,3]{0,1:T(4,128)S(1)}, f32[1024,3]{0,1:T(4,128)}, u32[]{:S(2)}) copy-start(f32[1024,3]{0,1:T(4,128)} %param.9) | copy-start | bytes 36868
  5.6 7.2 %copy-start.8 = (f32[1024,3]{0,1:T(4,128)S(1)}, f32[1024,3]{0,1:T(4,128)}, u32[]{:S(2)}) copy-start(f32[1024,3]{0,1:T(4,128)} %param.10) | copy-start | bytes 36868
  6.0 29.3 %copy-start.4 = (f32[32,27,3,3]{1,0,3,2:T(8,128)S(1)}, f32[32,27,3,3]{1,0,3,2:T(8,128)}, u32[]{:S(2)}) copy-start(f32[32,27,3,3]{1,0,3,2:T(8,128)} %param.17) | copy-start | bytes 93316
  6.1 29.3 %copy-start.11 = (s32[32,27]{1,0:T(8,128)S(1)}, s32[32,27]{1,0:T(8,128)}, u32[]{:S(2)}) copy-start(s32[32,27]{1,0:T(8,128)} %col.1) | copy-start | bytes 10372
  6.1 2.8 %collective-permute-start = (f32[288,256]{1,0:T(8,128)S(1)}, f32[288,256]{1,0:T(8,128)S(1)}, u32[]{:S(2)}, u32[]{:S(2)}) collective-permute-start(f32[288,256]{1,0:T(8,128)S(1)} %get-tuple-element.20), channel_id=1, source_target_pairs={{0,1},{1,2},{2,3},{3,4},{4,5},{5,6},{6,7},{7,8},{8,9},{9,10},{10,1... | collective-permute-start | bytes 884744 | tf_op jit(solution)/shard_map/ppermute | solution.py:432
  7.5 5.3 %collective-permute-start.1 = (f32[288,256]{1,0:T(8,128)S(1)}, f32[288,256]{1,0:T(8,128)S(1)}, u32[]{:S(2)}, u32[]{:S(2)}) collective-permute-start(f32[288,256]{1,0:T(8,128)S(1)} %get-tuple-element.21), channel_id=1, source_target_pairs={{1,0},{2,1},{3,2},{4,3},{5,4},{6,5},{7,6},{8,7},{9,8},{10,9},{11,1... | collective-permute-start | bytes 884744 | tf_op jit(solution)/shard_map/ppermute | solution.py:432
  17.3 27.4 %all-to-all-start = ((f32[128,2,128]{2,1,0:T(2,128)}), f32[128,2,128]{2,1,0:T(2,128)S(1)}, u32[]{:S(2)}, u32[]{:S(2)}) async-start(f32[128,2,128]{2,1,0:T(2,128)} %get-tuple-element.22), calls=%async_computation | async-start | bytes 262144 | tf_op jit(solution)/shard_map/all_to_all | solution.py:471
  44.7 17.6 %all-to-all-start.1 = ((f32[16,80,128]{2,1,0:T(8,128)}), f32[16,80,128]{2,1,0:T(8,128)S(1)}, u32[]{:S(2)}, u32[]{:S(2)}) async-start(f32[16,80,128]{2,1,0:T(8,128)} %shard_map.105), calls=%async_computation.1 | async-start | bytes 1310720 | tf_op jit(solution)/shard_map/all_to_all | solution.py:447
  49.0 2.8 %collective-permute-start.2 = (f32[3,256]{1,0:T(4,128)S(1)}, f32[3,256]{1,0:T(4,128)S(1)}, u32[]{:S(2)}, u32[]{:S(2)}) collective-permute-start(f32[3,256]{1,0:T(4,128)S(1)} %get-tuple-element.23), channel_id=1, source_target_pairs={{0,1},{1,2},{2,3},{3,4},{4,5},{5,6},{6,7},{7,8},{8,9},{9,10},{10,1... | collective-permute-start | bytes 9224 | tf_op jit(solution)/shard_map/ppermute | solution.py:432
  50.5 4.0 %collective-permute-start.3 = (f32[3,256]{1,0:T(4,128)S(1)}, f32[3,256]{1,0:T(4,128)S(1)}, u32[]{:S(2)}, u32[]{:S(2)}) collective-permute-start(f32[3,256]{1,0:T(4,128)S(1)} %get-tuple-element.24), channel_id=1, source_target_pairs={{1,0},{2,1},{3,2},{4,3},{5,4},{6,5},{7,6},{8,7},{9,8},{10,9},{11,1... | collective-permute-start | bytes 9224 | tf_op jit(solution)/shard_map/ppermute | solution.py:432
  65.9 1.3 collective-permute-start.4
  67.1 3.7 %collective-permute-start.5 = (f32[32,128]{1,0:T(8,128)S(1)}, f32[32,128]{1,0:T(8,128)S(1)}, u32[]{:S(2)}, u32[]{:S(2)}) collective-permute-start(f32[32,128]{1,0:T(8,128)S(1)} %pad_maximum_fusion.5), channel_id=1, source_target_pairs={{0,2},{2,0},{1,3},{3,1},{4,6},{6,4},{5,7},{7,5},{8,10},{10,8},{9,1... | collective-permute-start | bytes 49160 | tf_op jit(solution)/shard_map/ppermute | solution.py:422
  70.9 3.9 %collective-permute-start.6 = (f32[64,128]{1,0:T(8,128)S(1)}, f32[64,128]{1,0:T(8,128)S(1)}, u32[]{:S(2)}, u32[]{:S(2)}) collective-permute-start(f32[64,128]{1,0:T(8,128)S(1)} %pad_maximum_fusion), channel_id=1, source_target_pairs={{0,8},{8,0},{1,9},{9,1},{2,10},{10,2},{3,11},{11,3},{4,12},{12,4},... | collective-permute-start | bytes 98312 | tf_op jit(solution)/shard_map/ppermute | solution.py:424
  77.5 1.2 collective-permute-start.7
  78.7 3.7 %collective-permute-start.8 = (f32[32,128]{1,0:T(8,128)S(1)}, f32[32,128]{1,0:T(8,128)S(1)}, u32[]{:S(2)}, u32[]{:S(2)}) collective-permute-start(f32[32,128]{1,0:T(8,128)S(1)} %pad_maximum_fusion.6), channel_id=1, source_target_pairs={{0,2},{2,0},{1,3},{3,1},{4,6},{6,4},{5,7},{7,5},{8,10},{10,8},{9,1... | collective-permute-start | bytes 49160 | tf_op jit(solution)/shard_map/ppermute | solution.py:422
  82.4 3.9 %collective-permute-start.9 = (f32[64,128]{1,0:T(8,128)S(1)}, f32[64,128]{1,0:T(8,128)S(1)}, u32[]{:S(2)}, u32[]{:S(2)}) collective-permute-start(f32[64,128]{1,0:T(8,128)S(1)} %pad_maximum_fusion.1), channel_id=1, source_target_pairs={{0,8},{8,0},{1,9},{9,1},{2,10},{10,2},{3,11},{11,3},{4,12},{12,4},... | collective-permute-start | bytes 98312 | tf_op jit(solution)/shard_map/ppermute | solution.py:424
  89.1 1.2 collective-permute-start.10
  90.3 3.7 %collective-permute-start.11 = (f32[32,128]{1,0:T(8,128)S(1)}, f32[32,128]{1,0:T(8,128)S(1)}, u32[]{:S(2)}, u32[]{:S(2)}) collective-permute-start(f32[32,128]{1,0:T(8,128)S(1)} %pad_maximum_fusion.7), channel_id=1, source_target_pairs={{0,2},{2,0},{1,3},{3,1},{4,6},{6,4},{5,7},{7,5},{8,10},{10,8},{9,1... | collective-permute-start | bytes 49160 | tf_op jit(solution)/shard_map/ppermute | solution.py:422
  94.0 3.9 %collective-permute-start.12 = (f32[64,128]{1,0:T(8,128)S(1)}, f32[64,128]{1,0:T(8,128)S(1)}, u32[]{:S(2)}, u32[]{:S(2)}) collective-permute-start(f32[64,128]{1,0:T(8,128)S(1)} %pad_maximum_fusion.2), channel_id=1, source_target_pairs={{0,8},{8,0},{1,9},{9,1},{2,10},{10,2},{3,11},{11,3},{4,12},{12,4},... | collective-permute-start | bytes 98312 | tf_op jit(solution)/shard_map/ppermute | solution.py:424
  100.7 1.2 collective-permute-start.13
  101.8 3.7 %collective-permute-start.14 = (f32[32,128]{1,0:T(8,128)S(1)}, f32[32,128]{1,0:T(8,128)S(1)}, u32[]{:S(2)}, u32[]{:S(2)}) collective-permute-start(f32[32,128]{1,0:T(8,128)S(1)} %pad_maximum_fusion.8), channel_id=1, source_target_pairs={{0,2},{2,0},{1,3},{3,1},{4,6},{6,4},{5,7},{7,5},{8,10},{10,8},{9,1... | collective-permute-start | bytes 49160 | tf_op jit(solution)/shard_map/ppermute | solution.py:422
  105.6 3.9 %collective-permute-start.15 = (f32[64,128]{1,0:T(8,128)S(1)}, f32[64,128]{1,0:T(8,128)S(1)}, u32[]{:S(2)}, u32[]{:S(2)}) collective-permute-start(f32[64,128]{1,0:T(8,128)S(1)} %pad_maximum_fusion.3), channel_id=1, source_target_pairs={{0,8},{8,0},{1,9},{9,1},{2,10},{10,2},{3,11},{11,3},{4,12},{12,4},... | collective-permute-start | bytes 98312 | tf_op jit(solution)/shard_map/ppermute | solution.py:424
  112.2 1.2 collective-permute-start.16
  113.4 3.7 %collective-permute-start.17 = (f32[32,128]{1,0:T(8,128)S(1)}, f32[32,128]{1,0:T(8,128)S(1)}, u32[]{:S(2)}, u32[]{:S(2)}) collective-permute-start(f32[32,128]{1,0:T(8,128)S(1)} %pad_maximum_fusion.9), channel_id=1, source_target_pairs={{0,2},{2,0},{1,3},{3,1},{4,6},{6,4},{5,7},{7,5},{8,10},{10,8},{9,1... | collective-permute-start | bytes 49160 | tf_op jit(solution)/shard_map/ppermute | solution.py:422
  117.1 3.9 %collective-permute-start.18 = (f32[64,128]{1,0:T(8,128)S(1)}, f32[64,128]{1,0:T(8,128)S(1)}, u32[]{:S(2)}, u32[]{:S(2)}) collective-permute-start(f32[64,128]{1,0:T(8,128)S(1)} %pad_maximum_fusion.4), channel_id=1, source_target_pairs={{0,8},{8,0},{1,9},{9,1},{2,10},{10,2},{3,11},{11,3},{4,12},{12,4},... | collective-permute-start | bytes 98312 | tf_op jit(solution)/shard_map/ppermute | solution.py:424

commit v5 on v4

--- a/solution.py
+++ b/solution.py
@@ -8,8 +8,8 @@
 
 
 DOM = ("dom_0", "dom_1", "dom_2", "dom_3", "dom_4", "dom_5")
-OTHERS = ("dom_0", "dom_1", "dom_3")
-PEERS = 16
+OTHERS = ("dom_0", "dom_1", "dom_2", "dom_3")
+PEERS = 32
 UNROLL = 8
 CSWEEPS = 6
 damping = 0.7
@@ -212,20 +212,13 @@
 
 
 def lane_of_device(p, me):
-    p = lax.bitwise_xor(p, lax.bitwise_and(me, 11))
-
-    def bit(at, to, mask=1):
-        return lax.shift_left(lax.bitwise_and(lax.shift_right_logical(p, at), mask), to)
-
-    return bit(3, 6) + bit(1, 5) + bit(0, 4) + bit(5, 2, 3) + bit(4, 1) + bit(2, 0)
+    p = lax.bitwise_xor(p, lax.bitwise_and(me, 3))
+    return lax.shift_left(lax.bitwise_and(p, 3), 5) + lax.shift_right_logical(p, 2)
 
 
 def device_of_lane(q, me):
-    def bit(at, to, mask=1):
-        return lax.shift_left(lax.bitwise_and(lax.shift_right_logical(q, at), mask), to)
-
-    p = bit(6, 3) + bit(5, 1) + bit(4, 0) + bit(2, 5, 3) + bit(1, 4) + bit(0, 2)
-    return lax.bitwise_xor(p, lax.bitwise_and(me, 11))
+    p = lax.shift_left(lax.bitwise_and(q, 31), 2) + lax.shift_right_logical(q, 5)
+    return lax.bitwise_xor(p, lax.bitwise_and(me, 3))
 
 
 def coarse_pack_kernel(col, blk, send):
@@ -338,9 +331,9 @@
     table[...] = jnp.transpose(mine[...])
 
 
-def coarse_kernel(me_ref, p0, p1, p2, p3, rhs, dia, where, data, new, correction,
+def coarse_kernel(me_ref, p0, p1, p2, rhs, dia, where, data, new, correction,
                   table, mine, gather):
-    gathered(table, (p0, p1, p2, p3), mine)
+    gathered(table, (p0, p1, p2), mine)
     got = coarse_step(table, where, data, p0[...], rhs[...], dia[...], gather)
     new[...] = got
     mine[0:PEERS, :] = got
@@ -350,11 +343,11 @@
     correction[...] = jnp.concatenate([row[:, 32 * i : 32 * i + 32] for i in range(3)], axis=0)
 
 
-def post_kernel(base_ref, p0, p1, p2, p3, first_iter, rhs, dia, col, blk, node_row, before, after,
+def post_kernel(base_ref, p0, p1, p2, first_iter, rhs, dia, col, blk, node_row, before, after,
                 before2, after2, out, table, mine, one, two):
     base = base_ref[0]
     me = lax.shift_right_logical(base, 10)
-    gathered(table, (p0, p1, p2, p3), mine)
+    gathered(table, (p0, p1, p2), mine)
     one[...] = first_iter[...]
     one[:, lanes(0, HALO)] = before2[...]
     one[:, lanes(WIDE + ROWS + HALO, HALO)] = after2[...]
@@ -420,9 +413,7 @@
     p1 = lax.ppermute(new, "dom_5", swap)
     a = jnp.concatenate([new, p1], axis=0)
     p2 = lax.ppermute(a, "dom_4", swap)
-    b = jnp.concatenate([a, p2], axis=0)
-    p3 = lax.ppermute(b, "dom_2", swap)
-    return new, p1, p2, p3
+    return new, p1, p2
 
 
 def shifts(up, down):

time: 126 us -> 126 us (level)
  waiting for transfers between devices: 62 us -> 53.6 us
  Pallas kernels: 24.7 us -> 33 us
  starting transfers between devices: 32.8 us -> 31.5 us
    ppermute x5 -> x0, waiting for transfers between devices: 18.4 us -> none  [in_group(): p3 = lax.ppermute(b, 'dom_2', swap)]
    all_to_all x1, waiting for transfers between devices: 7.85 us -> 16.7 us  [cycle(): data = lax.all_to_all(dsend, OTHERS, 0, 0, tiled=True)]
    pallas_call x8, Pallas kernels: 24.3 us -> 32.6 us  [call(): pl.pallas_call(kernel, in_specs=specs, out_specs=[vmem] * len(outs), out_...]
    ppermute x5, waiting for transfers between devices: 14.9 us -> 16.2 us  [in_group(): p2 = lax.ppermute(a, 'dom_4', swap)]
  transfers between devices with their start and end apart: 21 -> 16, of which waited for: 19 -> 14; matrix products, arithmetic and copies ran while one was open for 0% -> 0% of each run, Pallas kernels for 1% -> 0%
where the time goes in v5:
time: 126 us; the launch traced here: 125 us
  waiting for transfers between devices  53.6 us (43%)
  Pallas kernels  33 us (26%)
  starting transfers between devices  31.5 us (25%)
  local copies, waits for them, and re-layouts  6.07 us (5%)
    pallas_call x8, Pallas kernels, call(): pl.pallas_call(kernel, in_specs=specs, out_specs=[vmem] * len(outs), out_...  32.6 us
    all_to_all x1, starting transfers between devices, cycle(): sums = lax.all_to_all(send, DOM, 0, 0, tiled=True)  18 us
    all_to_all x1, waiting for transfers between devices, cycle(): data = lax.all_to_all(dsend, OTHERS, 0, 0, tiled=True)  16.7 us
    ppermute x5, waiting for transfers between devices, in_group(): p2 = lax.ppermute(a, 'dom_4', swap)  16.2 us
    all_to_all x1, waiting for transfers between devices, cycle(): sums = lax.all_to_all(send, DOM, 0, 0, tiled=True)  8.04 us
    ppermute x4, waiting for transfers between devices, shifts(): return (lax.ppermute(up, DOM, forward), lax.ppermute(down, DOM, backward))  6.69 us
    unnamed x30, local copies, waits for them, and re-layouts  6.07 us
    ppermute x5, waiting for transfers between devices, in_group(): p1 = lax.ppermute(new, 'dom_5', swap)  5.89 us
  transfers between devices with their start and end apart: 16, of which 14 were waited for; matrix products, arithmetic and copies ran while one was open for 0% of the time, Pallas kernels for 0%

profile of v5, /device:TPU:0, one launch (start us, length us, event | category | flops | bytes accessed | tf_op | source)
XLA Modules:
  0.0 125.0 jit_solution(15492035885212081490)
XLA Ops:
  0.7 1.3 %copy-done = f32[1024,27,3,3]{0,1,3,2:T(8,128)S(1)} copy-done((f32[1024,27,3,3]{0,1,3,2:T(8,128)S(1)}, f32[1024,27,3,3]{0,1,3,2:T(8,128)}, u32[]{:S(2)}) %copy-start) | copy-done | bytes 995352
  1.9 0.9 copy-done.3
  2.8 0.7 copy-done.6
  3.6 0.7 copy-done.8
  4.3 0.7 copy-done.11
  5.0 0.7 copy-done.14
  5.6 0.4 pack.1
  6.0 0.0 copy-start.5
  6.0 0.0 copy-start.10
  6.1 1.4 %collective-permute-start = (f32[288,256]{1,0:T(8,128)S(1)}, f32[288,256]{1,0:T(8,128)S(1)}, u32[]{:S(2)}, u32[]{:S(2)}) collective-permute-start(f32[288,256]{1,0:T(8,128)S(1)} %get-tuple-element.20), channel_id=1, source_target_pairs={{0,1},{1,2},{2,3},{3,4},{4,5},{5,6},{6,7},{7,8},{8,9},{9,10},{10,1... | collective-permute-start | bytes 884744 | tf_op jit(solution)/shard_map/ppermute | solution.py:423
  7.5 1.3 %collective-permute-start.1 = (f32[288,256]{1,0:T(8,128)S(1)}, f32[288,256]{1,0:T(8,128)S(1)}, u32[]{:S(2)}, u32[]{:S(2)}) collective-permute-start(f32[288,256]{1,0:T(8,128)S(1)} %get-tuple-element.21), channel_id=1, source_target_pairs={{1,0},{2,1},{3,2},{4,3},{5,4},{6,5},{7,6},{8,7},{9,8},{10,9},{11,1... | collective-permute-start | bytes 884744 | tf_op jit(solution)/shard_map/ppermute | solution.py:423
  8.8 0.0 collective-permute-done.before
  8.8 4.0 %collective-permute-done.1.after = f32[288,256]{1,0:T(8,128)S(1)} collective-permute-done((f32[288,256]{1,0:T(8,128)S(1)}, f32[288,256]{1,0:T(8,128)S(1)}, u32[]{:S(2)}, u32[]{:S(2)}) %collective-permute-start.1) | collective-permute-done | bytes 294944 | tf_op jit(solution)/shard_map/ppermute | solution.py:423
  12.8 4.5 %shard_map.104 = (f32[128,2,128]{2,1,0:T(2,128)}, f32[3,2048]{1,0:T(4,128)S(1)}, f32[3,2048]{1,0:T(4,128)S(1)}, f32[3,2048]{1,0:T(4,128)S(1)}, f32[3,256]{1,0:T(4,128)S(1)}, /*index=5*/f32[3,256]{1,0:T(4,128)S(1)}) custom-call(s32[1]{0:T(128)S(6)} %mul.23.base_ref, f32[3,1024]{1,0:T(4,128)S(1)} %bitcast.19, f32[3,1024]{1,0:T(4,128)S(1)} %bitcast.21, ...), custom_call_target="tpu_custom_call" | custom-call | tf_op jit(solution)/shard_map/pallas_call | solution.py:399
  17.3 18.0 %all-to-all-start = ((f32[128,2,128]{2,1,0:T(2,128)}), f32[128,2,128]{2,1,0:T(2,128)S(1)}, u32[]{:S(2)}, u32[]{:S(2)}) async-start(f32[128,2,128]{2,1,0:T(2,128)} %get-tuple-element.22), calls=%async_computation | async-start | bytes 262144 | tf_op jit(solution)/shard_map/all_to_all | solution.py:462
  35.4 0.2 shard_map.105
  35.6 1.1 copy-done.2
  36.7 8.0 %all-to-all-done.sums = f32[128,2,128]{2,1,0:T(2,128)S(1)} async-done(((f32[128,2,128]{2,1,0:T(2,128)}), f32[128,2,128]{2,1,0:T(2,128)S(1)}, u32[]{:S(2)}, u32[]{:S(2)}) %all-to-all-start) | async-done | bytes 131104 | tf_op jit(solution)/shard_map/all_to_all | solution.py:462
  44.7 4.5 %all-to-all-start.1 = ((f32[32,80,128]{2,1,0:T(8,128)}), f32[32,80,128]{2,1,0:T(8,128)S(1)}, u32[]{:S(2)}, u32[]{:S(2)}) async-start(f32[32,80,128]{2,1,0:T(8,128)} %copy-done.2), calls=%async_computation.1 | async-start | bytes 2621440 | tf_op jit(solution)/shard_map/all_to_all | solution.py:438
  49.2 1.5 %collective-permute-start.2 = (f32[3,256]{1,0:T(4,128)S(1)}, f32[3,256]{1,0:T(4,128)S(1)}, u32[]{:S(2)}, u32[]{:S(2)}) collective-permute-start(f32[3,256]{1,0:T(4,128)S(1)} %get-tuple-element.23), channel_id=1, source_target_pairs={{0,1},{1,2},{2,3},{3,4},{4,5},{5,6},{6,7},{7,8},{8,9},{9,10},{10,1... | collective-permute-start | bytes 9224 | tf_op jit(solution)/shard_map/ppermute | solution.py:423
  50.7 1.3 %collective-permute-start.3 = (f32[3,256]{1,0:T(4,128)S(1)}, f32[3,256]{1,0:T(4,128)S(1)}, u32[]{:S(2)}, u32[]{:S(2)}) collective-permute-start(f32[3,256]{1,0:T(4,128)S(1)} %get-tuple-element.24), channel_id=1, source_target_pairs={{1,0},{2,1},{3,2},{4,3},{5,4},{6,5},{7,6},{8,7},{9,8},{10,9},{11,1... | collective-permute-start | bytes 9224 | tf_op jit(solution)/shard_map/ppermute | solution.py:423
  52.0 0.0 collective-permute-done.2.far_up.before2
  52.0 2.7 %collective-permute-done.3.far_down.after2 = f32[3,256]{1,0:T(4,128)S(1)} collective-permute-done((f32[3,256]{1,0:T(4,128)S(1)}, f32[3,256]{1,0:T(4,128)S(1)}, u32[]{:S(2)}, u32[]{:S(2)}) %collective-permute-start.3) | collective-permute-done | bytes 3104 | tf_op jit(solution)/shard_map/ppermute | solution.py:423
  54.8 16.7 %all-to-all-done.1.data = f32[32,80,128]{2,1,0:T(8,128)S(1)} async-done(((f32[32,80,128]{2,1,0:T(8,128)}), f32[32,80,128]{2,1,0:T(8,128)S(1)}, u32[]{:S(2)}, u32[]{:S(2)}) %all-to-all-start.1) | async-done | bytes 1310752 | tf_op jit(solution)/shard_map/all_to_all | solution.py:438
  71.5 5.3 %shard_map.106 = (f32[32,128]{1,0:T(8,128)S(1)}, f32[32,128]{1,0:T(8,128)S(1)}, f32[32,128]{1,0:T(8,128)S(1)}, s32[32,8,128]{2,1,0:T(8,128)S(1)}) custom-call(s32[1]{0:T(128)} %bitcast.me_ref, f32[128,2,128]{2,1,0:T(2,128)S(1)} %all-to-all-done.sums, f32[32,80,128]{2,1,0:T(8,128)S(1)} %all-to-all-done.1.data, ...), custom_call_target="tpu_custom_call" | custom-call | tf_op jit(solution)/shard_map/pallas_call | solution.py:399
  76.8 0.1 collective-permute-start.4
  76.9 1.2 collective-permute-done.4.p1
  78.1 0.7 collective-permute-start.5
  78.8 3.2 %collective-permute-done.5.p2 = f32[64,128]{1,0:T(8,128)S(1)} collective-permute-done((f32[64,128]{1,0:T(8,128)S(1)}, f32[64,128]{1,0:T(8,128)S(1)}, u32[]{:S(2)}, u32[]{:S(2)}) %collective-permute-start.5) | collective-permute-done | bytes 32800 | tf_op jit(solution)/shard_map/ppermute | solution.py:415
  82.0 4.6 %shard_map.107 = (f32[32,128]{1,0:T(8,128)S(1)}, f32[3,32]{1,0:T(4,128)}) custom-call(s32[1]{0:T(128)} %bitcast.me_ref, f32[32,128]{1,0:T(8,128)S(1)} %get-tuple-element.25.p0, f32[32,128]{1,0:T(8,128)S(1)} %collective-permute-done.4.p1, f32[64,128]{1,0:T(8,128)S(1)} %collective-permute-done.5.p2, f32[32,128]{1,0:T(8,128)S(1)} %get-tuple-element.26.rhs, ...), custom_call_target="tpu_custom_call" | custom-call | tf_op jit(solution)/shard_map/pallas_call | solution.py:399
  86.6 1.2 collective-permute-done.6.p1
  87.8 0.7 collective-permute-start.7
  88.4 3.2 %collective-permute-done.7.p2 = f32[64,128]{1,0:T(8,128)S(1)} collective-permute-done((f32[64,128]{1,0:T(8,128)S(1)}, f32[64,128]{1,0:T(8,128)S(1)}, u32[]{:S(2)}, u32[]{:S(2)}) %collective-permute-start.7) | collective-permute-done | bytes 32800 | tf_op jit(solution)/shard_map/ppermute | solution.py:415
  91.7 4.6 %shard_map.108 = (f32[32,128]{1,0:T(8,128)S(1)}, f32[3,32]{1,0:T(4,128)}) custom-call(s32[1]{0:T(128)} %bitcast.me_ref, f32[32,128]{1,0:T(8,128)S(1)} %get-tuple-element.29.p0, f32[32,128]{1,0:T(8,128)S(1)} %collective-permute-done.6.p1, f32[64,128]{1,0:T(8,128)S(1)} %collective-permute-done.7.p2, f32[32,128]{1,0:T(8,128)S(1)} %get-tuple-element.26.rhs, ...), custom_call_target="tpu_custom_call" | custom-call | tf_op jit(solution)/shard_map/pallas_call | solution.py:399
  96.2 1.2 collective-permute-done.8.p1
  97.4 0.7 collective-permute-start.9
  98.1 3.2 %collective-permute-done.9.p2 = f32[64,128]{1,0:T(8,128)S(1)} collective-permute-done((f32[64,128]{1,0:T(8,128)S(1)}, f32[64,128]{1,0:T(8,128)S(1)}, u32[]{:S(2)}, u32[]{:S(2)}) %collective-permute-start.9) | collective-permute-done | bytes 32800 | tf_op jit(solution)/shard_map/ppermute | solution.py:415
  101.3 4.6 %shard_map.109 = (f32[32,128]{1,0:T(8,128)S(1)}, f32[3,32]{1,0:T(4,128)}) custom-call(s32[1]{0:T(128)} %bitcast.me_ref, f32[32,128]{1,0:T(8,128)S(1)} %get-tuple-element.30.p0, f32[32,128]{1,0:T(8,128)S(1)} %collective-permute-done.8.p1, f32[64,128]{1,0:T(8,128)S(1)} %collective-permute-done.9.p2, f32[32,128]{1,0:T(8,128)S(1)} %get-tuple-element.26.rhs, ...), custom_call_target="tpu_custom_call" | custom-call | tf_op jit(solution)/shard_map/pallas_call | solution.py:399
  105.9 0.0 collective-permute-start.10
  105.9 1.2 collective-permute-done.10.p1
  107.1 0.7 collective-permute-start.11
  107.7 3.2 %collective-permute-done.11.p2 = f32[64,128]{1,0:T(8,128)S(1)} collective-permute-done((f32[64,128]{1,0:T(8,128)S(1)}, f32[64,128]{1,0:T(8,128)S(1)}, u32[]{:S(2)}, u32[]{:S(2)}) %collective-permute-start.11) | collective-permute-done | bytes 32800 | tf_op jit(solution)/shard_map/ppermute | solution.py:415
  111.0 4.6 %shard_map.110 = (f32[32,128]{1,0:T(8,128)S(1)}, f32[3,32]{1,0:T(4,128)}) custom-call(s32[1]{0:T(128)} %bitcast.me_ref, f32[32,128]{1,0:T(8,128)S(1)} %get-tuple-element.31.p0, f32[32,128]{1,0:T(8,128)S(1)} %collective-permute-done.10.p1, f32[64,128]{1,0:T(8,128)S(1)} %collective-permute-done.11.p2, f32[32,128]{1,0:T(8,128)S(1)} %get-tuple-element.26.rhs, ...), custom_call_target="tpu_custom_call" | custom-call | tf_op jit(solution)/shard_map/pallas_call | solution.py:399
  115.5 0.0 collective-permute-start.12
  115.6 1.2 collective-permute-done.12.p1
  116.7 0.7 collective-permute-start.13
  117.4 3.2 %collective-permute-done.13.p2 = f32[64,128]{1,0:T(8,128)S(1)} collective-permute-done((f32[64,128]{1,0:T(8,128)S(1)}, f32[64,128]{1,0:T(8,128)S(1)}, u32[]{:S(2)}, u32[]{:S(2)}) %collective-permute-start.13) | collective-permute-done | bytes 32800 | tf_op jit(solution)/shard_map/ppermute | solution.py:415
  120.7 4.3 %shard_map.111 = f32[3,1024]{1,0:T(4,128)} custom-call(s32[1]{0:T(128)S(6)} %mul.23.base_ref, f32[32,128]{1,0:T(8,128)S(1)} %get-tuple-element.32.p0, f32[32,128]{1,0:T(8,128)S(1)} %collective-permute-done.12.p1, f32[64,128]{1,0:T(8,128)S(1)} %collective-permute-done.13.p2, f32[3,2048]{1,0:T(4,128)S(1)} %get-tuple-element.33.first_iter, ...), custom_call_target="tpu_custom_call" | custom-call | tf_op jit(solution)/shard_map/pallas_call | solution.py:399
  (28 shorter events, 0.1 us)
Async XLA Ops:
  0.6 12.2 %copy-start.12 = (s32[1024]{0:T(1024)S(1)}, s32[1024]{0:T(1024)}, u32[]{:S(2)}) copy-start(s32[1024]{0:T(1024)} %param.13) | copy-start | bytes 12292
  0.6 12.2 %copy-start.13 = (f32[32,3]{0,1:T(4,128)S(1)}, f32[32,3]{0,1:T(4,128)}, u32[]{:S(2)}) copy-start(f32[32,3]{0,1:T(4,128)} %param.15) | copy-start | bytes 1156
  0.7 1.3 %copy-start = (f32[1024,27,3,3]{0,1,3,2:T(8,128)S(1)}, f32[1024,27,3,3]{0,1,3,2:T(8,128)}, u32[]{:S(2)}) copy-start(f32[1024,27,3,3]{0,1,3,2:T(8,128)} %param.12) | copy-start | bytes 2985988
  1.9 0.9 copy-start.3
  2.8 0.7 copy-start.6
  3.6 0.7 copy-start.8
  4.3 0.7 copy-start.11
  5.0 0.7 copy-start.14
  5.6 7.2 %copy-start.1 = (f32[1024,27,3,3]{0,1,3,2:T(8,128)S(1)}, f32[1024,27,3,3]{0,1,3,2:T(8,128)}, u32[]{:S(2)}) copy-start(f32[1024,27,3,3]{0,1,3,2:T(8,128)} %param.12) | copy-start | bytes 2985988
  5.6 7.2 %copy-start.4 = (s32[1024,27]{0,1:T(8,128)S(1)}, s32[1024,27]{0,1:T(8,128)}, u32[]{:S(2)}) copy-start(s32[1024,27]{0,1:T(8,128)} %param.11) | copy-start | bytes 331780
  5.6 7.2 %copy-start.7 = (f32[1024,3]{0,1:T(4,128)S(1)}, f32[1024,3]{0,1:T(4,128)}, u32[]{:S(2)}) copy-start(f32[1024,3]{0,1:T(4,128)} %param.9) | copy-start | bytes 36868
  5.6 7.2 %copy-start.9 = (f32[1024,3]{0,1:T(4,128)S(1)}, f32[1024,3]{0,1:T(4,128)}, u32[]{:S(2)}) copy-start(f32[1024,3]{0,1:T(4,128)} %param.10) | copy-start | bytes 36868
  6.0 29.3 %copy-start.5 = (f32[32,27,3,3]{1,0,3,2:T(8,128)S(1)}, f32[32,27,3,3]{1,0,3,2:T(8,128)}, u32[]{:S(2)}) copy-start(f32[32,27,3,3]{1,0,3,2:T(8,128)} %param.17) | copy-start | bytes 93316
  6.0 29.3 %copy-start.10 = (s32[32,27]{1,0:T(8,128)S(1)}, s32[32,27]{1,0:T(8,128)}, u32[]{:S(2)}) copy-start(s32[32,27]{1,0:T(8,128)} %col.1) | copy-start | bytes 10372
  6.1 2.8 %collective-permute-start = (f32[288,256]{1,0:T(8,128)S(1)}, f32[288,256]{1,0:T(8,128)S(1)}, u32[]{:S(2)}, u32[]{:S(2)}) collective-permute-start(f32[288,256]{1,0:T(8,128)S(1)} %get-tuple-element.20), channel_id=1, source_target_pairs={{0,1},{1,2},{2,3},{3,4},{4,5},{5,6},{6,7},{7,8},{8,9},{9,10},{10,1... | collective-permute-start | bytes 884744 | tf_op jit(solution)/shard_map/ppermute | solution.py:423
  7.5 5.3 %collective-permute-start.1 = (f32[288,256]{1,0:T(8,128)S(1)}, f32[288,256]{1,0:T(8,128)S(1)}, u32[]{:S(2)}, u32[]{:S(2)}) collective-permute-start(f32[288,256]{1,0:T(8,128)S(1)} %get-tuple-element.21), channel_id=1, source_target_pairs={{1,0},{2,1},{3,2},{4,3},{5,4},{6,5},{7,6},{8,7},{9,8},{10,9},{11,1... | collective-permute-start | bytes 884744 | tf_op jit(solution)/shard_map/ppermute | solution.py:423
  17.3 27.4 %all-to-all-start = ((f32[128,2,128]{2,1,0:T(2,128)}), f32[128,2,128]{2,1,0:T(2,128)S(1)}, u32[]{:S(2)}, u32[]{:S(2)}) async-start(f32[128,2,128]{2,1,0:T(2,128)} %get-tuple-element.22), calls=%async_computation | async-start | bytes 262144 | tf_op jit(solution)/shard_map/all_to_all | solution.py:462
  35.6 1.1 copy-start.2
  44.7 26.7 %all-to-all-start.1 = ((f32[32,80,128]{2,1,0:T(8,128)}), f32[32,80,128]{2,1,0:T(8,128)S(1)}, u32[]{:S(2)}, u32[]{:S(2)}) async-start(f32[32,80,128]{2,1,0:T(8,128)} %copy-done.2), calls=%async_computation.1 | async-start | bytes 2621440 | tf_op jit(solution)/shard_map/all_to_all | solution.py:438
  49.2 2.8 %collective-permute-start.2 = (f32[3,256]{1,0:T(4,128)S(1)}, f32[3,256]{1,0:T(4,128)S(1)}, u32[]{:S(2)}, u32[]{:S(2)}) collective-permute-start(f32[3,256]{1,0:T(4,128)S(1)} %get-tuple-element.23), channel_id=1, source_target_pairs={{0,1},{1,2},{2,3},{3,4},{4,5},{5,6},{6,7},{7,8},{8,9},{9,10},{10,1... | collective-permute-start | bytes 9224 | tf_op jit(solution)/shard_map/ppermute | solution.py:423
  50.7 4.0 %collective-permute-start.3 = (f32[3,256]{1,0:T(4,128)S(1)}, f32[3,256]{1,0:T(4,128)S(1)}, u32[]{:S(2)}, u32[]{:S(2)}) collective-permute-start(f32[3,256]{1,0:T(4,128)S(1)} %get-tuple-element.24), channel_id=1, source_target_pairs={{1,0},{2,1},{3,2},{4,3},{5,4},{6,5},{7,6},{8,7},{9,8},{10,9},{11,1... | collective-permute-start | bytes 9224 | tf_op jit(solution)/shard_map/ppermute | solution.py:423
  76.8 1.3 %collective-permute-start.4 = (f32[32,128]{1,0:T(8,128)S(1)}, f32[32,128]{1,0:T(8,128)S(1)}, u32[]{:S(2)}, u32[]{:S(2)}) collective-permute-start(f32[32,128]{1,0:T(8,128)S(1)} %get-tuple-element.25.p0), channel_id=1, source_target_pairs={{0,1},{1,0},{2,3},{3,2},{4,5},{5,4},{6,7},{7,6},{8,9},{9,8},{10,11... | collective-permute-start | bytes 49160 | tf_op jit(solution)/shard_map/ppermute | solution.py:413
  78.1 3.9 %collective-permute-start.5 = (f32[64,128]{1,0:T(8,128)S(1)}, f32[64,128]{1,0:T(8,128)S(1)}, u32[]{:S(2)}, u32[]{:S(2)}) collective-permute-start(f32[64,128]{1,0:T(8,128)S(1)} %pad_maximum_fusion), channel_id=1, source_target_pairs={{0,2},{2,0},{1,3},{3,1},{4,6},{6,4},{5,7},{7,5},{8,10},{10,8},{9,1... | collective-permute-start | bytes 98312 | tf_op jit(solution)/shard_map/ppermute | solution.py:415
  86.6 1.2 collective-permute-start.6
  87.8 3.9 %collective-permute-start.7 = (f32[64,128]{1,0:T(8,128)S(1)}, f32[64,128]{1,0:T(8,128)S(1)}, u32[]{:S(2)}, u32[]{:S(2)}) collective-permute-start(f32[64,128]{1,0:T(8,128)S(1)} %pad_maximum_fusion.1), channel_id=1, source_target_pairs={{0,2},{2,0},{1,3},{3,1},{4,6},{6,4},{5,7},{7,5},{8,10},{10,8},{9,1... | collective-permute-start | bytes 98312 | tf_op jit(solution)/shard_map/ppermute | solution.py:415
  96.2 1.2 collective-permute-start.8
  97.4 3.9 %collective-permute-start.9 = (f32[64,128]{1,0:T(8,128)S(1)}, f32[64,128]{1,0:T(8,128)S(1)}, u32[]{:S(2)}, u32[]{:S(2)}) collective-permute-start(f32[64,128]{1,0:T(8,128)S(1)} %pad_maximum_fusion.2), channel_id=1, source_target_pairs={{0,2},{2,0},{1,3},{3,1},{4,6},{6,4},{5,7},{7,5},{8,10},{10,8},{9,1... | collective-permute-start | bytes 98312 | tf_op jit(solution)/shard_map/ppermute | solution.py:415
  105.9 1.2 collective-permute-start.10
  107.1 3.9 %collective-permute-start.11 = (f32[64,128]{1,0:T(8,128)S(1)}, f32[64,128]{1,0:T(8,128)S(1)}, u32[]{:S(2)}, u32[]{:S(2)}) collective-permute-start(f32[64,128]{1,0:T(8,128)S(1)} %pad_maximum_fusion.3), channel_id=1, source_target_pairs={{0,2},{2,0},{1,3},{3,1},{4,6},{6,4},{5,7},{7,5},{8,10},{10,8},{9,1... | collective-permute-start | bytes 98312 | tf_op jit(solution)/shard_map/ppermute | solution.py:415
  115.5 1.2 collective-permute-start.12
  116.7 3.9 %collective-permute-start.13 = (f32[64,128]{1,0:T(8,128)S(1)}, f32[64,128]{1,0:T(8,128)S(1)}, u32[]{:S(2)}, u32[]{:S(2)}) collective-permute-start(f32[64,128]{1,0:T(8,128)S(1)} %pad_maximum_fusion.4), channel_id=1, source_target_pairs={{0,2},{2,0},{1,3},{3,1},{4,6},{6,4},{5,7},{7,5},{8,10},{10,8},{9,1... | collective-permute-start | bytes 98312 | tf_op jit(solution)/shard_map/ppermute | solution.py:415

commit v6 on v5

--- a/solution.py
+++ b/solution.py
@@ -10,7 +10,7 @@
 DOM = ("dom_0", "dom_1", "dom_2", "dom_3", "dom_4", "dom_5")
 OTHERS = ("dom_0", "dom_1", "dom_2", "dom_3")
 PEERS = 32
-UNROLL = 8
+UNROLL = 2
 CSWEEPS = 6
 damping = 0.7
 highest = lax.Precision.HIGHEST
@@ -154,6 +154,15 @@
         out[:, lanes(at)] = smoothed(table, pull, rhs, dia, at)
 
 
+def each_block(step):
+    def some(t, carry):
+        for u in range(UNROLL):
+            step(t * UNROLL + u)
+        return carry
+
+    lax.fori_loop(0, BLOCKS // UNROLL, some, 0)
+
+
 def own_block(table, col, blk, base, b):
     start = base + b * LANES - 2 * LANES
     cols, blks = local_getters(col, blk, start, b)
@@ -172,23 +181,21 @@
     sweep_halo(two, one, keep_rhs, keep_dia, before, base, WIDE - HALO)
     sweep_halo(two, one, keep_rhs, keep_dia, after, base, WIDE + ROWS)
 
-    def second(b, carry):
+    def second(b):
         at = WIDE + b * LANES
         pull = own_block(one, col, blk, base, b)
         two[:, lanes(at)] = smoothed(one, pull, keep_rhs, keep_dia, at)
-        return carry
-
-    lax.fori_loop(0, BLOCKS, second, 0)
-
-    def third(b, carry):
+
+    each_block(second)
+
+    def third(b):
         at = WIDE + b * LANES
         pull = jnp.concatenate(own_block(two, col, blk, base, b), axis=0)
         s, d = two[:, lanes(at)], keep_dia[:, lanes(at)]
         res[0:3, lanes(b * LANES)] = keep_rhs[:, lanes(at)] - (d * s - pull)
-        return carry
 
     res[...] = jnp.zeros(res.shape, f32)
-    lax.fori_loop(0, BLOCKS, third, 0)
+    each_block(third)
     first_iter[...] = two[...]
     up2[...] = two[:, lanes(WIDE + ROWS - WIDE, HALO)]
     down2[...] = two[:, lanes(WIDE + HALO, HALO)]
@@ -222,13 +229,46 @@
 
 
 def coarse_pack_kernel(col, blk, send):
-    def folded(a):
-        z = jnp.concatenate([a, jnp.zeros((32, 5), f32)], axis=1)
-        z = jnp.transpose(z)
-        return jnp.concatenate([z[8 * k : 8 * k + 8, :] for k in range(4)], axis=1)
-
-    parts = [folded(blk[i, j]) for i in range(3) for j in range(3)]
-    parts.append(folded(col[...].astype(f32)))
+    def turned(a):
+        z = jnp.transpose(jnp.concatenate([a, jnp.zeros((32, 5), f32)], axis=1))
+        return jnp.concatenate([z] * 4, axis=1)
+
+    columns = turned(col[...].astype(f32))
+    kind = lax.bitwise_and(columns.astype(i32), 7)
+    tile = (8, LANES)
+    sub = lax.broadcasted_iota(i32, tile, 0)
+    count = jnp.zeros(tile, i32)
+    match, earlier = [], []
+    for k in range(SLOTS):
+        here = sub == jnp.broadcast_to(kind[k : k + 1], tile)
+        match.append(here)
+        earlier.append(count)
+        count = count + here.astype(i32)
+    left = jnp.zeros((1, LANES), i32)
+    start = []
+    for n in range(16):
+        if n >= 8:
+            start.append(left)
+        left = jnp.maximum(left + count[n % 8 : n % 8 + 1] - 4, 0)
+    start = jnp.concatenate(start, axis=0) + 4 * sub
+    place = 4 * sub + lax.shift_right_logical(lax.broadcasted_iota(i32, tile, 1), 5)
+    slot = jnp.full(tile, 31, i32)
+    for k in range(SLOTS):
+        at = jnp.sum(jnp.where(match[k], start + earlier[k], 0), axis=0, keepdims=True)
+        slot = jnp.where(place == jnp.broadcast_to(lax.bitwise_and(at, 31), tile), k, slot)
+    inner, outer = lax.bitwise_and(slot, 7), lax.shift_right_logical(slot, 3)
+
+    def placed(z):
+        got = None
+        for g in range(4):
+            part = jnp.take_along_axis(
+                z[8 * g : 8 * g + 8], inner, axis=0, mode="promise_in_bounds"
+            )
+            got = part if got is None else jnp.where(outer == g, part, got)
+        return got
+
+    parts = [placed(turned(blk[i, j])) for i in range(3) for j in range(3)]
+    parts.append(jnp.where(slot == 31, sub.astype(f32), placed(columns)))
     for m in range(10):
         for d in range(PEERS):
             send[d, 8 * m : 8 * m + 8, :] = parts[m]
@@ -249,20 +289,30 @@
     return near
 
 
-def coarse_step(table, where, data, own, rhs, dia, gather):
-    def some(t, carry):
-        for u in range(UNROLL):
-            d = t * UNROLL + u
+def coarse_step(table, where, passes, data, own, rhs, dia, gather):
+    gather[...] = jnp.zeros(gather.shape, f32)
+
+    def one_pass(t, carry):
+        rows = [
+            [pltpu.roll(table[32 * j + 8 * v : 32 * j + 8 * v + 8, :], t, axis=0) for v in range(4)]
+            for j in range(3)
+        ]
+        for d in range(PEERS):
             w = where[d]
-            near = coarse_lookup(table, lax.bitwise_and(w, 31), lax.shift_right_logical(w, 5))
+            code, lane = lax.bitwise_and(w, 31), lax.shift_right_logical(w, 5)
+            near = [jnp.zeros((8, LANES), f32) for _ in range(3)]
+            for v in range(4):
+                here = code == 4 * t + v
+                for j in range(3):
+                    near[j] = jnp.where(here, picked(rows[j][v], lane), near[j])
             for i in range(3):
                 a = data[d, lanes8(3 * i), :] * near[0]
                 a = a + data[d, lanes8(3 * i + 1), :] * near[1]
                 a = a + data[d, lanes8(3 * i + 2), :] * near[2]
-                gather[i, pl.ds(d, 1), :] = jnp.sum(a, axis=0, keepdims=True)
+                gather[i, d : d + 1, :] += jnp.sum(a, axis=0, keepdims=True)
         return carry
 
-    lax.fori_loop(0, PEERS // UNROLL, some, 0)
+    lax.fori_loop(0, passes, one_pass, 0)
     parts = []
     for i in range(3):
         s = gather[i]
@@ -275,7 +325,7 @@
     return slice(8 * m, 8 * m + 8)
 
 
-def coarse_first_kernel(me_ref, sums, data, far_up, far_down, new, rhs, dia, where,
+def coarse_first_kernel(me_ref, sums, data, far_up, far_down, new, rhs, dia, where, passes,
                         table, gather, left, right):
     me = me_ref[0]
     got = jnp.transpose(sums[:, 0, :])
@@ -315,11 +365,19 @@
     own = jnp.transpose(first)[0:PEERS]
     rhs[...] = jnp.transpose(jnp.concatenate([crhs, pad], axis=0))[0:PEERS]
     dia[...] = jnp.transpose(jnp.concatenate([cdia, pad + 1.0], axis=0))[0:PEERS]
+    sub = lax.broadcasted_iota(i32, (8, LANES), 0)
+    most = jnp.zeros((8, LANES), i32)
     for d in range(PEERS):
         c = data[d, 72:80, :].astype(i32)
+        off = lax.bitwise_and(sub - c, 7)
+        most = jnp.maximum(most, off)
         at = lane_of_device(lax.shift_right_logical(c, 5), me)
-        where[d] = lax.bitwise_and(c, 31) + lax.shift_left(at, 5)
-    new[...] = coarse_step(table, where, data, own, rhs[...], dia[...], gather)
+        code = lax.bitwise_and(lax.shift_right_logical(c, 3), 3) + lax.shift_left(off, 2)
+        where[d] = code + lax.shift_left(at, 5)
+    passes[0] = jnp.max(most) + 1
+    new[...] = coarse_step(
+        table, where, passes[0], data, own, rhs[...], dia[...], gather
+    )
 
 
 def gathered(table, pieces, mine):
@@ -331,10 +389,10 @@
     table[...] = jnp.transpose(mine[...])
 
 
-def coarse_kernel(me_ref, p0, p1, p2, rhs, dia, where, data, new, correction,
+def coarse_kernel(me_ref, passes, p0, p1, p2, rhs, dia, where, data, new, correction,
                   table, mine, gather):
     gathered(table, (p0, p1, p2), mine)
-    got = coarse_step(table, where, data, p0[...], rhs[...], dia[...], gather)
+    got = coarse_step(table, where, passes[0], data, p0[...], rhs[...], dia[...], gather)
     new[...] = got
     mine[0:PEERS, :] = got
     me = me_ref[0]
@@ -375,31 +433,27 @@
     sweep_halo(two, one, rhs, dia, before, base, WIDE - HALO)
     sweep_halo(two, one, rhs, dia, after, base, WIDE + ROWS)
 
-    def first(b, carry):
+    def first(b):
         at = WIDE + b * LANES
         pull = own_block(one, col, blk, base, b)
         two[:, lanes(at)] = smoothed(one, pull, rhs, dia, at)
-        return carry
-
-    def second(b, carry):
+
+    def second(b):
         at = WIDE + b * LANES
         pull = own_block(two, col, blk, base, b)
         out[:, lanes(b * LANES)] = smoothed(two, pull, rhs, dia, at)
-        return carry
-
-    lax.fori_loop(0, BLOCKS, first, 0)
-    lax.fori_loop(0, BLOCKS, second, 0)
-
-
-def call(kernel, outs, args, scratch=(), scalar=False):
+
+    each_block(first)
+    each_block(second)
+
+
+def call(kernel, outs, args, scratch=(), scalars=0, scalar_outs=0):
     vmem = pl.BlockSpec(memory_space=pltpu.VMEM)
-    specs = [vmem] * len(args)
-    if scalar:
-        specs[0] = pl.BlockSpec(memory_space=pltpu.SMEM)
+    smem = pl.BlockSpec(memory_space=pltpu.SMEM)
     return pl.pallas_call(
         kernel,
-        in_specs=specs,
-        out_specs=[vmem] * len(outs),
+        in_specs=[smem] * scalars + [vmem] * (len(args) - scalars),
+        out_specs=[vmem] * (len(outs) - scalar_outs) + [smem] * scalar_outs,
         out_shape=[jax.ShapeDtypeStruct(o, t) for o, t in outs],
         scratch_shapes=[
             pltpu.VMEM(*s) if isinstance(s[0], tuple) else pltpu.VMEM(s, f32) for s in scratch
@@ -456,31 +510,31 @@
         [((LANES, 2, LANES), f32), ((3, wide), f32), ((3, wide), f32), ((3, wide), f32),
          ((3, HALO), f32), ((3, HALO), f32)],
         [base, rhs, dia, col, blk, agg, owner, cdia, before, after],
-        scratch=[(3, wide), (3, wide), (8, ROWS)], scalar=True,
+        scratch=[(3, wide), (3, wide), (8, ROWS)], scalars=1,
     )
     before2, after2 = shifts(up2, down2)
     sums = lax.all_to_all(send, DOM, 0, 0, tiled=True)
     peers = ((PEERS, LANES), f32)
     gather = (3, PEERS, LANES)
     square = (LANES, LANES)
-    new, crhs, cd, where = call(
+    new, crhs, cd, where, passes = call(
         coarse_first_kernel,
-        [peers, peers, peers, ((PEERS, 8, LANES), i32)],
+        [peers, peers, peers, ((PEERS, 8, LANES), i32), ((1,), i32)],
         [me, sums, data, before2, after2],
         scratch=[square, gather, ((288, 4096), jnp.bfloat16), ((LANES, 4096), jnp.bfloat16)],
-        scalar=True,
+        scalars=1, scalar_outs=1,
     )
     for _ in range(CSWEEPS - 2):
         new, mine = call(
             coarse_kernel, [peers, ((3, 32), f32)],
-            [me, *in_group(new), crhs, cd, where, data],
-            scratch=[square, square, gather], scalar=True,
+            [me, passes, *in_group(new), crhs, cd, where, data],
+            scratch=[square, square, gather], scalars=2,
         )
     solution, = call(
         post_kernel, [((3, ROWS), f32)],
         [base, *in_group(new), first_iter, wrhs, wdia, col, blk, node_row,
          before, after, before2, after2],
-        scratch=[square, square, (3, wide), (3, wide)], scalar=True,
+        scratch=[square, square, (3, wide), (3, wide)], scalars=1,
     )
     return solution.T, mine.T
 

time: 126 us -> 120 us (0.952)
  Pallas kernels: 33 us -> 25.2 us
  starting transfers between devices: 31.5 us -> 39 us
  waiting for transfers between devices: 53.6 us -> 47.5 us
    pallas_call x8, Pallas kernels: 32.6 us -> 24.8 us  [call(): pl.pallas_call(kernel, in_specs=[smem] * scalars + [vmem] * (len(args) -...]
    ppermute x5, starting transfers between devices: 3.34 us -> 10.9 us  [in_group(): p2 = lax.ppermute(a, 'dom_4', swap)]
    ppermute x5, waiting for transfers between devices: 16.2 us -> 10.4 us  [in_group(): p2 = lax.ppermute(a, 'dom_4', swap)]
where the time goes in v6:
time: 120 us; the launch traced here: 119 us
  waiting for transfers between devices  47.5 us (40%)
  starting transfers between devices  39 us (32%)
  Pallas kernels  25.2 us (21%)
  local copies, waits for them, and re-layouts  6.07 us (5%)
    pallas_call x8, Pallas kernels, call(): pl.pallas_call(kernel, in_specs=[smem] * scalars + [vmem] * (len(args) -...  24.8 us
    all_to_all x1, starting transfers between devices, cycle(): sums = lax.all_to_all(send, DOM, 0, 0, tiled=True)  18 us
    all_to_all x1, waiting for transfers between devices, cycle(): data = lax.all_to_all(dsend, OTHERS, 0, 0, tiled=True)  16.7 us
    ppermute x5, starting transfers between devices, in_group(): p2 = lax.ppermute(a, 'dom_4', swap)  10.9 us
    ppermute x5, waiting for transfers between devices, in_group(): p2 = lax.ppermute(a, 'dom_4', swap)  10.4 us
    all_to_all x1, waiting for transfers between devices, cycle(): sums = lax.all_to_all(send, DOM, 0, 0, tiled=True)  7.83 us
    ppermute x4, waiting for transfers between devices, shifts(): return (lax.ppermute(up, DOM, forward), lax.ppermute(down, DOM, backward))  6.69 us
    unnamed x30, local copies, waits for them, and re-layouts  6.07 us
  transfers between devices with their start and end apart: 16, of which 14 were waited for; matrix products, arithmetic and copies ran while one was open for 0% of the time, Pallas kernels for 0%

profile of v6, /device:TPU:0, one launch (start us, length us, event | category | flops | bytes accessed | tf_op | source)
XLA Modules:
  0.0 118.6 jit_solution(9605011051779971741)
XLA Ops:
  0.7 1.3 %copy-done = f32[1024,27,3,3]{0,1,3,2:T(8,128)S(1)} copy-done((f32[1024,27,3,3]{0,1,3,2:T(8,128)S(1)}, f32[1024,27,3,3]{0,1,3,2:T(8,128)}, u32[]{:S(2)}) %copy-start) | copy-done | bytes 995352
  1.9 0.9 copy-done.3
  2.8 0.7 copy-done.6
  3.6 0.7 copy-done.8
  4.3 0.7 copy-done.11
  5.0 0.7 copy-done.14
  5.6 0.4 pack.1
  6.0 0.0 copy-start.5
  6.0 0.0 copy-start.10
  6.1 1.4 %collective-permute-start = (f32[288,256]{1,0:T(8,128)S(1)}, f32[288,256]{1,0:T(8,128)S(1)}, u32[]{:S(2)}, u32[]{:S(2)}) collective-permute-start(f32[288,256]{1,0:T(8,128)S(1)} %get-tuple-element.21), channel_id=1, source_target_pairs={{0,1},{1,2},{2,3},{3,4},{4,5},{5,6},{6,7},{7,8},{8,9},{9,10},{10,1... | collective-permute-start | bytes 884744 | tf_op jit(solution)/shard_map/ppermute | solution.py:477
  7.5 1.3 %collective-permute-start.1 = (f32[288,256]{1,0:T(8,128)S(1)}, f32[288,256]{1,0:T(8,128)S(1)}, u32[]{:S(2)}, u32[]{:S(2)}) collective-permute-start(f32[288,256]{1,0:T(8,128)S(1)} %get-tuple-element.22), channel_id=1, source_target_pairs={{1,0},{2,1},{3,2},{4,3},{5,4},{6,5},{7,6},{8,7},{9,8},{10,9},{11,1... | collective-permute-start | bytes 884744 | tf_op jit(solution)/shard_map/ppermute | solution.py:477
  8.8 0.0 collective-permute-done.before
  8.8 4.0 %collective-permute-done.1.after = f32[288,256]{1,0:T(8,128)S(1)} collective-permute-done((f32[288,256]{1,0:T(8,128)S(1)}, f32[288,256]{1,0:T(8,128)S(1)}, u32[]{:S(2)}, u32[]{:S(2)}) %collective-permute-start.1) | collective-permute-done | bytes 294944 | tf_op jit(solution)/shard_map/ppermute | solution.py:477
  12.8 3.6 %shard_map.104 = (f32[128,2,128]{2,1,0:T(2,128)}, f32[3,2048]{1,0:T(4,128)S(1)}, f32[3,2048]{1,0:T(4,128)S(1)}, f32[3,2048]{1,0:T(4,128)S(1)}, f32[3,256]{1,0:T(4,128)S(1)}, /*index=5*/f32[3,256]{1,0:T(4,128)S(1)}) custom-call(s32[1]{0:T(128)S(6)} %mul.23.base_ref, f32[3,1024]{1,0:T(4,128)S(1)} %bitcast.19, f32[3,1024]{1,0:T(4,128)S(1)} %bitcast.21, ...), custom_call_target="tpu_custom_call" | custom-call | tf_op jit(solution)/shard_map/pallas_call | solution.py:453
  16.5 18.0 %all-to-all-start = ((f32[128,2,128]{2,1,0:T(2,128)}), f32[128,2,128]{2,1,0:T(2,128)S(1)}, u32[]{:S(2)}, u32[]{:S(2)}) async-start(f32[128,2,128]{2,1,0:T(2,128)} %get-tuple-element.23), calls=%async_computation | async-start | bytes 262144 | tf_op jit(solution)/shard_map/all_to_all | solution.py:516
  34.5 0.4 shard_map.105
  35.0 1.1 copy-done.2
  36.0 7.8 %all-to-all-done.sums = f32[128,2,128]{2,1,0:T(2,128)S(1)} async-done(((f32[128,2,128]{2,1,0:T(2,128)}), f32[128,2,128]{2,1,0:T(2,128)S(1)}, u32[]{:S(2)}, u32[]{:S(2)}) %all-to-all-start) | async-done | bytes 131104 | tf_op jit(solution)/shard_map/all_to_all | solution.py:516
  43.9 4.5 %all-to-all-start.1 = ((f32[32,80,128]{2,1,0:T(8,128)}), f32[32,80,128]{2,1,0:T(8,128)S(1)}, u32[]{:S(2)}, u32[]{:S(2)}) async-start(f32[32,80,128]{2,1,0:T(8,128)} %copy-done.2), calls=%async_computation.1 | async-start | bytes 2621440 | tf_op jit(solution)/shard_map/all_to_all | solution.py:492
  48.4 1.5 %collective-permute-start.2 = (f32[3,256]{1,0:T(4,128)S(1)}, f32[3,256]{1,0:T(4,128)S(1)}, u32[]{:S(2)}, u32[]{:S(2)}) collective-permute-start(f32[3,256]{1,0:T(4,128)S(1)} %get-tuple-element.24), channel_id=1, source_target_pairs={{0,1},{1,2},{2,3},{3,4},{4,5},{5,6},{6,7},{7,8},{8,9},{9,10},{10,1... | collective-permute-start | bytes 9224 | tf_op jit(solution)/shard_map/ppermute | solution.py:477
  49.9 1.3 %collective-permute-start.3 = (f32[3,256]{1,0:T(4,128)S(1)}, f32[3,256]{1,0:T(4,128)S(1)}, u32[]{:S(2)}, u32[]{:S(2)}) collective-permute-start(f32[3,256]{1,0:T(4,128)S(1)} %get-tuple-element.25), channel_id=1, source_target_pairs={{1,0},{2,1},{3,2},{4,3},{5,4},{6,5},{7,6},{8,7},{9,8},{10,9},{11,1... | collective-permute-start | bytes 9224 | tf_op jit(solution)/shard_map/ppermute | solution.py:477
  51.2 0.0 collective-permute-done.2.far_up.before2
  51.2 2.7 %collective-permute-done.3.far_down.after2 = f32[3,256]{1,0:T(4,128)S(1)} collective-permute-done((f32[3,256]{1,0:T(4,128)S(1)}, f32[3,256]{1,0:T(4,128)S(1)}, u32[]{:S(2)}, u32[]{:S(2)}) %collective-permute-start.3) | collective-permute-done | bytes 3104 | tf_op jit(solution)/shard_map/ppermute | solution.py:477
  53.9 16.7 %all-to-all-done.1.data = f32[32,80,128]{2,1,0:T(8,128)S(1)} async-done(((f32[32,80,128]{2,1,0:T(8,128)}), f32[32,80,128]{2,1,0:T(8,128)S(1)}, u32[]{:S(2)}, u32[]{:S(2)}) %all-to-all-start.1) | async-done | bytes 1310752 | tf_op jit(solution)/shard_map/all_to_all | solution.py:492
  70.6 3.9 %shard_map.106 = (f32[32,128]{1,0:T(8,128)S(1)}, f32[32,128]{1,0:T(8,128)S(1)}, f32[32,128]{1,0:T(8,128)S(1)}, s32[32,8,128]{2,1,0:T(8,128)S(1)}, s32[1]{0:T(128)}) custom-call(s32[1]{0:T(128)} %bitcast.me_ref, f32[128,2,128]{2,1,0:T(2,128)S(1)} %all-to-all-done.sums, f32[32,80,128]{2,1,0:T(8,128)S(1)} %all-to-all-done.1.data, ...), custom_call_target="tpu_custom_call" | custom-call | tf_op jit(solution)/shard_map/pallas_call | solution.py:453
  74.6 0.1 collective-permute-start.4
  74.6 1.2 collective-permute-done.4.p1
  75.8 1.3 %collective-permute-start.5 = (f32[64,128]{1,0:T(8,128)S(1)}, f32[64,128]{1,0:T(8,128)S(1)}, u32[]{:S(2)}, u32[]{:S(2)}) collective-permute-start(f32[64,128]{1,0:T(8,128)S(1)} %pad_maximum_fusion), channel_id=1, source_target_pairs={{0,2},{2,0},{1,3},{3,1},{4,6},{6,4},{5,7},{7,5},{8,10},{10,8},{9,1... | collective-permute-start | bytes 98312 | tf_op jit(solution)/shard_map/ppermute | solution.py:469
  77.1 2.6 %collective-permute-done.5.p2 = f32[64,128]{1,0:T(8,128)S(1)} collective-permute-done((f32[64,128]{1,0:T(8,128)S(1)}, f32[64,128]{1,0:T(8,128)S(1)}, u32[]{:S(2)}, u32[]{:S(2)}) %collective-permute-start.5) | collective-permute-done | bytes 32800 | tf_op jit(solution)/shard_map/ppermute | solution.py:469
  79.7 3.3 %shard_map.107 = (f32[32,128]{1,0:T(8,128)S(1)}, f32[3,32]{1,0:T(4,128)}) custom-call(s32[1]{0:T(128)} %bitcast.me_ref, s32[1]{0:T(128)} %get-tuple-element.26.passes, f32[32,128]{1,0:T(8,128)S(1)} %get-tuple-element.27.p0, f32[32,128]{1,0:T(8,128)S(1)} %collective-permute-done.4.p1, f32[64,128]{1,0:T(8,128)S(1)} %collective-permute-done.5.p2, ...), custom_call_target="tpu_custom_call" | custom-call | tf_op jit(solution)/shard_map/pallas_call | solution.py:453
  83.1 0.0 collective-permute-start.6
  83.1 1.2 collective-permute-done.6.p1
  84.3 1.9 %collective-permute-start.7 = (f32[64,128]{1,0:T(8,128)S(1)}, f32[64,128]{1,0:T(8,128)S(1)}, u32[]{:S(2)}, u32[]{:S(2)}) collective-permute-start(f32[64,128]{1,0:T(8,128)S(1)} %pad_maximum_fusion.1), channel_id=1, source_target_pairs={{0,2},{2,0},{1,3},{3,1},{4,6},{6,4},{5,7},{7,5},{8,10},{10,8},{9,1... | collective-permute-start | bytes 98312 | tf_op jit(solution)/shard_map/ppermute | solution.py:469
  86.1 2.0 %collective-permute-done.7.p2 = f32[64,128]{1,0:T(8,128)S(1)} collective-permute-done((f32[64,128]{1,0:T(8,128)S(1)}, f32[64,128]{1,0:T(8,128)S(1)}, u32[]{:S(2)}, u32[]{:S(2)}) %collective-permute-start.7) | collective-permute-done | bytes 32800 | tf_op jit(solution)/shard_map/ppermute | solution.py:469
  88.2 3.3 %shard_map.108 = (f32[32,128]{1,0:T(8,128)S(1)}, f32[3,32]{1,0:T(4,128)}) custom-call(s32[1]{0:T(128)} %bitcast.me_ref, s32[1]{0:T(128)} %get-tuple-element.26.passes, f32[32,128]{1,0:T(8,128)S(1)} %get-tuple-element.31.p0, f32[32,128]{1,0:T(8,128)S(1)} %collective-permute-done.6.p1, f32[64,128]{1,0:T(8,128)S(1)} %collective-permute-done.7.p2, ...), custom_call_target="tpu_custom_call" | custom-call | tf_op jit(solution)/shard_map/pallas_call | solution.py:453
  91.5 0.0 collective-permute-start.8
  91.5 1.2 collective-permute-done.8.p1
  92.7 2.5 %collective-permute-start.9 = (f32[64,128]{1,0:T(8,128)S(1)}, f32[64,128]{1,0:T(8,128)S(1)}, u32[]{:S(2)}, u32[]{:S(2)}) collective-permute-start(f32[64,128]{1,0:T(8,128)S(1)} %pad_maximum_fusion.2), channel_id=1, source_target_pairs={{0,2},{2,0},{1,3},{3,1},{4,6},{6,4},{5,7},{7,5},{8,10},{10,8},{9,1... | collective-permute-start | bytes 98312 | tf_op jit(solution)/shard_map/ppermute | solution.py:469
  95.2 1.9 %collective-permute-done.9.p2 = f32[64,128]{1,0:T(8,128)S(1)} collective-permute-done((f32[64,128]{1,0:T(8,128)S(1)}, f32[64,128]{1,0:T(8,128)S(1)}, u32[]{:S(2)}, u32[]{:S(2)}) %collective-permute-start.9) | collective-permute-done | bytes 32800 | tf_op jit(solution)/shard_map/ppermute | solution.py:469
  97.1 3.3 %shard_map.109 = (f32[32,128]{1,0:T(8,128)S(1)}, f32[3,32]{1,0:T(4,128)}) custom-call(s32[1]{0:T(128)} %bitcast.me_ref, s32[1]{0:T(128)} %get-tuple-element.26.passes, f32[32,128]{1,0:T(8,128)S(1)} %get-tuple-element.32.p0, f32[32,128]{1,0:T(8,128)S(1)} %collective-permute-done.8.p1, f32[64,128]{1,0:T(8,128)S(1)} %collective-permute-done.9.p2, ...), custom_call_target="tpu_custom_call" | custom-call | tf_op jit(solution)/shard_map/pallas_call | solution.py:453
  100.4 1.2 collective-permute-done.10.p1
  101.6 2.6 %collective-permute-start.11 = (f32[64,128]{1,0:T(8,128)S(1)}, f32[64,128]{1,0:T(8,128)S(1)}, u32[]{:S(2)}, u32[]{:S(2)}) collective-permute-start(f32[64,128]{1,0:T(8,128)S(1)} %pad_maximum_fusion.3), channel_id=1, source_target_pairs={{0,2},{2,0},{1,3},{3,1},{4,6},{6,4},{5,7},{7,5},{8,10},{10,8},{9,1... | collective-permute-start | bytes 98312 | tf_op jit(solution)/shard_map/ppermute | solution.py:469
  104.2 1.9 %collective-permute-done.11.p2 = f32[64,128]{1,0:T(8,128)S(1)} collective-permute-done((f32[64,128]{1,0:T(8,128)S(1)}, f32[64,128]{1,0:T(8,128)S(1)}, u32[]{:S(2)}, u32[]{:S(2)}) %collective-permute-start.11) | collective-permute-done | bytes 32800 | tf_op jit(solution)/shard_map/ppermute | solution.py:469
  106.1 3.3 %shard_map.110 = (f32[32,128]{1,0:T(8,128)S(1)}, f32[3,32]{1,0:T(4,128)}) custom-call(s32[1]{0:T(128)} %bitcast.me_ref, s32[1]{0:T(128)} %get-tuple-element.26.passes, f32[32,128]{1,0:T(8,128)S(1)} %get-tuple-element.33.p0, f32[32,128]{1,0:T(8,128)S(1)} %collective-permute-done.10.p1, f32[64,128]{1,0:T(8,128)S(1)} %collective-permute-done.11.p2, ...), custom_call_target="tpu_custom_call" | custom-call | tf_op jit(solution)/shard_map/pallas_call | solution.py:453
  109.4 1.2 collective-permute-done.12.p1
  110.6 2.6 %collective-permute-start.13 = (f32[64,128]{1,0:T(8,128)S(1)}, f32[64,128]{1,0:T(8,128)S(1)}, u32[]{:S(2)}, u32[]{:S(2)}) collective-permute-start(f32[64,128]{1,0:T(8,128)S(1)} %pad_maximum_fusion.4), channel_id=1, source_target_pairs={{0,2},{2,0},{1,3},{3,1},{4,6},{6,4},{5,7},{7,5},{8,10},{10,8},{9,1... | collective-permute-start | bytes 98312 | tf_op jit(solution)/shard_map/ppermute | solution.py:469
  113.2 1.9 %collective-permute-done.13.p2 = f32[64,128]{1,0:T(8,128)S(1)} collective-permute-done((f32[64,128]{1,0:T(8,128)S(1)}, f32[64,128]{1,0:T(8,128)S(1)}, u32[]{:S(2)}, u32[]{:S(2)}) %collective-permute-start.13) | collective-permute-done | bytes 32800 | tf_op jit(solution)/shard_map/ppermute | solution.py:469
  115.1 3.5 %shard_map.111 = f32[3,1024]{1,0:T(4,128)} custom-call(s32[1]{0:T(128)S(6)} %mul.23.base_ref, f32[32,128]{1,0:T(8,128)S(1)} %get-tuple-element.34.p0, f32[32,128]{1,0:T(8,128)S(1)} %collective-permute-done.12.p1, f32[64,128]{1,0:T(8,128)S(1)} %collective-permute-done.13.p2, f32[3,2048]{1,0:T(4,128)S(1)} %get-tuple-element.35.first_iter, ...), custom_call_target="tpu_custom_call" | custom-call | tf_op jit(solution)/shard_map/pallas_call | solution.py:453
  (28 shorter events, 0.1 us)
Async XLA Ops:
  0.6 12.2 %copy-start.12 = (s32[1024]{0:T(1024)S(1)}, s32[1024]{0:T(1024)}, u32[]{:S(2)}) copy-start(s32[1024]{0:T(1024)} %param.13) | copy-start | bytes 12292
  0.6 12.2 %copy-start.13 = (f32[32,3]{0,1:T(4,128)S(1)}, f32[32,3]{0,1:T(4,128)}, u32[]{:S(2)}) copy-start(f32[32,3]{0,1:T(4,128)} %param.15) | copy-start | bytes 1156
  0.7 1.3 %copy-start = (f32[1024,27,3,3]{0,1,3,2:T(8,128)S(1)}, f32[1024,27,3,3]{0,1,3,2:T(8,128)}, u32[]{:S(2)}) copy-start(f32[1024,27,3,3]{0,1,3,2:T(8,128)} %param.12) | copy-start | bytes 2985988
  1.9 0.9 copy-start.3
  2.8 0.7 copy-start.6
  3.6 0.7 copy-start.8
  4.3 0.7 copy-start.11
  5.0 0.7 copy-start.14
  5.6 7.2 %copy-start.1 = (f32[1024,27,3,3]{0,1,3,2:T(8,128)S(1)}, f32[1024,27,3,3]{0,1,3,2:T(8,128)}, u32[]{:S(2)}) copy-start(f32[1024,27,3,3]{0,1,3,2:T(8,128)} %param.12) | copy-start | bytes 2985988
  5.6 7.2 %copy-start.4 = (s32[1024,27]{0,1:T(8,128)S(1)}, s32[1024,27]{0,1:T(8,128)}, u32[]{:S(2)}) copy-start(s32[1024,27]{0,1:T(8,128)} %param.11) | copy-start | bytes 331780
  5.6 7.2 %copy-start.7 = (f32[1024,3]{0,1:T(4,128)S(1)}, f32[1024,3]{0,1:T(4,128)}, u32[]{:S(2)}) copy-start(f32[1024,3]{0,1:T(4,128)} %param.9) | copy-start | bytes 36868
  5.6 7.2 %copy-start.9 = (f32[1024,3]{0,1:T(4,128)S(1)}, f32[1024,3]{0,1:T(4,128)}, u32[]{:S(2)}) copy-start(f32[1024,3]{0,1:T(4,128)} %param.10) | copy-start | bytes 36868
  6.0 28.5 %copy-start.5 = (f32[32,27,3,3]{1,0,3,2:T(8,128)S(1)}, f32[32,27,3,3]{1,0,3,2:T(8,128)}, u32[]{:S(2)}) copy-start(f32[32,27,3,3]{1,0,3,2:T(8,128)} %param.17) | copy-start | bytes 93316
  6.0 28.5 %copy-start.10 = (s32[32,27]{1,0:T(8,128)S(1)}, s32[32,27]{1,0:T(8,128)}, u32[]{:S(2)}) copy-start(s32[32,27]{1,0:T(8,128)} %col.1) | copy-start | bytes 10372
  6.1 2.8 %collective-permute-start = (f32[288,256]{1,0:T(8,128)S(1)}, f32[288,256]{1,0:T(8,128)S(1)}, u32[]{:S(2)}, u32[]{:S(2)}) collective-permute-start(f32[288,256]{1,0:T(8,128)S(1)} %get-tuple-element.21), channel_id=1, source_target_pairs={{0,1},{1,2},{2,3},{3,4},{4,5},{5,6},{6,7},{7,8},{8,9},{9,10},{10,1... | collective-permute-start | bytes 884744 | tf_op jit(solution)/shard_map/ppermute | solution.py:477
  7.5 5.3 %collective-permute-start.1 = (f32[288,256]{1,0:T(8,128)S(1)}, f32[288,256]{1,0:T(8,128)S(1)}, u32[]{:S(2)}, u32[]{:S(2)}) collective-permute-start(f32[288,256]{1,0:T(8,128)S(1)} %get-tuple-element.22), channel_id=1, source_target_pairs={{1,0},{2,1},{3,2},{4,3},{5,4},{6,5},{7,6},{8,7},{9,8},{10,9},{11,1... | collective-permute-start | bytes 884744 | tf_op jit(solution)/shard_map/ppermute | solution.py:477
  16.5 27.4 %all-to-all-start = ((f32[128,2,128]{2,1,0:T(2,128)}), f32[128,2,128]{2,1,0:T(2,128)S(1)}, u32[]{:S(2)}, u32[]{:S(2)}) async-start(f32[128,2,128]{2,1,0:T(2,128)} %get-tuple-element.23), calls=%async_computation | async-start | bytes 262144 | tf_op jit(solution)/shard_map/all_to_all | solution.py:516
  34.9 1.1 copy-start.2
  43.9 26.7 %all-to-all-start.1 = ((f32[32,80,128]{2,1,0:T(8,128)}), f32[32,80,128]{2,1,0:T(8,128)S(1)}, u32[]{:S(2)}, u32[]{:S(2)}) async-start(f32[32,80,128]{2,1,0:T(8,128)} %copy-done.2), calls=%async_computation.1 | async-start | bytes 2621440 | tf_op jit(solution)/shard_map/all_to_all | solution.py:492
  48.4 2.8 %collective-permute-start.2 = (f32[3,256]{1,0:T(4,128)S(1)}, f32[3,256]{1,0:T(4,128)S(1)}, u32[]{:S(2)}, u32[]{:S(2)}) collective-permute-start(f32[3,256]{1,0:T(4,128)S(1)} %get-tuple-element.24), channel_id=1, source_target_pairs={{0,1},{1,2},{2,3},{3,4},{4,5},{5,6},{6,7},{7,8},{8,9},{9,10},{10,1... | collective-permute-start | bytes 9224 | tf_op jit(solution)/shard_map/ppermute | solution.py:477
  49.9 4.0 %collective-permute-start.3 = (f32[3,256]{1,0:T(4,128)S(1)}, f32[3,256]{1,0:T(4,128)S(1)}, u32[]{:S(2)}, u32[]{:S(2)}) collective-permute-start(f32[3,256]{1,0:T(4,128)S(1)} %get-tuple-element.25), channel_id=1, source_target_pairs={{1,0},{2,1},{3,2},{4,3},{5,4},{6,5},{7,6},{8,7},{9,8},{10,9},{11,1... | collective-permute-start | bytes 9224 | tf_op jit(solution)/shard_map/ppermute | solution.py:477
  74.6 1.3 %collective-permute-start.4 = (f32[32,128]{1,0:T(8,128)S(1)}, f32[32,128]{1,0:T(8,128)S(1)}, u32[]{:S(2)}, u32[]{:S(2)}) collective-permute-start(f32[32,128]{1,0:T(8,128)S(1)} %get-tuple-element.27.p0), channel_id=1, source_target_pairs={{0,1},{1,0},{2,3},{3,2},{4,5},{5,4},{6,7},{7,6},{8,9},{9,8},{10,11... | collective-permute-start | bytes 49160 | tf_op jit(solution)/shard_map/ppermute | solution.py:467
  75.8 3.9 %collective-permute-start.5 = (f32[64,128]{1,0:T(8,128)S(1)}, f32[64,128]{1,0:T(8,128)S(1)}, u32[]{:S(2)}, u32[]{:S(2)}) collective-permute-start(f32[64,128]{1,0:T(8,128)S(1)} %pad_maximum_fusion), channel_id=1, source_target_pairs={{0,2},{2,0},{1,3},{3,1},{4,6},{6,4},{5,7},{7,5},{8,10},{10,8},{9,1... | collective-permute-start | bytes 98312 | tf_op jit(solution)/shard_map/ppermute | solution.py:469
  83.1 1.2 collective-permute-start.6
  84.3 3.9 %collective-permute-start.7 = (f32[64,128]{1,0:T(8,128)S(1)}, f32[64,128]{1,0:T(8,128)S(1)}, u32[]{:S(2)}, u32[]{:S(2)}) collective-permute-start(f32[64,128]{1,0:T(8,128)S(1)} %pad_maximum_fusion.1), channel_id=1, source_target_pairs={{0,2},{2,0},{1,3},{3,1},{4,6},{6,4},{5,7},{7,5},{8,10},{10,8},{9,1... | collective-permute-start | bytes 98312 | tf_op jit(solution)/shard_map/ppermute | solution.py:469
  91.5 1.2 collective-permute-start.8
  92.7 4.4 %collective-permute-start.9 = (f32[64,128]{1,0:T(8,128)S(1)}, f32[64,128]{1,0:T(8,128)S(1)}, u32[]{:S(2)}, u32[]{:S(2)}) collective-permute-start(f32[64,128]{1,0:T(8,128)S(1)} %pad_maximum_fusion.2), channel_id=1, source_target_pairs={{0,2},{2,0},{1,3},{3,1},{4,6},{6,4},{5,7},{7,5},{8,10},{10,8},{9,1... | collective-permute-start | bytes 98312 | tf_op jit(solution)/shard_map/ppermute | solution.py:469
  100.4 1.2 collective-permute-start.10
  101.6 4.5 %collective-permute-start.11 = (f32[64,128]{1,0:T(8,128)S(1)}, f32[64,128]{1,0:T(8,128)S(1)}, u32[]{:S(2)}, u32[]{:S(2)}) collective-permute-start(f32[64,128]{1,0:T(8,128)S(1)} %pad_maximum_fusion.3), channel_id=1, source_target_pairs={{0,2},{2,0},{1,3},{3,1},{4,6},{6,4},{5,7},{7,5},{8,10},{10,8},{9,1... | collective-permute-start | bytes 98312 | tf_op jit(solution)/shard_map/ppermute | solution.py:469
  109.4 1.2 collective-permute-start.12
  110.6 4.5 %collective-permute-start.13 = (f32[64,128]{1,0:T(8,128)S(1)}, f32[64,128]{1,0:T(8,128)S(1)}, u32[]{:S(2)}, u32[]{:S(2)}) collective-permute-start(f32[64,128]{1,0:T(8,128)S(1)} %pad_maximum_fusion.4), channel_id=1, source_target_pairs={{0,2},{2,0},{1,3},{3,1},{4,6},{6,4},{5,7},{7,5},{8,10},{10,8},{9,1... | collective-permute-start | bytes 98312 | tf_op jit(solution)/shard_map/ppermute | solution.py:469

commit v7 on v6

--- a/solution.py
+++ b/solution.py
@@ -325,9 +325,9 @@
     return slice(8 * m, 8 * m + 8)
 
 
-def coarse_first_kernel(me_ref, sums, data, far_up, far_down, new, rhs, dia, where, passes,
+def coarse_first_kernel(base_ref, sums, data, far_up, far_down, new, rhs, dia, where, passes,
                         table, gather, left, right):
-    me = me_ref[0]
+    me = lax.shift_right_logical(base_ref[0], 10)
     got = jnp.transpose(sums[:, 0, :])
     rows = got[96:128].astype(i32)
     s = got[0:96]
@@ -374,9 +374,10 @@
         at = lane_of_device(lax.shift_right_logical(c, 5), me)
         code = lax.bitwise_and(lax.shift_right_logical(c, 3), 3) + lax.shift_left(off, 2)
         where[d] = code + lax.shift_left(at, 5)
-    passes[0] = jnp.max(most) + 1
+    most = jnp.max(most.astype(f32)).astype(i32) + 1
+    passes[...] = jnp.broadcast_to(most, passes.shape)
     new[...] = coarse_step(
-        table, where, passes[0], data, own, rhs[...], dia[...], gather
+        table, where, most, data, own, rhs[...], dia[...], gather
     )
 
 
@@ -389,23 +390,20 @@
     table[...] = jnp.transpose(mine[...])
 
 
-def coarse_kernel(me_ref, passes, p0, p1, p2, rhs, dia, where, data, new, correction,
-                  table, mine, gather):
+def coarse_kernel(base_ref, passes, p0, p1, p2, rhs, dia, where, data, new, table, mine, gather):
     gathered(table, (p0, p1, p2), mine)
-    got = coarse_step(table, where, passes[0], data, p0[...], rhs[...], dia[...], gather)
-    new[...] = got
-    mine[0:PEERS, :] = got
-    me = me_ref[0]
-    at = lane_of_device(me, me)
-    row = mine[pl.ds(at, 1), :]
-    correction[...] = jnp.concatenate([row[:, 32 * i : 32 * i + 32] for i in range(3)], axis=0)
+    new[...] = coarse_step(
+        table, where, passes[...][0, 0], data, p0[...], rhs[...], dia[...], gather
+    )
 
 
 def post_kernel(base_ref, p0, p1, p2, first_iter, rhs, dia, col, blk, node_row, before, after,
-                before2, after2, out, table, mine, one, two):
+                before2, after2, out, correction, table, mine, one, two):
     base = base_ref[0]
     me = lax.shift_right_logical(base, 10)
     gathered(table, (p0, p1, p2), mine)
+    row = mine[pl.ds(lane_of_device(me, me), 1), :]
+    correction[...] = jnp.concatenate([row[:, 32 * i : 32 * i + 32] for i in range(3)], axis=0)
     one[...] = first_iter[...]
     one[:, lanes(0, HALO)] = before2[...]
     one[:, lanes(WIDE + ROWS + HALO, HALO)] = after2[...]
@@ -447,18 +445,18 @@
     each_block(second)
 
 
-def call(kernel, outs, args, scratch=(), scalars=0, scalar_outs=0):
+def call(kernel, outs, args, scratch=(), scalars=0, limit=12):
     vmem = pl.BlockSpec(memory_space=pltpu.VMEM)
     smem = pl.BlockSpec(memory_space=pltpu.SMEM)
     return pl.pallas_call(
         kernel,
         in_specs=[smem] * scalars + [vmem] * (len(args) - scalars),
-        out_specs=[vmem] * (len(outs) - scalar_outs) + [smem] * scalar_outs,
+        out_specs=[vmem] * len(outs),
         out_shape=[jax.ShapeDtypeStruct(o, t) for o, t in outs],
         scratch_shapes=[
             pltpu.VMEM(*s) if isinstance(s[0], tuple) else pltpu.VMEM(s, f32) for s in scratch
         ],
-        compiler_params=pltpu.CompilerParams(vmem_limit_bytes=12 * 2**20),
+        compiler_params=pltpu.CompilerParams(vmem_limit_bytes=limit * 2**20),
     )(*args)
 
 
@@ -488,7 +486,10 @@
     base = me * ROWS
     wide = WIDE + ROWS + WIDE
 
-    dsend, = call(coarse_pack_kernel, [((PEERS, 80, LANES), f32)], [coarse_columns, cblk])
+    dsend, = call(
+        coarse_pack_kernel, [((PEERS, 80, LANES), f32)], [coarse_columns, cblk],
+        limit=60,
+    )
     data = lax.all_to_all(dsend, OTHERS, 0, 0, tiled=True)
     vmem, far = pl.BlockSpec(memory_space=pltpu.VMEM), pl.BlockSpec(memory_space=pltpu.HBM)
     up, down, node_row = pl.pallas_call(
@@ -519,19 +520,19 @@
     square = (LANES, LANES)
     new, crhs, cd, where, passes = call(
         coarse_first_kernel,
-        [peers, peers, peers, ((PEERS, 8, LANES), i32), ((1,), i32)],
-        [me, sums, data, before2, after2],
+        [peers, peers, peers, ((PEERS, 8, LANES), i32), ((8, LANES), i32)],
+        [base, sums, data, before2, after2],
         scratch=[square, gather, ((288, 4096), jnp.bfloat16), ((LANES, 4096), jnp.bfloat16)],
-        scalars=1, scalar_outs=1,
+        scalars=1,
     )
     for _ in range(CSWEEPS - 2):
-        new, mine = call(
-            coarse_kernel, [peers, ((3, 32), f32)],
-            [me, passes, *in_group(new), crhs, cd, where, data],
-            scratch=[square, square, gather], scalars=2,
+        new, = call(
+            coarse_kernel, [peers],
+            [base, passes, *in_group(new), crhs, cd, where, data],
+            scratch=[square, square, gather], scalars=1,
         )
-    solution, = call(
-        post_kernel, [((3, ROWS), f32)],
+    solution, mine = call(
+        post_kernel, [((3, ROWS), f32), ((3, 32), f32)],
         [base, *in_group(new), first_iter, wrhs, wdia, col, blk, node_row,
          before, after, before2, after2],
         scratch=[square, square, (3, wide), (3, wide)], scalars=1,

time: 120 us -> 115 us (0.958)
  Pallas kernels: 25.2 us -> 21.8 us
    pallas_call x8, Pallas kernels: 24.8 us -> 21.4 us  [call(): pl.pallas_call(kernel, in_specs=[smem] * scalars + [vmem] * (len(args) -...]
    unnamed x30 -> x26, local copies, waits for them, and re-layouts: 6.07 us -> 4.99 us
  transfers between devices with their start and end apart: 16 -> 16, of which waited for: 14 -> 14; matrix products, arithmetic and copies ran while one was open for 0% -> 0% of each run, Pallas kernels for 0% -> 2%
where the time goes in v7:
time: 115 us; the launch traced here: 114 us
  waiting for transfers between devices  46.6 us (41%)
  starting transfers between devices  39.3 us (34%)
  Pallas kernels  21.8 us (19%)
  local copies, waits for them, and re-layouts  4.99 us (4%)
    pallas_call x8, Pallas kernels, call(): pl.pallas_call(kernel, in_specs=[smem] * scalars + [vmem] * (len(args) -...  21.4 us
    all_to_all x1, starting transfers between devices, cycle(): sums = lax.all_to_all(send, DOM, 0, 0, tiled=True)  18 us
    all_to_all x1, waiting for transfers between devices, cycle(): data = lax.all_to_all(dsend, OTHERS, 0, 0, tiled=True)  16.7 us
    ppermute x5, starting transfers between devices, in_group(): p2 = lax.ppermute(a, 'dom_4', swap)  10.8 us
    ppermute x5, waiting for transfers between devices, in_group(): p2 = lax.ppermute(a, 'dom_4', swap)  10.4 us
    all_to_all x1, waiting for transfers between devices, cycle(): sums = lax.all_to_all(send, DOM, 0, 0, tiled=True)  6.93 us
    ppermute x4, waiting for transfers between devices, shifts(): return (lax.ppermute(up, DOM, forward), lax.ppermute(down, DOM, backward))  6.67 us
    ppermute x5, waiting for transfers between devices, in_group(): p1 = lax.ppermute(new, 'dom_5', swap)  5.85 us
  transfers between devices with their start and end apart: 16, of which 14 were waited for; matrix products, arithmetic and copies ran while one was open for 0% of the time, Pallas kernels for 2%

profile of v7, /device:TPU:0, one launch (start us, length us, event | category | flops | bytes accessed | tf_op | source)
XLA Modules:
  0.0 113.5 jit_solution(1421557818698927448)
XLA Ops:
  0.7 1.3 %copy-done = f32[1024,27,3,3]{0,1,3,2:T(8,128)S(1)} copy-done((f32[1024,27,3,3]{0,1,3,2:T(8,128)S(1)}, f32[1024,27,3,3]{0,1,3,2:T(8,128)}, u32[]{:S(2)}) %copy-start) | copy-done | bytes 995352
  2.0 0.9 copy-done.2
  2.9 0.7 copy-done.4
  3.6 0.7 copy-done.6
  4.3 0.7 copy-done.8
  5.0 0.7 copy-done.11
  5.6 0.4 pack.1
  6.0 1.4 %collective-permute-start = (f32[288,256]{1,0:T(8,128)S(1)}, f32[288,256]{1,0:T(8,128)S(1)}, u32[]{:S(2)}, u32[]{:S(2)}) collective-permute-start(f32[288,256]{1,0:T(8,128)S(1)} %get-tuple-element.18), channel_id=1, source_target_pairs={{0,1},{1,2},{2,3},{3,4},{4,5},{5,6},{6,7},{7,8},{8,9},{9,10},{10,1... | collective-permute-start | bytes 884744 | tf_op jit(solution)/shard_map/ppermute | solution.py:475
  7.5 1.3 %collective-permute-start.1 = (f32[288,256]{1,0:T(8,128)S(1)}, f32[288,256]{1,0:T(8,128)S(1)}, u32[]{:S(2)}, u32[]{:S(2)}) collective-permute-start(f32[288,256]{1,0:T(8,128)S(1)} %get-tuple-element.19), channel_id=1, source_target_pairs={{1,0},{2,1},{3,2},{4,3},{5,4},{6,5},{7,6},{8,7},{9,8},{10,9},{11,1... | collective-permute-start | bytes 884744 | tf_op jit(solution)/shard_map/ppermute | solution.py:475
  8.8 0.0 collective-permute-done.before
  8.8 4.0 %collective-permute-done.1.after = f32[288,256]{1,0:T(8,128)S(1)} collective-permute-done((f32[288,256]{1,0:T(8,128)S(1)}, f32[288,256]{1,0:T(8,128)S(1)}, u32[]{:S(2)}, u32[]{:S(2)}) %collective-permute-start.1) | collective-permute-done | bytes 294944 | tf_op jit(solution)/shard_map/ppermute | solution.py:475
  12.8 0.0 copy-done.9
  12.8 3.6 %shard_map.104 = (f32[128,2,128]{2,1,0:T(2,128)}, f32[3,2048]{1,0:T(4,128)S(1)}, f32[3,2048]{1,0:T(4,128)S(1)}, f32[3,2048]{1,0:T(4,128)S(1)}, f32[3,256]{1,0:T(4,128)S(1)}, /*index=5*/f32[3,256]{1,0:T(4,128)S(1)}) custom-call(s32[1]{0:T(128)} %bitcast.base_ref, f32[3,1024]{1,0:T(4,128)S(1)} %bitcast.18, f32[3,1024]{1,0:T(4,128)S(1)} %bitcast.20, ...), custom_call_target="tpu_custom_call" | custom-call | tf_op jit(solution)/shard_map/pallas_call | solution.py:451
  16.5 18.0 %all-to-all-start = ((f32[128,2,128]{2,1,0:T(2,128)}), f32[128,2,128]{2,1,0:T(2,128)S(1)}, u32[]{:S(2)}, u32[]{:S(2)}) async-start(f32[128,2,128]{2,1,0:T(2,128)} %get-tuple-element.20), calls=%async_computation | async-start | bytes 262144 | tf_op jit(solution)/shard_map/all_to_all | solution.py:517
  34.5 2.4 %shard_map.105 = f32[32,80,128]{2,1,0:T(8,128)} custom-call(s32[32,27]{1,0:T(8,128)} %col.1, f32[3,3,32,27]{3,2,1,0:T(8,128)} %bitcast.26), custom_call_target="tpu_custom_call" | custom-call | tf_op jit(solution)/shard_map/pallas_call | solution.py:451
  36.9 6.9 %all-to-all-done.sums = f32[128,2,128]{2,1,0:T(2,128)S(1)} async-done(((f32[128,2,128]{2,1,0:T(2,128)}), f32[128,2,128]{2,1,0:T(2,128)S(1)}, u32[]{:S(2)}, u32[]{:S(2)}) %all-to-all-start) | async-done | bytes 131104 | tf_op jit(solution)/shard_map/all_to_all | solution.py:517
  43.9 4.5 %all-to-all-start.1 = ((f32[32,80,128]{2,1,0:T(8,128)}), f32[32,80,128]{2,1,0:T(8,128)S(1)}, u32[]{:S(2)}, u32[]{:S(2)}) async-start(f32[32,80,128]{2,1,0:T(8,128)} %shard_map.105), calls=%async_computation.1 | async-start | bytes 2621440 | tf_op jit(solution)/shard_map/all_to_all | solution.py:493
  48.4 1.5 %collective-permute-start.2 = (f32[3,256]{1,0:T(4,128)S(1)}, f32[3,256]{1,0:T(4,128)S(1)}, u32[]{:S(2)}, u32[]{:S(2)}) collective-permute-start(f32[3,256]{1,0:T(4,128)S(1)} %get-tuple-element.21), channel_id=1, source_target_pairs={{0,1},{1,2},{2,3},{3,4},{4,5},{5,6},{6,7},{7,8},{8,9},{9,10},{10,1... | collective-permute-start | bytes 9224 | tf_op jit(solution)/shard_map/ppermute | solution.py:475
  49.9 1.3 %collective-permute-start.3 = (f32[3,256]{1,0:T(4,128)S(1)}, f32[3,256]{1,0:T(4,128)S(1)}, u32[]{:S(2)}, u32[]{:S(2)}) collective-permute-start(f32[3,256]{1,0:T(4,128)S(1)} %get-tuple-element.22), channel_id=1, source_target_pairs={{1,0},{2,1},{3,2},{4,3},{5,4},{6,5},{7,6},{8,7},{9,8},{10,9},{11,1... | collective-permute-start | bytes 9224 | tf_op jit(solution)/shard_map/ppermute | solution.py:475
  51.2 0.0 collective-permute-done.2.far_up.before2
  51.2 2.7 %collective-permute-done.3.far_down.after2 = f32[3,256]{1,0:T(4,128)S(1)} collective-permute-done((f32[3,256]{1,0:T(4,128)S(1)}, f32[3,256]{1,0:T(4,128)S(1)}, u32[]{:S(2)}, u32[]{:S(2)}) %collective-permute-start.3) | collective-permute-done | bytes 3104 | tf_op jit(solution)/shard_map/ppermute | solution.py:475
  53.9 16.7 %all-to-all-done.1.data = f32[32,80,128]{2,1,0:T(8,128)S(1)} async-done(((f32[32,80,128]{2,1,0:T(8,128)}), f32[32,80,128]{2,1,0:T(8,128)S(1)}, u32[]{:S(2)}, u32[]{:S(2)}) %all-to-all-start.1) | async-done | bytes 1310752 | tf_op jit(solution)/shard_map/all_to_all | solution.py:493
  70.6 3.5 %shard_map.106 = (f32[32,128]{1,0:T(8,128)S(1)}, f32[32,128]{1,0:T(8,128)S(1)}, f32[32,128]{1,0:T(8,128)S(1)}, s32[32,8,128]{2,1,0:T(8,128)S(1)}, s32[8,128]{1,0:T(8,128)S(1)}) custom-call(s32[1]{0:T(128)} %bitcast.base_ref, f32[128,2,128]{2,1,0:T(2,128)S(1)} %all-to-all-done.sums, f32[32,80,128]{2,1,0:T(8,128)S(1)} %all-to-all-done.1.data, ...), custom_call_target="tpu_custom_call" | custom-call | tf_op jit(solution)/shard_map/pallas_call | solution.py:451
  74.2 0.1 collective-permute-start.4
  74.2 1.2 %collective-permute-done.4.p1 = f32[32,128]{1,0:T(8,128)S(1)} collective-permute-done((f32[32,128]{1,0:T(8,128)S(1)}, f32[32,128]{1,0:T(8,128)S(1)}, u32[]{:S(2)}, u32[]{:S(2)}) %collective-permute-start.4) | collective-permute-done | bytes 16416 | tf_op jit(solution)/shard_map/ppermute | solution.py:465
  75.4 1.3 %collective-permute-start.5 = (f32[64,128]{1,0:T(8,128)S(1)}, f32[64,128]{1,0:T(8,128)S(1)}, u32[]{:S(2)}, u32[]{:S(2)}) collective-permute-start(f32[64,128]{1,0:T(8,128)S(1)} %pad_maximum_fusion), channel_id=1, source_target_pairs={{0,2},{2,0},{1,3},{3,1},{4,6},{6,4},{5,7},{7,5},{8,10},{10,8},{9,1... | collective-permute-start | bytes 98312 | tf_op jit(solution)/shard_map/ppermute | solution.py:467
  76.7 2.7 %collective-permute-done.5.p2 = f32[64,128]{1,0:T(8,128)S(1)} collective-permute-done((f32[64,128]{1,0:T(8,128)S(1)}, f32[64,128]{1,0:T(8,128)S(1)}, u32[]{:S(2)}, u32[]{:S(2)}) %collective-permute-start.5) | collective-permute-done | bytes 32800 | tf_op jit(solution)/shard_map/ppermute | solution.py:467
  79.3 2.1 %shard_map.107.p0 = f32[32,128]{1,0:T(8,128)S(1)} custom-call(s32[1]{0:T(128)} %bitcast.base_ref, s32[8,128]{1,0:T(8,128)S(1)} %get-tuple-element.23.passes, f32[32,128]{1,0:T(8,128)S(1)} %get-tuple-element.24.p0, f32[32,128]{1,0:T(8,128)S(1)} %collective-permute-done.4.p1, f32[64,128]{1,0:T(8,128)S(1)} %collective-permute-done.5.p2, ...), custom_call_target="tpu_custom_call" | custom-call | tf_op jit(solution)/shard_map/pallas_call | solution.py:451
  81.4 0.1 collective-permute-start.6
  81.5 1.2 %collective-permute-done.6.p1 = f32[32,128]{1,0:T(8,128)S(1)} collective-permute-done((f32[32,128]{1,0:T(8,128)S(1)}, f32[32,128]{1,0:T(8,128)S(1)}, u32[]{:S(2)}, u32[]{:S(2)}) %collective-permute-start.6) | collective-permute-done | bytes 16416 | tf_op jit(solution)/shard_map/ppermute | solution.py:465
  82.7 1.9 %collective-permute-start.7 = (f32[64,128]{1,0:T(8,128)S(1)}, f32[64,128]{1,0:T(8,128)S(1)}, u32[]{:S(2)}, u32[]{:S(2)}) collective-permute-start(f32[64,128]{1,0:T(8,128)S(1)} %pad_maximum_fusion.1), channel_id=1, source_target_pairs={{0,2},{2,0},{1,3},{3,1},{4,6},{6,4},{5,7},{7,5},{8,10},{10,8},{9,1... | collective-permute-start | bytes 98312 | tf_op jit(solution)/shard_map/ppermute | solution.py:467
  84.5 2.1 %collective-permute-done.7.p2 = f32[64,128]{1,0:T(8,128)S(1)} collective-permute-done((f32[64,128]{1,0:T(8,128)S(1)}, f32[64,128]{1,0:T(8,128)S(1)}, u32[]{:S(2)}, u32[]{:S(2)}) %collective-permute-start.7) | collective-permute-done | bytes 32800 | tf_op jit(solution)/shard_map/ppermute | solution.py:467
  86.6 2.1 %shard_map.108.p0 = f32[32,128]{1,0:T(8,128)S(1)} custom-call(s32[1]{0:T(128)} %bitcast.base_ref, s32[8,128]{1,0:T(8,128)S(1)} %get-tuple-element.23.passes, f32[32,128]{1,0:T(8,128)S(1)} %shard_map.107.p0, f32[32,128]{1,0:T(8,128)S(1)} %collective-permute-done.6.p1, f32[64,128]{1,0:T(8,128)S(1)} %collective-permute-done.7.p2, ...), custom_call_target="tpu_custom_call" | custom-call | tf_op jit(solution)/shard_map/pallas_call | solution.py:451
  88.7 0.1 collective-permute-start.8
  88.8 1.2 %collective-permute-done.8.p1 = f32[32,128]{1,0:T(8,128)S(1)} collective-permute-done((f32[32,128]{1,0:T(8,128)S(1)}, f32[32,128]{1,0:T(8,128)S(1)}, u32[]{:S(2)}, u32[]{:S(2)}) %collective-permute-start.8) | collective-permute-done | bytes 16416 | tf_op jit(solution)/shard_map/ppermute | solution.py:465
  90.0 2.5 %collective-permute-start.9 = (f32[64,128]{1,0:T(8,128)S(1)}, f32[64,128]{1,0:T(8,128)S(1)}, u32[]{:S(2)}, u32[]{:S(2)}) collective-permute-start(f32[64,128]{1,0:T(8,128)S(1)} %pad_maximum_fusion.2), channel_id=1, source_target_pairs={{0,2},{2,0},{1,3},{3,1},{4,6},{6,4},{5,7},{7,5},{8,10},{10,8},{9,1... | collective-permute-start | bytes 98312 | tf_op jit(solution)/shard_map/ppermute | solution.py:467
  92.4 1.9 %collective-permute-done.9.p2 = f32[64,128]{1,0:T(8,128)S(1)} collective-permute-done((f32[64,128]{1,0:T(8,128)S(1)}, f32[64,128]{1,0:T(8,128)S(1)}, u32[]{:S(2)}, u32[]{:S(2)}) %collective-permute-start.9) | collective-permute-done | bytes 32800 | tf_op jit(solution)/shard_map/ppermute | solution.py:467
  94.3 2.1 %shard_map.109.p0 = f32[32,128]{1,0:T(8,128)S(1)} custom-call(s32[1]{0:T(128)} %bitcast.base_ref, s32[8,128]{1,0:T(8,128)S(1)} %get-tuple-element.23.passes, f32[32,128]{1,0:T(8,128)S(1)} %shard_map.108.p0, f32[32,128]{1,0:T(8,128)S(1)} %collective-permute-done.8.p1, f32[64,128]{1,0:T(8,128)S(1)} %collective-permute-done.9.p2, ...), custom_call_target="tpu_custom_call" | custom-call | tf_op jit(solution)/shard_map/pallas_call | solution.py:451
  96.4 0.1 collective-permute-start.10
  96.5 1.2 %collective-permute-done.10.p1 = f32[32,128]{1,0:T(8,128)S(1)} collective-permute-done((f32[32,128]{1,0:T(8,128)S(1)}, f32[32,128]{1,0:T(8,128)S(1)}, u32[]{:S(2)}, u32[]{:S(2)}) %collective-permute-start.10) | collective-permute-done | bytes 16416 | tf_op jit(solution)/shard_map/ppermute | solution.py:465
  97.7 2.6 %collective-permute-start.11 = (f32[64,128]{1,0:T(8,128)S(1)}, f32[64,128]{1,0:T(8,128)S(1)}, u32[]{:S(2)}, u32[]{:S(2)}) collective-permute-start(f32[64,128]{1,0:T(8,128)S(1)} %pad_maximum_fusion.3), channel_id=1, source_target_pairs={{0,2},{2,0},{1,3},{3,1},{4,6},{6,4},{5,7},{7,5},{8,10},{10,8},{9,1... | collective-permute-start | bytes 98312 | tf_op jit(solution)/shard_map/ppermute | solution.py:467
  100.3 1.9 %collective-permute-done.11.p2 = f32[64,128]{1,0:T(8,128)S(1)} collective-permute-done((f32[64,128]{1,0:T(8,128)S(1)}, f32[64,128]{1,0:T(8,128)S(1)}, u32[]{:S(2)}, u32[]{:S(2)}) %collective-permute-start.11) | collective-permute-done | bytes 32800 | tf_op jit(solution)/shard_map/ppermute | solution.py:467
  102.2 2.1 %shard_map.110.p0 = f32[32,128]{1,0:T(8,128)S(1)} custom-call(s32[1]{0:T(128)} %bitcast.base_ref, s32[8,128]{1,0:T(8,128)S(1)} %get-tuple-element.23.passes, f32[32,128]{1,0:T(8,128)S(1)} %shard_map.109.p0, f32[32,128]{1,0:T(8,128)S(1)} %collective-permute-done.10.p1, f32[64,128]{1,0:T(8,128)S(1)} %collective-permute-done.11.p2, ...), custom_call_target="tpu_custom_call" | custom-call | tf_op jit(solution)/shard_map/pallas_call | solution.py:451
  104.3 0.1 collective-permute-start.12
  104.4 1.2 %collective-permute-done.12.p1 = f32[32,128]{1,0:T(8,128)S(1)} collective-permute-done((f32[32,128]{1,0:T(8,128)S(1)}, f32[32,128]{1,0:T(8,128)S(1)}, u32[]{:S(2)}, u32[]{:S(2)}) %collective-permute-start.12) | collective-permute-done | bytes 16416 | tf_op jit(solution)/shard_map/ppermute | solution.py:465
  105.5 2.6 %collective-permute-start.13 = (f32[64,128]{1,0:T(8,128)S(1)}, f32[64,128]{1,0:T(8,128)S(1)}, u32[]{:S(2)}, u32[]{:S(2)}) collective-permute-start(f32[64,128]{1,0:T(8,128)S(1)} %pad_maximum_fusion.4), channel_id=1, source_target_pairs={{0,2},{2,0},{1,3},{3,1},{4,6},{6,4},{5,7},{7,5},{8,10},{10,8},{9,1... | collective-permute-start | bytes 98312 | tf_op jit(solution)/shard_map/ppermute | solution.py:467
  108.2 1.9 %collective-permute-done.13.p2 = f32[64,128]{1,0:T(8,128)S(1)} collective-permute-done((f32[64,128]{1,0:T(8,128)S(1)}, f32[64,128]{1,0:T(8,128)S(1)}, u32[]{:S(2)}, u32[]{:S(2)}) %collective-permute-start.13) | collective-permute-done | bytes 32800 | tf_op jit(solution)/shard_map/ppermute | solution.py:467
  110.1 3.5 %shard_map.111 = (f32[3,1024]{1,0:T(4,128)}, f32[3,32]{1,0:T(4,128)}) custom-call(s32[1]{0:T(128)} %bitcast.base_ref, f32[32,128]{1,0:T(8,128)S(1)} %shard_map.110.p0, f32[32,128]{1,0:T(8,128)S(1)} %collective-permute-done.12.p1, f32[64,128]{1,0:T(8,128)S(1)} %collective-permute-done.13.p2, f32[3,2048]{1,0:T(4,128)S(1)} %get-tuple-element.28.first_iter, ...), custom_call_target="tpu_custom_call" | custom-call | tf_op jit(solution)/shard_map/pallas_call | solution.py:451
  (24 shorter events, 0.1 us)
Async XLA Ops:
  0.6 12.2 %copy-start.12 = (s32[32]{0:T(128)S(1)}, s32[32]{0:T(128)}, u32[]{:S(2)}) copy-start(s32[32]{0:T(128)} %param.14) | copy-start | bytes 388
  0.6 12.2 %copy-start.9 = (s32[1024]{0:T(1024)S(1)}, s32[1024]{0:T(1024)}, u32[]{:S(2)}) copy-start(s32[1024]{0:T(1024)} %param.13) | copy-start | bytes 12292
  0.7 12.1 %copy-start.10 = (f32[32,3]{0,1:T(4,128)S(1)}, f32[32,3]{0,1:T(4,128)}, u32[]{:S(2)}) copy-start(f32[32,3]{0,1:T(4,128)} %param.15) | copy-start | bytes 1156
  0.7 1.3 %copy-start = (f32[1024,27,3,3]{0,1,3,2:T(8,128)S(1)}, f32[1024,27,3,3]{0,1,3,2:T(8,128)}, u32[]{:S(2)}) copy-start(f32[1024,27,3,3]{0,1,3,2:T(8,128)} %param.12) | copy-start | bytes 2985988
  2.0 0.9 copy-start.2
  2.9 0.7 copy-start.4
  3.6 0.7 copy-start.6
  4.3 0.7 copy-start.8
  5.0 0.7 copy-start.11
  5.6 7.2 %copy-start.1 = (f32[1024,27,3,3]{0,1,3,2:T(8,128)S(1)}, f32[1024,27,3,3]{0,1,3,2:T(8,128)}, u32[]{:S(2)}) copy-start(f32[1024,27,3,3]{0,1,3,2:T(8,128)} %param.12) | copy-start | bytes 2985988
  5.6 7.2 %copy-start.3 = (s32[1024,27]{0,1:T(8,128)S(1)}, s32[1024,27]{0,1:T(8,128)}, u32[]{:S(2)}) copy-start(s32[1024,27]{0,1:T(8,128)} %param.11) | copy-start | bytes 331780
  5.6 7.2 %copy-start.5 = (f32[1024,3]{0,1:T(4,128)S(1)}, f32[1024,3]{0,1:T(4,128)}, u32[]{:S(2)}) copy-start(f32[1024,3]{0,1:T(4,128)} %param.9) | copy-start | bytes 36868
  5.6 7.2 %copy-start.7 = (f32[1024,3]{0,1:T(4,128)S(1)}, f32[1024,3]{0,1:T(4,128)}, u32[]{:S(2)}) copy-start(f32[1024,3]{0,1:T(4,128)} %param.10) | copy-start | bytes 36868
  6.0 2.8 %collective-permute-start = (f32[288,256]{1,0:T(8,128)S(1)}, f32[288,256]{1,0:T(8,128)S(1)}, u32[]{:S(2)}, u32[]{:S(2)}) collective-permute-start(f32[288,256]{1,0:T(8,128)S(1)} %get-tuple-element.18), channel_id=1, source_target_pairs={{0,1},{1,2},{2,3},{3,4},{4,5},{5,6},{6,7},{7,8},{8,9},{9,10},{10,1... | collective-permute-start | bytes 884744 | tf_op jit(solution)/shard_map/ppermute | solution.py:475
  7.5 5.3 %collective-permute-start.1 = (f32[288,256]{1,0:T(8,128)S(1)}, f32[288,256]{1,0:T(8,128)S(1)}, u32[]{:S(2)}, u32[]{:S(2)}) collective-permute-start(f32[288,256]{1,0:T(8,128)S(1)} %get-tuple-element.19), channel_id=1, source_target_pairs={{1,0},{2,1},{3,2},{4,3},{5,4},{6,5},{7,6},{8,7},{9,8},{10,9},{11,1... | collective-permute-start | bytes 884744 | tf_op jit(solution)/shard_map/ppermute | solution.py:475
  16.5 27.4 %all-to-all-start = ((f32[128,2,128]{2,1,0:T(2,128)}), f32[128,2,128]{2,1,0:T(2,128)S(1)}, u32[]{:S(2)}, u32[]{:S(2)}) async-start(f32[128,2,128]{2,1,0:T(2,128)} %get-tuple-element.20), calls=%async_computation | async-start | bytes 262144 | tf_op jit(solution)/shard_map/all_to_all | solution.py:517
  43.9 26.8 %all-to-all-start.1 = ((f32[32,80,128]{2,1,0:T(8,128)}), f32[32,80,128]{2,1,0:T(8,128)S(1)}, u32[]{:S(2)}, u32[]{:S(2)}) async-start(f32[32,80,128]{2,1,0:T(8,128)} %shard_map.105), calls=%async_computation.1 | async-start | bytes 2621440 | tf_op jit(solution)/shard_map/all_to_all | solution.py:493
  48.4 2.8 %collective-permute-start.2 = (f32[3,256]{1,0:T(4,128)S(1)}, f32[3,256]{1,0:T(4,128)S(1)}, u32[]{:S(2)}, u32[]{:S(2)}) collective-permute-start(f32[3,256]{1,0:T(4,128)S(1)} %get-tuple-element.21), channel_id=1, source_target_pairs={{0,1},{1,2},{2,3},{3,4},{4,5},{5,6},{6,7},{7,8},{8,9},{9,10},{10,1... | collective-permute-start | bytes 9224 | tf_op jit(solution)/shard_map/ppermute | solution.py:475
  49.9 4.0 %collective-permute-start.3 = (f32[3,256]{1,0:T(4,128)S(1)}, f32[3,256]{1,0:T(4,128)S(1)}, u32[]{:S(2)}, u32[]{:S(2)}) collective-permute-start(f32[3,256]{1,0:T(4,128)S(1)} %get-tuple-element.22), channel_id=1, source_target_pairs={{1,0},{2,1},{3,2},{4,3},{5,4},{6,5},{7,6},{8,7},{9,8},{10,9},{11,1... | collective-permute-start | bytes 9224 | tf_op jit(solution)/shard_map/ppermute | solution.py:475
  74.2 1.3 %collective-permute-start.4 = (f32[32,128]{1,0:T(8,128)S(1)}, f32[32,128]{1,0:T(8,128)S(1)}, u32[]{:S(2)}, u32[]{:S(2)}) collective-permute-start(f32[32,128]{1,0:T(8,128)S(1)} %get-tuple-element.24.p0), channel_id=1, source_target_pairs={{0,1},{1,0},{2,3},{3,2},{4,5},{5,4},{6,7},{7,6},{8,9},{9,8},{10,11... | collective-permute-start | bytes 49160 | tf_op jit(solution)/shard_map/ppermute | solution.py:465
  75.4 3.9 %collective-permute-start.5 = (f32[64,128]{1,0:T(8,128)S(1)}, f32[64,128]{1,0:T(8,128)S(1)}, u32[]{:S(2)}, u32[]{:S(2)}) collective-permute-start(f32[64,128]{1,0:T(8,128)S(1)} %pad_maximum_fusion), channel_id=1, source_target_pairs={{0,2},{2,0},{1,3},{3,1},{4,6},{6,4},{5,7},{7,5},{8,10},{10,8},{9,1... | collective-permute-start | bytes 98312 | tf_op jit(solution)/shard_map/ppermute | solution.py:467
  81.4 1.3 %collective-permute-start.6 = (f32[32,128]{1,0:T(8,128)S(1)}, f32[32,128]{1,0:T(8,128)S(1)}, u32[]{:S(2)}, u32[]{:S(2)}) collective-permute-start(f32[32,128]{1,0:T(8,128)S(1)} %shard_map.107.p0), channel_id=1, source_target_pairs={{0,1},{1,0},{2,3},{3,2},{4,5},{5,4},{6,7},{7,6},{8,9},{9,8},{10,11... | collective-permute-start | bytes 49160 | tf_op jit(solution)/shard_map/ppermute | solution.py:465
  82.7 3.9 %collective-permute-start.7 = (f32[64,128]{1,0:T(8,128)S(1)}, f32[64,128]{1,0:T(8,128)S(1)}, u32[]{:S(2)}, u32[]{:S(2)}) collective-permute-start(f32[64,128]{1,0:T(8,128)S(1)} %pad_maximum_fusion.1), channel_id=1, source_target_pairs={{0,2},{2,0},{1,3},{3,1},{4,6},{6,4},{5,7},{7,5},{8,10},{10,8},{9,1... | collective-permute-start | bytes 98312 | tf_op jit(solution)/shard_map/ppermute | solution.py:467
  88.7 1.3 %collective-permute-start.8 = (f32[32,128]{1,0:T(8,128)S(1)}, f32[32,128]{1,0:T(8,128)S(1)}, u32[]{:S(2)}, u32[]{:S(2)}) collective-permute-start(f32[32,128]{1,0:T(8,128)S(1)} %shard_map.108.p0), channel_id=1, source_target_pairs={{0,1},{1,0},{2,3},{3,2},{4,5},{5,4},{6,7},{7,6},{8,9},{9,8},{10,11... | collective-permute-start | bytes 49160 | tf_op jit(solution)/shard_map/ppermute | solution.py:465
  90.0 4.4 %collective-permute-start.9 = (f32[64,128]{1,0:T(8,128)S(1)}, f32[64,128]{1,0:T(8,128)S(1)}, u32[]{:S(2)}, u32[]{:S(2)}) collective-permute-start(f32[64,128]{1,0:T(8,128)S(1)} %pad_maximum_fusion.2), channel_id=1, source_target_pairs={{0,2},{2,0},{1,3},{3,1},{4,6},{6,4},{5,7},{7,5},{8,10},{10,8},{9,1... | collective-permute-start | bytes 98312 | tf_op jit(solution)/shard_map/ppermute | solution.py:467
  96.4 1.3 %collective-permute-start.10 = (f32[32,128]{1,0:T(8,128)S(1)}, f32[32,128]{1,0:T(8,128)S(1)}, u32[]{:S(2)}, u32[]{:S(2)}) collective-permute-start(f32[32,128]{1,0:T(8,128)S(1)} %shard_map.109.p0), channel_id=1, source_target_pairs={{0,1},{1,0},{2,3},{3,2},{4,5},{5,4},{6,7},{7,6},{8,9},{9,8},{10,11... | collective-permute-start | bytes 49160 | tf_op jit(solution)/shard_map/ppermute | solution.py:465
  97.7 4.5 %collective-permute-start.11 = (f32[64,128]{1,0:T(8,128)S(1)}, f32[64,128]{1,0:T(8,128)S(1)}, u32[]{:S(2)}, u32[]{:S(2)}) collective-permute-start(f32[64,128]{1,0:T(8,128)S(1)} %pad_maximum_fusion.3), channel_id=1, source_target_pairs={{0,2},{2,0},{1,3},{3,1},{4,6},{6,4},{5,7},{7,5},{8,10},{10,8},{9,1... | collective-permute-start | bytes 98312 | tf_op jit(solution)/shard_map/ppermute | solution.py:467
  104.3 1.3 %collective-permute-start.12 = (f32[32,128]{1,0:T(8,128)S(1)}, f32[32,128]{1,0:T(8,128)S(1)}, u32[]{:S(2)}, u32[]{:S(2)}) collective-permute-start(f32[32,128]{1,0:T(8,128)S(1)} %shard_map.110.p0), channel_id=1, source_target_pairs={{0,1},{1,0},{2,3},{3,2},{4,5},{5,4},{6,7},{7,6},{8,9},{9,8},{10,11... | collective-permute-start | bytes 49160 | tf_op jit(solution)/shard_map/ppermute | solution.py:465
  105.5 4.5 %collective-permute-start.13 = (f32[64,128]{1,0:T(8,128)S(1)}, f32[64,128]{1,0:T(8,128)S(1)}, u32[]{:S(2)}, u32[]{:S(2)}) collective-permute-start(f32[64,128]{1,0:T(8,128)S(1)} %pad_maximum_fusion.4), channel_id=1, source_target_pairs={{0,2},{2,0},{1,3},{3,1},{4,6},{6,4},{5,7},{7,5},{8,10},{10,8},{9,1... | collective-permute-start | bytes 98312 | tf_op jit(solution)/shard_map/ppermute | solution.py:467

commit v8 on v7

--- a/solution.py
+++ b/solution.py
@@ -10,7 +10,7 @@
 DOM = ("dom_0", "dom_1", "dom_2", "dom_3", "dom_4", "dom_5")
 OTHERS = ("dom_0", "dom_1", "dom_2", "dom_3")
 PEERS = 32
-UNROLL = 2
+UNROLL = 8
 CSWEEPS = 6
 damping = 0.7
 highest = lax.Precision.HIGHEST
@@ -390,18 +390,18 @@
     table[...] = jnp.transpose(mine[...])
 
 
-def coarse_kernel(base_ref, passes, p0, p1, p2, rhs, dia, where, data, new, table, mine, gather):
-    gathered(table, (p0, p1, p2), mine)
+def coarse_kernel(base_ref, passes, p0, p1, p2, p3, rhs, dia, where, data, new, table, mine, gather):
+    gathered(table, (p0, p1, p2, p3), mine)
     new[...] = coarse_step(
         table, where, passes[...][0, 0], data, p0[...], rhs[...], dia[...], gather
     )
 
 
-def post_kernel(base_ref, p0, p1, p2, first_iter, rhs, dia, col, blk, node_row, before, after,
+def post_kernel(base_ref, p0, p1, p2, p3, first_iter, rhs, dia, col, blk, node_row, before, after,
                 before2, after2, out, correction, table, mine, one, two):
     base = base_ref[0]
     me = lax.shift_right_logical(base, 10)
-    gathered(table, (p0, p1, p2), mine)
+    gathered(table, (p0, p1, p2, p3), mine)
     row = mine[pl.ds(lane_of_device(me, me), 1), :]
     correction[...] = jnp.concatenate([row[:, 32 * i : 32 * i + 32] for i in range(3)], axis=0)
     one[...] = first_iter[...]
@@ -462,10 +462,11 @@
 
 def in_group(new):
     swap = [(0, 1), (1, 0)]
+    both = [(i, 3 - i) for i in range(4)]
+    p2 = lax.ppermute(new, "dom_4", swap)
+    p3 = lax.ppermute(new, ("dom_4", "dom_5"), both)
     p1 = lax.ppermute(new, "dom_5", swap)
-    a = jnp.concatenate([new, p1], axis=0)
-    p2 = lax.ppermute(a, "dom_4", swap)
-    return new, p1, p2
+    return new, p1, p2, p3
 
 
 def shifts(up, down):

time: 115 us -> 108 us (0.939)
  waiting for transfers between devices: 46.6 us -> 42.9 us
  Pallas kernels: 21.8 us -> 20.1 us
  starting transfers between devices: 39.3 us -> 37.9 us
    ppermute x5, waiting for transfers between devices: 5.85 us -> 0.01 us  [in_group(): p1 = lax.ppermute(new, 'dom_5', swap)]
    ppermute x5 -> x10, waiting for transfers between devices: 10.4 us -> 12.6 us  [the longest x5 6.36 us: in_group(): p3 = lax.ppermute(new, ('dom_4', 'dom_5'), both)]
    ppermute x5 -> x10, starting transfers between devices: 10.8 us -> 9.08 us  [the longest x5 5.64 us: in_group(): p2 = lax.ppermute(new, 'dom_4', swap)]
    pallas_call x8, Pallas kernels: 21.4 us -> 19.7 us  [call(): pl.pallas_call(kernel, in_specs=[smem] * scalars + [vmem] * (len(args) -...]
  transfers between devices with their start and end apart: 16 -> 21, of which waited for: 14 -> 14; matrix products, arithmetic and copies ran while one was open for 0% -> 0% of each run, Pallas kernels for 2% -> 2%
where the time goes in v8:
time: 108 us; the launch traced here: 107 us
  waiting for transfers between devices  42.9 us (40%)
  starting transfers between devices  37.9 us (35%)
  Pallas kernels  20.1 us (19%)
  local copies, waits for them, and re-layouts  4.99 us (5%)
    pallas_call x8, Pallas kernels, call(): pl.pallas_call(kernel, in_specs=[smem] * scalars + [vmem] * (len(args) -...  19.7 us
    all_to_all x1, starting transfers between devices, cycle(): sums = lax.all_to_all(send, DOM, 0, 0, tiled=True)  18 us
    all_to_all x1, waiting for transfers between devices, cycle(): data = lax.all_to_all(dsend, OTHERS, 0, 0, tiled=True)  16.7 us
    all_to_all x1, waiting for transfers between devices, cycle(): sums = lax.all_to_all(send, DOM, 0, 0, tiled=True)  6.92 us
    ppermute x4, waiting for transfers between devices, shifts(): return (lax.ppermute(up, DOM, forward), lax.ppermute(down, DOM, backward))  6.69 us
    ppermute x5, waiting for transfers between devices, in_group(): p3 = lax.ppermute(new, ('dom_4', 'dom_5'), both)  6.36 us
    ppermute x5, waiting for transfers between devices, in_group(): p2 = lax.ppermute(new, 'dom_4', swap)  6.25 us
    ppermute x5, starting transfers between devices, in_group(): p2 = lax.ppermute(new, 'dom_4', swap)  5.64 us
  transfers between devices with their start and end apart: 21, of which 14 were waited for; matrix products, arithmetic and copies ran while one was open for 0% of the time, Pallas kernels for 2%

profile of v8, /device:TPU:0, one launch (start us, length us, event | category | flops | bytes accessed | tf_op | source)
XLA Modules:
  0.0 106.8 jit_solution(10934625895729796891)
XLA Ops:
  0.7 1.3 %copy-done = f32[1024,27,3,3]{0,1,3,2:T(8,128)S(1)} copy-done((f32[1024,27,3,3]{0,1,3,2:T(8,128)S(1)}, f32[1024,27,3,3]{0,1,3,2:T(8,128)}, u32[]{:S(2)}) %copy-start) | copy-done | bytes 995352
  2.0 0.9 copy-done.2
  2.9 0.7 copy-done.4
  3.6 0.7 copy-done.6
  4.3 0.7 copy-done.8
  5.0 0.7 copy-done.11
  5.6 0.4 pack.1
  6.0 1.4 %collective-permute-start = (f32[288,256]{1,0:T(8,128)S(1)}, f32[288,256]{1,0:T(8,128)S(1)}, u32[]{:S(2)}, u32[]{:S(2)}) collective-permute-start(f32[288,256]{1,0:T(8,128)S(1)} %get-tuple-element.18), channel_id=1, source_target_pairs={{0,1},{1,2},{2,3},{3,4},{4,5},{5,6},{6,7},{7,8},{8,9},{9,10},{10,1... | collective-permute-start | bytes 884744 | tf_op jit(solution)/shard_map/ppermute | solution.py:476
  7.5 1.3 %collective-permute-start.1 = (f32[288,256]{1,0:T(8,128)S(1)}, f32[288,256]{1,0:T(8,128)S(1)}, u32[]{:S(2)}, u32[]{:S(2)}) collective-permute-start(f32[288,256]{1,0:T(8,128)S(1)} %get-tuple-element.19), channel_id=1, source_target_pairs={{1,0},{2,1},{3,2},{4,3},{5,4},{6,5},{7,6},{8,7},{9,8},{10,9},{11,1... | collective-permute-start | bytes 884744 | tf_op jit(solution)/shard_map/ppermute | solution.py:476
  8.8 4.0 %collective-permute-done.1.after = f32[288,256]{1,0:T(8,128)S(1)} collective-permute-done((f32[288,256]{1,0:T(8,128)S(1)}, f32[288,256]{1,0:T(8,128)S(1)}, u32[]{:S(2)}, u32[]{:S(2)}) %collective-permute-start.1) | collective-permute-done | bytes 294944 | tf_op jit(solution)/shard_map/ppermute | solution.py:476
  12.8 2.8 %shard_map.104 = (f32[128,2,128]{2,1,0:T(2,128)}, f32[3,2048]{1,0:T(4,128)S(1)}, f32[3,2048]{1,0:T(4,128)S(1)}, f32[3,2048]{1,0:T(4,128)S(1)}, f32[3,256]{1,0:T(4,128)S(1)}, /*index=5*/f32[3,256]{1,0:T(4,128)S(1)}) custom-call(s32[1]{0:T(128)} %bitcast.base_ref, f32[3,1024]{1,0:T(4,128)S(1)} %bitcast.18, f32[3,1024]{1,0:T(4,128)S(1)} %bitcast.20, ...), custom_call_target="tpu_custom_call" | custom-call | tf_op jit(solution)/shard_map/pallas_call | solution.py:451
  15.6 18.0 %all-to-all-start = ((f32[128,2,128]{2,1,0:T(2,128)}), f32[128,2,128]{2,1,0:T(2,128)S(1)}, u32[]{:S(2)}, u32[]{:S(2)}) async-start(f32[128,2,128]{2,1,0:T(2,128)} %get-tuple-element.20), calls=%async_computation | async-start | bytes 262144 | tf_op jit(solution)/shard_map/all_to_all | solution.py:518
  33.7 2.5 %shard_map.105 = f32[32,80,128]{2,1,0:T(8,128)} custom-call(s32[32,27]{1,0:T(8,128)} %col.1, f32[3,3,32,27]{3,2,1,0:T(8,128)} %bitcast.26), custom_call_target="tpu_custom_call" | custom-call | tf_op jit(solution)/shard_map/pallas_call | solution.py:451
  36.1 6.9 %all-to-all-done.sums = f32[128,2,128]{2,1,0:T(2,128)S(1)} async-done(((f32[128,2,128]{2,1,0:T(2,128)}), f32[128,2,128]{2,1,0:T(2,128)S(1)}, u32[]{:S(2)}, u32[]{:S(2)}) %all-to-all-start) | async-done | bytes 131104 | tf_op jit(solution)/shard_map/all_to_all | solution.py:518
  43.0 4.5 %all-to-all-start.1 = ((f32[32,80,128]{2,1,0:T(8,128)}), f32[32,80,128]{2,1,0:T(8,128)S(1)}, u32[]{:S(2)}, u32[]{:S(2)}) async-start(f32[32,80,128]{2,1,0:T(8,128)} %shard_map.105), calls=%async_computation.1 | async-start | bytes 2621440 | tf_op jit(solution)/shard_map/all_to_all | solution.py:494
  47.5 1.5 %collective-permute-start.2 = (f32[3,256]{1,0:T(4,128)S(1)}, f32[3,256]{1,0:T(4,128)S(1)}, u32[]{:S(2)}, u32[]{:S(2)}) collective-permute-start(f32[3,256]{1,0:T(4,128)S(1)} %get-tuple-element.21), channel_id=1, source_target_pairs={{0,1},{1,2},{2,3},{3,4},{4,5},{5,6},{6,7},{7,8},{8,9},{9,10},{10,1... | collective-permute-start | bytes 9224 | tf_op jit(solution)/shard_map/ppermute | solution.py:476
  49.1 1.3 %collective-permute-start.3 = (f32[3,256]{1,0:T(4,128)S(1)}, f32[3,256]{1,0:T(4,128)S(1)}, u32[]{:S(2)}, u32[]{:S(2)}) collective-permute-start(f32[3,256]{1,0:T(4,128)S(1)} %get-tuple-element.22), channel_id=1, source_target_pairs={{1,0},{2,1},{3,2},{4,3},{5,4},{6,5},{7,6},{8,7},{9,8},{10,9},{11,1... | collective-permute-start | bytes 9224 | tf_op jit(solution)/shard_map/ppermute | solution.py:476
  50.4 2.7 %collective-permute-done.3.far_down.after2 = f32[3,256]{1,0:T(4,128)S(1)} collective-permute-done((f32[3,256]{1,0:T(4,128)S(1)}, f32[3,256]{1,0:T(4,128)S(1)}, u32[]{:S(2)}, u32[]{:S(2)}) %collective-permute-start.3) | collective-permute-done | bytes 3104 | tf_op jit(solution)/shard_map/ppermute | solution.py:476
  53.1 16.7 %all-to-all-done.1.data = f32[32,80,128]{2,1,0:T(8,128)S(1)} async-done(((f32[32,80,128]{2,1,0:T(8,128)}), f32[32,80,128]{2,1,0:T(8,128)S(1)}, u32[]{:S(2)}, u32[]{:S(2)}) %all-to-all-start.1) | async-done | bytes 1310752 | tf_op jit(solution)/shard_map/all_to_all | solution.py:494
  69.8 3.5 %shard_map.106 = (f32[32,128]{1,0:T(8,128)S(1)}, f32[32,128]{1,0:T(8,128)S(1)}, f32[32,128]{1,0:T(8,128)S(1)}, s32[32,8,128]{2,1,0:T(8,128)S(1)}, s32[8,128]{1,0:T(8,128)S(1)}) custom-call(s32[1]{0:T(128)} %bitcast.base_ref, f32[128,2,128]{2,1,0:T(2,128)S(1)} %all-to-all-done.sums, f32[32,80,128]{2,1,0:T(8,128)S(1)} %all-to-all-done.1.data, ...), custom_call_target="tpu_custom_call" | custom-call | tf_op jit(solution)/shard_map/pallas_call | solution.py:451
  73.3 0.1 collective-permute-start.6
  73.4 1.4 %collective-permute-start.5 = (f32[32,128]{1,0:T(8,128)S(1)}, f32[32,128]{1,0:T(8,128)S(1)}, u32[]{:S(2)}, u32[]{:S(2)}) collective-permute-start(f32[32,128]{1,0:T(8,128)S(1)} %get-tuple-element.24.p0), channel_id=1, source_target_pairs={{0,2},{2,0},{1,3},{3,1},{4,6},{6,4},{5,7},{7,5},{8,10},{10,8},{9,1... | collective-permute-start | bytes 49160 | tf_op jit(solution)/shard_map/ppermute | solution.py:466
  74.7 0.5 collective-permute-start.4
  75.2 1.3 %collective-permute-done.6.p3 = f32[32,128]{1,0:T(8,128)S(1)} collective-permute-done((f32[32,128]{1,0:T(8,128)S(1)}, f32[32,128]{1,0:T(8,128)S(1)}, u32[]{:S(2)}, u32[]{:S(2)}) %collective-permute-start.6) | collective-permute-done | bytes 16416 | tf_op jit(solution)/shard_map/ppermute | solution.py:467
  76.5 0.7 collective-permute-done.5.p2
  77.2 2.1 %shard_map.107.p0 = f32[32,128]{1,0:T(8,128)S(1)} custom-call(s32[1]{0:T(128)} %bitcast.base_ref, s32[8,128]{1,0:T(8,128)S(1)} %get-tuple-element.23.passes, f32[32,128]{1,0:T(8,128)S(1)} %get-tuple-element.24.p0, f32[32,128]{1,0:T(8,128)S(1)} %collective-permute-done.4.p1, f32[32,128]{1,0:T(8,128)S(1)} %collective-permute-done.5.p2, ...), custom_call_target="tpu_custom_call" | custom-call | tf_op jit(solution)/shard_map/pallas_call | solution.py:451
  79.3 1.2 %collective-permute-start.9 = (f32[32,128]{1,0:T(8,128)S(1)}, f32[32,128]{1,0:T(8,128)S(1)}, u32[]{:S(2)}, u32[]{:S(2)}) collective-permute-start(f32[32,128]{1,0:T(8,128)S(1)} %shard_map.107.p0), channel_id=1, source_target_pairs={{0,3},{1,2},{2,1},{3,0},{4,7},{5,6},{6,5},{7,4},{8,11},{9,10},{10,... | collective-permute-start | bytes 49160 | tf_op jit(solution)/shard_map/ppermute | solution.py:467
  80.5 0.9 collective-permute-start.8
  81.4 1.2 %collective-permute-done.9.p3 = f32[32,128]{1,0:T(8,128)S(1)} collective-permute-done((f32[32,128]{1,0:T(8,128)S(1)}, f32[32,128]{1,0:T(8,128)S(1)}, u32[]{:S(2)}, u32[]{:S(2)}) %collective-permute-start.9) | collective-permute-done | bytes 16416 | tf_op jit(solution)/shard_map/ppermute | solution.py:467
  82.5 1.8 %collective-permute-done.8.p2 = f32[32,128]{1,0:T(8,128)S(1)} collective-permute-done((f32[32,128]{1,0:T(8,128)S(1)}, f32[32,128]{1,0:T(8,128)S(1)}, u32[]{:S(2)}, u32[]{:S(2)}) %collective-permute-start.8) | collective-permute-done | bytes 16416 | tf_op jit(solution)/shard_map/ppermute | solution.py:466
  84.3 2.1 %shard_map.108.p0 = f32[32,128]{1,0:T(8,128)S(1)} custom-call(s32[1]{0:T(128)} %bitcast.base_ref, s32[8,128]{1,0:T(8,128)S(1)} %get-tuple-element.23.passes, f32[32,128]{1,0:T(8,128)S(1)} %shard_map.107.p0, f32[32,128]{1,0:T(8,128)S(1)} %collective-permute-done.7.p1, f32[32,128]{1,0:T(8,128)S(1)} %collective-permute-done.8.p2, ...), custom_call_target="tpu_custom_call" | custom-call | tf_op jit(solution)/shard_map/pallas_call | solution.py:451
  86.4 0.5 collective-permute-start.12
  86.9 1.2 %collective-permute-start.11 = (f32[32,128]{1,0:T(8,128)S(1)}, f32[32,128]{1,0:T(8,128)S(1)}, u32[]{:S(2)}, u32[]{:S(2)}) collective-permute-start(f32[32,128]{1,0:T(8,128)S(1)} %shard_map.108.p0), channel_id=1, source_target_pairs={{0,2},{2,0},{1,3},{3,1},{4,6},{6,4},{5,7},{7,5},{8,10},{10,8},{9,1... | collective-permute-start | bytes 49160 | tf_op jit(solution)/shard_map/ppermute | solution.py:466
  88.1 0.2 collective-permute-start.10
  88.3 1.3 %collective-permute-done.12.p3 = f32[32,128]{1,0:T(8,128)S(1)} collective-permute-done((f32[32,128]{1,0:T(8,128)S(1)}, f32[32,128]{1,0:T(8,128)S(1)}, u32[]{:S(2)}, u32[]{:S(2)}) %collective-permute-start.12) | collective-permute-done | bytes 16416 | tf_op jit(solution)/shard_map/ppermute | solution.py:467
  89.6 1.1 %collective-permute-done.11.p2 = f32[32,128]{1,0:T(8,128)S(1)} collective-permute-done((f32[32,128]{1,0:T(8,128)S(1)}, f32[32,128]{1,0:T(8,128)S(1)}, u32[]{:S(2)}, u32[]{:S(2)}) %collective-permute-start.11) | collective-permute-done | bytes 16416 | tf_op jit(solution)/shard_map/ppermute | solution.py:466
  90.7 2.1 %shard_map.109.p0 = f32[32,128]{1,0:T(8,128)S(1)} custom-call(s32[1]{0:T(128)} %bitcast.base_ref, s32[8,128]{1,0:T(8,128)S(1)} %get-tuple-element.23.passes, f32[32,128]{1,0:T(8,128)S(1)} %shard_map.108.p0, f32[32,128]{1,0:T(8,128)S(1)} %collective-permute-done.10.p1, f32[32,128]{1,0:T(8,128)S(1)} %collective-permute-done.11.p2, ...), custom_call_target="tpu_custom_call" | custom-call | tf_op jit(solution)/shard_map/pallas_call | solution.py:451
  92.8 0.8 collective-permute-start.15
  93.6 1.2 %collective-permute-start.14 = (f32[32,128]{1,0:T(8,128)S(1)}, f32[32,128]{1,0:T(8,128)S(1)}, u32[]{:S(2)}, u32[]{:S(2)}) collective-permute-start(f32[32,128]{1,0:T(8,128)S(1)} %shard_map.109.p0), channel_id=1, source_target_pairs={{0,2},{2,0},{1,3},{3,1},{4,6},{6,4},{5,7},{7,5},{8,10},{10,8},{9,1... | collective-permute-start | bytes 49160 | tf_op jit(solution)/shard_map/ppermute | solution.py:466
  94.7 0.0 collective-permute-start.13
  94.8 1.3 %collective-permute-done.15.p3 = f32[32,128]{1,0:T(8,128)S(1)} collective-permute-done((f32[32,128]{1,0:T(8,128)S(1)}, f32[32,128]{1,0:T(8,128)S(1)}, u32[]{:S(2)}, u32[]{:S(2)}) %collective-permute-start.15) | collective-permute-done | bytes 16416 | tf_op jit(solution)/shard_map/ppermute | solution.py:467
  96.0 1.3 %collective-permute-done.14.p2 = f32[32,128]{1,0:T(8,128)S(1)} collective-permute-done((f32[32,128]{1,0:T(8,128)S(1)}, f32[32,128]{1,0:T(8,128)S(1)}, u32[]{:S(2)}, u32[]{:S(2)}) %collective-permute-start.14) | collective-permute-done | bytes 16416 | tf_op jit(solution)/shard_map/ppermute | solution.py:466
  97.3 2.1 %shard_map.110.p0 = f32[32,128]{1,0:T(8,128)S(1)} custom-call(s32[1]{0:T(128)} %bitcast.base_ref, s32[8,128]{1,0:T(8,128)S(1)} %get-tuple-element.23.passes, f32[32,128]{1,0:T(8,128)S(1)} %shard_map.109.p0, f32[32,128]{1,0:T(8,128)S(1)} %collective-permute-done.13.p1, f32[32,128]{1,0:T(8,128)S(1)} %collective-permute-done.14.p2, ...), custom_call_target="tpu_custom_call" | custom-call | tf_op jit(solution)/shard_map/pallas_call | solution.py:451
  99.4 0.9 collective-permute-start.18
  100.3 1.0 collective-permute-start.17
  101.3 1.3 %collective-permute-done.18.p3 = f32[32,128]{1,0:T(8,128)S(1)} collective-permute-done((f32[32,128]{1,0:T(8,128)S(1)}, f32[32,128]{1,0:T(8,128)S(1)}, u32[]{:S(2)}, u32[]{:S(2)}) %collective-permute-start.18) | collective-permute-done | bytes 16416 | tf_op jit(solution)/shard_map/ppermute | solution.py:467
  102.6 1.5 %collective-permute-done.17.p2 = f32[32,128]{1,0:T(8,128)S(1)} collective-permute-done((f32[32,128]{1,0:T(8,128)S(1)}, f32[32,128]{1,0:T(8,128)S(1)}, u32[]{:S(2)}, u32[]{:S(2)}) %collective-permute-start.17) | collective-permute-done | bytes 16416 | tf_op jit(solution)/shard_map/ppermute | solution.py:466
  104.1 2.7 %shard_map.111 = (f32[3,1024]{1,0:T(4,128)}, f32[3,32]{1,0:T(4,128)}) custom-call(s32[1]{0:T(128)} %bitcast.base_ref, f32[32,128]{1,0:T(8,128)S(1)} %shard_map.110.p0, f32[32,128]{1,0:T(8,128)S(1)} %collective-permute-done.16.p1, f32[32,128]{1,0:T(8,128)S(1)} %collective-permute-done.17.p2, f32[32,128]{1,0:T(8,128)S(1)} %collective-permute-done.18.p3, ...), custom_call_target="tpu_custom_call" | custom-call | tf_op jit(solution)/shard_map/pallas_call | solution.py:451
  (29 shorter events, 0.1 us)
Async XLA Ops:
  0.6 12.2 %copy-start.12 = (s32[32]{0:T(128)S(1)}, s32[32]{0:T(128)}, u32[]{:S(2)}) copy-start(s32[32]{0:T(128)} %param.14) | copy-start | bytes 388
  0.6 12.2 %copy-start.9 = (s32[1024]{0:T(1024)S(1)}, s32[1024]{0:T(1024)}, u32[]{:S(2)}) copy-start(s32[1024]{0:T(1024)} %param.13) | copy-start | bytes 12292
  0.7 12.1 %copy-start.10 = (f32[32,3]{0,1:T(4,128)S(1)}, f32[32,3]{0,1:T(4,128)}, u32[]{:S(2)}) copy-start(f32[32,3]{0,1:T(4,128)} %param.15) | copy-start | bytes 1156
  0.7 1.3 %copy-start = (f32[1024,27,3,3]{0,1,3,2:T(8,128)S(1)}, f32[1024,27,3,3]{0,1,3,2:T(8,128)}, u32[]{:S(2)}) copy-start(f32[1024,27,3,3]{0,1,3,2:T(8,128)} %param.12) | copy-start | bytes 2985988
  2.0 0.9 copy-start.2
  2.9 0.7 copy-start.4
  3.6 0.7 copy-start.6
  4.3 0.7 copy-start.8
  5.0 0.7 copy-start.11
  5.6 7.2 %copy-start.1 = (f32[1024,27,3,3]{0,1,3,2:T(8,128)S(1)}, f32[1024,27,3,3]{0,1,3,2:T(8,128)}, u32[]{:S(2)}) copy-start(f32[1024,27,3,3]{0,1,3,2:T(8,128)} %param.12) | copy-start | bytes 2985988
  5.6 7.2 %copy-start.3 = (s32[1024,27]{0,1:T(8,128)S(1)}, s32[1024,27]{0,1:T(8,128)}, u32[]{:S(2)}) copy-start(s32[1024,27]{0,1:T(8,128)} %param.11) | copy-start | bytes 331780
  5.6 7.2 %copy-start.5 = (f32[1024,3]{0,1:T(4,128)S(1)}, f32[1024,3]{0,1:T(4,128)}, u32[]{:S(2)}) copy-start(f32[1024,3]{0,1:T(4,128)} %param.9) | copy-start | bytes 36868
  5.6 7.2 %copy-start.7 = (f32[1024,3]{0,1:T(4,128)S(1)}, f32[1024,3]{0,1:T(4,128)}, u32[]{:S(2)}) copy-start(f32[1024,3]{0,1:T(4,128)} %param.10) | copy-start | bytes 36868
  6.0 2.8 %collective-permute-start = (f32[288,256]{1,0:T(8,128)S(1)}, f32[288,256]{1,0:T(8,128)S(1)}, u32[]{:S(2)}, u32[]{:S(2)}) collective-permute-start(f32[288,256]{1,0:T(8,128)S(1)} %get-tuple-element.18), channel_id=1, source_target_pairs={{0,1},{1,2},{2,3},{3,4},{4,5},{5,6},{6,7},{7,8},{8,9},{9,10},{10,1... | collective-permute-start | bytes 884744 | tf_op jit(solution)/shard_map/ppermute | solution.py:476
  7.5 5.3 %collective-permute-start.1 = (f32[288,256]{1,0:T(8,128)S(1)}, f32[288,256]{1,0:T(8,128)S(1)}, u32[]{:S(2)}, u32[]{:S(2)}) collective-permute-start(f32[288,256]{1,0:T(8,128)S(1)} %get-tuple-element.19), channel_id=1, source_target_pairs={{1,0},{2,1},{3,2},{4,3},{5,4},{6,5},{7,6},{8,7},{9,8},{10,9},{11,1... | collective-permute-start | bytes 884744 | tf_op jit(solution)/shard_map/ppermute | solution.py:476
  15.6 27.4 %all-to-all-start = ((f32[128,2,128]{2,1,0:T(2,128)}), f32[128,2,128]{2,1,0:T(2,128)S(1)}, u32[]{:S(2)}, u32[]{:S(2)}) async-start(f32[128,2,128]{2,1,0:T(2,128)} %get-tuple-element.20), calls=%async_computation | async-start | bytes 262144 | tf_op jit(solution)/shard_map/all_to_all | solution.py:518
  43.0 26.7 %all-to-all-start.1 = ((f32[32,80,128]{2,1,0:T(8,128)}), f32[32,80,128]{2,1,0:T(8,128)S(1)}, u32[]{:S(2)}, u32[]{:S(2)}) async-start(f32[32,80,128]{2,1,0:T(8,128)} %shard_map.105), calls=%async_computation.1 | async-start | bytes 2621440 | tf_op jit(solution)/shard_map/all_to_all | solution.py:494
  47.5 2.8 %collective-permute-start.2 = (f32[3,256]{1,0:T(4,128)S(1)}, f32[3,256]{1,0:T(4,128)S(1)}, u32[]{:S(2)}, u32[]{:S(2)}) collective-permute-start(f32[3,256]{1,0:T(4,128)S(1)} %get-tuple-element.21), channel_id=1, source_target_pairs={{0,1},{1,2},{2,3},{3,4},{4,5},{5,6},{6,7},{7,8},{8,9},{9,10},{10,1... | collective-permute-start | bytes 9224 | tf_op jit(solution)/shard_map/ppermute | solution.py:476
  49.1 4.0 %collective-permute-start.3 = (f32[3,256]{1,0:T(4,128)S(1)}, f32[3,256]{1,0:T(4,128)S(1)}, u32[]{:S(2)}, u32[]{:S(2)}) collective-permute-start(f32[3,256]{1,0:T(4,128)S(1)} %get-tuple-element.22), channel_id=1, source_target_pairs={{1,0},{2,1},{3,2},{4,3},{5,4},{6,5},{7,6},{8,7},{9,8},{10,9},{11,1... | collective-permute-start | bytes 9224 | tf_op jit(solution)/shard_map/ppermute | solution.py:476
  73.3 3.2 %collective-permute-start.6 = (f32[32,128]{1,0:T(8,128)S(1)}, f32[32,128]{1,0:T(8,128)S(1)}, u32[]{:S(2)}, u32[]{:S(2)}) collective-permute-start(f32[32,128]{1,0:T(8,128)S(1)} %get-tuple-element.24.p0), channel_id=1, source_target_pairs={{0,3},{1,2},{2,1},{3,0},{4,7},{5,6},{6,5},{7,4},{8,11},{9,10},{10,... | collective-permute-start | bytes 49160 | tf_op jit(solution)/shard_map/ppermute | solution.py:467
  73.4 3.8 %collective-permute-start.5 = (f32[32,128]{1,0:T(8,128)S(1)}, f32[32,128]{1,0:T(8,128)S(1)}, u32[]{:S(2)}, u32[]{:S(2)}) collective-permute-start(f32[32,128]{1,0:T(8,128)S(1)} %get-tuple-element.24.p0), channel_id=1, source_target_pairs={{0,2},{2,0},{1,3},{3,1},{4,6},{6,4},{5,7},{7,5},{8,10},{10,8},{9,1... | collective-permute-start | bytes 49160 | tf_op jit(solution)/shard_map/ppermute | solution.py:466
  74.7 2.5 %collective-permute-start.4 = (f32[32,128]{1,0:T(8,128)S(1)}, f32[32,128]{1,0:T(8,128)S(1)}, u32[]{:S(2)}, u32[]{:S(2)}) collective-permute-start(f32[32,128]{1,0:T(8,128)S(1)} %get-tuple-element.24.p0), channel_id=1, source_target_pairs={{0,1},{1,0},{2,3},{3,2},{4,5},{5,4},{6,7},{7,6},{8,9},{9,8},{10,11... | collective-permute-start | bytes 49160 | tf_op jit(solution)/shard_map/ppermute | solution.py:468
  79.3 3.2 %collective-permute-start.9 = (f32[32,128]{1,0:T(8,128)S(1)}, f32[32,128]{1,0:T(8,128)S(1)}, u32[]{:S(2)}, u32[]{:S(2)}) collective-permute-start(f32[32,128]{1,0:T(8,128)S(1)} %shard_map.107.p0), channel_id=1, source_target_pairs={{0,3},{1,2},{2,1},{3,0},{4,7},{5,6},{6,5},{7,4},{8,11},{9,10},{10,... | collective-permute-start | bytes 49160 | tf_op jit(solution)/shard_map/ppermute | solution.py:467
  80.5 3.8 %collective-permute-start.8 = (f32[32,128]{1,0:T(8,128)S(1)}, f32[32,128]{1,0:T(8,128)S(1)}, u32[]{:S(2)}, u32[]{:S(2)}) collective-permute-start(f32[32,128]{1,0:T(8,128)S(1)} %shard_map.107.p0), channel_id=1, source_target_pairs={{0,2},{2,0},{1,3},{3,1},{4,6},{6,4},{5,7},{7,5},{8,10},{10,8},{9,1... | collective-permute-start | bytes 49160 | tf_op jit(solution)/shard_map/ppermute | solution.py:466
  81.3 3.0 %collective-permute-start.7 = (f32[32,128]{1,0:T(8,128)S(1)}, f32[32,128]{1,0:T(8,128)S(1)}, u32[]{:S(2)}, u32[]{:S(2)}) collective-permute-start(f32[32,128]{1,0:T(8,128)S(1)} %shard_map.107.p0), channel_id=1, source_target_pairs={{0,1},{1,0},{2,3},{3,2},{4,5},{5,4},{6,7},{7,6},{8,9},{9,8},{10,11... | collective-permute-start | bytes 49160 | tf_op jit(solution)/shard_map/ppermute | solution.py:468
  86.4 3.2 %collective-permute-start.12 = (f32[32,128]{1,0:T(8,128)S(1)}, f32[32,128]{1,0:T(8,128)S(1)}, u32[]{:S(2)}, u32[]{:S(2)}) collective-permute-start(f32[32,128]{1,0:T(8,128)S(1)} %shard_map.108.p0), channel_id=1, source_target_pairs={{0,3},{1,2},{2,1},{3,0},{4,7},{5,6},{6,5},{7,4},{8,11},{9,10},{10,... | collective-permute-start | bytes 49160 | tf_op jit(solution)/shard_map/ppermute | solution.py:467
  86.9 3.8 %collective-permute-start.11 = (f32[32,128]{1,0:T(8,128)S(1)}, f32[32,128]{1,0:T(8,128)S(1)}, u32[]{:S(2)}, u32[]{:S(2)}) collective-permute-start(f32[32,128]{1,0:T(8,128)S(1)} %shard_map.108.p0), channel_id=1, source_target_pairs={{0,2},{2,0},{1,3},{3,1},{4,6},{6,4},{5,7},{7,5},{8,10},{10,8},{9,1... | collective-permute-start | bytes 49160 | tf_op jit(solution)/shard_map/ppermute | solution.py:466
  88.1 2.6 %collective-permute-start.10 = (f32[32,128]{1,0:T(8,128)S(1)}, f32[32,128]{1,0:T(8,128)S(1)}, u32[]{:S(2)}, u32[]{:S(2)}) collective-permute-start(f32[32,128]{1,0:T(8,128)S(1)} %shard_map.108.p0), channel_id=1, source_target_pairs={{0,1},{1,0},{2,3},{3,2},{4,5},{5,4},{6,7},{7,6},{8,9},{9,8},{10,11... | collective-permute-start | bytes 49160 | tf_op jit(solution)/shard_map/ppermute | solution.py:468
  92.8 3.2 %collective-permute-start.15 = (f32[32,128]{1,0:T(8,128)S(1)}, f32[32,128]{1,0:T(8,128)S(1)}, u32[]{:S(2)}, u32[]{:S(2)}) collective-permute-start(f32[32,128]{1,0:T(8,128)S(1)} %shard_map.109.p0), channel_id=1, source_target_pairs={{0,3},{1,2},{2,1},{3,0},{4,7},{5,6},{6,5},{7,4},{8,11},{9,10},{10,... | collective-permute-start | bytes 49160 | tf_op jit(solution)/shard_map/ppermute | solution.py:467
  93.6 3.7 %collective-permute-start.14 = (f32[32,128]{1,0:T(8,128)S(1)}, f32[32,128]{1,0:T(8,128)S(1)}, u32[]{:S(2)}, u32[]{:S(2)}) collective-permute-start(f32[32,128]{1,0:T(8,128)S(1)} %shard_map.109.p0), channel_id=1, source_target_pairs={{0,2},{2,0},{1,3},{3,1},{4,6},{6,4},{5,7},{7,5},{8,10},{10,8},{9,1... | collective-permute-start | bytes 49160 | tf_op jit(solution)/shard_map/ppermute | solution.py:466
  94.7 2.6 %collective-permute-start.13 = (f32[32,128]{1,0:T(8,128)S(1)}, f32[32,128]{1,0:T(8,128)S(1)}, u32[]{:S(2)}, u32[]{:S(2)}) collective-permute-start(f32[32,128]{1,0:T(8,128)S(1)} %shard_map.109.p0), channel_id=1, source_target_pairs={{0,1},{1,0},{2,3},{3,2},{4,5},{5,4},{6,7},{7,6},{8,9},{9,8},{10,11... | collective-permute-start | bytes 49160 | tf_op jit(solution)/shard_map/ppermute | solution.py:468
  99.4 3.2 %collective-permute-start.18 = (f32[32,128]{1,0:T(8,128)S(1)}, f32[32,128]{1,0:T(8,128)S(1)}, u32[]{:S(2)}, u32[]{:S(2)}) collective-permute-start(f32[32,128]{1,0:T(8,128)S(1)} %shard_map.110.p0), channel_id=1, source_target_pairs={{0,3},{1,2},{2,1},{3,0},{4,7},{5,6},{6,5},{7,4},{8,11},{9,10},{10,... | collective-permute-start | bytes 49160 | tf_op jit(solution)/shard_map/ppermute | solution.py:467
  100.3 3.8 %collective-permute-start.17 = (f32[32,128]{1,0:T(8,128)S(1)}, f32[32,128]{1,0:T(8,128)S(1)}, u32[]{:S(2)}, u32[]{:S(2)}) collective-permute-start(f32[32,128]{1,0:T(8,128)S(1)} %shard_map.110.p0), channel_id=1, source_target_pairs={{0,2},{2,0},{1,3},{3,1},{4,6},{6,4},{5,7},{7,5},{8,10},{10,8},{9,1... | collective-permute-start | bytes 49160 | tf_op jit(solution)/shard_map/ppermute | solution.py:466
  101.3 2.8 %collective-permute-start.16 = (f32[32,128]{1,0:T(8,128)S(1)}, f32[32,128]{1,0:T(8,128)S(1)}, u32[]{:S(2)}, u32[]{:S(2)}) collective-permute-start(f32[32,128]{1,0:T(8,128)S(1)} %shard_map.110.p0), channel_id=1, source_target_pairs={{0,1},{1,0},{2,3},{3,2},{4,5},{5,4},{6,7},{7,6},{8,9},{9,8},{10,11... | collective-permute-start | bytes 49160 | tf_op jit(solution)/shard_map/ppermute | solution.py:468

commit v9 on v8

--- a/solution.py
+++ b/solution.py
@@ -3,12 +3,10 @@
 from jax import lax
 from jax.experimental import pallas as pl
 from jax.experimental.pallas import tpu as pltpu
-from jax.sharding import Mesh
 from jax.sharding import PartitionSpec as P
 
 
-DOM = ("dom_0", "dom_1", "dom_2", "dom_3", "dom_4", "dom_5")
-OTHERS = ("dom_0", "dom_1", "dom_2", "dom_3")
+DOM = "dom"
 PEERS = 32
 UNROLL = 8
 CSWEEPS = 6
@@ -218,14 +216,30 @@
     send[:, 1, :] = jnp.broadcast_to(row, (LANES, LANES))
 
 
+def parity(p):
+    return lax.bitwise_and(
+        lax.bitwise_xor(lax.shift_right_logical(p, 1), lax.shift_right_logical(p, 2)), 1
+    )
+
+
 def lane_of_device(p, me):
-    p = lax.bitwise_xor(p, lax.bitwise_and(me, 3))
-    return lax.shift_left(lax.bitwise_and(p, 3), 5) + lax.shift_right_logical(p, 2)
+    side = lax.shift_left(lax.bitwise_xor(parity(p), parity(me)), 6)
+    core = lax.shift_left(lax.bitwise_and(lax.bitwise_xor(p, me), 1), 5)
+    return side + core + lax.shift_right_logical(p, 2)
 
 
 def device_of_lane(q, me):
-    p = lax.shift_left(lax.bitwise_and(q, 31), 2) + lax.shift_right_logical(q, 5)
-    return lax.bitwise_xor(p, lax.bitwise_and(me, 3))
+    side = lax.bitwise_xor(lax.shift_right_logical(q, 6), parity(me))
+    side = lax.bitwise_xor(side, lax.bitwise_and(q, 1))
+    core = lax.bitwise_and(lax.bitwise_xor(lax.shift_right_logical(q, 5), me), 1)
+    return lax.shift_left(lax.bitwise_and(q, 31), 2) + lax.shift_left(side, 1) + core
+
+
+def row_groups():
+    return [
+        [4 * m + 2 * (side ^ (m & 1)) + core for m in range(PEERS)]
+        for side in range(2) for core in range(2)
+    ]
 
 
 def coarse_pack_kernel(col, blk, send):
@@ -461,11 +475,10 @@
 
 
 def in_group(new):
-    swap = [(0, 1), (1, 0)]
-    both = [(i, 3 - i) for i in range(4)]
-    p2 = lax.ppermute(new, "dom_4", swap)
-    p3 = lax.ppermute(new, ("dom_4", "dom_5"), both)
-    p1 = lax.ppermute(new, "dom_5", swap)
+    def partner(bits):
+        return lax.ppermute(new, DOM, [(i, i ^ bits) for i in range(lax.axis_size(DOM))])
+
+    p2, p3, p1 = partner(2), partner(3), partner(1)
     return new, p1, p2, p3
 
 
@@ -491,7 +504,9 @@
         coarse_pack_kernel, [((PEERS, 80, LANES), f32)], [coarse_columns, cblk],
         limit=60,
     )
-    data = lax.all_to_all(dsend, OTHERS, 0, 0, tiled=True)
+    data = lax.all_to_all(
+        dsend, DOM, 0, 0, axis_index_groups=row_groups(), tiled=True
+    )
     vmem, far = pl.BlockSpec(memory_space=pltpu.VMEM), pl.BlockSpec(memory_space=pltpu.HBM)
     up, down, node_row = pl.pallas_call(
         pack_kernel,
@@ -542,10 +557,9 @@
 
 
 def solution(mesh):
-    torus = Mesh(mesh.devices.reshape(4, 2, 2, 2, 2, 2), DOM)
     return jax.shard_map(
         cycle,
-        mesh=torus,
+        mesh=mesh,
         in_specs=(
             P(DOM, None),
             P(DOM, None),

time: 108 us -> 108 us (level)
  Pallas kernels: 20.1 us -> 23.1 us
  waiting for transfers between devices: 42.9 us -> 40.7 us
    pallas_call x8, Pallas kernels: 19.7 us -> 22.7 us  [call(): pl.pallas_call(kernel, in_specs=[smem] * scalars + [vmem] * (len(args) -...]
    ppermute x15, waiting for transfers between devices: 12.6 us -> 10.7 us  [partner(): lax.ppermute(new, DOM, [(i, i ^ bits) for i in range(lax.axis_size(DOM))])]
where the time goes in v9:
time: 108 us; the launch traced here: 107 us
  waiting for transfers between devices  40.7 us (38%)
  starting transfers between devices  37.6 us (35%)
  Pallas kernels  23.1 us (21%)
  local copies, waits for them, and re-layouts  4.99 us (5%)
    pallas_call x8, Pallas kernels, call(): pl.pallas_call(kernel, in_specs=[smem] * scalars + [vmem] * (len(args) -...  22.7 us
    all_to_all x1, starting transfers between devices, cycle(): sums = lax.all_to_all(send, DOM, 0, 0, tiled=True)  18 us
    all_to_all x1, waiting for transfers between devices, cycle(): lax.all_to_all(dsend, DOM, 0, 0, axis_index_groups=row_groups(), tiled=True)  17.2 us
    ppermute x15, waiting for transfers between devices, partner(): lax.ppermute(new, DOM, [(i, i ^ bits) for i in range(lax.axis_size(DOM))])  10.7 us
    ppermute x15, starting transfers between devices, partner(): lax.ppermute(new, DOM, [(i, i ^ bits) for i in range(lax.axis_size(DOM))])  9.67 us
    all_to_all x1, waiting for transfers between devices, cycle(): sums = lax.all_to_all(send, DOM, 0, 0, tiled=True)  6.92 us
    ppermute x4, waiting for transfers between devices, shifts(): return (lax.ppermute(up, DOM, forward), lax.ppermute(down, DOM, backward))  5.88 us
    ppermute x4, starting transfers between devices, shifts(): return (lax.ppermute(up, DOM, forward), lax.ppermute(down, DOM, backward))  5.35 us
  transfers between devices with their start and end apart: 21, of which 14 were waited for; matrix products, arithmetic and copies ran while one was open for 0% of the time, Pallas kernels for 2%

profile of v9, /device:TPU:0, one launch (start us, length us, event | category | flops | bytes accessed | tf_op | source)
XLA Modules:
  0.0 107.3 jit_solution(6687712373811406780)
XLA Ops:
  0.7 1.3 %copy-done = f32[1024,27,3,3]{0,1,3,2:T(8,128)S(1)} copy-done((f32[1024,27,3,3]{0,1,3,2:T(8,128)S(1)}, f32[1024,27,3,3]{0,1,3,2:T(8,128)}, u32[]{:S(2)}) %copy-start) | copy-done | bytes 995352
  2.0 0.9 copy-done.2
  2.9 0.7 copy-done.4
  3.6 0.7 copy-done.6
  4.3 0.7 copy-done.8
  5.0 0.7 copy-done.11
  5.6 0.4 pack.1
  6.0 1.4 %collective-permute-start = (f32[288,256]{1,0:T(8,128)S(1)}, f32[288,256]{1,0:T(8,128)S(1)}, u32[]{:S(2)}, u32[]{:S(2)}) collective-permute-start(f32[288,256]{1,0:T(8,128)S(1)} %get-tuple-element.18), channel_id=1, source_target_pairs={{0,1},{1,2},{2,3},{3,4},{4,5},{5,6},{6,7},{7,8},{8,9},{9,10},{10,1... | collective-permute-start | bytes 884744 | tf_op jit(solution)/shard_map/ppermute | solution.py:489
  7.5 1.3 %collective-permute-start.1 = (f32[288,256]{1,0:T(8,128)S(1)}, f32[288,256]{1,0:T(8,128)S(1)}, u32[]{:S(2)}, u32[]{:S(2)}) collective-permute-start(f32[288,256]{1,0:T(8,128)S(1)} %get-tuple-element.19), channel_id=1, source_target_pairs={{1,0},{2,1},{3,2},{4,3},{5,4},{6,5},{7,6},{8,7},{9,8},{10,9},{11,1... | collective-permute-start | bytes 884744 | tf_op jit(solution)/shard_map/ppermute | solution.py:489
  8.8 4.0 %collective-permute-done.1.after = f32[288,256]{1,0:T(8,128)S(1)} collective-permute-done((f32[288,256]{1,0:T(8,128)S(1)}, f32[288,256]{1,0:T(8,128)S(1)}, u32[]{:S(2)}, u32[]{:S(2)}) %collective-permute-start.1) | collective-permute-done | bytes 294944 | tf_op jit(solution)/shard_map/ppermute | solution.py:489
  12.8 2.8 %shard_map.104 = (f32[128,2,128]{2,1,0:T(2,128)}, f32[3,2048]{1,0:T(4,128)S(1)}, f32[3,2048]{1,0:T(4,128)S(1)}, f32[3,2048]{1,0:T(4,128)S(1)}, f32[3,256]{1,0:T(4,128)S(1)}, /*index=5*/f32[3,256]{1,0:T(4,128)S(1)}) custom-call(s32[1]{0:T(128)} %bitcast.base_ref, f32[3,1024]{1,0:T(4,128)S(1)} %bitcast.18, f32[3,1024]{1,0:T(4,128)S(1)} %bitcast.20, ...), custom_call_target="tpu_custom_call" | custom-call | tf_op jit(solution)/shard_map/pallas_call | solution.py:465
  15.6 18.0 %all-to-all-start = ((f32[128,2,128]{2,1,0:T(2,128)}), f32[128,2,128]{2,1,0:T(2,128)S(1)}, u32[]{:S(2)}, u32[]{:S(2)}) async-start(f32[128,2,128]{2,1,0:T(2,128)} %get-tuple-element.20), calls=%async_computation | async-start | bytes 262144 | tf_op jit(solution)/shard_map/all_to_all | solution.py:533
  33.7 2.5 %shard_map.105 = f32[32,80,128]{2,1,0:T(8,128)} custom-call(s32[32,27]{1,0:T(8,128)} %col.1, f32[3,3,32,27]{3,2,1,0:T(8,128)} %bitcast.26), custom_call_target="tpu_custom_call" | custom-call | tf_op jit(solution)/shard_map/pallas_call | solution.py:465
  36.1 6.9 %all-to-all-done.sums = f32[128,2,128]{2,1,0:T(2,128)S(1)} async-done(((f32[128,2,128]{2,1,0:T(2,128)}), f32[128,2,128]{2,1,0:T(2,128)S(1)}, u32[]{:S(2)}, u32[]{:S(2)}) %all-to-all-start) | async-done | bytes 131104 | tf_op jit(solution)/shard_map/all_to_all | solution.py:533
  43.0 4.6 %all-to-all-start.1 = ((f32[32,80,128]{2,1,0:T(8,128)}), f32[32,80,128]{2,1,0:T(8,128)S(1)}, u32[]{:S(2)}, u32[]{:S(2)}) async-start(f32[32,80,128]{2,1,0:T(8,128)} %shard_map.105), calls=%async_computation.1 | async-start | bytes 2621440 | tf_op jit(solution)/shard_map/all_to_all | solution.py:507
  47.6 1.3 %collective-permute-start.2 = (f32[3,256]{1,0:T(4,128)S(1)}, f32[3,256]{1,0:T(4,128)S(1)}, u32[]{:S(2)}, u32[]{:S(2)}) collective-permute-start(f32[3,256]{1,0:T(4,128)S(1)} %get-tuple-element.21), channel_id=1, source_target_pairs={{0,1},{1,2},{2,3},{3,4},{4,5},{5,6},{6,7},{7,8},{8,9},{9,10},{10,1... | collective-permute-start | bytes 9224 | tf_op jit(solution)/shard_map/ppermute | solution.py:489
  49.0 1.3 %collective-permute-start.3 = (f32[3,256]{1,0:T(4,128)S(1)}, f32[3,256]{1,0:T(4,128)S(1)}, u32[]{:S(2)}, u32[]{:S(2)}) collective-permute-start(f32[3,256]{1,0:T(4,128)S(1)} %get-tuple-element.22), channel_id=1, source_target_pairs={{1,0},{2,1},{3,2},{4,3},{5,4},{6,5},{7,6},{8,7},{9,8},{10,9},{11,1... | collective-permute-start | bytes 9224 | tf_op jit(solution)/shard_map/ppermute | solution.py:489
  50.3 1.9 %collective-permute-done.3.far_down.after2 = f32[3,256]{1,0:T(4,128)S(1)} collective-permute-done((f32[3,256]{1,0:T(4,128)S(1)}, f32[3,256]{1,0:T(4,128)S(1)}, u32[]{:S(2)}, u32[]{:S(2)}) %collective-permute-start.3) | collective-permute-done | bytes 3104 | tf_op jit(solution)/shard_map/ppermute | solution.py:489
  52.2 17.2 %all-to-all-done.1.data = f32[32,80,128]{2,1,0:T(8,128)S(1)} async-done(((f32[32,80,128]{2,1,0:T(8,128)}), f32[32,80,128]{2,1,0:T(8,128)S(1)}, u32[]{:S(2)}, u32[]{:S(2)}) %all-to-all-start.1) | async-done | bytes 1310752 | tf_op jit(solution)/shard_map/all_to_all | solution.py:507
  69.4 4.1 %shard_map.106 = (f32[32,128]{1,0:T(8,128)S(1)}, f32[32,128]{1,0:T(8,128)S(1)}, f32[32,128]{1,0:T(8,128)S(1)}, s32[32,8,128]{2,1,0:T(8,128)S(1)}, s32[8,128]{1,0:T(8,128)S(1)}) custom-call(s32[1]{0:T(128)} %bitcast.base_ref, f32[128,2,128]{2,1,0:T(2,128)S(1)} %all-to-all-done.sums, f32[32,80,128]{2,1,0:T(8,128)S(1)} %all-to-all-done.1.data, ...), custom_call_target="tpu_custom_call" | custom-call | tf_op jit(solution)/shard_map/pallas_call | solution.py:465
  73.5 0.1 collective-permute-start.6
  73.6 0.1 collective-permute-start.5
  73.7 1.8 %collective-permute-start.4 = (f32[32,128]{1,0:T(8,128)S(1)}, f32[32,128]{1,0:T(8,128)S(1)}, u32[]{:S(2)}, u32[]{:S(2)}) collective-permute-start(f32[32,128]{1,0:T(8,128)S(1)} %get-tuple-element.24.p0), channel_id=1, source_target_pairs={{0,1},{1,0},{2,3},{3,2},{4,5},{5,4},{6,7},{7,6},{8,9},{9,8},{10,11... | collective-permute-start | bytes 49160 | tf_op jit(solution)/shard_map/ppermute | solution.py:479
  75.5 1.3 %collective-permute-done.6.p3 = f32[32,128]{1,0:T(8,128)S(1)} collective-permute-done((f32[32,128]{1,0:T(8,128)S(1)}, f32[32,128]{1,0:T(8,128)S(1)}, u32[]{:S(2)}, u32[]{:S(2)}) %collective-permute-start.6) | collective-permute-done | bytes 16416 | tf_op jit(solution)/shard_map/ppermute | solution.py:479
  76.8 0.7 collective-permute-done.5.p2
  77.4 2.7 %shard_map.107.p0 = f32[32,128]{1,0:T(8,128)S(1)} custom-call(s32[1]{0:T(128)} %bitcast.base_ref, s32[8,128]{1,0:T(8,128)S(1)} %get-tuple-element.23.passes, f32[32,128]{1,0:T(8,128)S(1)} %get-tuple-element.24.p0, f32[32,128]{1,0:T(8,128)S(1)} %collective-permute-done.4.p1, f32[32,128]{1,0:T(8,128)S(1)} %collective-permute-done.5.p2, ...), custom_call_target="tpu_custom_call" | custom-call | tf_op jit(solution)/shard_map/pallas_call | solution.py:465
  80.1 0.6 collective-permute-start.9
  80.7 1.4 %collective-permute-start.7 = (f32[32,128]{1,0:T(8,128)S(1)}, f32[32,128]{1,0:T(8,128)S(1)}, u32[]{:S(2)}, u32[]{:S(2)}) collective-permute-start(f32[32,128]{1,0:T(8,128)S(1)} %shard_map.107.p0), channel_id=1, source_target_pairs={{0,1},{1,0},{2,3},{3,2},{4,5},{5,4},{6,7},{7,6},{8,9},{9,8},{10,11... | collective-permute-start | bytes 49160 | tf_op jit(solution)/shard_map/ppermute | solution.py:479
  82.1 1.3 %collective-permute-done.9.p3 = f32[32,128]{1,0:T(8,128)S(1)} collective-permute-done((f32[32,128]{1,0:T(8,128)S(1)}, f32[32,128]{1,0:T(8,128)S(1)}, u32[]{:S(2)}, u32[]{:S(2)}) %collective-permute-start.9) | collective-permute-done | bytes 16416 | tf_op jit(solution)/shard_map/ppermute | solution.py:479
  83.4 1.1 %collective-permute-done.8.p2 = f32[32,128]{1,0:T(8,128)S(1)} collective-permute-done((f32[32,128]{1,0:T(8,128)S(1)}, f32[32,128]{1,0:T(8,128)S(1)}, u32[]{:S(2)}, u32[]{:S(2)}) %collective-permute-start.8) | collective-permute-done | bytes 16416 | tf_op jit(solution)/shard_map/ppermute | solution.py:479
  84.4 2.7 %shard_map.108.p0 = f32[32,128]{1,0:T(8,128)S(1)} custom-call(s32[1]{0:T(128)} %bitcast.base_ref, s32[8,128]{1,0:T(8,128)S(1)} %get-tuple-element.23.passes, f32[32,128]{1,0:T(8,128)S(1)} %shard_map.107.p0, f32[32,128]{1,0:T(8,128)S(1)} %collective-permute-done.7.p1, f32[32,128]{1,0:T(8,128)S(1)} %collective-permute-done.8.p2, ...), custom_call_target="tpu_custom_call" | custom-call | tf_op jit(solution)/shard_map/pallas_call | solution.py:465
  87.1 0.2 collective-permute-start.12
  87.3 0.0 collective-permute-start.11
  87.3 1.8 %collective-permute-start.10 = (f32[32,128]{1,0:T(8,128)S(1)}, f32[32,128]{1,0:T(8,128)S(1)}, u32[]{:S(2)}, u32[]{:S(2)}) collective-permute-start(f32[32,128]{1,0:T(8,128)S(1)} %shard_map.108.p0), channel_id=1, source_target_pairs={{0,1},{1,0},{2,3},{3,2},{4,5},{5,4},{6,7},{7,6},{8,9},{9,8},{10,11... | collective-permute-start | bytes 49160 | tf_op jit(solution)/shard_map/ppermute | solution.py:479
  89.1 1.3 %collective-permute-done.12.p3 = f32[32,128]{1,0:T(8,128)S(1)} collective-permute-done((f32[32,128]{1,0:T(8,128)S(1)}, f32[32,128]{1,0:T(8,128)S(1)}, u32[]{:S(2)}, u32[]{:S(2)}) %collective-permute-start.12) | collective-permute-done | bytes 16416 | tf_op jit(solution)/shard_map/ppermute | solution.py:479
  90.4 0.7 collective-permute-done.11.p2
  91.0 2.7 %shard_map.109.p0 = f32[32,128]{1,0:T(8,128)S(1)} custom-call(s32[1]{0:T(128)} %bitcast.base_ref, s32[8,128]{1,0:T(8,128)S(1)} %get-tuple-element.23.passes, f32[32,128]{1,0:T(8,128)S(1)} %shard_map.108.p0, f32[32,128]{1,0:T(8,128)S(1)} %collective-permute-done.10.p1, f32[32,128]{1,0:T(8,128)S(1)} %collective-permute-done.11.p2, ...), custom_call_target="tpu_custom_call" | custom-call | tf_op jit(solution)/shard_map/pallas_call | solution.py:465
  93.7 0.6 collective-permute-start.15
  94.3 1.4 %collective-permute-start.13 = (f32[32,128]{1,0:T(8,128)S(1)}, f32[32,128]{1,0:T(8,128)S(1)}, u32[]{:S(2)}, u32[]{:S(2)}) collective-permute-start(f32[32,128]{1,0:T(8,128)S(1)} %shard_map.109.p0), channel_id=1, source_target_pairs={{0,1},{1,0},{2,3},{3,2},{4,5},{5,4},{6,7},{7,6},{8,9},{9,8},{10,11... | collective-permute-start | bytes 49160 | tf_op jit(solution)/shard_map/ppermute | solution.py:479
  95.7 1.3 %collective-permute-done.15.p3 = f32[32,128]{1,0:T(8,128)S(1)} collective-permute-done((f32[32,128]{1,0:T(8,128)S(1)}, f32[32,128]{1,0:T(8,128)S(1)}, u32[]{:S(2)}, u32[]{:S(2)}) %collective-permute-start.15) | collective-permute-done | bytes 16416 | tf_op jit(solution)/shard_map/ppermute | solution.py:479
  97.0 1.1 %collective-permute-done.14.p2 = f32[32,128]{1,0:T(8,128)S(1)} collective-permute-done((f32[32,128]{1,0:T(8,128)S(1)}, f32[32,128]{1,0:T(8,128)S(1)}, u32[]{:S(2)}, u32[]{:S(2)}) %collective-permute-start.14) | collective-permute-done | bytes 16416 | tf_op jit(solution)/shard_map/ppermute | solution.py:479
  98.0 2.7 %shard_map.110.p0 = f32[32,128]{1,0:T(8,128)S(1)} custom-call(s32[1]{0:T(128)} %bitcast.base_ref, s32[8,128]{1,0:T(8,128)S(1)} %get-tuple-element.23.passes, f32[32,128]{1,0:T(8,128)S(1)} %shard_map.109.p0, f32[32,128]{1,0:T(8,128)S(1)} %collective-permute-done.13.p1, f32[32,128]{1,0:T(8,128)S(1)} %collective-permute-done.14.p2, ...), custom_call_target="tpu_custom_call" | custom-call | tf_op jit(solution)/shard_map/pallas_call | solution.py:465
  100.7 0.2 collective-permute-start.18
  100.9 0.0 collective-permute-start.17
  100.9 1.8 %collective-permute-start.16 = (f32[32,128]{1,0:T(8,128)S(1)}, f32[32,128]{1,0:T(8,128)S(1)}, u32[]{:S(2)}, u32[]{:S(2)}) collective-permute-start(f32[32,128]{1,0:T(8,128)S(1)} %shard_map.110.p0), channel_id=1, source_target_pairs={{0,1},{1,0},{2,3},{3,2},{4,5},{5,4},{6,7},{7,6},{8,9},{9,8},{10,11... | collective-permute-start | bytes 49160 | tf_op jit(solution)/shard_map/ppermute | solution.py:479
  102.7 1.3 %collective-permute-done.18.p3 = f32[32,128]{1,0:T(8,128)S(1)} collective-permute-done((f32[32,128]{1,0:T(8,128)S(1)}, f32[32,128]{1,0:T(8,128)S(1)}, u32[]{:S(2)}, u32[]{:S(2)}) %collective-permute-start.18) | collective-permute-done | bytes 16416 | tf_op jit(solution)/shard_map/ppermute | solution.py:479
  104.0 0.7 collective-permute-done.17.p2
  104.6 2.7 %shard_map.111 = (f32[3,1024]{1,0:T(4,128)}, f32[3,32]{1,0:T(4,128)}) custom-call(s32[1]{0:T(128)} %bitcast.base_ref, f32[32,128]{1,0:T(8,128)S(1)} %shard_map.110.p0, f32[32,128]{1,0:T(8,128)S(1)} %collective-permute-done.16.p1, f32[32,128]{1,0:T(8,128)S(1)} %collective-permute-done.17.p2, f32[32,128]{1,0:T(8,128)S(1)} %collective-permute-done.18.p3, ...), custom_call_target="tpu_custom_call" | custom-call | tf_op jit(solution)/shard_map/pallas_call | solution.py:465
  (29 shorter events, 0.1 us)
Async XLA Ops:
  0.6 12.2 %copy-start.12 = (s32[32]{0:T(128)S(1)}, s32[32]{0:T(128)}, u32[]{:S(2)}) copy-start(s32[32]{0:T(128)} %param.14) | copy-start | bytes 388
  0.6 12.2 %copy-start.9 = (s32[1024]{0:T(1024)S(1)}, s32[1024]{0:T(1024)}, u32[]{:S(2)}) copy-start(s32[1024]{0:T(1024)} %param.13) | copy-start | bytes 12292
  0.7 12.1 %copy-start.10 = (f32[32,3]{0,1:T(4,128)S(1)}, f32[32,3]{0,1:T(4,128)}, u32[]{:S(2)}) copy-start(f32[32,3]{0,1:T(4,128)} %param.15) | copy-start | bytes 1156
  0.7 1.3 %copy-start = (f32[1024,27,3,3]{0,1,3,2:T(8,128)S(1)}, f32[1024,27,3,3]{0,1,3,2:T(8,128)}, u32[]{:S(2)}) copy-start(f32[1024,27,3,3]{0,1,3,2:T(8,128)} %param.12) | copy-start | bytes 2985988
  2.0 0.9 copy-start.2
  2.9 0.7 copy-start.4
  3.6 0.7 copy-start.6
  4.3 0.7 copy-start.8
  5.0 0.7 copy-start.11
  5.6 7.2 %copy-start.1 = (f32[1024,27,3,3]{0,1,3,2:T(8,128)S(1)}, f32[1024,27,3,3]{0,1,3,2:T(8,128)}, u32[]{:S(2)}) copy-start(f32[1024,27,3,3]{0,1,3,2:T(8,128)} %param.12) | copy-start | bytes 2985988
  5.6 7.2 %copy-start.3 = (s32[1024,27]{0,1:T(8,128)S(1)}, s32[1024,27]{0,1:T(8,128)}, u32[]{:S(2)}) copy-start(s32[1024,27]{0,1:T(8,128)} %param.11) | copy-start | bytes 331780
  5.6 7.2 %copy-start.5 = (f32[1024,3]{0,1:T(4,128)S(1)}, f32[1024,3]{0,1:T(4,128)}, u32[]{:S(2)}) copy-start(f32[1024,3]{0,1:T(4,128)} %param.9) | copy-start | bytes 36868
  5.6 7.2 %copy-start.7 = (f32[1024,3]{0,1:T(4,128)S(1)}, f32[1024,3]{0,1:T(4,128)}, u32[]{:S(2)}) copy-start(f32[1024,3]{0,1:T(4,128)} %param.10) | copy-start | bytes 36868
  6.0 2.8 %collective-permute-start = (f32[288,256]{1,0:T(8,128)S(1)}, f32[288,256]{1,0:T(8,128)S(1)}, u32[]{:S(2)}, u32[]{:S(2)}) collective-permute-start(f32[288,256]{1,0:T(8,128)S(1)} %get-tuple-element.18), channel_id=1, source_target_pairs={{0,1},{1,2},{2,3},{3,4},{4,5},{5,6},{6,7},{7,8},{8,9},{9,10},{10,1... | collective-permute-start | bytes 884744 | tf_op jit(solution)/shard_map/ppermute | solution.py:489
  7.5 5.3 %collective-permute-start.1 = (f32[288,256]{1,0:T(8,128)S(1)}, f32[288,256]{1,0:T(8,128)S(1)}, u32[]{:S(2)}, u32[]{:S(2)}) collective-permute-start(f32[288,256]{1,0:T(8,128)S(1)} %get-tuple-element.19), channel_id=1, source_target_pairs={{1,0},{2,1},{3,2},{4,3},{5,4},{6,5},{7,6},{8,7},{9,8},{10,9},{11,1... | collective-permute-start | bytes 884744 | tf_op jit(solution)/shard_map/ppermute | solution.py:489
  15.6 27.4 %all-to-all-start = ((f32[128,2,128]{2,1,0:T(2,128)}), f32[128,2,128]{2,1,0:T(2,128)S(1)}, u32[]{:S(2)}, u32[]{:S(2)}) async-start(f32[128,2,128]{2,1,0:T(2,128)} %get-tuple-element.20), calls=%async_computation | async-start | bytes 262144 | tf_op jit(solution)/shard_map/all_to_all | solution.py:533
  43.0 26.4 %all-to-all-start.1 = ((f32[32,80,128]{2,1,0:T(8,128)}), f32[32,80,128]{2,1,0:T(8,128)S(1)}, u32[]{:S(2)}, u32[]{:S(2)}) async-start(f32[32,80,128]{2,1,0:T(8,128)} %shard_map.105), calls=%async_computation.1 | async-start | bytes 2621440 | tf_op jit(solution)/shard_map/all_to_all | solution.py:507
  47.6 2.6 %collective-permute-start.2 = (f32[3,256]{1,0:T(4,128)S(1)}, f32[3,256]{1,0:T(4,128)S(1)}, u32[]{:S(2)}, u32[]{:S(2)}) collective-permute-start(f32[3,256]{1,0:T(4,128)S(1)} %get-tuple-element.21), channel_id=1, source_target_pairs={{0,1},{1,2},{2,3},{3,4},{4,5},{5,6},{6,7},{7,8},{8,9},{9,10},{10,1... | collective-permute-start | bytes 9224 | tf_op jit(solution)/shard_map/ppermute | solution.py:489
  49.0 3.2 %collective-permute-start.3 = (f32[3,256]{1,0:T(4,128)S(1)}, f32[3,256]{1,0:T(4,128)S(1)}, u32[]{:S(2)}, u32[]{:S(2)}) collective-permute-start(f32[3,256]{1,0:T(4,128)S(1)} %get-tuple-element.22), channel_id=1, source_target_pairs={{1,0},{2,1},{3,2},{4,3},{5,4},{6,5},{7,6},{8,7},{9,8},{10,9},{11,1... | collective-permute-start | bytes 9224 | tf_op jit(solution)/shard_map/ppermute | solution.py:489
  73.5 3.2 %collective-permute-start.6 = (f32[32,128]{1,0:T(8,128)S(1)}, f32[32,128]{1,0:T(8,128)S(1)}, u32[]{:S(2)}, u32[]{:S(2)}) collective-permute-start(f32[32,128]{1,0:T(8,128)S(1)} %get-tuple-element.24.p0), channel_id=1, source_target_pairs={{0,3},{1,2},{2,1},{3,0},{4,7},{5,6},{6,5},{7,4},{8,11},{9,10},{10,... | collective-permute-start | bytes 49160 | tf_op jit(solution)/shard_map/ppermute | solution.py:479
  73.6 3.8 %collective-permute-start.5 = (f32[32,128]{1,0:T(8,128)S(1)}, f32[32,128]{1,0:T(8,128)S(1)}, u32[]{:S(2)}, u32[]{:S(2)}) collective-permute-start(f32[32,128]{1,0:T(8,128)S(1)} %get-tuple-element.24.p0), channel_id=1, source_target_pairs={{0,2},{1,3},{2,0},{3,1},{4,6},{5,7},{6,4},{7,5},{8,10},{9,11},{10,... | collective-permute-start | bytes 49160 | tf_op jit(solution)/shard_map/ppermute | solution.py:479
  73.7 3.7 %collective-permute-start.4 = (f32[32,128]{1,0:T(8,128)S(1)}, f32[32,128]{1,0:T(8,128)S(1)}, u32[]{:S(2)}, u32[]{:S(2)}) collective-permute-start(f32[32,128]{1,0:T(8,128)S(1)} %get-tuple-element.24.p0), channel_id=1, source_target_pairs={{0,1},{1,0},{2,3},{3,2},{4,5},{5,4},{6,7},{7,6},{8,9},{9,8},{10,11... | collective-permute-start | bytes 49160 | tf_op jit(solution)/shard_map/ppermute | solution.py:479
  80.1 3.2 %collective-permute-start.9 = (f32[32,128]{1,0:T(8,128)S(1)}, f32[32,128]{1,0:T(8,128)S(1)}, u32[]{:S(2)}, u32[]{:S(2)}) collective-permute-start(f32[32,128]{1,0:T(8,128)S(1)} %shard_map.107.p0), channel_id=1, source_target_pairs={{0,3},{1,2},{2,1},{3,0},{4,7},{5,6},{6,5},{7,4},{8,11},{9,10},{10,... | collective-permute-start | bytes 49160 | tf_op jit(solution)/shard_map/ppermute | solution.py:479
  80.7 3.7 %collective-permute-start.8 = (f32[32,128]{1,0:T(8,128)S(1)}, f32[32,128]{1,0:T(8,128)S(1)}, u32[]{:S(2)}, u32[]{:S(2)}) collective-permute-start(f32[32,128]{1,0:T(8,128)S(1)} %shard_map.107.p0), channel_id=1, source_target_pairs={{0,2},{1,3},{2,0},{3,1},{4,6},{5,7},{6,4},{7,5},{8,10},{9,11},{10,... | collective-permute-start | bytes 49160 | tf_op jit(solution)/shard_map/ppermute | solution.py:479
  80.7 3.7 %collective-permute-start.7 = (f32[32,128]{1,0:T(8,128)S(1)}, f32[32,128]{1,0:T(8,128)S(1)}, u32[]{:S(2)}, u32[]{:S(2)}) collective-permute-start(f32[32,128]{1,0:T(8,128)S(1)} %shard_map.107.p0), channel_id=1, source_target_pairs={{0,1},{1,0},{2,3},{3,2},{4,5},{5,4},{6,7},{7,6},{8,9},{9,8},{10,11... | collective-permute-start | bytes 49160 | tf_op jit(solution)/shard_map/ppermute | solution.py:479
  87.1 3.2 %collective-permute-start.12 = (f32[32,128]{1,0:T(8,128)S(1)}, f32[32,128]{1,0:T(8,128)S(1)}, u32[]{:S(2)}, u32[]{:S(2)}) collective-permute-start(f32[32,128]{1,0:T(8,128)S(1)} %shard_map.108.p0), channel_id=1, source_target_pairs={{0,3},{1,2},{2,1},{3,0},{4,7},{5,6},{6,5},{7,4},{8,11},{9,10},{10,... | collective-permute-start | bytes 49160 | tf_op jit(solution)/shard_map/ppermute | solution.py:479
  87.3 3.7 %collective-permute-start.11 = (f32[32,128]{1,0:T(8,128)S(1)}, f32[32,128]{1,0:T(8,128)S(1)}, u32[]{:S(2)}, u32[]{:S(2)}) collective-permute-start(f32[32,128]{1,0:T(8,128)S(1)} %shard_map.108.p0), channel_id=1, source_target_pairs={{0,2},{1,3},{2,0},{3,1},{4,6},{5,7},{6,4},{7,5},{8,10},{9,11},{10,... | collective-permute-start | bytes 49160 | tf_op jit(solution)/shard_map/ppermute | solution.py:479
  87.3 3.7 %collective-permute-start.10 = (f32[32,128]{1,0:T(8,128)S(1)}, f32[32,128]{1,0:T(8,128)S(1)}, u32[]{:S(2)}, u32[]{:S(2)}) collective-permute-start(f32[32,128]{1,0:T(8,128)S(1)} %shard_map.108.p0), channel_id=1, source_target_pairs={{0,1},{1,0},{2,3},{3,2},{4,5},{5,4},{6,7},{7,6},{8,9},{9,8},{10,11... | collective-permute-start | bytes 49160 | tf_op jit(solution)/shard_map/ppermute | solution.py:479
  93.7 3.2 %collective-permute-start.15 = (f32[32,128]{1,0:T(8,128)S(1)}, f32[32,128]{1,0:T(8,128)S(1)}, u32[]{:S(2)}, u32[]{:S(2)}) collective-permute-start(f32[32,128]{1,0:T(8,128)S(1)} %shard_map.109.p0), channel_id=1, source_target_pairs={{0,3},{1,2},{2,1},{3,0},{4,7},{5,6},{6,5},{7,4},{8,11},{9,10},{10,... | collective-permute-start | bytes 49160 | tf_op jit(solution)/shard_map/ppermute | solution.py:479
  94.3 3.7 %collective-permute-start.14 = (f32[32,128]{1,0:T(8,128)S(1)}, f32[32,128]{1,0:T(8,128)S(1)}, u32[]{:S(2)}, u32[]{:S(2)}) collective-permute-start(f32[32,128]{1,0:T(8,128)S(1)} %shard_map.109.p0), channel_id=1, source_target_pairs={{0,2},{1,3},{2,0},{3,1},{4,6},{5,7},{6,4},{7,5},{8,10},{9,11},{10,... | collective-permute-start | bytes 49160 | tf_op jit(solution)/shard_map/ppermute | solution.py:479
  94.3 3.7 %collective-permute-start.13 = (f32[32,128]{1,0:T(8,128)S(1)}, f32[32,128]{1,0:T(8,128)S(1)}, u32[]{:S(2)}, u32[]{:S(2)}) collective-permute-start(f32[32,128]{1,0:T(8,128)S(1)} %shard_map.109.p0), channel_id=1, source_target_pairs={{0,1},{1,0},{2,3},{3,2},{4,5},{5,4},{6,7},{7,6},{8,9},{9,8},{10,11... | collective-permute-start | bytes 49160 | tf_op jit(solution)/shard_map/ppermute | solution.py:479
  100.7 3.2 %collective-permute-start.18 = (f32[32,128]{1,0:T(8,128)S(1)}, f32[32,128]{1,0:T(8,128)S(1)}, u32[]{:S(2)}, u32[]{:S(2)}) collective-permute-start(f32[32,128]{1,0:T(8,128)S(1)} %shard_map.110.p0), channel_id=1, source_target_pairs={{0,3},{1,2},{2,1},{3,0},{4,7},{5,6},{6,5},{7,4},{8,11},{9,10},{10,... | collective-permute-start | bytes 49160 | tf_op jit(solution)/shard_map/ppermute | solution.py:479
  100.9 3.7 %collective-permute-start.17 = (f32[32,128]{1,0:T(8,128)S(1)}, f32[32,128]{1,0:T(8,128)S(1)}, u32[]{:S(2)}, u32[]{:S(2)}) collective-permute-start(f32[32,128]{1,0:T(8,128)S(1)} %shard_map.110.p0), channel_id=1, source_target_pairs={{0,2},{1,3},{2,0},{3,1},{4,6},{5,7},{6,4},{7,5},{8,10},{9,11},{10,... | collective-permute-start | bytes 49160 | tf_op jit(solution)/shard_map/ppermute | solution.py:479
  100.9 3.7 %collective-permute-start.16 = (f32[32,128]{1,0:T(8,128)S(1)}, f32[32,128]{1,0:T(8,128)S(1)}, u32[]{:S(2)}, u32[]{:S(2)}) collective-permute-start(f32[32,128]{1,0:T(8,128)S(1)} %shard_map.110.p0), channel_id=1, source_target_pairs={{0,1},{1,0},{2,3},{3,2},{4,5},{5,4},{6,7},{7,6},{8,9},{9,8},{10,11... | collective-permute-start | bytes 49160 | tf_op jit(solution)/shard_map/ppermute | solution.py:479

commit v10 on v9

--- a/solution.py
+++ b/solution.py
@@ -209,11 +209,11 @@
     row = jnp.concatenate(
         [sums[0:1], sums[1:2], sums[2:3], owner_row[...].astype(f32)], axis=1
     )
-    send[:, 0, :] = jnp.broadcast_to(row, (LANES, LANES))
+    send[0, 0:1, :] = row
     row = jnp.concatenate(
         [cdia[0:1], cdia[1:2], cdia[2:3], jnp.ones((1, 32), f32)], axis=1
     )
-    send[:, 1, :] = jnp.broadcast_to(row, (LANES, LANES))
+    send[0, 1:2, :] = row
 
 
 def parity(p):
@@ -233,6 +233,13 @@
     side = lax.bitwise_xor(side, lax.bitwise_and(q, 1))
     core = lax.bitwise_and(lax.bitwise_xor(lax.shift_right_logical(q, 5), me), 1)
     return lax.shift_left(lax.bitwise_and(q, 31), 2) + lax.shift_left(side, 1) + core
+
+
+def row_of_device(p, me):
+    p = lax.bitwise_xor(p, me)
+    far = lax.shift_left(lax.bitwise_and(lax.shift_right_logical(p, 2), 1), 6)
+    yz = lax.shift_left(lax.shift_right_logical(p, 3), 2)
+    return far + yz + lax.bitwise_and(p, 3)
 
 
 def row_groups():
@@ -369,7 +376,7 @@
         left[...], right[...], (((1,), (1,)), ((), ())), preferred_element_type=f32
     )
     crhs = both[0:96] + both[96:192] + both[192:288]
-    order = device_of_lane(lax.broadcasted_iota(i32, (96, LANES), 1), me)
+    order = row_of_device(device_of_lane(lax.broadcasted_iota(i32, (96, LANES), 1), me), me)
     cdia = jnp.take_along_axis(
         jnp.transpose(sums[:, 1, :])[0:96], order, axis=1, mode="promise_in_bounds"
     )
@@ -474,11 +481,12 @@
     )(*args)
 
 
+def partner(value, bits):
+    return lax.ppermute(value, DOM, [(i, i ^ bits) for i in range(lax.axis_size(DOM))])
+
+
 def in_group(new):
-    def partner(bits):
-        return lax.ppermute(new, DOM, [(i, i ^ bits) for i in range(lax.axis_size(DOM))])
-
-    p2, p3, p1 = partner(2), partner(3), partner(1)
+    p2, p3, p1 = partner(new, 2), partner(new, 3), partner(new, 1)
     return new, p1, p2, p3
 
 
@@ -519,18 +527,20 @@
             pltpu.VMEM((2, SLOTS, HALO), i32), pltpu.VMEM((2, 3, 3, SLOTS, HALO), f32),
             pltpu.VMEM((8, LANES), i32), pltpu.VMEM((1, 32), i32), pltpu.SemaphoreType.DMA((8,)),
         ],
-        compiler_params=pltpu.CompilerParams(vmem_limit_bytes=12 * 2**20),
+        compiler_params=pltpu.CompilerParams(vmem_limit_bytes=60 * 2**20),
     )(rhs, dia, col, blk, agg, owner)
     before, after = shifts(up, down)
     send, first_iter, wrhs, wdia, up2, down2 = call(
         pre_kernel,
-        [((LANES, 2, LANES), f32), ((3, wide), f32), ((3, wide), f32), ((3, wide), f32),
+        [((1, 2, LANES), f32), ((3, wide), f32), ((3, wide), f32), ((3, wide), f32),
          ((3, HALO), f32), ((3, HALO), f32)],
         [base, rhs, dia, col, blk, agg, owner, cdia, before, after],
         scratch=[(3, wide), (3, wide), (8, ROWS)], scalars=1,
     )
     before2, after2 = shifts(up2, down2)
-    sums = lax.all_to_all(send, DOM, 0, 0, tiled=True)
+    sums = send
+    for bits in ((1, 2, 3), (8, 16, 24), (32, 64, 96), (4,)):
+        sums = jnp.concatenate([sums] + [partner(sums, b) for b in bits], axis=0)
     peers = ((PEERS, LANES), f32)
     gather = (3, PEERS, LANES)
     square = (LANES, LANES)

time: 108 us -> 99.3 us (0.919)
  the two profiles are of different devices: /device:TPU:0 before, /device:TPU:16 now
where the time goes in v10:
time: 99.3 us; the launch traced here: 98.9 us
  starting transfers between devices  49.6 us (50%)
  Pallas kernels  24.2 us (24%)
  waiting for transfers between devices  24 us (24%)
    ppermute x25, starting transfers between devices, partner(): lax.ppermute(value, DOM, [(i, i ^ bits) for i in range(lax.axis_size(DOM))])  23.5 us
    ppermute x25, waiting for transfers between devices, partner(): lax.ppermute(value, DOM, [(i, i ^ bits) for i in range(lax.axis_size(DOM))])  22.7 us
    pallas_call x8, Pallas kernels, call(): pl.pallas_call(kernel, in_specs=[smem] * scalars + [vmem] * (len(args) -...  22 us
    ppermute x4, starting transfers between devices, shifts(): return (lax.ppermute(up, DOM, forward), lax.ppermute(down, DOM, backward))  19.6 us
    all_to_all x1, starting transfers between devices, cycle(): lax.all_to_all(dsend, DOM, 0, 0, axis_index_groups=row_groups(), tiled=True)  6.56 us
    pallas_call x1, Pallas kernels, cycle(): pl.pallas_call(pack_kernel, name='pack', in_specs=[far] * 6, out_specs=[v...  2.21 us
  transfers between devices with their start and end apart: 30, of which 16 were waited for; matrix products, arithmetic and copies ran while one was open for 0% of the time, Pallas kernels for 5%

profile of v10, /device:TPU:16, one launch (start us, length us, event | category | flops | bytes accessed | tf_op | source)
XLA Modules:
  0.0 98.9 jit_solution(12795668438893154979)
XLA Ops:
  0.6 2.2 %pack.1 = (f32[288,256]{1,0:T(8,128)}, f32[288,256]{1,0:T(8,128)}, f32[8,128]{1,0:T(8,128)}) custom-call(f32[3,1024]{1,0:T(4,128)} %bitcast.17, f32[3,1024]{1,0:T(4,128)} %bitcast.19, s32[27,1024]{1,0:T(8,128)} %bitcast.14, f32[3,3,27,1024]{3,2,1,0:T(8,128)} %bitcast.11, s32[8,128]{1,0:T(8,128)} %bitcast.21, s32[1,32]{1,0:T(1,128)} %bitcast.24), custom_call_target="tpu_custom_call" | custom-call | tf_op jit(solution)/shard_map/pack/pallas_call | solution.py:519
  2.8 1.9 %collective-permute-start = (f32[288,256]{1,0:T(8,128)}, f32[288,256]{1,0:T(8,128)S(1)}, u32[]{:S(2)}, u32[]{:S(2)}) collective-permute-start(f32[288,256]{1,0:T(8,128)} %get-tuple-element.18), channel_id=1, source_target_pairs={{0,1},{1,2},{2,3},{3,4},{4,5},{5,6},{6,7},{7,8},{8,9},{9,10},{10,1... | collective-permute-start | bytes 884744 | tf_op jit(solution)/shard_map/ppermute | solution.py:497
  4.8 7.9 %collective-permute-start.1 = (f32[288,256]{1,0:T(8,128)}, f32[288,256]{1,0:T(8,128)S(1)}, u32[]{:S(2)}, u32[]{:S(2)}) collective-permute-start(f32[288,256]{1,0:T(8,128)} %get-tuple-element.19), channel_id=1, source_target_pairs={{1,0},{2,1},{3,2},{4,3},{5,4},{6,5},{7,6},{8,7},{9,8},{10,9},{11,1... | collective-permute-start | bytes 884744 | tf_op jit(solution)/shard_map/ppermute | solution.py:497
  12.6 2.5 %shard_map.105 = f32[32,80,128]{2,1,0:T(8,128)} custom-call(s32[32,27]{1,0:T(8,128)} %col.1, f32[3,3,32,27]{3,2,1,0:T(8,128)} %bitcast.26), custom_call_target="tpu_custom_call" | custom-call | tf_op jit(solution)/shard_map/pallas_call | solution.py:472
  15.2 6.6 %all-to-all-start = ((f32[32,80,128]{2,1,0:T(8,128)}), f32[32,80,128]{2,1,0:T(8,128)S(1)}, u32[]{:S(2)}, u32[]{:S(2)}) async-start(f32[32,80,128]{2,1,0:T(8,128)} %shard_map.105), calls=%async_computation | async-start | bytes 2621440 | tf_op jit(solution)/shard_map/all_to_all | solution.py:515
  21.8 2.1 %shard_map.104 = (f32[1,2,128]{2,1,0:T(2,128)S(1)}, f32[3,2048]{1,0:T(4,128)S(1)}, f32[3,2048]{1,0:T(4,128)S(1)}, f32[3,2048]{1,0:T(4,128)S(1)}, f32[3,256]{1,0:T(4,128)S(1)}, /*index=5*/f32[3,256]{1,0:T(4,128)S(1)}) custom-call(s32[1]{0:T(128)} %bitcast.base_ref, f32[3,1024]{1,0:T(4,128)S(1)} %bitcast.18, f32[3,1024]{1,0:T(4,128)S(1)} %bitcast.20, ...), custom_call_target="tpu_custom_call" | custom-call | tf_op jit(solution)/shard_map/pallas_call | solution.py:472
  23.9 0.9 collective-permute-start.3
  24.7 1.0 %collective-permute-start.2 = (f32[1,2,128]{2,1,0:T(2,128)S(1)}, f32[1,2,128]{2,1,0:T(2,128)S(1)}, u32[]{:S(2)}, u32[]{:S(2)}) collective-permute-start(f32[1,2,128]{2,1,0:T(2,128)S(1)} %get-tuple-element.20), channel_id=1, source_target_pairs={{0,1},{1,0},{2,3},{3,2},{4,5},{5,4},{6,7},{7,6},{8,9},{9,8},{10,11... | collective-permute-start | bytes 3080 | tf_op jit(solution)/shard_map/ppermute | solution.py:485
  25.8 0.8 collective-permute-done.2
  26.6 0.9 collective-permute-done.3
  27.5 1.5 %collective-permute-start.5 = (f32[4,2,128]{2,1,0:T(2,128)S(1)}, f32[4,2,128]{2,1,0:T(2,128)S(1)}, u32[]{:S(2)}, u32[]{:S(2)}) collective-permute-start(f32[4,2,128]{2,1,0:T(2,128)S(1)} %get-tuple-element.52), channel_id=1, source_target_pairs={{0,8},{1,9},{2,10},{3,11},{4,12},{5,13},{6,14},{7,15},{8,0},{9,1},... | collective-permute-start | bytes 12296 | tf_op jit(solution)/shard_map/ppermute | solution.py:485
  29.1 2.1 %collective-permute-start.7 = (f32[4,2,128]{2,1,0:T(2,128)S(1)}, f32[4,2,128]{2,1,0:T(2,128)S(1)}, u32[]{:S(2)}, u32[]{:S(2)}) collective-permute-start(f32[4,2,128]{2,1,0:T(2,128)S(1)} %get-tuple-element.52), channel_id=1, source_target_pairs={{0,24},{1,25},{2,26},{3,27},{4,28},{5,29},{6,30},{7,31},{8,16},{9,... | collective-permute-start | bytes 12296 | tf_op jit(solution)/shard_map/ppermute | solution.py:485
  31.1 0.6 collective-permute-start.6
  31.8 2.5 %collective-permute-done.5 = f32[4,2,128]{2,1,0:T(2,128)S(1)} collective-permute-done((f32[4,2,128]{2,1,0:T(2,128)S(1)}, f32[4,2,128]{2,1,0:T(2,128)S(1)}, u32[]{:S(2)}, u32[]{:S(2)}) %collective-permute-start.5) | collective-permute-done | bytes 4128 | tf_op jit(solution)/shard_map/ppermute | solution.py:485
  34.3 3.9 %collective-permute-done.6 = f32[4,2,128]{2,1,0:T(2,128)S(1)} collective-permute-done((f32[4,2,128]{2,1,0:T(2,128)S(1)}, f32[4,2,128]{2,1,0:T(2,128)S(1)}, u32[]{:S(2)}, u32[]{:S(2)}) %collective-permute-start.6) | collective-permute-done | bytes 4128 | tf_op jit(solution)/shard_map/ppermute | solution.py:485
  38.2 1.3 %collective-permute-start.8 = (f32[16,2,128]{2,1,0:T(2,128)S(1)}, f32[16,2,128]{2,1,0:T(2,128)S(1)}, u32[]{:S(2)}, u32[]{:S(2)}) collective-permute-start(f32[16,2,128]{2,1,0:T(2,128)S(1)} %get-tuple-element.42), channel_id=1, source_target_pairs={{0,32},{1,33},{2,34},{3,35},{4,36},{5,37},{6,38},{7,39},{8,40},{9,... | collective-permute-start | bytes 49160 | tf_op jit(solution)/shard_map/ppermute | solution.py:485
  39.5 1.5 %collective-permute-start.10 = (f32[16,2,128]{2,1,0:T(2,128)S(1)}, f32[16,2,128]{2,1,0:T(2,128)S(1)}, u32[]{:S(2)}, u32[]{:S(2)}) collective-permute-start(f32[16,2,128]{2,1,0:T(2,128)S(1)} %get-tuple-element.42), channel_id=1, source_target_pairs={{0,96},{1,97},{2,98},{3,99},{4,100},{5,101},{6,102},{7,103},{8,104... | collective-permute-start | bytes 49160 | tf_op jit(solution)/shard_map/ppermute | solution.py:485
  41.0 1.4 %collective-permute-start.9 = (f32[16,2,128]{2,1,0:T(2,128)S(1)}, f32[16,2,128]{2,1,0:T(2,128)S(1)}, u32[]{:S(2)}, u32[]{:S(2)}) collective-permute-start(f32[16,2,128]{2,1,0:T(2,128)S(1)} %get-tuple-element.42), channel_id=1, source_target_pairs={{0,64},{1,65},{2,66},{3,67},{4,68},{5,69},{6,70},{7,71},{8,72},{9,... | collective-permute-start | bytes 49160 | tf_op jit(solution)/shard_map/ppermute | solution.py:485
  42.4 3.9 %collective-permute-done.9 = f32[16,2,128]{2,1,0:T(2,128)S(1)} collective-permute-done((f32[16,2,128]{2,1,0:T(2,128)S(1)}, f32[16,2,128]{2,1,0:T(2,128)S(1)}, u32[]{:S(2)}, u32[]{:S(2)}) %collective-permute-start.9) | collective-permute-done | bytes 16416 | tf_op jit(solution)/shard_map/ppermute | solution.py:485
  46.3 3.4 %collective-permute-start.11 = (f32[64,2,128]{2,1,0:T(2,128)S(1)}, f32[64,2,128]{2,1,0:T(2,128)S(1)}, u32[]{:S(2)}, u32[]{:S(2)}) collective-permute-start(f32[64,2,128]{2,1,0:T(2,128)S(1)} %get-tuple-element.34), channel_id=1, source_target_pairs={{0,4},{1,5},{2,6},{3,7},{4,0},{5,1},{6,2},{7,3},{8,12},{9,13},{10,... | collective-permute-start | bytes 196616 | tf_op jit(solution)/shard_map/ppermute | solution.py:485
  49.7 1.9 %collective-permute-start.12 = (f32[3,256]{1,0:T(4,128)S(1)}, f32[3,256]{1,0:T(4,128)S(1)}, u32[]{:S(2)}, u32[]{:S(2)}) collective-permute-start(f32[3,256]{1,0:T(4,128)S(1)} %get-tuple-element.21), channel_id=1, source_target_pairs={{0,1},{1,2},{2,3},{3,4},{4,5},{5,6},{6,7},{7,8},{8,9},{9,10},{10,1... | collective-permute-start | bytes 9224 | tf_op jit(solution)/shard_map/ppermute | solution.py:497
  51.6 7.9 %collective-permute-start.13 = (f32[3,256]{1,0:T(4,128)S(1)}, f32[3,256]{1,0:T(4,128)S(1)}, u32[]{:S(2)}, u32[]{:S(2)}) collective-permute-start(f32[3,256]{1,0:T(4,128)S(1)} %get-tuple-element.22), channel_id=1, source_target_pairs={{1,0},{2,1},{3,2},{4,3},{5,4},{6,5},{7,6},{8,7},{9,8},{10,9},{11,1... | collective-permute-start | bytes 9224 | tf_op jit(solution)/shard_map/ppermute | solution.py:497
  59.5 1.3 %collective-permute-done.13.far_down.after2 = f32[3,256]{1,0:T(4,128)S(1)} collective-permute-done((f32[3,256]{1,0:T(4,128)S(1)}, f32[3,256]{1,0:T(4,128)S(1)}, u32[]{:S(2)}, u32[]{:S(2)}) %collective-permute-start.13) | collective-permute-done | bytes 3104 | tf_op jit(solution)/shard_map/ppermute | solution.py:497
  60.8 4.1 %shard_map.106 = (f32[32,128]{1,0:T(8,128)S(1)}, f32[32,128]{1,0:T(8,128)S(1)}, f32[32,128]{1,0:T(8,128)S(1)}, s32[32,8,128]{2,1,0:T(8,128)S(1)}, s32[8,128]{1,0:T(8,128)S(1)}) custom-call(s32[1]{0:T(128)} %bitcast.base_ref, f32[128,2,128]{2,1,0:T(2,128)S(1)} %constant_dynamic-update-slice_fusion.21.sums, f32[32,80,128]{2,1,0:T(8,128)S(1)} %all-to-all-done.data, ...), custom_call_target="tpu_custom_call" | custom-call | tf_op jit(solution)/shard_map/pallas_call | solution.py:472
  65.1 1.8 %collective-permute-start.14 = (f32[32,128]{1,0:T(8,128)S(1)}, f32[32,128]{1,0:T(8,128)S(1)}, u32[]{:S(2)}, u32[]{:S(2)}) collective-permute-start(f32[32,128]{1,0:T(8,128)S(1)} %get-tuple-element.24.p0), channel_id=1, source_target_pairs={{0,1},{1,0},{2,3},{3,2},{4,5},{5,4},{6,7},{7,6},{8,9},{9,8},{10,11... | collective-permute-start | bytes 49160 | tf_op jit(solution)/shard_map/ppermute | solution.py:485
  66.9 1.3 %collective-permute-done.16.p3 = f32[32,128]{1,0:T(8,128)S(1)} collective-permute-done((f32[32,128]{1,0:T(8,128)S(1)}, f32[32,128]{1,0:T(8,128)S(1)}, u32[]{:S(2)}, u32[]{:S(2)}) %collective-permute-start.16) | collective-permute-done | bytes 16416 | tf_op jit(solution)/shard_map/ppermute | solution.py:485
  68.2 0.7 collective-permute-done.15.p2
  68.8 2.7 %shard_map.107.p0 = f32[32,128]{1,0:T(8,128)S(1)} custom-call(s32[1]{0:T(128)} %bitcast.base_ref, s32[8,128]{1,0:T(8,128)S(1)} %get-tuple-element.23.passes, f32[32,128]{1,0:T(8,128)S(1)} %get-tuple-element.24.p0, f32[32,128]{1,0:T(8,128)S(1)} %collective-permute-done.14.p1, f32[32,128]{1,0:T(8,128)S(1)} %collective-permute-done.15.p2, ...), custom_call_target="tpu_custom_call" | custom-call | tf_op jit(solution)/shard_map/pallas_call | solution.py:472
  71.5 0.6 collective-permute-start.19
  72.1 1.4 %collective-permute-start.17 = (f32[32,128]{1,0:T(8,128)S(1)}, f32[32,128]{1,0:T(8,128)S(1)}, u32[]{:S(2)}, u32[]{:S(2)}) collective-permute-start(f32[32,128]{1,0:T(8,128)S(1)} %shard_map.107.p0), channel_id=1, source_target_pairs={{0,1},{1,0},{2,3},{3,2},{4,5},{5,4},{6,7},{7,6},{8,9},{9,8},{10,11... | collective-permute-start | bytes 49160 | tf_op jit(solution)/shard_map/ppermute | solution.py:485
  73.5 1.3 %collective-permute-done.19.p3 = f32[32,128]{1,0:T(8,128)S(1)} collective-permute-done((f32[32,128]{1,0:T(8,128)S(1)}, f32[32,128]{1,0:T(8,128)S(1)}, u32[]{:S(2)}, u32[]{:S(2)}) %collective-permute-start.19) | collective-permute-done | bytes 16416 | tf_op jit(solution)/shard_map/ppermute | solution.py:485
  74.8 1.1 %collective-permute-done.18.p2 = f32[32,128]{1,0:T(8,128)S(1)} collective-permute-done((f32[32,128]{1,0:T(8,128)S(1)}, f32[32,128]{1,0:T(8,128)S(1)}, u32[]{:S(2)}, u32[]{:S(2)}) %collective-permute-start.18) | collective-permute-done | bytes 16416 | tf_op jit(solution)/shard_map/ppermute | solution.py:485
  75.8 2.7 %shard_map.108.p0 = f32[32,128]{1,0:T(8,128)S(1)} custom-call(s32[1]{0:T(128)} %bitcast.base_ref, s32[8,128]{1,0:T(8,128)S(1)} %get-tuple-element.23.passes, f32[32,128]{1,0:T(8,128)S(1)} %shard_map.107.p0, f32[32,128]{1,0:T(8,128)S(1)} %collective-permute-done.17.p1, f32[32,128]{1,0:T(8,128)S(1)} %collective-permute-done.18.p2, ...), custom_call_target="tpu_custom_call" | custom-call | tf_op jit(solution)/shard_map/pallas_call | solution.py:472
  78.5 0.2 collective-permute-start.22
  78.7 1.8 %collective-permute-start.20 = (f32[32,128]{1,0:T(8,128)S(1)}, f32[32,128]{1,0:T(8,128)S(1)}, u32[]{:S(2)}, u32[]{:S(2)}) collective-permute-start(f32[32,128]{1,0:T(8,128)S(1)} %shard_map.108.p0), channel_id=1, source_target_pairs={{0,1},{1,0},{2,3},{3,2},{4,5},{5,4},{6,7},{7,6},{8,9},{9,8},{10,11... | collective-permute-start | bytes 49160 | tf_op jit(solution)/shard_map/ppermute | solution.py:485
  80.5 1.3 %collective-permute-done.22.p3 = f32[32,128]{1,0:T(8,128)S(1)} collective-permute-done((f32[32,128]{1,0:T(8,128)S(1)}, f32[32,128]{1,0:T(8,128)S(1)}, u32[]{:S(2)}, u32[]{:S(2)}) %collective-permute-start.22) | collective-permute-done | bytes 16416 | tf_op jit(solution)/shard_map/ppermute | solution.py:485
  81.8 0.7 collective-permute-done.21.p2
  82.4 2.7 %shard_map.109.p0 = f32[32,128]{1,0:T(8,128)S(1)} custom-call(s32[1]{0:T(128)} %bitcast.base_ref, s32[8,128]{1,0:T(8,128)S(1)} %get-tuple-element.23.passes, f32[32,128]{1,0:T(8,128)S(1)} %shard_map.108.p0, f32[32,128]{1,0:T(8,128)S(1)} %collective-permute-done.20.p1, f32[32,128]{1,0:T(8,128)S(1)} %collective-permute-done.21.p2, ...), custom_call_target="tpu_custom_call" | custom-call | tf_op jit(solution)/shard_map/pallas_call | solution.py:472
  85.1 0.8 collective-permute-start.25
  85.9 1.4 %collective-permute-start.23 = (f32[32,128]{1,0:T(8,128)S(1)}, f32[32,128]{1,0:T(8,128)S(1)}, u32[]{:S(2)}, u32[]{:S(2)}) collective-permute-start(f32[32,128]{1,0:T(8,128)S(1)} %shard_map.109.p0), channel_id=1, source_target_pairs={{0,1},{1,0},{2,3},{3,2},{4,5},{5,4},{6,7},{7,6},{8,9},{9,8},{10,11... | collective-permute-start | bytes 49160 | tf_op jit(solution)/shard_map/ppermute | solution.py:485
  87.2 1.3 %collective-permute-done.25.p3 = f32[32,128]{1,0:T(8,128)S(1)} collective-permute-done((f32[32,128]{1,0:T(8,128)S(1)}, f32[32,128]{1,0:T(8,128)S(1)}, u32[]{:S(2)}, u32[]{:S(2)}) %collective-permute-start.25) | collective-permute-done | bytes 16416 | tf_op jit(solution)/shard_map/ppermute | solution.py:485
  88.5 1.1 %collective-permute-done.24.p2 = f32[32,128]{1,0:T(8,128)S(1)} collective-permute-done((f32[32,128]{1,0:T(8,128)S(1)}, f32[32,128]{1,0:T(8,128)S(1)}, u32[]{:S(2)}, u32[]{:S(2)}) %collective-permute-start.24) | collective-permute-done | bytes 16416 | tf_op jit(solution)/shard_map/ppermute | solution.py:485
  89.6 2.7 %shard_map.110.p0 = f32[32,128]{1,0:T(8,128)S(1)} custom-call(s32[1]{0:T(128)} %bitcast.base_ref, s32[8,128]{1,0:T(8,128)S(1)} %get-tuple-element.23.passes, f32[32,128]{1,0:T(8,128)S(1)} %shard_map.109.p0, f32[32,128]{1,0:T(8,128)S(1)} %collective-permute-done.23.p1, f32[32,128]{1,0:T(8,128)S(1)} %collective-permute-done.24.p2, ...), custom_call_target="tpu_custom_call" | custom-call | tf_op jit(solution)/shard_map/pallas_call | solution.py:472
  92.3 0.2 collective-permute-start.28
  92.5 1.8 %collective-permute-start.26 = (f32[32,128]{1,0:T(8,128)S(1)}, f32[32,128]{1,0:T(8,128)S(1)}, u32[]{:S(2)}, u32[]{:S(2)}) collective-permute-start(f32[32,128]{1,0:T(8,128)S(1)} %shard_map.110.p0), channel_id=1, source_target_pairs={{0,1},{1,0},{2,3},{3,2},{4,5},{5,4},{6,7},{7,6},{8,9},{9,8},{10,11... | collective-permute-start | bytes 49160 | tf_op jit(solution)/shard_map/ppermute | solution.py:485
  94.2 1.3 %collective-permute-done.28.p3 = f32[32,128]{1,0:T(8,128)S(1)} collective-permute-done((f32[32,128]{1,0:T(8,128)S(1)}, f32[32,128]{1,0:T(8,128)S(1)}, u32[]{:S(2)}, u32[]{:S(2)}) %collective-permute-start.28) | collective-permute-done | bytes 16416 | tf_op jit(solution)/shard_map/ppermute | solution.py:485
  95.5 0.7 collective-permute-done.27.p2
  96.2 2.6 %shard_map.111 = (f32[3,1024]{1,0:T(4,128)}, f32[3,32]{1,0:T(4,128)}) custom-call(s32[1]{0:T(128)} %bitcast.base_ref, f32[32,128]{1,0:T(8,128)S(1)} %shard_map.110.p0, f32[32,128]{1,0:T(8,128)S(1)} %collective-permute-done.26.p1, f32[32,128]{1,0:T(8,128)S(1)} %collective-permute-done.27.p2, f32[32,128]{1,0:T(8,128)S(1)} %collective-permute-done.28.p3, ...), custom_call_target="tpu_custom_call" | custom-call | tf_op jit(solution)/shard_map/pallas_call | solution.py:472
  (48 shorter events, 0.4 us)
Async XLA Ops:
  2.8 18.9 %collective-permute-start = (f32[288,256]{1,0:T(8,128)}, f32[288,256]{1,0:T(8,128)S(1)}, u32[]{:S(2)}, u32[]{:S(2)}) collective-permute-start(f32[288,256]{1,0:T(8,128)} %get-tuple-element.18), channel_id=1, source_target_pairs={{0,1},{1,2},{2,3},{3,4},{4,5},{5,6},{6,7},{7,8},{8,9},{9,10},{10,1... | collective-permute-start | bytes 884744 | tf_op jit(solution)/shard_map/ppermute | solution.py:497
  4.8 17.0 %collective-permute-start.1 = (f32[288,256]{1,0:T(8,128)}, f32[288,256]{1,0:T(8,128)S(1)}, u32[]{:S(2)}, u32[]{:S(2)}) collective-permute-start(f32[288,256]{1,0:T(8,128)} %get-tuple-element.19), channel_id=1, source_target_pairs={{1,0},{2,1},{3,2},{4,3},{5,4},{6,5},{7,6},{8,7},{9,8},{10,9},{11,1... | collective-permute-start | bytes 884744 | tf_op jit(solution)/shard_map/ppermute | solution.py:497
  15.1 6.6 %copy-start = (f32[1024,27,3,3]{0,1,3,2:T(8,128)S(1)}, f32[1024,27,3,3]{0,1,3,2:T(8,128)}, u32[]{:S(2)}) copy-start(f32[1024,27,3,3]{0,1,3,2:T(8,128)} %param.12) | copy-start | bytes 2985988
  15.1 6.7 %copy-start.1 = (s32[1024,27]{0,1:T(8,128)S(1)}, s32[1024,27]{0,1:T(8,128)}, u32[]{:S(2)}) copy-start(s32[1024,27]{0,1:T(8,128)} %param.11) | copy-start | bytes 331780
  15.1 6.7 %copy-start.2 = (f32[1024,3]{0,1:T(4,128)S(1)}, f32[1024,3]{0,1:T(4,128)}, u32[]{:S(2)}) copy-start(f32[1024,3]{0,1:T(4,128)} %param.9) | copy-start | bytes 36868
  15.1 6.7 %copy-start.3 = (f32[1024,3]{0,1:T(4,128)S(1)}, f32[1024,3]{0,1:T(4,128)}, u32[]{:S(2)}) copy-start(f32[1024,3]{0,1:T(4,128)} %param.10) | copy-start | bytes 36868
  15.1 6.7 %copy-start.4 = (s32[1024]{0:T(1024)S(1)}, s32[1024]{0:T(1024)}, u32[]{:S(2)}) copy-start(s32[1024]{0:T(1024)} %param.13) | copy-start | bytes 12292
  15.1 6.7 %copy-start.6 = (f32[32,3]{0,1:T(4,128)S(1)}, f32[32,3]{0,1:T(4,128)}, u32[]{:S(2)}) copy-start(f32[32,3]{0,1:T(4,128)} %param.15) | copy-start | bytes 1156
  15.1 6.7 %copy-start.7 = (s32[32]{0:T(128)S(1)}, s32[32]{0:T(128)}, u32[]{:S(2)}) copy-start(s32[32]{0:T(128)} %param.14) | copy-start | bytes 388
  15.2 45.6 %all-to-all-start = ((f32[32,80,128]{2,1,0:T(8,128)}), f32[32,80,128]{2,1,0:T(8,128)S(1)}, u32[]{:S(2)}, u32[]{:S(2)}) async-start(f32[32,80,128]{2,1,0:T(8,128)} %shard_map.105), calls=%async_computation | async-start | bytes 2621440 | tf_op jit(solution)/shard_map/all_to_all | solution.py:515
  23.9 3.6 %collective-permute-start.4 = (f32[1,2,128]{2,1,0:T(2,128)S(1)}, f32[1,2,128]{2,1,0:T(2,128)S(1)}, u32[]{:S(2)}, u32[]{:S(2)}) collective-permute-start(f32[1,2,128]{2,1,0:T(2,128)S(1)} %get-tuple-element.20), channel_id=1, source_target_pairs={{0,3},{1,2},{2,1},{3,0},{4,7},{5,6},{6,5},{7,4},{8,11},{9,10},{10,... | collective-permute-start | bytes 3080 | tf_op jit(solution)/shard_map/ppermute | solution.py:485
  23.9 3.6 %collective-permute-start.3 = (f32[1,2,128]{2,1,0:T(2,128)S(1)}, f32[1,2,128]{2,1,0:T(2,128)S(1)}, u32[]{:S(2)}, u32[]{:S(2)}) collective-permute-start(f32[1,2,128]{2,1,0:T(2,128)S(1)} %get-tuple-element.20), channel_id=1, source_target_pairs={{0,2},{1,3},{2,0},{3,1},{4,6},{5,7},{6,4},{7,5},{8,10},{9,11},{10,... | collective-permute-start | bytes 3080 | tf_op jit(solution)/shard_map/ppermute | solution.py:485
  24.7 1.9 %collective-permute-start.2 = (f32[1,2,128]{2,1,0:T(2,128)S(1)}, f32[1,2,128]{2,1,0:T(2,128)S(1)}, u32[]{:S(2)}, u32[]{:S(2)}) collective-permute-start(f32[1,2,128]{2,1,0:T(2,128)S(1)} %get-tuple-element.20), channel_id=1, source_target_pairs={{0,1},{1,0},{2,3},{3,2},{4,5},{5,4},{6,7},{7,6},{8,9},{9,8},{10,11... | collective-permute-start | bytes 3080 | tf_op jit(solution)/shard_map/ppermute | solution.py:485
  27.5 6.8 %collective-permute-start.5 = (f32[4,2,128]{2,1,0:T(2,128)S(1)}, f32[4,2,128]{2,1,0:T(2,128)S(1)}, u32[]{:S(2)}, u32[]{:S(2)}) collective-permute-start(f32[4,2,128]{2,1,0:T(2,128)S(1)} %get-tuple-element.52), channel_id=1, source_target_pairs={{0,8},{1,9},{2,10},{3,11},{4,12},{5,13},{6,14},{7,15},{8,0},{9,1},... | collective-permute-start | bytes 12296 | tf_op jit(solution)/shard_map/ppermute | solution.py:485
  29.1 9.1 %collective-permute-start.7 = (f32[4,2,128]{2,1,0:T(2,128)S(1)}, f32[4,2,128]{2,1,0:T(2,128)S(1)}, u32[]{:S(2)}, u32[]{:S(2)}) collective-permute-start(f32[4,2,128]{2,1,0:T(2,128)S(1)} %get-tuple-element.52), channel_id=1, source_target_pairs={{0,24},{1,25},{2,26},{3,27},{4,28},{5,29},{6,30},{7,31},{8,16},{9,... | collective-permute-start | bytes 12296 | tf_op jit(solution)/shard_map/ppermute | solution.py:485
  31.1 7.0 %collective-permute-start.6 = (f32[4,2,128]{2,1,0:T(2,128)S(1)}, f32[4,2,128]{2,1,0:T(2,128)S(1)}, u32[]{:S(2)}, u32[]{:S(2)}) collective-permute-start(f32[4,2,128]{2,1,0:T(2,128)S(1)} %get-tuple-element.52), channel_id=1, source_target_pairs={{0,16},{1,17},{2,18},{3,19},{4,20},{5,21},{6,22},{7,23},{8,24},{9,... | collective-permute-start | bytes 12296 | tf_op jit(solution)/shard_map/ppermute | solution.py:485
  38.2 4.2 %collective-permute-start.8 = (f32[16,2,128]{2,1,0:T(2,128)S(1)}, f32[16,2,128]{2,1,0:T(2,128)S(1)}, u32[]{:S(2)}, u32[]{:S(2)}) collective-permute-start(f32[16,2,128]{2,1,0:T(2,128)S(1)} %get-tuple-element.42), channel_id=1, source_target_pairs={{0,32},{1,33},{2,34},{3,35},{4,36},{5,37},{6,38},{7,39},{8,40},{9,... | collective-permute-start | bytes 49160 | tf_op jit(solution)/shard_map/ppermute | solution.py:485
  39.5 6.8 %collective-permute-start.10 = (f32[16,2,128]{2,1,0:T(2,128)S(1)}, f32[16,2,128]{2,1,0:T(2,128)S(1)}, u32[]{:S(2)}, u32[]{:S(2)}) collective-permute-start(f32[16,2,128]{2,1,0:T(2,128)S(1)} %get-tuple-element.42), channel_id=1, source_target_pairs={{0,96},{1,97},{2,98},{3,99},{4,100},{5,101},{6,102},{7,103},{8,104... | collective-permute-start | bytes 49160 | tf_op jit(solution)/shard_map/ppermute | solution.py:485
  41.0 5.2 %collective-permute-start.9 = (f32[16,2,128]{2,1,0:T(2,128)S(1)}, f32[16,2,128]{2,1,0:T(2,128)S(1)}, u32[]{:S(2)}, u32[]{:S(2)}) collective-permute-start(f32[16,2,128]{2,1,0:T(2,128)S(1)} %get-tuple-element.42), channel_id=1, source_target_pairs={{0,64},{1,65},{2,66},{3,67},{4,68},{5,69},{6,70},{7,71},{8,72},{9,... | collective-permute-start | bytes 49160 | tf_op jit(solution)/shard_map/ppermute | solution.py:485
  46.3 13.2 %collective-permute-start.11 = (f32[64,2,128]{2,1,0:T(2,128)S(1)}, f32[64,2,128]{2,1,0:T(2,128)S(1)}, u32[]{:S(2)}, u32[]{:S(2)}) collective-permute-start(f32[64,2,128]{2,1,0:T(2,128)S(1)} %get-tuple-element.34), channel_id=1, source_target_pairs={{0,4},{1,5},{2,6},{3,7},{4,0},{5,1},{6,2},{7,3},{8,12},{9,13},{10,... | collective-permute-start | bytes 196616 | tf_op jit(solution)/shard_map/ppermute | solution.py:485
  49.7 9.8 %collective-permute-start.12 = (f32[3,256]{1,0:T(4,128)S(1)}, f32[3,256]{1,0:T(4,128)S(1)}, u32[]{:S(2)}, u32[]{:S(2)}) collective-permute-start(f32[3,256]{1,0:T(4,128)S(1)} %get-tuple-element.21), channel_id=1, source_target_pairs={{0,1},{1,2},{2,3},{3,4},{4,5},{5,6},{6,7},{7,8},{8,9},{9,10},{10,1... | collective-permute-start | bytes 9224 | tf_op jit(solution)/shard_map/ppermute | solution.py:497
  51.6 9.2 %collective-permute-start.13 = (f32[3,256]{1,0:T(4,128)S(1)}, f32[3,256]{1,0:T(4,128)S(1)}, u32[]{:S(2)}, u32[]{:S(2)}) collective-permute-start(f32[3,256]{1,0:T(4,128)S(1)} %get-tuple-element.22), channel_id=1, source_target_pairs={{1,0},{2,1},{3,2},{4,3},{5,4},{6,5},{7,6},{8,7},{9,8},{10,9},{11,1... | collective-permute-start | bytes 9224 | tf_op jit(solution)/shard_map/ppermute | solution.py:497
  64.9 3.2 %collective-permute-start.16 = (f32[32,128]{1,0:T(8,128)S(1)}, f32[32,128]{1,0:T(8,128)S(1)}, u32[]{:S(2)}, u32[]{:S(2)}) collective-permute-start(f32[32,128]{1,0:T(8,128)S(1)} %get-tuple-element.24.p0), channel_id=1, source_target_pairs={{0,3},{1,2},{2,1},{3,0},{4,7},{5,6},{6,5},{7,4},{8,11},{9,10},{10,... | collective-permute-start | bytes 49160 | tf_op jit(solution)/shard_map/ppermute | solution.py:485
  65.0 3.8 %collective-permute-start.15 = (f32[32,128]{1,0:T(8,128)S(1)}, f32[32,128]{1,0:T(8,128)S(1)}, u32[]{:S(2)}, u32[]{:S(2)}) collective-permute-start(f32[32,128]{1,0:T(8,128)S(1)} %get-tuple-element.24.p0), channel_id=1, source_target_pairs={{0,2},{1,3},{2,0},{3,1},{4,6},{5,7},{6,4},{7,5},{8,10},{9,11},{10,... | collective-permute-start | bytes 49160 | tf_op jit(solution)/shard_map/ppermute | solution.py:485
  65.1 3.7 %collective-permute-start.14 = (f32[32,128]{1,0:T(8,128)S(1)}, f32[32,128]{1,0:T(8,128)S(1)}, u32[]{:S(2)}, u32[]{:S(2)}) collective-permute-start(f32[32,128]{1,0:T(8,128)S(1)} %get-tuple-element.24.p0), channel_id=1, source_target_pairs={{0,1},{1,0},{2,3},{3,2},{4,5},{5,4},{6,7},{7,6},{8,9},{9,8},{10,11... | collective-permute-start | bytes 49160 | tf_op jit(solution)/shard_map/ppermute | solution.py:485
  71.5 3.2 %collective-permute-start.19 = (f32[32,128]{1,0:T(8,128)S(1)}, f32[32,128]{1,0:T(8,128)S(1)}, u32[]{:S(2)}, u32[]{:S(2)}) collective-permute-start(f32[32,128]{1,0:T(8,128)S(1)} %shard_map.107.p0), channel_id=1, source_target_pairs={{0,3},{1,2},{2,1},{3,0},{4,7},{5,6},{6,5},{7,4},{8,11},{9,10},{10,... | collective-permute-start | bytes 49160 | tf_op jit(solution)/shard_map/ppermute | solution.py:485
  72.1 3.7 %collective-permute-start.18 = (f32[32,128]{1,0:T(8,128)S(1)}, f32[32,128]{1,0:T(8,128)S(1)}, u32[]{:S(2)}, u32[]{:S(2)}) collective-permute-start(f32[32,128]{1,0:T(8,128)S(1)} %shard_map.107.p0), channel_id=1, source_target_pairs={{0,2},{1,3},{2,0},{3,1},{4,6},{5,7},{6,4},{7,5},{8,10},{9,11},{10,... | collective-permute-start | bytes 49160 | tf_op jit(solution)/shard_map/ppermute | solution.py:485
  72.1 3.7 %collective-permute-start.17 = (f32[32,128]{1,0:T(8,128)S(1)}, f32[32,128]{1,0:T(8,128)S(1)}, u32[]{:S(2)}, u32[]{:S(2)}) collective-permute-start(f32[32,128]{1,0:T(8,128)S(1)} %shard_map.107.p0), channel_id=1, source_target_pairs={{0,1},{1,0},{2,3},{3,2},{4,5},{5,4},{6,7},{7,6},{8,9},{9,8},{10,11... | collective-permute-start | bytes 49160 | tf_op jit(solution)/shard_map/ppermute | solution.py:485
  78.5 17.7 %copy-start.5 = (f32[8,128]{1,0:T(8,128)S(1)}, f32[8,128]{1,0:T(8,128)}, u32[]{:S(2)}) copy-start(f32[8,128]{1,0:T(8,128)} %get-tuple-element.31.node_row) | copy-start | bytes 12292
  78.5 3.2 %collective-permute-start.22 = (f32[32,128]{1,0:T(8,128)S(1)}, f32[32,128]{1,0:T(8,128)S(1)}, u32[]{:S(2)}, u32[]{:S(2)}) collective-permute-start(f32[32,128]{1,0:T(8,128)S(1)} %shard_map.108.p0), channel_id=1, source_target_pairs={{0,3},{1,2},{2,1},{3,0},{4,7},{5,6},{6,5},{7,4},{8,11},{9,10},{10,... | collective-permute-start | bytes 49160 | tf_op jit(solution)/shard_map/ppermute | solution.py:485
  78.7 3.7 %collective-permute-start.21 = (f32[32,128]{1,0:T(8,128)S(1)}, f32[32,128]{1,0:T(8,128)S(1)}, u32[]{:S(2)}, u32[]{:S(2)}) collective-permute-start(f32[32,128]{1,0:T(8,128)S(1)} %shard_map.108.p0), channel_id=1, source_target_pairs={{0,2},{1,3},{2,0},{3,1},{4,6},{5,7},{6,4},{7,5},{8,10},{9,11},{10,... | collective-permute-start | bytes 49160 | tf_op jit(solution)/shard_map/ppermute | solution.py:485
  78.7 3.7 %collective-permute-start.20 = (f32[32,128]{1,0:T(8,128)S(1)}, f32[32,128]{1,0:T(8,128)S(1)}, u32[]{:S(2)}, u32[]{:S(2)}) collective-permute-start(f32[32,128]{1,0:T(8,128)S(1)} %shard_map.108.p0), channel_id=1, source_target_pairs={{0,1},{1,0},{2,3},{3,2},{4,5},{5,4},{6,7},{7,6},{8,9},{9,8},{10,11... | collective-permute-start | bytes 49160 | tf_op jit(solution)/shard_map/ppermute | solution.py:485
  85.1 3.4 %collective-permute-start.25 = (f32[32,128]{1,0:T(8,128)S(1)}, f32[32,128]{1,0:T(8,128)S(1)}, u32[]{:S(2)}, u32[]{:S(2)}) collective-permute-start(f32[32,128]{1,0:T(8,128)S(1)} %shard_map.109.p0), channel_id=1, source_target_pairs={{0,3},{1,2},{2,1},{3,0},{4,7},{5,6},{6,5},{7,4},{8,11},{9,10},{10,... | collective-permute-start | bytes 49160 | tf_op jit(solution)/shard_map/ppermute | solution.py:485
  85.9 3.7 %collective-permute-start.24 = (f32[32,128]{1,0:T(8,128)S(1)}, f32[32,128]{1,0:T(8,128)S(1)}, u32[]{:S(2)}, u32[]{:S(2)}) collective-permute-start(f32[32,128]{1,0:T(8,128)S(1)} %shard_map.109.p0), channel_id=1, source_target_pairs={{0,2},{1,3},{2,0},{3,1},{4,6},{5,7},{6,4},{7,5},{8,10},{9,11},{10,... | collective-permute-start | bytes 49160 | tf_op jit(solution)/shard_map/ppermute | solution.py:485
  85.9 3.7 %collective-permute-start.23 = (f32[32,128]{1,0:T(8,128)S(1)}, f32[32,128]{1,0:T(8,128)S(1)}, u32[]{:S(2)}, u32[]{:S(2)}) collective-permute-start(f32[32,128]{1,0:T(8,128)S(1)} %shard_map.109.p0), channel_id=1, source_target_pairs={{0,1},{1,0},{2,3},{3,2},{4,5},{5,4},{6,7},{7,6},{8,9},{9,8},{10,11... | collective-permute-start | bytes 49160 | tf_op jit(solution)/shard_map/ppermute | solution.py:485
  92.3 3.2 %collective-permute-start.28 = (f32[32,128]{1,0:T(8,128)S(1)}, f32[32,128]{1,0:T(8,128)S(1)}, u32[]{:S(2)}, u32[]{:S(2)}) collective-permute-start(f32[32,128]{1,0:T(8,128)S(1)} %shard_map.110.p0), channel_id=1, source_target_pairs={{0,3},{1,2},{2,1},{3,0},{4,7},{5,6},{6,5},{7,4},{8,11},{9,10},{10,... | collective-permute-start | bytes 49160 | tf_op jit(solution)/shard_map/ppermute | solution.py:485
  92.5 3.7 %collective-permute-start.27 = (f32[32,128]{1,0:T(8,128)S(1)}, f32[32,128]{1,0:T(8,128)S(1)}, u32[]{:S(2)}, u32[]{:S(2)}) collective-permute-start(f32[32,128]{1,0:T(8,128)S(1)} %shard_map.110.p0), channel_id=1, source_target_pairs={{0,2},{1,3},{2,0},{3,1},{4,6},{5,7},{6,4},{7,5},{8,10},{9,11},{10,... | collective-permute-start | bytes 49160 | tf_op jit(solution)/shard_map/ppermute | solution.py:485
  92.5 3.7 %collective-permute-start.26 = (f32[32,128]{1,0:T(8,128)S(1)}, f32[32,128]{1,0:T(8,128)S(1)}, u32[]{:S(2)}, u32[]{:S(2)}) collective-permute-start(f32[32,128]{1,0:T(8,128)S(1)} %shard_map.110.p0), channel_id=1, source_target_pairs={{0,1},{1,0},{2,3},{3,2},{4,5},{5,4},{6,7},{7,6},{8,9},{9,8},{10,11... | collective-permute-start | bytes 49160 | tf_op jit(solution)/shard_map/ppermute | solution.py:485

commit v11 on v10

--- a/solution.py
+++ b/solution.py
@@ -346,7 +346,7 @@
     return slice(8 * m, 8 * m + 8)
 
 
-def coarse_first_kernel(base_ref, sums, data, far_up, far_down, new, rhs, dia, where, passes,
+def coarse_first_kernel(base_ref, sums, data, new, rhs, dia, where, passes,
                         table, gather, left, right):
     me = lax.shift_right_logical(base_ref[0], 10)
     got = jnp.transpose(sums[:, 0, :])
@@ -411,7 +411,8 @@
     table[...] = jnp.transpose(mine[...])
 
 
-def coarse_kernel(base_ref, passes, p0, p1, p2, p3, rhs, dia, where, data, new, table, mine, gather):
+def coarse_kernel(base_ref, passes, p0, p1, p2, p3, rhs, dia, where, data, *rest):
+    new, table, mine, gather = rest[-4:]
     gathered(table, (p0, p1, p2, p3), mine)
     new[...] = coarse_step(
         table, where, passes[...][0, 0], data, p0[...], rhs[...], dia[...], gather
@@ -547,14 +548,15 @@
     new, crhs, cd, where, passes = call(
         coarse_first_kernel,
         [peers, peers, peers, ((PEERS, 8, LANES), i32), ((8, LANES), i32)],
-        [base, sums, data, before2, after2],
+        [base, sums, data],
         scratch=[square, gather, ((288, 4096), jnp.bfloat16), ((LANES, 4096), jnp.bfloat16)],
         scalars=1,
     )
-    for _ in range(CSWEEPS - 2):
+    awaited = [(), (before2,), (after2,)] + [()] * CSWEEPS
+    for sweep in range(CSWEEPS - 2):
         new, = call(
             coarse_kernel, [peers],
-            [base, passes, *in_group(new), crhs, cd, where, data],
+            [base, passes, *in_group(new), crhs, cd, where, data, *awaited[sweep]],
             scratch=[square, square, gather], scalars=1,
         )
     solution, mine = call(

time: 99.3 us -> 100 us (level)
  the two profiles are of different devices: /device:TPU:16 before, /device:TPU:0 now
where the time goes in v11:
time: 100 us; the launch traced here: 98.7 us
  starting transfers between devices  47.6 us (48%)
  waiting for transfers between devices  25.8 us (26%)
  Pallas kernels  24.2 us (24%)
    ppermute x25, starting transfers between devices, partner(): lax.ppermute(value, DOM, [(i, i ^ bits) for i in range(lax.axis_size(DOM))])  28 us
    ppermute x25, waiting for transfers between devices, partner(): lax.ppermute(value, DOM, [(i, i ^ bits) for i in range(lax.axis_size(DOM))])  23.2 us
    pallas_call x8, Pallas kernels, call(): pl.pallas_call(kernel, in_specs=[smem] * scalars + [vmem] * (len(args) -...  22 us
    all_to_all x1, starting transfers between devices, cycle(): lax.all_to_all(dsend, DOM, 0, 0, axis_index_groups=row_groups(), tiled=True)  13.7 us
    ppermute x4, starting transfers between devices, shifts(): return (lax.ppermute(up, DOM, forward), lax.ppermute(down, DOM, backward))  5.91 us
    ppermute x4, waiting for transfers between devices, shifts(): return (lax.ppermute(up, DOM, forward), lax.ppermute(down, DOM, backward))  2.57 us
    pallas_call x1, Pallas kernels, cycle(): pl.pallas_call(pack_kernel, name='pack', in_specs=[far] * 6, out_specs=[v...  2.21 us
  transfers between devices with their start and end apart: 30, of which 16 were waited for; matrix products, arithmetic and copies ran while one was open for 0% of the time, Pallas kernels for 5%

profile of v11, /device:TPU:0, one launch (start us, length us, event | category | flops | bytes accessed | tf_op | source)
XLA Modules:
  0.0 98.7 jit_solution(8818293049600246637)
XLA Ops:
  0.6 2.2 %pack.1 = (f32[288,256]{1,0:T(8,128)}, f32[288,256]{1,0:T(8,128)}, f32[8,128]{1,0:T(8,128)}) custom-call(f32[3,1024]{1,0:T(4,128)} %bitcast.17, f32[3,1024]{1,0:T(4,128)} %bitcast.19, s32[27,1024]{1,0:T(8,128)} %bitcast.14, f32[3,3,27,1024]{3,2,1,0:T(8,128)} %bitcast.11, s32[8,128]{1,0:T(8,128)} %bitcast.21, s32[1,32]{1,0:T(1,128)} %bitcast.24), custom_call_target="tpu_custom_call" | custom-call | tf_op jit(solution)/shard_map/pack/pallas_call | solution.py:520
  2.8 1.3 %collective-permute-start = (f32[288,256]{1,0:T(8,128)}, f32[288,256]{1,0:T(8,128)S(1)}, u32[]{:S(2)}, u32[]{:S(2)}) collective-permute-start(f32[288,256]{1,0:T(8,128)} %get-tuple-element.18), channel_id=1, source_target_pairs={{0,1},{1,2},{2,3},{3,4},{4,5},{5,6},{6,7},{7,8},{8,9},{9,10},{10,1... | collective-permute-start | bytes 884744 | tf_op jit(solution)/shard_map/ppermute | solution.py:498
  4.2 1.3 %collective-permute-start.1 = (f32[288,256]{1,0:T(8,128)}, f32[288,256]{1,0:T(8,128)S(1)}, u32[]{:S(2)}, u32[]{:S(2)}) collective-permute-start(f32[288,256]{1,0:T(8,128)} %get-tuple-element.19), channel_id=1, source_target_pairs={{1,0},{2,1},{3,2},{4,3},{5,4},{6,5},{7,6},{8,7},{9,8},{10,9},{11,1... | collective-permute-start | bytes 884744 | tf_op jit(solution)/shard_map/ppermute | solution.py:498
  5.5 2.5 %shard_map.105 = f32[32,80,128]{2,1,0:T(8,128)} custom-call(s32[32,27]{1,0:T(8,128)} %col.1, f32[3,3,32,27]{3,2,1,0:T(8,128)} %bitcast.26), custom_call_target="tpu_custom_call" | custom-call | tf_op jit(solution)/shard_map/pallas_call | solution.py:473
  8.0 13.7 %all-to-all-start = ((f32[32,80,128]{2,1,0:T(8,128)}), f32[32,80,128]{2,1,0:T(8,128)S(1)}, u32[]{:S(2)}, u32[]{:S(2)}) async-start(f32[32,80,128]{2,1,0:T(8,128)} %shard_map.105), calls=%async_computation | async-start | bytes 2621440 | tf_op jit(solution)/shard_map/all_to_all | solution.py:516
  21.8 2.1 %shard_map.104 = (f32[1,2,128]{2,1,0:T(2,128)S(1)}, f32[3,2048]{1,0:T(4,128)S(1)}, f32[3,2048]{1,0:T(4,128)S(1)}, f32[3,2048]{1,0:T(4,128)S(1)}, f32[3,256]{1,0:T(4,128)S(1)}, /*index=5*/f32[3,256]{1,0:T(4,128)S(1)}) custom-call(s32[1]{0:T(128)} %bitcast.base_ref, f32[3,1024]{1,0:T(4,128)S(1)} %bitcast.18, f32[3,1024]{1,0:T(4,128)S(1)} %bitcast.20, ...), custom_call_target="tpu_custom_call" | custom-call | tf_op jit(solution)/shard_map/pallas_call | solution.py:473
  23.9 1.1 %collective-permute-start.3 = (f32[1,2,128]{2,1,0:T(2,128)S(1)}, f32[1,2,128]{2,1,0:T(2,128)S(1)}, u32[]{:S(2)}, u32[]{:S(2)}) collective-permute-start(f32[1,2,128]{2,1,0:T(2,128)S(1)} %get-tuple-element.20), channel_id=1, source_target_pairs={{0,2},{1,3},{2,0},{3,1},{4,6},{5,7},{6,4},{7,5},{8,10},{9,11},{10,... | collective-permute-start | bytes 3080 | tf_op jit(solution)/shard_map/ppermute | solution.py:486
  25.0 0.8 collective-permute-start.2
  25.8 0.8 collective-permute-done.2
  26.6 0.9 collective-permute-done.3
  27.5 1.9 %collective-permute-start.5 = (f32[4,2,128]{2,1,0:T(2,128)S(1)}, f32[4,2,128]{2,1,0:T(2,128)S(1)}, u32[]{:S(2)}, u32[]{:S(2)}) collective-permute-start(f32[4,2,128]{2,1,0:T(2,128)S(1)} %get-tuple-element.52), channel_id=1, source_target_pairs={{0,8},{1,9},{2,10},{3,11},{4,12},{5,13},{6,14},{7,15},{8,0},{9,1},... | collective-permute-start | bytes 12296 | tf_op jit(solution)/shard_map/ppermute | solution.py:486
  29.4 2.1 %collective-permute-start.7 = (f32[4,2,128]{2,1,0:T(2,128)S(1)}, f32[4,2,128]{2,1,0:T(2,128)S(1)}, u32[]{:S(2)}, u32[]{:S(2)}) collective-permute-start(f32[4,2,128]{2,1,0:T(2,128)S(1)} %get-tuple-element.52), channel_id=1, source_target_pairs={{0,24},{1,25},{2,26},{3,27},{4,28},{5,29},{6,30},{7,31},{8,16},{9,... | collective-permute-start | bytes 12296 | tf_op jit(solution)/shard_map/ppermute | solution.py:486
  31.5 0.6 collective-permute-start.6
  32.1 2.9 %collective-permute-done.5 = f32[4,2,128]{2,1,0:T(2,128)S(1)} collective-permute-done((f32[4,2,128]{2,1,0:T(2,128)S(1)}, f32[4,2,128]{2,1,0:T(2,128)S(1)}, u32[]{:S(2)}, u32[]{:S(2)}) %collective-permute-start.5) | collective-permute-done | bytes 4128 | tf_op jit(solution)/shard_map/ppermute | solution.py:486
  35.0 5.2 %collective-permute-done.6 = f32[4,2,128]{2,1,0:T(2,128)S(1)} collective-permute-done((f32[4,2,128]{2,1,0:T(2,128)S(1)}, f32[4,2,128]{2,1,0:T(2,128)S(1)}, u32[]{:S(2)}, u32[]{:S(2)}) %collective-permute-start.6) | collective-permute-done | bytes 4128 | tf_op jit(solution)/shard_map/ppermute | solution.py:486
  40.2 0.1 collective-permute-start.8
  40.3 1.9 %collective-permute-start.10 = (f32[16,2,128]{2,1,0:T(2,128)S(1)}, f32[16,2,128]{2,1,0:T(2,128)S(1)}, u32[]{:S(2)}, u32[]{:S(2)}) collective-permute-start(f32[16,2,128]{2,1,0:T(2,128)S(1)} %get-tuple-element.42), channel_id=1, source_target_pairs={{0,96},{1,97},{2,98},{3,99},{4,100},{5,101},{6,102},{7,103},{8,104... | collective-permute-start | bytes 49160 | tf_op jit(solution)/shard_map/ppermute | solution.py:486
  42.2 2.2 %collective-permute-start.9 = (f32[16,2,128]{2,1,0:T(2,128)S(1)}, f32[16,2,128]{2,1,0:T(2,128)S(1)}, u32[]{:S(2)}, u32[]{:S(2)}) collective-permute-start(f32[16,2,128]{2,1,0:T(2,128)S(1)} %get-tuple-element.42), channel_id=1, source_target_pairs={{0,64},{1,65},{2,66},{3,67},{4,68},{5,69},{6,70},{7,71},{8,72},{9,... | collective-permute-start | bytes 49160 | tf_op jit(solution)/shard_map/ppermute | solution.py:486
  44.4 3.1 %collective-permute-done.9 = f32[16,2,128]{2,1,0:T(2,128)S(1)} collective-permute-done((f32[16,2,128]{2,1,0:T(2,128)S(1)}, f32[16,2,128]{2,1,0:T(2,128)S(1)}, u32[]{:S(2)}, u32[]{:S(2)}) %collective-permute-start.9) | collective-permute-done | bytes 16416 | tf_op jit(solution)/shard_map/ppermute | solution.py:486
  47.5 3.4 %collective-permute-start.11 = (f32[64,2,128]{2,1,0:T(2,128)S(1)}, f32[64,2,128]{2,1,0:T(2,128)S(1)}, u32[]{:S(2)}, u32[]{:S(2)}) collective-permute-start(f32[64,2,128]{2,1,0:T(2,128)S(1)} %get-tuple-element.34), channel_id=1, source_target_pairs={{0,4},{1,5},{2,6},{3,7},{4,0},{5,1},{6,2},{7,3},{8,12},{9,13},{10,... | collective-permute-start | bytes 196616 | tf_op jit(solution)/shard_map/ppermute | solution.py:486
  50.9 2.4 %collective-permute-done.11 = f32[64,2,128]{2,1,0:T(2,128)S(1)} collective-permute-done((f32[64,2,128]{2,1,0:T(2,128)S(1)}, f32[64,2,128]{2,1,0:T(2,128)S(1)}, u32[]{:S(2)}, u32[]{:S(2)}) %collective-permute-start.11) | collective-permute-done | bytes 65568 | tf_op jit(solution)/shard_map/ppermute | solution.py:486
  53.3 4.1 %shard_map.106 = (f32[32,128]{1,0:T(8,128)S(1)}, f32[32,128]{1,0:T(8,128)S(1)}, f32[32,128]{1,0:T(8,128)S(1)}, s32[32,8,128]{2,1,0:T(8,128)S(1)}, s32[8,128]{1,0:T(8,128)S(1)}) custom-call(s32[1]{0:T(128)} %bitcast.base_ref, f32[128,2,128]{2,1,0:T(2,128)S(1)} %constant_dynamic-update-slice_fusion.21.sums, f32[32,80,128]{2,1,0:T(8,128)S(1)} %all-to-all-done.data), custom_call_target="tpu_custom_call" | custom-call | tf_op jit(solution)/shard_map/pallas_call | solution.py:473
  57.6 1.2 %collective-permute-start.13 = (f32[32,128]{1,0:T(8,128)S(1)}, f32[32,128]{1,0:T(8,128)S(1)}, u32[]{:S(2)}, u32[]{:S(2)}) collective-permute-start(f32[32,128]{1,0:T(8,128)S(1)} %get-tuple-element.22.p0), channel_id=1, source_target_pairs={{0,2},{1,3},{2,0},{3,1},{4,6},{5,7},{6,4},{7,5},{8,10},{9,11},{10,... | collective-permute-start | bytes 49160 | tf_op jit(solution)/shard_map/ppermute | solution.py:486
  58.7 0.7 collective-permute-start.12
  59.4 1.3 %collective-permute-done.14.p3 = f32[32,128]{1,0:T(8,128)S(1)} collective-permute-done((f32[32,128]{1,0:T(8,128)S(1)}, f32[32,128]{1,0:T(8,128)S(1)}, u32[]{:S(2)}, u32[]{:S(2)}) %collective-permute-start.14) | collective-permute-done | bytes 16416 | tf_op jit(solution)/shard_map/ppermute | solution.py:486
  60.7 0.7 collective-permute-done.13.p2
  61.4 2.7 %shard_map.107.p0 = f32[32,128]{1,0:T(8,128)S(1)} custom-call(s32[1]{0:T(128)} %bitcast.base_ref, s32[8,128]{1,0:T(8,128)S(1)} %get-tuple-element.21.passes, f32[32,128]{1,0:T(8,128)S(1)} %get-tuple-element.22.p0, f32[32,128]{1,0:T(8,128)S(1)} %collective-permute-done.12.p1, f32[32,128]{1,0:T(8,128)S(1)} %collective-permute-done.13.p2, ...), custom_call_target="tpu_custom_call" | custom-call | tf_op jit(solution)/shard_map/pallas_call | solution.py:473
  64.1 1.0 %collective-permute-start.17 = (f32[32,128]{1,0:T(8,128)S(1)}, f32[32,128]{1,0:T(8,128)S(1)}, u32[]{:S(2)}, u32[]{:S(2)}) collective-permute-start(f32[32,128]{1,0:T(8,128)S(1)} %shard_map.107.p0), channel_id=1, source_target_pairs={{0,3},{1,2},{2,1},{3,0},{4,7},{5,6},{6,5},{7,4},{8,11},{9,10},{10,... | collective-permute-start | bytes 49160 | tf_op jit(solution)/shard_map/ppermute | solution.py:486
  65.1 0.2 collective-permute-start.16
  65.3 0.7 collective-permute-start.15
  66.0 1.9 %collective-permute-start.18 = (f32[3,256]{1,0:T(4,128)S(1)}, f32[3,256]{1,0:T(4,128)S(1)}, u32[]{:S(2)}, u32[]{:S(2)}) collective-permute-start(f32[3,256]{1,0:T(4,128)S(1)} %get-tuple-element.26), channel_id=1, source_target_pairs={{0,1},{1,2},{2,3},{3,4},{4,5},{5,6},{6,7},{7,8},{8,9},{9,10},{10,1... | collective-permute-start | bytes 9224 | tf_op jit(solution)/shard_map/ppermute | solution.py:498
  67.9 0.8 collective-permute-done.18.rest_0_.before2
  68.8 2.7 %shard_map.108.p0 = f32[32,128]{1,0:T(8,128)S(1)} custom-call(s32[1]{0:T(128)} %bitcast.base_ref, s32[8,128]{1,0:T(8,128)S(1)} %get-tuple-element.21.passes, f32[32,128]{1,0:T(8,128)S(1)} %shard_map.107.p0, f32[32,128]{1,0:T(8,128)S(1)} %collective-permute-done.15.p1, f32[32,128]{1,0:T(8,128)S(1)} %collective-permute-done.16.p2, ...), custom_call_target="tpu_custom_call" | custom-call | tf_op jit(solution)/shard_map/pallas_call | solution.py:473
  71.5 4.0 %collective-permute-start.21 = (f32[32,128]{1,0:T(8,128)S(1)}, f32[32,128]{1,0:T(8,128)S(1)}, u32[]{:S(2)}, u32[]{:S(2)}) collective-permute-start(f32[32,128]{1,0:T(8,128)S(1)} %shard_map.108.p0), channel_id=1, source_target_pairs={{0,3},{1,2},{2,1},{3,0},{4,7},{5,6},{6,5},{7,4},{8,11},{9,10},{10,... | collective-permute-start | bytes 49160 | tf_op jit(solution)/shard_map/ppermute | solution.py:486
  75.5 0.2 collective-permute-start.19
  75.7 1.4 %collective-permute-start.22 = (f32[3,256]{1,0:T(4,128)S(1)}, f32[3,256]{1,0:T(4,128)S(1)}, u32[]{:S(2)}, u32[]{:S(2)}) collective-permute-start(f32[3,256]{1,0:T(4,128)S(1)} %get-tuple-element.27), channel_id=1, source_target_pairs={{1,0},{2,1},{3,2},{4,3},{5,4},{6,5},{7,6},{8,7},{9,8},{10,9},{11,1... | collective-permute-start | bytes 9224 | tf_op jit(solution)/shard_map/ppermute | solution.py:498
  77.2 1.8 %collective-permute-done.22.rest_0_.after2 = f32[3,256]{1,0:T(4,128)S(1)} collective-permute-done((f32[3,256]{1,0:T(4,128)S(1)}, f32[3,256]{1,0:T(4,128)S(1)}, u32[]{:S(2)}, u32[]{:S(2)}) %collective-permute-start.22) | collective-permute-done | bytes 3104 | tf_op jit(solution)/shard_map/ppermute | solution.py:498
  78.9 0.3 collective-permute-done.20.p2
  79.3 2.7 %shard_map.109.p0 = f32[32,128]{1,0:T(8,128)S(1)} custom-call(s32[1]{0:T(128)} %bitcast.base_ref, s32[8,128]{1,0:T(8,128)S(1)} %get-tuple-element.21.passes, f32[32,128]{1,0:T(8,128)S(1)} %shard_map.108.p0, f32[32,128]{1,0:T(8,128)S(1)} %collective-permute-done.19.p1, f32[32,128]{1,0:T(8,128)S(1)} %collective-permute-done.20.p2, ...), custom_call_target="tpu_custom_call" | custom-call | tf_op jit(solution)/shard_map/pallas_call | solution.py:473
  82.0 3.7 %collective-permute-start.25 = (f32[32,128]{1,0:T(8,128)S(1)}, f32[32,128]{1,0:T(8,128)S(1)}, u32[]{:S(2)}, u32[]{:S(2)}) collective-permute-start(f32[32,128]{1,0:T(8,128)S(1)} %shard_map.109.p0), channel_id=1, source_target_pairs={{0,3},{1,2},{2,1},{3,0},{4,7},{5,6},{6,5},{7,4},{8,11},{9,10},{10,... | collective-permute-start | bytes 49160 | tf_op jit(solution)/shard_map/ppermute | solution.py:486
  85.7 0.2 collective-permute-start.23
  85.9 1.2 %collective-permute-done.25.p3 = f32[32,128]{1,0:T(8,128)S(1)} collective-permute-done((f32[32,128]{1,0:T(8,128)S(1)}, f32[32,128]{1,0:T(8,128)S(1)}, u32[]{:S(2)}, u32[]{:S(2)}) %collective-permute-start.25) | collective-permute-done | bytes 16416 | tf_op jit(solution)/shard_map/ppermute | solution.py:486
  87.1 2.3 %collective-permute-done.24.p2 = f32[32,128]{1,0:T(8,128)S(1)} collective-permute-done((f32[32,128]{1,0:T(8,128)S(1)}, f32[32,128]{1,0:T(8,128)S(1)}, u32[]{:S(2)}, u32[]{:S(2)}) %collective-permute-start.24) | collective-permute-done | bytes 16416 | tf_op jit(solution)/shard_map/ppermute | solution.py:486
  89.4 2.7 %shard_map.110.p0 = f32[32,128]{1,0:T(8,128)S(1)} custom-call(s32[1]{0:T(128)} %bitcast.base_ref, s32[8,128]{1,0:T(8,128)S(1)} %get-tuple-element.21.passes, f32[32,128]{1,0:T(8,128)S(1)} %shard_map.109.p0, f32[32,128]{1,0:T(8,128)S(1)} %collective-permute-done.23.p1, f32[32,128]{1,0:T(8,128)S(1)} %collective-permute-done.24.p2, ...), custom_call_target="tpu_custom_call" | custom-call | tf_op jit(solution)/shard_map/pallas_call | solution.py:473
  92.3 1.8 %collective-permute-start.26 = (f32[32,128]{1,0:T(8,128)S(1)}, f32[32,128]{1,0:T(8,128)S(1)}, u32[]{:S(2)}, u32[]{:S(2)}) collective-permute-start(f32[32,128]{1,0:T(8,128)S(1)} %shard_map.110.p0), channel_id=1, source_target_pairs={{0,1},{1,0},{2,3},{3,2},{4,5},{5,4},{6,7},{7,6},{8,9},{9,8},{10,11... | collective-permute-start | bytes 49160 | tf_op jit(solution)/shard_map/ppermute | solution.py:486
  94.0 1.3 %collective-permute-done.28.p3 = f32[32,128]{1,0:T(8,128)S(1)} collective-permute-done((f32[32,128]{1,0:T(8,128)S(1)}, f32[32,128]{1,0:T(8,128)S(1)}, u32[]{:S(2)}, u32[]{:S(2)}) %collective-permute-start.28) | collective-permute-done | bytes 16416 | tf_op jit(solution)/shard_map/ppermute | solution.py:486
  95.3 0.7 collective-permute-done.27.p2
  96.0 2.6 %shard_map.111 = (f32[3,1024]{1,0:T(4,128)}, f32[3,32]{1,0:T(4,128)}) custom-call(s32[1]{0:T(128)} %bitcast.base_ref, f32[32,128]{1,0:T(8,128)S(1)} %shard_map.110.p0, f32[32,128]{1,0:T(8,128)S(1)} %collective-permute-done.26.p1, f32[32,128]{1,0:T(8,128)S(1)} %collective-permute-done.27.p2, f32[32,128]{1,0:T(8,128)S(1)} %collective-permute-done.28.p3, ...), custom_call_target="tpu_custom_call" | custom-call | tf_op jit(solution)/shard_map/pallas_call | solution.py:473
  (48 shorter events, 0.6 us)
Async XLA Ops:
  2.8 18.9 %collective-permute-start = (f32[288,256]{1,0:T(8,128)}, f32[288,256]{1,0:T(8,128)S(1)}, u32[]{:S(2)}, u32[]{:S(2)}) collective-permute-start(f32[288,256]{1,0:T(8,128)} %get-tuple-element.18), channel_id=1, source_target_pairs={{0,1},{1,2},{2,3},{3,4},{4,5},{5,6},{6,7},{7,8},{8,9},{9,10},{10,1... | collective-permute-start | bytes 884744 | tf_op jit(solution)/shard_map/ppermute | solution.py:498
  4.2 17.6 %collective-permute-start.1 = (f32[288,256]{1,0:T(8,128)}, f32[288,256]{1,0:T(8,128)S(1)}, u32[]{:S(2)}, u32[]{:S(2)}) collective-permute-start(f32[288,256]{1,0:T(8,128)} %get-tuple-element.19), channel_id=1, source_target_pairs={{1,0},{2,1},{3,2},{4,3},{5,4},{6,5},{7,6},{8,7},{9,8},{10,9},{11,1... | collective-permute-start | bytes 884744 | tf_op jit(solution)/shard_map/ppermute | solution.py:498
  7.9 13.8 %copy-start = (f32[1024,27,3,3]{0,1,3,2:T(8,128)S(1)}, f32[1024,27,3,3]{0,1,3,2:T(8,128)}, u32[]{:S(2)}) copy-start(f32[1024,27,3,3]{0,1,3,2:T(8,128)} %param.12) | copy-start | bytes 2985988
  7.9 13.8 %copy-start.1 = (s32[1024,27]{0,1:T(8,128)S(1)}, s32[1024,27]{0,1:T(8,128)}, u32[]{:S(2)}) copy-start(s32[1024,27]{0,1:T(8,128)} %param.11) | copy-start | bytes 331780
  7.9 13.8 %copy-start.2 = (f32[1024,3]{0,1:T(4,128)S(1)}, f32[1024,3]{0,1:T(4,128)}, u32[]{:S(2)}) copy-start(f32[1024,3]{0,1:T(4,128)} %param.9) | copy-start | bytes 36868
  7.9 13.9 %copy-start.3 = (f32[1024,3]{0,1:T(4,128)S(1)}, f32[1024,3]{0,1:T(4,128)}, u32[]{:S(2)}) copy-start(f32[1024,3]{0,1:T(4,128)} %param.10) | copy-start | bytes 36868
  7.9 13.9 %copy-start.4 = (s32[1024]{0:T(1024)S(1)}, s32[1024]{0:T(1024)}, u32[]{:S(2)}) copy-start(s32[1024]{0:T(1024)} %param.13) | copy-start | bytes 12292
  7.9 13.9 %copy-start.6 = (f32[32,3]{0,1:T(4,128)S(1)}, f32[32,3]{0,1:T(4,128)}, u32[]{:S(2)}) copy-start(f32[32,3]{0,1:T(4,128)} %param.15) | copy-start | bytes 1156
  8.0 13.9 %copy-start.7 = (s32[32]{0:T(128)S(1)}, s32[32]{0:T(128)}, u32[]{:S(2)}) copy-start(s32[32]{0:T(128)} %param.14) | copy-start | bytes 388
  8.0 45.4 %all-to-all-start = ((f32[32,80,128]{2,1,0:T(8,128)}), f32[32,80,128]{2,1,0:T(8,128)S(1)}, u32[]{:S(2)}, u32[]{:S(2)}) async-start(f32[32,80,128]{2,1,0:T(8,128)} %shard_map.105), calls=%async_computation | async-start | bytes 2621440 | tf_op jit(solution)/shard_map/all_to_all | solution.py:516
  23.9 3.6 %collective-permute-start.4 = (f32[1,2,128]{2,1,0:T(2,128)S(1)}, f32[1,2,128]{2,1,0:T(2,128)S(1)}, u32[]{:S(2)}, u32[]{:S(2)}) collective-permute-start(f32[1,2,128]{2,1,0:T(2,128)S(1)} %get-tuple-element.20), channel_id=1, source_target_pairs={{0,3},{1,2},{2,1},{3,0},{4,7},{5,6},{6,5},{7,4},{8,11},{9,10},{10,... | collective-permute-start | bytes 3080 | tf_op jit(solution)/shard_map/ppermute | solution.py:486
  23.9 3.6 %collective-permute-start.3 = (f32[1,2,128]{2,1,0:T(2,128)S(1)}, f32[1,2,128]{2,1,0:T(2,128)S(1)}, u32[]{:S(2)}, u32[]{:S(2)}) collective-permute-start(f32[1,2,128]{2,1,0:T(2,128)S(1)} %get-tuple-element.20), channel_id=1, source_target_pairs={{0,2},{1,3},{2,0},{3,1},{4,6},{5,7},{6,4},{7,5},{8,10},{9,11},{10,... | collective-permute-start | bytes 3080 | tf_op jit(solution)/shard_map/ppermute | solution.py:486
  25.0 1.6 %collective-permute-start.2 = (f32[1,2,128]{2,1,0:T(2,128)S(1)}, f32[1,2,128]{2,1,0:T(2,128)S(1)}, u32[]{:S(2)}, u32[]{:S(2)}) collective-permute-start(f32[1,2,128]{2,1,0:T(2,128)S(1)} %get-tuple-element.20), channel_id=1, source_target_pairs={{0,1},{1,0},{2,3},{3,2},{4,5},{5,4},{6,7},{7,6},{8,9},{9,8},{10,11... | collective-permute-start | bytes 3080 | tf_op jit(solution)/shard_map/ppermute | solution.py:486
  27.5 7.4 %collective-permute-start.5 = (f32[4,2,128]{2,1,0:T(2,128)S(1)}, f32[4,2,128]{2,1,0:T(2,128)S(1)}, u32[]{:S(2)}, u32[]{:S(2)}) collective-permute-start(f32[4,2,128]{2,1,0:T(2,128)S(1)} %get-tuple-element.52), channel_id=1, source_target_pairs={{0,8},{1,9},{2,10},{3,11},{4,12},{5,13},{6,14},{7,15},{8,0},{9,1},... | collective-permute-start | bytes 12296 | tf_op jit(solution)/shard_map/ppermute | solution.py:486
  29.4 10.7 %collective-permute-start.7 = (f32[4,2,128]{2,1,0:T(2,128)S(1)}, f32[4,2,128]{2,1,0:T(2,128)S(1)}, u32[]{:S(2)}, u32[]{:S(2)}) collective-permute-start(f32[4,2,128]{2,1,0:T(2,128)S(1)} %get-tuple-element.52), channel_id=1, source_target_pairs={{0,24},{1,25},{2,26},{3,27},{4,28},{5,29},{6,30},{7,31},{8,16},{9,... | collective-permute-start | bytes 12296 | tf_op jit(solution)/shard_map/ppermute | solution.py:486
  31.5 8.7 %collective-permute-start.6 = (f32[4,2,128]{2,1,0:T(2,128)S(1)}, f32[4,2,128]{2,1,0:T(2,128)S(1)}, u32[]{:S(2)}, u32[]{:S(2)}) collective-permute-start(f32[4,2,128]{2,1,0:T(2,128)S(1)} %get-tuple-element.52), channel_id=1, source_target_pairs={{0,16},{1,17},{2,18},{3,19},{4,20},{5,21},{6,22},{7,23},{8,24},{9,... | collective-permute-start | bytes 12296 | tf_op jit(solution)/shard_map/ppermute | solution.py:486
  40.2 4.2 %collective-permute-start.8 = (f32[16,2,128]{2,1,0:T(2,128)S(1)}, f32[16,2,128]{2,1,0:T(2,128)S(1)}, u32[]{:S(2)}, u32[]{:S(2)}) collective-permute-start(f32[16,2,128]{2,1,0:T(2,128)S(1)} %get-tuple-element.42), channel_id=1, source_target_pairs={{0,32},{1,33},{2,34},{3,35},{4,36},{5,37},{6,38},{7,39},{8,40},{9,... | collective-permute-start | bytes 49160 | tf_op jit(solution)/shard_map/ppermute | solution.py:486
  40.3 7.1 %collective-permute-start.10 = (f32[16,2,128]{2,1,0:T(2,128)S(1)}, f32[16,2,128]{2,1,0:T(2,128)S(1)}, u32[]{:S(2)}, u32[]{:S(2)}) collective-permute-start(f32[16,2,128]{2,1,0:T(2,128)S(1)} %get-tuple-element.42), channel_id=1, source_target_pairs={{0,96},{1,97},{2,98},{3,99},{4,100},{5,101},{6,102},{7,103},{8,104... | collective-permute-start | bytes 49160 | tf_op jit(solution)/shard_map/ppermute | solution.py:486
  42.2 5.2 %collective-permute-start.9 = (f32[16,2,128]{2,1,0:T(2,128)S(1)}, f32[16,2,128]{2,1,0:T(2,128)S(1)}, u32[]{:S(2)}, u32[]{:S(2)}) collective-permute-start(f32[16,2,128]{2,1,0:T(2,128)S(1)} %get-tuple-element.42), channel_id=1, source_target_pairs={{0,64},{1,65},{2,66},{3,67},{4,68},{5,69},{6,70},{7,71},{8,72},{9,... | collective-permute-start | bytes 49160 | tf_op jit(solution)/shard_map/ppermute | solution.py:486
  47.5 5.8 %collective-permute-start.11 = (f32[64,2,128]{2,1,0:T(2,128)S(1)}, f32[64,2,128]{2,1,0:T(2,128)S(1)}, u32[]{:S(2)}, u32[]{:S(2)}) collective-permute-start(f32[64,2,128]{2,1,0:T(2,128)S(1)} %get-tuple-element.34), channel_id=1, source_target_pairs={{0,4},{1,5},{2,6},{3,7},{4,0},{5,1},{6,2},{7,3},{8,12},{9,13},{10,... | collective-permute-start | bytes 196616 | tf_op jit(solution)/shard_map/ppermute | solution.py:486
  57.5 3.2 %collective-permute-start.14 = (f32[32,128]{1,0:T(8,128)S(1)}, f32[32,128]{1,0:T(8,128)S(1)}, u32[]{:S(2)}, u32[]{:S(2)}) collective-permute-start(f32[32,128]{1,0:T(8,128)S(1)} %get-tuple-element.22.p0), channel_id=1, source_target_pairs={{0,3},{1,2},{2,1},{3,0},{4,7},{5,6},{6,5},{7,4},{8,11},{9,10},{10,... | collective-permute-start | bytes 49160 | tf_op jit(solution)/shard_map/ppermute | solution.py:486
  57.6 3.9 %collective-permute-start.13 = (f32[32,128]{1,0:T(8,128)S(1)}, f32[32,128]{1,0:T(8,128)S(1)}, u32[]{:S(2)}, u32[]{:S(2)}) collective-permute-start(f32[32,128]{1,0:T(8,128)S(1)} %get-tuple-element.22.p0), channel_id=1, source_target_pairs={{0,2},{1,3},{2,0},{3,1},{4,6},{5,7},{6,4},{7,5},{8,10},{9,11},{10,... | collective-permute-start | bytes 49160 | tf_op jit(solution)/shard_map/ppermute | solution.py:486
  58.7 2.7 %collective-permute-start.12 = (f32[32,128]{1,0:T(8,128)S(1)}, f32[32,128]{1,0:T(8,128)S(1)}, u32[]{:S(2)}, u32[]{:S(2)}) collective-permute-start(f32[32,128]{1,0:T(8,128)S(1)} %get-tuple-element.22.p0), channel_id=1, source_target_pairs={{0,1},{1,0},{2,3},{3,2},{4,5},{5,4},{6,7},{7,6},{8,9},{9,8},{10,11... | collective-permute-start | bytes 49160 | tf_op jit(solution)/shard_map/ppermute | solution.py:486
  64.1 4.7 %collective-permute-start.17 = (f32[32,128]{1,0:T(8,128)S(1)}, f32[32,128]{1,0:T(8,128)S(1)}, u32[]{:S(2)}, u32[]{:S(2)}) collective-permute-start(f32[32,128]{1,0:T(8,128)S(1)} %shard_map.107.p0), channel_id=1, source_target_pairs={{0,3},{1,2},{2,1},{3,0},{4,7},{5,6},{6,5},{7,4},{8,11},{9,10},{10,... | collective-permute-start | bytes 49160 | tf_op jit(solution)/shard_map/ppermute | solution.py:486
  65.1 3.7 %collective-permute-start.16 = (f32[32,128]{1,0:T(8,128)S(1)}, f32[32,128]{1,0:T(8,128)S(1)}, u32[]{:S(2)}, u32[]{:S(2)}) collective-permute-start(f32[32,128]{1,0:T(8,128)S(1)} %shard_map.107.p0), channel_id=1, source_target_pairs={{0,2},{1,3},{2,0},{3,1},{4,6},{5,7},{6,4},{7,5},{8,10},{9,11},{10,... | collective-permute-start | bytes 49160 | tf_op jit(solution)/shard_map/ppermute | solution.py:486
  65.3 3.5 %collective-permute-start.15 = (f32[32,128]{1,0:T(8,128)S(1)}, f32[32,128]{1,0:T(8,128)S(1)}, u32[]{:S(2)}, u32[]{:S(2)}) collective-permute-start(f32[32,128]{1,0:T(8,128)S(1)} %shard_map.107.p0), channel_id=1, source_target_pairs={{0,1},{1,0},{2,3},{3,2},{4,5},{5,4},{6,7},{7,6},{8,9},{9,8},{10,11... | collective-permute-start | bytes 49160 | tf_op jit(solution)/shard_map/ppermute | solution.py:486
  66.0 2.7 %collective-permute-start.18 = (f32[3,256]{1,0:T(4,128)S(1)}, f32[3,256]{1,0:T(4,128)S(1)}, u32[]{:S(2)}, u32[]{:S(2)}) collective-permute-start(f32[3,256]{1,0:T(4,128)S(1)} %get-tuple-element.26), channel_id=1, source_target_pairs={{0,1},{1,2},{2,3},{3,4},{4,5},{5,6},{6,7},{7,8},{8,9},{9,10},{10,1... | collective-permute-start | bytes 9224 | tf_op jit(solution)/shard_map/ppermute | solution.py:498
  71.5 7.4 %collective-permute-start.21 = (f32[32,128]{1,0:T(8,128)S(1)}, f32[32,128]{1,0:T(8,128)S(1)}, u32[]{:S(2)}, u32[]{:S(2)}) collective-permute-start(f32[32,128]{1,0:T(8,128)S(1)} %shard_map.108.p0), channel_id=1, source_target_pairs={{0,3},{1,2},{2,1},{3,0},{4,7},{5,6},{6,5},{7,4},{8,11},{9,10},{10,... | collective-permute-start | bytes 49160 | tf_op jit(solution)/shard_map/ppermute | solution.py:486
  75.5 3.7 %collective-permute-start.20 = (f32[32,128]{1,0:T(8,128)S(1)}, f32[32,128]{1,0:T(8,128)S(1)}, u32[]{:S(2)}, u32[]{:S(2)}) collective-permute-start(f32[32,128]{1,0:T(8,128)S(1)} %shard_map.108.p0), channel_id=1, source_target_pairs={{0,2},{1,3},{2,0},{3,1},{4,6},{5,7},{6,4},{7,5},{8,10},{9,11},{10,... | collective-permute-start | bytes 49160 | tf_op jit(solution)/shard_map/ppermute | solution.py:486
  75.5 3.7 %collective-permute-start.19 = (f32[32,128]{1,0:T(8,128)S(1)}, f32[32,128]{1,0:T(8,128)S(1)}, u32[]{:S(2)}, u32[]{:S(2)}) collective-permute-start(f32[32,128]{1,0:T(8,128)S(1)} %shard_map.108.p0), channel_id=1, source_target_pairs={{0,1},{1,0},{2,3},{3,2},{4,5},{5,4},{6,7},{7,6},{8,9},{9,8},{10,11... | collective-permute-start | bytes 49160 | tf_op jit(solution)/shard_map/ppermute | solution.py:486
  75.7 20.3 %copy-start.5 = (f32[8,128]{1,0:T(8,128)S(1)}, f32[8,128]{1,0:T(8,128)}, u32[]{:S(2)}) copy-start(f32[8,128]{1,0:T(8,128)} %get-tuple-element.31.node_row) | copy-start | bytes 12292
  75.7 3.2 %collective-permute-start.22 = (f32[3,256]{1,0:T(4,128)S(1)}, f32[3,256]{1,0:T(4,128)S(1)}, u32[]{:S(2)}, u32[]{:S(2)}) collective-permute-start(f32[3,256]{1,0:T(4,128)S(1)} %get-tuple-element.27), channel_id=1, source_target_pairs={{1,0},{2,1},{3,2},{4,3},{5,4},{6,5},{7,6},{8,7},{9,8},{10,9},{11,1... | collective-permute-start | bytes 9224 | tf_op jit(solution)/shard_map/ppermute | solution.py:498
  82.0 5.2 %collective-permute-start.25 = (f32[32,128]{1,0:T(8,128)S(1)}, f32[32,128]{1,0:T(8,128)S(1)}, u32[]{:S(2)}, u32[]{:S(2)}) collective-permute-start(f32[32,128]{1,0:T(8,128)S(1)} %shard_map.109.p0), channel_id=1, source_target_pairs={{0,3},{1,2},{2,1},{3,0},{4,7},{5,6},{6,5},{7,4},{8,11},{9,10},{10,... | collective-permute-start | bytes 49160 | tf_op jit(solution)/shard_map/ppermute | solution.py:486
  85.7 3.7 %collective-permute-start.24 = (f32[32,128]{1,0:T(8,128)S(1)}, f32[32,128]{1,0:T(8,128)S(1)}, u32[]{:S(2)}, u32[]{:S(2)}) collective-permute-start(f32[32,128]{1,0:T(8,128)S(1)} %shard_map.109.p0), channel_id=1, source_target_pairs={{0,2},{1,3},{2,0},{3,1},{4,6},{5,7},{6,4},{7,5},{8,10},{9,11},{10,... | collective-permute-start | bytes 49160 | tf_op jit(solution)/shard_map/ppermute | solution.py:486
  85.7 3.7 %collective-permute-start.23 = (f32[32,128]{1,0:T(8,128)S(1)}, f32[32,128]{1,0:T(8,128)S(1)}, u32[]{:S(2)}, u32[]{:S(2)}) collective-permute-start(f32[32,128]{1,0:T(8,128)S(1)} %shard_map.109.p0), channel_id=1, source_target_pairs={{0,1},{1,0},{2,3},{3,2},{4,5},{5,4},{6,7},{7,6},{8,9},{9,8},{10,11... | collective-permute-start | bytes 49160 | tf_op jit(solution)/shard_map/ppermute | solution.py:486
  92.1 3.2 %collective-permute-start.28 = (f32[32,128]{1,0:T(8,128)S(1)}, f32[32,128]{1,0:T(8,128)S(1)}, u32[]{:S(2)}, u32[]{:S(2)}) collective-permute-start(f32[32,128]{1,0:T(8,128)S(1)} %shard_map.110.p0), channel_id=1, source_target_pairs={{0,3},{1,2},{2,1},{3,0},{4,7},{5,6},{6,5},{7,4},{8,11},{9,10},{10,... | collective-permute-start | bytes 49160 | tf_op jit(solution)/shard_map/ppermute | solution.py:486
  92.2 3.8 %collective-permute-start.27 = (f32[32,128]{1,0:T(8,128)S(1)}, f32[32,128]{1,0:T(8,128)S(1)}, u32[]{:S(2)}, u32[]{:S(2)}) collective-permute-start(f32[32,128]{1,0:T(8,128)S(1)} %shard_map.110.p0), channel_id=1, source_target_pairs={{0,2},{1,3},{2,0},{3,1},{4,6},{5,7},{6,4},{7,5},{8,10},{9,11},{10,... | collective-permute-start | bytes 49160 | tf_op jit(solution)/shard_map/ppermute | solution.py:486
  92.3 3.7 %collective-permute-start.26 = (f32[32,128]{1,0:T(8,128)S(1)}, f32[32,128]{1,0:T(8,128)S(1)}, u32[]{:S(2)}, u32[]{:S(2)}) collective-permute-start(f32[32,128]{1,0:T(8,128)S(1)} %shard_map.110.p0), channel_id=1, source_target_pairs={{0,1},{1,0},{2,3},{3,2},{4,5},{5,4},{6,7},{7,6},{8,9},{9,8},{10,11... | collective-permute-start | bytes 49160 | tf_op jit(solution)/shard_map/ppermute | solution.py:486
